TPU v7x, 8 devices: a whole 2x2x1 slice. The times are simulated.
8 devices in a mesh: dp: 1 (over z), cp: 8 (over y, x, core).
Axes of the slice: x: 2, y: 2, z: 1, core: 2. Of those that a mesh axis runs over, the one named last changes fastest.
Arguments:
- vis_feat: bfloat16 [8, 4096, 1152], P(('dp', 'cp'))
- text_emb: bfloat16 [4096, 3584], P(('dp', 'cp'))
- img_pos: int32 [8], P('dp')
- grad_y: bfloat16 [4096, 3584], P(('dp', 'cp'))
- pn_gain: bfloat16 [1152], replicated
- w_proj: bfloat16 [1152, 3584], replicated
- pre_gain: bfloat16 [3584], replicated
- w_query: bfloat16 [3584, 4096], replicated
- w_key: bfloat16 [3584, 2048], replicated
- w_value: bfloat16 [3584, 2048], replicated
- q_gain: bfloat16 [256], replicated
- k_gain: bfloat16 [256], replicated
- w_out: bfloat16 [4096, 3584], replicated
- post_gain: bfloat16 [3584], replicated
Outputs:
- output 1: bfloat16 [4096, 3584], P(('dp', 'cp'))
- output 2: bfloat16 [4096, 3584], P(('dp', 'cp'))
- output 3: bfloat16 [8, 4096, 1152], P(('dp', 'cp'))
- output 4: bfloat16 [1152], P('dp')
- output 5: bfloat16 [1152, 3584], P('dp')
- output 6: bfloat16 [3584], P('dp')
- output 7: bfloat16 [3584, 4096], P('dp')
- output 8: bfloat16 [3584, 2048], P('dp')
- output 9: bfloat16 [3584, 2048], P('dp')
- output 10: bfloat16 [256], P('dp')
- output 11: bfloat16 [256], P('dp')
- output 12: bfloat16 [4096, 3584], P('dp')
- output 13: bfloat16 [3584], P('dp')
All inputs are finite; a program needn't handle non-finite values.
Results may differ from a plain program's by a relative error of at most 0.02.
Values are sent between devices in bfloat16 or wider.
A program may use at most 1 GiB of HBM per device.

v0:
```python
import functools
import jax
import jax.numpy as jnp
from jax import lax
from jax.sharding import PartitionSpec as P

GRID = 64
POOL = 4
EPS = 1e-6
ROPE_BASE = 1000000.0
ROPE_SCALE = 8.0
NEG_BIG = -1e30


def rms_scale(values, gain_vec):
    wide_vals = values.astype(jnp.float32)
    mean_sq = jnp.mean(wide_vals * wide_vals, axis=-1, keepdims=True)
    return wide_vals * lax.rsqrt(mean_sq + EPS) * (1.0 + gain_vec)


def gain_norm(values, gain_vec):
    return rms_scale(values, gain_vec).astype(jnp.bfloat16)


def rope_tables(positions, head_dim):
    inv_freq = ROPE_BASE ** (-jnp.arange(0, head_dim, 2).astype(jnp.float32) / head_dim)
    rot_angle = (positions.astype(jnp.float32) / ROPE_SCALE)[:, None] * inv_freq[None, :]
    rot_angle = jnp.concatenate([rot_angle, rot_angle], axis=-1)
    return jnp.cos(rot_angle)[:, None, :], jnp.sin(rot_angle)[:, None, :]


def apply_rope(values, cos_t, sin_t):
    half_dim = values.shape[-1] // 2
    rotated = jnp.concatenate([-values[..., half_dim:], values[..., :half_dim]], axis=-1)
    return values * cos_t + rotated * sin_t


def qk_rotate(q_raw, k_raw, q_gain, k_gain, cos_t, sin_t):
    q_heads = apply_rope(rms_scale(q_raw, q_gain), cos_t, sin_t).astype(jnp.bfloat16)
    k_heads = apply_rope(rms_scale(k_raw, k_gain), cos_t, sin_t).astype(jnp.bfloat16)
    return q_heads, k_heads


def post_residual(merged, proj_out, gain_vec):
    return (merged.astype(jnp.float32) + rms_scale(proj_out, gain_vec)).astype(jnp.bfloat16)


def pool_patches(vis_loc):
    img_count = vis_loc.shape[0]
    dim_v = vis_loc.shape[2]
    side_len = GRID // POOL
    patch_grid = vis_loc.reshape(img_count, side_len, POOL, side_len, POOL, dim_v)
    pooled = jnp.sum(patch_grid, axis=(2, 4), dtype=jnp.float32) / (POOL * POOL)
    return pooled.astype(jnp.bfloat16).reshape(img_count * side_len * side_len, dim_v)


def unpool_grad(d_pooled, img_count):
    side_len = GRID // POOL
    dim_v = d_pooled.shape[-1]
    spread = (d_pooled.astype(jnp.float32) / (POOL * POOL)).reshape(img_count, side_len, 1, side_len, 1, dim_v)
    spread = jnp.broadcast_to(spread, (img_count, side_len, POOL, side_len, POOL, dim_v))
    return spread.astype(jnp.bfloat16).reshape(img_count, GRID * GRID, dim_v)


def merge_layout(img_pos, dev_rank, seq_loc, block_len):
    q_pos = dev_rank * seq_loc + jnp.arange(seq_loc)
    offset = q_pos[:, None] - img_pos[None, :]
    in_blk = (offset >= 0) & (offset < block_len)
    is_img = jnp.any(in_blk, axis=1)
    flat_row = jnp.sum(jnp.where(in_blk, jnp.arange(img_pos.shape[0])[None, :] * block_len + offset, 0), axis=1)
    blk_start = jnp.where(is_img, q_pos - jnp.sum(jnp.where(in_blk, offset, 0), axis=1), -block_len)
    return q_pos, is_img, flat_row, blk_start


def attn_forward(q_heads, k_all, v_all, visible):
    seq_loc = q_heads.shape[0]
    head_dim = q_heads.shape[-1]
    q_grp = q_heads.reshape(seq_loc, k_all.shape[1], -1, head_dim)
    scores = jnp.einsum('qkgd,skd->kgqs', q_grp, k_all, preferred_element_type=jnp.float32) * head_dim ** -0.5
    probs_hi = jax.nn.softmax(jnp.where(visible, scores, NEG_BIG), axis=-1)
    probs_lo = probs_hi.astype(jnp.bfloat16)
    attn_out = jnp.einsum('kgqs,skd->qkgd', probs_lo, v_all, preferred_element_type=jnp.float32)
    return attn_out.astype(jnp.bfloat16).reshape(seq_loc, -1), probs_hi, probs_lo


def attn_backward(d_attn, q_heads, k_all, v_all, probs_hi, probs_lo):
    seq_loc = q_heads.shape[0]
    head_dim = q_heads.shape[-1]
    q_grp = q_heads.reshape(seq_loc, k_all.shape[1], -1, head_dim)
    d_grp = d_attn.reshape(q_grp.shape)
    d_probs = jnp.einsum('qkgd,skd->kgqs', d_grp, v_all, preferred_element_type=jnp.float32)
    d_v_part = jnp.einsum('kgqs,qkgd->skd', probs_lo, d_grp, preferred_element_type=jnp.float32)
    d_scores = probs_hi * (d_probs - jnp.sum(d_probs * probs_hi, axis=-1, keepdims=True)) * head_dim ** -0.5
    d_scores = d_scores.astype(jnp.bfloat16)
    d_q = jnp.einsum('kgqs,skd->qkgd', d_scores, k_all, preferred_element_type=jnp.float32).astype(jnp.bfloat16).reshape(q_heads.shape)
    d_k_part = jnp.einsum('kgqs,qkgd->skd', d_scores, q_grp, preferred_element_type=jnp.float32)
    return d_q, d_k_part, d_v_part


def solution(mesh):
    group_size = mesh.shape['cp']
    seq_spec = P(('dp', 'cp'))
    part_spec = P('dp')
    rep_spec = P()

    def device_body(vis_loc, text_loc, img_pos, grad_y, pn_gain, w_proj, pre_gain, w_query, w_key, w_value, q_gain, k_gain, w_out, post_gain):
        dev_rank = lax.axis_index('cp')
        seq_loc = text_loc.shape[0]
        img_loc = vis_loc.shape[0]
        head_dim = q_gain.shape[0]
        block_len = (GRID // POOL) ** 2
        pooled = pool_patches(vis_loc)
        normed, norm_pull = jax.vjp(gain_norm, pooled, pn_gain.astype(jnp.float32))
        soft_loc = jnp.dot(normed, w_proj, preferred_element_type=jnp.float32).astype(jnp.bfloat16)
        soft_all = lax.all_gather(soft_loc, 'cp', tiled=True)
        q_pos, is_img, flat_row, blk_start = merge_layout(img_pos, dev_rank, seq_loc, block_len)
        img_mask = is_img[:, None]
        merged = jnp.where(img_mask, jnp.take(soft_all, flat_row, axis=0), text_loc)
        hidden, pre_pull = jax.vjp(gain_norm, merged, pre_gain.astype(jnp.float32))
        q_raw = jnp.dot(hidden, w_query, preferred_element_type=jnp.float32).astype(jnp.bfloat16).reshape(seq_loc, -1, head_dim)
        k_raw = jnp.dot(hidden, w_key, preferred_element_type=jnp.float32).astype(jnp.bfloat16).reshape(seq_loc, -1, head_dim)
        v_loc = jnp.dot(hidden, w_value, preferred_element_type=jnp.float32).astype(jnp.bfloat16).reshape(seq_loc, -1, head_dim)
        cos_t, sin_t = rope_tables(q_pos, head_dim)
        rotate_fn = functools.partial(qk_rotate, cos_t=cos_t, sin_t=sin_t)
        (q_heads, k_loc), qk_pull = jax.vjp(rotate_fn, q_raw, k_raw, q_gain.astype(jnp.float32), k_gain.astype(jnp.float32))
        k_all = lax.all_gather(k_loc, 'cp', tiled=True)
        v_all = lax.all_gather(v_loc, 'cp', tiled=True)
        key_pos = jnp.arange(seq_loc * group_size)
        visible = (key_pos[None, :] <= q_pos[:, None]) | ((key_pos[None, :] >= blk_start[:, None]) & (key_pos[None, :] < blk_start[:, None] + block_len))
        attn_out, probs_hi, probs_lo = attn_forward(q_heads, k_all, v_all, visible)
        proj_out = jnp.dot(attn_out, w_out, preferred_element_type=jnp.float32).astype(jnp.bfloat16)
        y_loc, post_pull = jax.vjp(post_residual, merged, proj_out, post_gain.astype(jnp.float32))
        d_resid, d_proj, g_post = post_pull(grad_y)
        g_out = jnp.einsum('sh,sd->hd', attn_out, d_proj, preferred_element_type=jnp.float32)
        d_attn = jnp.einsum('sd,hd->sh', d_proj, w_out, preferred_element_type=jnp.float32).astype(jnp.bfloat16)
        d_q, d_k_part, d_v_part = attn_backward(d_attn, q_heads, k_all, v_all, probs_hi, probs_lo)
        d_k_loc = lax.psum_scatter(d_k_part, 'cp', scatter_dimension=0, tiled=True).astype(jnp.bfloat16)
        d_v_loc = lax.psum_scatter(d_v_part, 'cp', scatter_dimension=0, tiled=True).astype(jnp.bfloat16)
        d_q_raw, d_k_raw, g_q_gain, g_k_gain = qk_pull((d_q, d_k_loc))
        d_q_flat = d_q_raw.reshape(seq_loc, -1)
        d_k_flat = d_k_raw.reshape(seq_loc, -1)
        d_v_flat = d_v_loc.reshape(seq_loc, -1)
        d_hidden = jnp.einsum('sh,dh->sd', d_q_flat, w_query, preferred_element_type=jnp.float32)
        d_hidden = d_hidden + jnp.einsum('sh,dh->sd', d_k_flat, w_key, preferred_element_type=jnp.float32)
        d_hidden = (d_hidden + jnp.einsum('sh,dh->sd', d_v_flat, w_value, preferred_element_type=jnp.float32)).astype(jnp.bfloat16)
        g_query = jnp.einsum('sd,sh->dh', hidden, d_q_flat, preferred_element_type=jnp.float32)
        g_key = jnp.einsum('sd,sh->dh', hidden, d_k_flat, preferred_element_type=jnp.float32)
        g_value = jnp.einsum('sd,sh->dh', hidden, d_v_flat, preferred_element_type=jnp.float32)
        d_merged_attn, g_pre = pre_pull(d_hidden)
        d_merged = (d_resid.astype(jnp.float32) + d_merged_attn.astype(jnp.float32)).astype(jnp.bfloat16)
        grad_text = jnp.where(img_mask, 0.0, d_merged).astype(jnp.bfloat16)
        d_soft_all = jnp.zeros_like(soft_all).at[flat_row].add(jnp.where(img_mask, d_merged, 0.0).astype(jnp.bfloat16))
        d_soft_loc = lax.psum_scatter(d_soft_all, 'cp', scatter_dimension=0, tiled=True)
        g_proj = jnp.einsum('nc,nd->cd', normed, d_soft_loc, preferred_element_type=jnp.float32)
        d_normed = jnp.einsum('nd,cd->nc', d_soft_loc, w_proj, preferred_element_type=jnp.float32).astype(jnp.bfloat16)
        d_pooled, g_pn = norm_pull(d_normed)
        grad_vis = unpool_grad(d_pooled, img_loc)
        weight_grads = lax.psum((g_pn, g_proj, g_pre, g_query, g_key, g_value, g_q_gain, g_k_gain, g_out, g_post), 'cp')
        return (y_loc, grad_text, grad_vis) + tuple(grad_part.astype(jnp.bfloat16) for grad_part in weight_grads)

    in_specs = (seq_spec, seq_spec, part_spec, seq_spec) + (rep_spec,) * 10
    out_specs = (seq_spec, seq_spec, seq_spec) + (part_spec,) * 10
    return jax.shard_map(device_body, mesh=mesh, in_specs=in_specs, out_specs=out_specs, check_vma=False)
```

profile of v0, /device:TPU:0, one launch (start us, length us, event | category | flops | bytes accessed | tf_op | source)
XLA Modules:
  0.0 3589.9 jit_solution(5123569243655212582)
XLA Ops:
  7.2 17.8 reshape.340
  25.0 11.6 reduce_sum.181
  38.1 7.1 convolution_convert_fusion.3
  46.5 1.9 fusion.73
  48.5 74.9 %all-gather.4.cloned.1.call-done = bf16[2048,3584]{1,0:T(8,128)(2,1)} async-done(((bf16[256,3584]{1,0:T(8,128)(2,1)}), bf16[2048,3584]{1,0:T(8,128)(2,1)}) %all-gather.4.cloned.1.call-update) | async-done | bytes 14680080 | tf_op jit(solution)/shard_map/all_gather | solution.py:115
  123.4 14.9 gather_fusion
  138.4 4.1 fusion.43
  142.5 12.8 fusion.56
  155.3 2.0 copy-done.2
  157.3 2.0 copy.223
  160.1 2.7 fusion.55
  163.5 1.9 fusion.54
  165.5 12.2 convolution_convert_fusion.5
  177.7 2.5 copy.214
  181.3 3.9 fusion.33
  185.2 23.8 fusion.48
  209.0 8.9 copy.215
  217.9 7.3 copy.224
  225.2 3.4 copy-done
  230.1 5.2 multiply_multiply_fusion
  235.3 4.1 slice_negate_fusion.1
  239.3 7.2 copy.184
  246.5 7.2 copy.183
  253.8 9.0 fusion.32
  262.7 52.0 %fusion.16 = f32[8,4096,512,2]{2,1,3,0:T(8,128)} fusion(bf16[512,8,2,256]{0,3,2,1:T(8,128)(2,1)} %fusion.32, bf16[4096,8,256]{2,0,1:T(8,128)(2,1)} %all-gather.8.cloned.1.call-done), kind=kOutput, calls=%fused_computation.23 | convolution fusion | flops 17179869184 | bytes 155189248 | tf_op jit(solution)/shard_map/qkgd,skd->kgqs/dot_general | solution.py:79
  314.8 129.1 %fusion.105 = (f32[8,2,512]{2,1,0:T(2,128)S(1)}, f32[8,2,512,4096]{2,3,1,0:T(8,128)}) fusion(f32[8,4096,512,2]{2,1,3,0:T(8,128)} %fusion.16, pred[512,4096]{0,1:T(8,128)(4,1)S(1)} %copy-done.23), kind=kOutput, calls=%fused_computation.184 | output fusion | flops 201330688 | bytes 270565376 | tf_op jit(solution)/shard_map/sub | solution.py:80
  443.9 48.8 %fusion.57 = bf16[8,256,2,512]{3,1,2,0:T(8,128)(2,1)} fusion(bf16[4096,8,256]{0,2,1:T(8,128)(2,1)} %all-gather.6.cloned.1.call-done, f32[8,2,512,4096]{2,3,1,0:T(8,128)} %get-tuple-element.57, f32[8,2,512]{2,1,0:T(2,128)S(1)} %get-tuple-element.56), kind=kOutput, calls=%fused_computation.111 | convolution fusion | flops 17249075200 | bytes 155222016 | tf_op jit(solution)/shard_map/kgqs,skd->qkgd/dot_general | solution.py:82
  492.7 22.8 fusion.41
  515.6 6.6 fusion.38
  522.2 25.2 convolution_convert_fusion
  547.5 6.4 copy.221
  553.9 52.2 %fusion.19 = f32[8,4096,512,2]{2,1,3,0:T(8,128)} fusion(bf16[512,8,2,256]{0,3,2,1:T(8,128)(2,1)} %bitcast.169, bf16[4096,8,256]{0,2,1:T(8,128)(2,1)} %all-gather.6.cloned.1.call-done), kind=kOutput, calls=%fused_computation.26 | convolution fusion | flops 17179869184 | bytes 155189248 | tf_op jit(solution)/shard_map/qkgd,skd->kgqs/dot_general | solution.py:91
  606.0 171.9 %fusion.22 = f32[4096,8,256]{2,0,1:T(8,128)} fusion(bf16[512,8,2,256]{0,3,2,1:T(8,128)(2,1)} %fusion.32, f32[8,4096,512,2]{2,1,3,0:T(8,128)} %fusion.19, f32[8,2,512,4096]{2,3,1,0:T(8,128)} %get-tuple-element.57, f32[8,2,512]{2,1,0:T(2,128)S(1)} %get-tuple-element.56), kind=kOutput, calls=%fused_computation.38 | convolution fusion | flops 17414762496 | bytes 306216960 | tf_op jit(solution)/shard_map/kgqs,qkgd->skd/dot_general | solution.py:96
  778.0 55.6 %fusion.23 = f32[4096,8,256]{0,2,1:T(8,128)} fusion(bf16[512,8,2,256]{0,3,2,1:T(8,128)(2,1)} %bitcast.170, f32[8,2,512,4096]{2,3,1,0:T(8,128)} %get-tuple-element.57, f32[8,2,512]{2,1,0:T(2,128)S(1)} %get-tuple-element.56), kind=kOutput, calls=%fused_computation.39 | convolution fusion | flops 17246978048 | bytes 171999232 | tf_op jit(solution)/shard_map/kgqs,qkgd->skd/dot_general | solution.py:92
  833.7 167.1 %convert_convert_fusion = f32[8,256,2,512]{3,1,2,0:T(8,128)} fusion(f32[8,4096,512,2]{2,1,3,0:T(8,128)} %fusion.19, bf16[4096,8,256]{2,0,1:T(8,128)(2,1)} %all-gather.8.cloned.1.call-done, f32[8,2,512,4096]{2,3,1,0:T(8,128)} %get-tuple-element.57, f32[8,2,512]{2,1,0:T(2,128)S(1)} %get-tuple-element.56), kind=kOutput, calls=%fused_computation.102 | convolution fusion | flops 17418956800 | bytes 293634048 | tf_op jit(solution)/shard_map/kgqs,skd->qkgd/dot_general | solution.py:95
  1000.8 10.3 copy.192
  1011.1 8.2 broadcast_multiply_fusion
  1019.3 6.3 fusion.103
  1026.6 2.4 copy-done.5
  1029.0 8.4 multiply_reduce_fusion
  1037.7 7.2 fusion.30
  1044.9 4.2 copy.225
  1049.2 23.6 fusion.106
  1072.7 2.6 convert_multiply_fusion.12
  1077.5 2.1 multiply_reduce_fusion.3
  1079.6 1.5 fusion.51
  1081.1 2.4 copy.200
  1083.5 13.6 fusion.107
  1097.1 76.9 %reduce-scatter.6.cloned.1.call-done = f32[512,8,256]{0,2,1:T(8,128)} async-done(((f32[4096,8,256]{0,2,1:T(8,128)}), f32[512,8,256]{0,2,1:T(8,128)}) %reduce-scatter.6.cloned.1.call-update) | async-done | bytes 4194320 | tf_op jit(solution)/shard_map/reduce_scatter | solution.py:138
  1173.9 2.5 convert_element_type.295
  1176.4 30.4 fusion.36
  1206.8 8.1 broadcast_select_fusion
  1214.9 21.3 scatter_custom_fusion
  1236.2 25.8 fusion.96
  1262.0 28.1 fusion.89
  1290.0 16.4 fusion.94
  1306.5 13.7 fusion.92
  1320.2 2.1 broadcast_select_fusion.1
  1322.4 6.5 reduce-scatter.8.cloned.1.call-done
  1328.9 6.6 fusion.69
  1335.8 5.6 broadcast_in_dim.117
  1341.5 15.6 broadcast_in_dim.118
  1357.1 8.0 fusion.108
  1365.1 2217.5 %all-reduce.6 = (bf16[1152]{0:T(1024)(128)(2,1)}, bf16[1152,3584]{1,0:T(8,128)(2,1)}, bf16[3584]{0:T(1024)(128)(2,1)}, bf16[3584,4096]{1,0:T(8,128)(2,1)}, bf16[...) all-reduce(f32[1152]{0:T(1024)S(1)} %get-tuple-element.21, ...), channel_id=1, replica_groups=mesh['dp'=1,'cp'=8] {'cp'}, use_global_device_ids=true, to_apply=%region_22.23 | all-reduce | flops 48177792 | bytes 289066752 | tf_op jit(solution)/shard_map/psum | solution.py:158
  (185 shorter events, 10.7 us)
Async XLA Ops:
  7.2 116.3 %all-gather.4.cloned.1.call-start = ((), (), s32[]{:S(2)}) async-start(), calls=%async_computation.3 | async-start | bytes 16515072 | tf_op jit(solution)/shard_map/all_gather | solution.py:115
  25.0 11.8 copy-start.57
  36.8 8.4 copy-start.16
  36.9 8.4 copy-start.31
  37.0 8.3 copy-start.46
  37.0 8.3 copy-start.48
  38.1 7.5 copy-start.60
  38.1 10.3 copy-start.63
  38.1 10.4 copy-start.54
  45.3 217.5 %all-gather.8.cloned.1.call-start = ((), (), s32[]{:S(2)}) async-start(), calls=%async_computation.5 | async-start | bytes 18874368 | tf_op jit(solution)/shard_map/all_gather | solution.py:126
  46.4 134.3 %copy-start.44 = (pred[512]{0:T(512)(128)(4,1)}, pred[512]{0:T(512)(128)(4,1)S(1)}, u32[]{:S(2)}) copy-start(pred[512]{0:T(512)(128)(4,1)S(1)} %fusion.80) | copy-start | bytes 1540
  48.4 131.8 %copy-start.14 = (f32[512,256]{1,0:T(8,128)}, f32[512,256]{1,0:T(8,128)S(1)}, u32[]{:S(2)}) copy-start(f32[512,256]{1,0:T(8,128)S(1)} %get-tuple-element.55) | copy-start | bytes 1572868
  48.4 132.0 %copy-start.12 = (f32[512,256]{1,0:T(8,128)}, f32[512,256]{1,0:T(8,128)S(1)}, u32[]{:S(2)}) copy-start(f32[512,256]{1,0:T(8,128)S(1)} %get-tuple-element.54) | copy-start | bytes 1572868
  48.4 114.8 %copy-start.42 = (f32[256]{0:T(256)}, f32[256]{0:T(256)S(1)}, u32[]{:S(2)}) copy-start(f32[256]{0:T(256)S(1)} %convert_add_fusion.6) | copy-start | bytes 3076
  48.5 136.7 %copy-start.33 = (f32[3584]{0:T(1024)}, f32[3584]{0:T(1024)S(1)}, u32[]{:S(2)}) copy-start(f32[3584]{0:T(1024)S(1)} %convert_add_fusion.3) | copy-start | bytes 43012
  142.5 12.8 copy-start.6
  142.5 12.8 copy-start.38
  142.5 42.7 %copy-start.50 = (f32[512]{0:T(512)}, f32[512]{0:T(512)S(1)}, u32[]{:S(2)}) copy-start(f32[512]{0:T(512)S(1)} %fusion.81) | copy-start | bytes 6148
  160.0 3.3 copy-start.29
  160.0 3.2 copy-start.25
  160.0 3.5 copy-start.3
  165.4 278.5 %all-gather.6.cloned.1.call-start = ((), (), s32[]{:S(2)}) async-start(), calls=%async_computation.4 | async-start | bytes 18874368 | tf_op jit(solution)/shard_map/all_gather | solution.py:127
  180.2 892.5 %reduce-scatter.4.cloned.1.call-start = ((), (), s32[]{:S(2)}) async-start(), calls=%async_computation.6 | async-start | bytes 37748736 | tf_op jit(solution)/shard_map/reduce_scatter | solution.py:137
  180.7 73.1 %copy-start.40 = (f32[256]{0:T(256)}, f32[256]{0:T(256)S(1)}, u32[]{:S(2)}) copy-start(f32[256]{0:T(256)S(1)} %convert_add_fusion.5) | copy-start | bytes 3076
  225.2 3.4 copy-start
  229.9 5.4 copy-start.27
  230.0 5.2 copy-start.18
  262.7 52.0 %copy-start.23 = (pred[512,4096]{0,1:T(8,128)(4,1)S(1)}, pred[512,4096]{0,1:T(8,128)(4,1)}, u32[]{:S(2)}) copy-start(pred[512,4096]{0,1:T(8,128)(4,1)} %fusion.33) | copy-start | bytes 6291460
  492.7 22.8 copy-start.7
  492.7 22.9 copy-start.11
  492.7 22.9 copy-start.36
  515.5 6.7 copy-start.20
  515.5 6.7 copy-start.52
  522.2 25.3 copy-start.61
  778.0 396.0 %reduce-scatter.6.cloned.1.call-start = ((), (), s32[]{:S(2)}) async-start(), calls=%async_computation.7 | async-start | bytes 37748736 | tf_op jit(solution)/shard_map/reduce_scatter | solution.py:138
  833.7 495.2 %reduce-scatter.8.cloned.1.call-start = ((), (), s32[]{:S(2)}) async-start(), calls=%async_computation.8 | async-start | bytes 16515072 | tf_op jit(solution)/shard_map/reduce_scatter | solution.py:153
  1000.8 10.3 copy-start.15
  1011.1 14.5 copy-start.13
  1011.1 14.5 copy-start.19
  1019.3 7.3 copy-start.1
  1019.3 9.7 copy-start.5
  1019.3 9.7 copy-start.41
  1029.0 8.5 copy-start.28
  1072.7 3.1 copy-start.43
  1072.7 3.5 copy-start.4
  1072.7 4.7 copy-start.9
  1083.5 92.9 %copy-start.34 = (f32[3584]{0:T(1024)S(1)}, f32[3584]{0:T(1024)}, u32[]{:S(2)}) copy-start(f32[3584]{0:T(1024)} %copy-done.33) | copy-start | bytes 43012
  1083.5 92.9 %copy-start.51 = (f32[512]{0:T(512)S(1)}, f32[512]{0:T(512)}, u32[]{:S(2)}) copy-start(f32[512]{0:T(512)} %copy-done.50) | copy-start | bytes 6148
  1176.4 30.4 copy-start.39
  1176.4 30.4 copy-start.45
  1236.2 25.8 copy-start.37
  1236.2 25.8 copy-start.53
  1236.2 25.8 copy-start.62
  1290.0 16.4 copy-start.8
  1306.5 13.8 copy-start.10
  1320.2 8.6 copy-start.17
  1320.2 8.6 copy-start.32
  1320.2 8.6 copy-start.49
  1322.4 13.1 copy-start.47
  1341.5 15.6 copy-start.22
  1341.5 15.6 copy-start.24
  1357.1 8.0 copy-start.35
  1357.1 8.0 copy-start.58
  1357.1 8.0 copy-start.59
  (7 other events, 14.8 us)
Sparse Core Ops, SparseCore 0:
  45.4 77.9 all-gather.3
  165.5 84.0 all-gather.7
  252.0 87.3 all-gather.5
  778.1 196.2 reduce-scatter.3
  977.7 196.2 reduce-scatter.5
  1236.3 92.5 reduce-scatter.7
where the time goes:
time: 3600 us; the launch traced here: 3590 us
  blocking collectives  2220 us (62%)
  matrix products  818 us (23%)
  other arithmetic  255 us (7%)
  waiting for transfers between devices  158 us (4%)
  local copies, waits for them, and re-layouts  126 us (4%)
    psum x1, blocking collectives, device_body(): lax.psum((g_pn, g_proj, g_pre, g_query, g_key, g_value, g_q_gain, g_k_gai...  2220 us
    dot_general x1, matrix products, attn_backward(): jnp.einsum('kgqs,qkgd->skd', d_scores, q_grp, preferred_element_type=jnp....  172 us
    dot_general x1, matrix products, attn_backward(): jnp.einsum('kgqs,skd->qkgd', d_scores, k_all, preferred_element_type=jnp....  167 us
    sub x1, other arithmetic, attn_forward(): probs_hi = jax.nn.softmax(jnp.where(visible, scores, NEG_BIG), axis=-1)  129 us
    reduce_scatter x1, waiting for transfers between devices, device_body(): lax.psum_scatter(d_v_part, 'cp', scatter_dimension=0, tiled=True)  76.9 us
    all_gather x1, waiting for transfers between devices, device_body(): soft_all = lax.all_gather(soft_loc, 'cp', tiled=True)  74.9 us
  transfers between devices with their start and end apart: 6, of which 3 were waited for; matrix products, arithmetic and copies ran while one was open for 19% of the time, Pallas kernels for 0%

commit v1 on v0

v1 whole, which is shorter than its diff:
```python
import functools
import math
import jax
import jax.numpy as jnp
from jax import lax
from jax.experimental import pallas as pl
from jax.experimental.pallas import tpu as pltpu
from jax.sharding import PartitionSpec as P

GRID = 64
POOL = 4
SIDE = GRID // POOL
BLOCK = SIDE * SIDE
EPS = 1e-6
ROPE_BASE = 1000000.0
ROPE_SCALE = 8.0
NEG_BIG = -1e30
F32 = jnp.float32
BF16 = jnp.bfloat16
LOG2E = math.log2(math.e)


def rms_scale(values, gain_vec):
    wide_vals = values.astype(F32)
    mean_sq = jnp.mean(wide_vals * wide_vals, axis=-1, keepdims=True)
    return wide_vals * lax.rsqrt(mean_sq + EPS) * (1.0 + gain_vec)


def gain_norm(values, gain_vec):
    return rms_scale(values, gain_vec).astype(BF16)


def post_residual(merged, proj_out, gain_vec):
    return (merged.astype(F32) + rms_scale(proj_out, gain_vec)).astype(BF16)


def dot(a, b):
    return jnp.dot(a, b, preferred_element_type=F32)


def dot_nt(a, b):
    return lax.dot_general(a, b, (((1,), (1,)), ((), ())), preferred_element_type=F32)


def dot_tn(a, b):
    return lax.dot_general(a, b, (((0,), (0,)), ((), ())), preferred_element_type=F32)


def rope_tables(seq, head_dim):
    inv_freq = ROPE_BASE ** (-jnp.arange(0, head_dim, 2).astype(F32) / head_dim)
    rot_angle = (jnp.arange(seq).astype(F32) / ROPE_SCALE)[:, None] * inv_freq[None, :]
    return jnp.cos(rot_angle), jnp.sin(rot_angle)


def rope_fwd_kernel(hd, raw_ref, cos_ref, sin_ref, gq_ref, gk_ref, q_ref, k_ref, kt_ref):
    cos, sin = cos_ref[...], sin_ref[...]
    half = hd // 2
    n_q = q_ref.shape[1] // hd

    def one(col, gain):
        x = raw_ref[:, col:col + hd].astype(F32)
        r = lax.rsqrt(jnp.mean(x * x, axis=-1, keepdims=True) + EPS)
        x = x * r * (1.0 + gain)
        a, b = x[:, :half], x[:, half:]
        return (a * cos - b * sin), (b * cos + a * sin)

    for h in range(n_q):
        a, b = one(h * hd, gq_ref[...])
        q_ref[:, h * hd:h * hd + half] = a.astype(BF16)
        q_ref[:, h * hd + half:(h + 1) * hd] = b.astype(BF16)
    a, b = one(n_q * hd, gk_ref[...])
    k_ref[:, :half] = a.astype(BF16)
    k_ref[:, half:] = b.astype(BF16)
    kt_ref[:half, :] = a.T.astype(BF16)
    kt_ref[half:, :] = b.T.astype(BF16)


def rope_fwd(raw, cos, sin, gq, gk, hd, n_q):
    seq, width = raw.shape
    bm = 512
    row = lambda w: pl.BlockSpec((bm, w), lambda i: (i, 0))
    fix = pl.BlockSpec((1, hd), lambda i: (0, 0))
    return pl.pallas_call(
        functools.partial(rope_fwd_kernel, hd),
        grid=(seq // bm,),
        in_specs=[row(width), row(hd // 2), row(hd // 2), fix, fix],
        out_specs=[row(n_q * hd), row(hd), pl.BlockSpec((hd, bm), lambda i: (0, i))],
        out_shape=[jax.ShapeDtypeStruct((seq, n_q * hd), BF16), jax.ShapeDtypeStruct((seq, hd), BF16), jax.ShapeDtypeStruct((hd, seq), BF16)],
        cost_estimate=pl.CostEstimate(flops=20 * seq * width, bytes_accessed=4 * seq * width, transcendentals=0),
        name="rope_fwd",
    )(raw, cos, sin, gq, gk)


def rope_bwd_kernel(hd, raw_ref, dq_ref, dk_ref, dv_ref, cos_ref, sin_ref, gq_ref, gk_ref, out_ref, sq_ref, sk_ref):
    cos, sin = cos_ref[...], sin_ref[...]
    half = hd // 2
    n_q = dq_ref.shape[1] // hd

    @pl.when(pl.program_id(0) == 0)
    def _():
        sq_ref[...] = jnp.zeros_like(sq_ref)
        sk_ref[...] = jnp.zeros_like(sk_ref)

    def one(col, d_ref, dcol, gain, acc_ref):
        da = d_ref[:, dcol:dcol + half].astype(F32)
        db = d_ref[:, dcol + half:dcol + hd].astype(F32)
        d = jnp.concatenate([da * cos + db * sin, db * cos - da * sin], axis=1)
        x = raw_ref[:, col:col + hd].astype(F32)
        r = lax.rsqrt(jnp.mean(x * x, axis=-1, keepdims=True) + EPS)
        xr = x * r
        acc_ref[...] += jnp.sum(d * xr, axis=0, keepdims=True)
        gd = d * (1.0 + gain)
        dx = r * (gd - xr * jnp.mean(xr * gd, axis=-1, keepdims=True))
        out_ref[:, col:col + hd] = dx.astype(BF16)

    for h in range(n_q):
        one(h * hd, dq_ref, h * hd, gq_ref[...], sq_ref)
    one(n_q * hd, dk_ref, 0, gk_ref[...], sk_ref)
    out_ref[:, (n_q + 1) * hd:] = dv_ref[...]


def rope_bwd(raw, dq, dk, dv, cos, sin, gq, gk, hd, n_q):
    seq, width = raw.shape
    bm = 512
    row = lambda w: pl.BlockSpec((bm, w), lambda i: (i, 0))
    fix = pl.BlockSpec((1, hd), lambda i: (0, 0))
    return pl.pallas_call(
        functools.partial(rope_bwd_kernel, hd),
        grid=(seq // bm,),
        in_specs=[row(width), row(n_q * hd), row(hd), row(hd), row(hd // 2), row(hd // 2), fix, fix],
        out_specs=[row(width), fix, fix],
        out_shape=[jax.ShapeDtypeStruct((seq, width), BF16), jax.ShapeDtypeStruct((1, hd), F32), jax.ShapeDtypeStruct((1, hd), F32)],
        cost_estimate=pl.CostEstimate(flops=30 * seq * width, bytes_accessed=6 * seq * width, transcendentals=0),
        name="rope_bwd",
    )(raw, dq, dk, dv, cos, sin, gq, gk)


BQ = 256
KB = 512


def stack_heads(blk, hd):
    return jnp.concatenate([blk[:, h * hd:(h + 1) * hd] for h in range(blk.shape[1] // hd)], axis=0)


def fold_lanes(x, op):
    out = x[:, :128]
    for c in range(1, x.shape[1] // 128):
        out = op(out, x[:, c * 128:(c + 1) * 128])
    return out


def attn_fwd_kernel(hd, lim_ref, q_ref, kt_ref, v_ref, o_ref, o32_ref, lse_ref, s_ref):
    qb = pl.program_id(0)
    seq = kt_ref.shape[1]
    coef = hd ** -0.5 * LOG2E
    n_q = q_ref.shape[1] // hd
    rows = n_q * BQ
    q2 = stack_heads(q_ref[...], hd)
    lim = lim_ref[...]
    lim2 = jnp.concatenate([lim] * n_q, axis=0)
    n_full = (qb * BQ) // KB
    n_all = jnp.minimum((qb * BQ + BQ + BLOCK + KB - 1) // KB, seq // KB)

    def score(kb):
        cols = pl.ds(pl.multiple_of(kb * KB, KB), KB)
        return dot(q2, kt_ref[:, cols]), cols

    def full_body(kb, m):
        s, cols = score(kb)
        s_ref[:, cols] = s
        return jnp.maximum(m, fold_lanes(s, jnp.maximum))

    def mask_body(kb, m):
        s, cols = score(kb)
        key = kb * KB + lax.broadcasted_iota(jnp.int32, s.shape, 1)
        s = jnp.where(key <= lim2, s, NEG_BIG)
        s_ref[:, cols] = s
        return jnp.maximum(m, fold_lanes(s, jnp.maximum))

    m = lax.fori_loop(0, n_full, full_body, jnp.full((rows, 128), NEG_BIG, F32))
    m = lax.fori_loop(n_full, n_all, mask_body, m)
    m = jnp.max(m, axis=1, keepdims=True)

    def exp_body(kb, l):
        cols = pl.ds(pl.multiple_of(kb * KB, KB), KB)
        e = jnp.exp2((s_ref[:, cols] - m) * coef)
        s_ref[:, cols] = e
        return l + fold_lanes(e, jnp.add)

    l = lax.fori_loop(0, n_all, exp_body, jnp.zeros((rows, 128), F32))
    l = jnp.sum(l, axis=1, keepdims=True)
    inv = 1.0 / l

    def pv_body(kb, acc):
        cols = pl.ds(pl.multiple_of(kb * KB, KB), KB)
        p = (s_ref[:, cols] * inv).astype(BF16)
        return acc + dot(p, v_ref[cols, :])

    acc = lax.fori_loop(0, n_all, pv_body, jnp.zeros((rows, hd), F32))
    for h in range(n_q):
        part = acc[h * BQ:(h + 1) * BQ]
        o32_ref[:, h * hd:(h + 1) * hd] = part
        o_ref[:, h * hd:(h + 1) * hd] = part.astype(BF16)
    lse = jnp.broadcast_to(m * coef + jnp.log2(l), (rows, 128))
    lse_ref[0] = lse.T[:8, :]


def attn_fwd(lim, q, kt, raw, hd):
    seq, width = q.shape
    n_q = width // hd
    v_col = raw.shape[1] // hd - 1
    row = lambda w: pl.BlockSpec((BQ, w), lambda i: (i, 0))
    return pl.pallas_call(
        functools.partial(attn_fwd_kernel, hd),
        grid=(seq // BQ,),
        in_specs=[row(1), row(width), pl.BlockSpec((hd, seq), lambda i: (0, 0)), pl.BlockSpec((seq, hd), lambda i: (0, v_col))],
        out_specs=[row(width), row(width), pl.BlockSpec((1, 8, n_q * BQ), lambda i: (i, 0, 0))],
        out_shape=[jax.ShapeDtypeStruct((seq, width), BF16), jax.ShapeDtypeStruct((seq, width), F32), jax.ShapeDtypeStruct((seq // BQ, 8, n_q * BQ), F32)],
        scratch_shapes=[pltpu.VMEM((n_q * BQ, seq), F32)],
        cost_estimate=pl.CostEstimate(flops=int(2.2 * seq * seq * width), bytes_accessed=8 * seq * width, transcendentals=seq * seq),
        compiler_params=pltpu.CompilerParams(vmem_limit_bytes=40 * 1024 * 1024),
        name="attn_fwd",
    )(lim, q, kt, raw)


def attn_bwd_kernel(hd, lim_ref, q_ref, k_ref, kt_ref, v_ref, do_ref, o32_ref, lse_ref, dq_ref, dk_ref, dv_ref, dk_acc, dv_acc):
    qb = pl.program_id(0)
    seq = kt_ref.shape[1]
    scale = hd ** -0.5
    coef = scale * LOG2E
    n_q = q_ref.shape[1] // hd
    rows = n_q * BQ

    @pl.when(qb == 0)
    def _():
        dk_acc[...] = jnp.zeros_like(dk_acc)
        dv_acc[...] = jnp.zeros_like(dv_acc)

    q2 = stack_heads(q_ref[...], hd)
    do2 = stack_heads(do_ref[...], hd)
    o2 = stack_heads(o32_ref[...], hd)
    qt = q2.T
    dot_ = do2.T
    delta = jnp.sum(fold_lanes(do2.astype(F32) * o2, jnp.add).T, axis=0, keepdims=True)
    lse = lse_ref[0][0:1, :]
    lim = lim_ref[0]
    lim2 = jnp.concatenate([lim] * n_q, axis=1)
    n_full = (qb * BQ) // KB
    n_all = jnp.minimum((qb * BQ + BQ + BLOCK + KB - 1) // KB, seq // KB)

    def body(masked, kb, dqt):
        cols = pl.ds(pl.multiple_of(kb * KB, KB), KB)
        st = dot(k_ref[cols, :], qt)
        pt = jnp.exp2(st * coef - lse)
        if masked:
            key = kb * KB + lax.broadcasted_iota(jnp.int32, st.shape, 0)
            pt = jnp.where(key <= lim2, pt, 0.0)
        dpt = dot(v_ref[cols, :], dot_)
        dst = (pt * (dpt - delta) * scale).astype(BF16)
        dv_acc[cols, :] += dot(pt.astype(BF16), do2)
        dk_acc[cols, :] += dot(dst, q2)
        return dqt + dot(kt_ref[:, cols], dst)

    dqt = lax.fori_loop(0, n_full, functools.partial(body, False), jnp.zeros((hd, rows), F32))
    dqt = lax.fori_loop(n_full, n_all, functools.partial(body, True), dqt)
    dq = dqt.T.astype(BF16)
    for h in range(n_q):
        dq_ref[:, h * hd:(h + 1) * hd] = dq[h * BQ:(h + 1) * BQ]

    @pl.when(qb == pl.num_programs(0) - 1)
    def _():
        dk_ref[...] = dk_acc[...].astype(BF16)
        dv_ref[...] = dv_acc[...].astype(BF16)


def attn_bwd(lim_row, q, k, kt, raw, d_o, o32, lse, hd):
    seq, width = q.shape
    n_q = width // hd
    v_col = raw.shape[1] // hd - 1
    row = lambda w: pl.BlockSpec((BQ, w), lambda i: (i, 0))
    whole = pl.BlockSpec((seq, hd), lambda i: (0, 0))
    return pl.pallas_call(
        functools.partial(attn_bwd_kernel, hd),
        grid=(seq // BQ,),
        in_specs=[pl.BlockSpec((1, 1, BQ), lambda i: (i, 0, 0)), row(width), whole, pl.BlockSpec((hd, seq), lambda i: (0, 0)),
                  pl.BlockSpec((seq, hd), lambda i: (0, v_col)), row(width), row(width), pl.BlockSpec((1, 8, n_q * BQ), lambda i: (i, 0, 0))],
        out_specs=[row(width), whole, whole],
        out_shape=[jax.ShapeDtypeStruct((seq, width), BF16), jax.ShapeDtypeStruct((seq, hd), BF16), jax.ShapeDtypeStruct((seq, hd), BF16)],
        scratch_shapes=[pltpu.VMEM((seq, hd), F32), pltpu.VMEM((seq, hd), F32)],
        cost_estimate=pl.CostEstimate(flops=int(5.5 * seq * seq * width), bytes_accessed=12 * seq * width, transcendentals=seq * seq),
        compiler_params=pltpu.CompilerParams(vmem_limit_bytes=48 * 1024 * 1024),
        name="attn_bwd",
    )(lim_row, q, k, kt, raw, d_o, o32, lse)


def solution(mesh):
    n_dev = mesh.shape['cp']
    seq_spec = P(('dp', 'cp'))
    part_spec = P('dp')
    rep_spec = P()

    def gather_rows(x):
        return lax.all_gather(x, 'cp', tiled=True)

    def to_seq(x):
        return lax.all_to_all(x, 'cp', split_axis=0, concat_axis=1, tiled=True)

    def to_heads(x):
        return lax.all_to_all(x, 'cp', split_axis=1, concat_axis=0, tiled=True)

    def device_body(vis_loc, text_loc, img_pos, grad_y, pn_gain, w_proj, pre_gain, w_query, w_key, w_value, q_gain, k_gain, w_out, post_gain):
        rank = lax.axis_index('cp')
        seq_loc, d_model = text_loc.shape
        seq = seq_loc * n_dev
        img_loc, patches, dim_v = vis_loc.shape
        n_img = img_pos.shape[0]
        hd = q_gain.shape[0]
        wq_loc = w_query.shape[1] // n_dev
        wk_loc = w_key.shape[1] // n_dev
        n_q = wq_loc // hd
        pn32, pre32, post32 = pn_gain.astype(F32), pre_gain.astype(F32), post_gain.astype(F32)
        gq32 = q_gain.astype(F32)[None, :]
        gk32 = k_gain.astype(F32)[None, :]

        patch = jnp.arange(patches)
        patch_cell = (patch // (GRID * POOL)) * SIDE + (patch % GRID) // POOL
        pool_mat = (jnp.arange(BLOCK)[:, None] == patch_cell[None, :]).astype(BF16)
        pooled = jnp.einsum('cp,npd->ncd', pool_mat, vis_loc, preferred_element_type=F32) / (POOL * POOL)
        pooled = pooled.astype(BF16).reshape(img_loc * BLOCK, dim_v)
        normed, norm_pull = jax.vjp(gain_norm, pooled, pn32)
        normed_all = gather_rows(normed)

        q_pos = rank * seq_loc + jnp.arange(seq_loc)
        offset = q_pos[:, None] - img_pos[None, :]
        in_blk = (offset >= 0) & (offset < BLOCK)
        is_img = jnp.any(in_blk, axis=1)
        img_mask = is_img[:, None]
        flat_row = jnp.sum(jnp.where(in_blk, jnp.arange(n_img)[None, :] * BLOCK + offset, 0), axis=1)
        flat_row = jnp.where(is_img, flat_row, -1)
        select = (flat_row[:, None] == jnp.arange(n_img * BLOCK)[None, :]).astype(BF16)
        all_pos = jnp.arange(seq)
        all_off = all_pos[:, None] - img_pos[None, :]
        all_in = (all_off >= 0) & (all_off < BLOCK)
        limit = all_pos + jnp.sum(jnp.where(all_in, BLOCK - 1 - all_off, 0), axis=1)

        normed_rows = dot(select, normed_all).astype(BF16)
        soft_rows = dot(normed_rows, w_proj).astype(BF16)
        merged = jnp.where(img_mask, soft_rows, text_loc)
        hidden, pre_pull = jax.vjp(gain_norm, merged, pre32)
        hidden_all = gather_rows(hidden)

        w_qkv = jnp.concatenate([
            lax.dynamic_slice_in_dim(w_query, rank * wq_loc, wq_loc, 1),
            lax.dynamic_slice_in_dim(w_key, rank * wk_loc, wk_loc, 1),
            lax.dynamic_slice_in_dim(w_value, rank * wk_loc, wk_loc, 1)], axis=1)
        raw = dot(hidden_all, w_qkv).astype(BF16)
        cos_t, sin_t = rope_tables(seq, hd)
        q, k, kt = rope_fwd(raw, cos_t, sin_t, gq32, gk32, hd, n_q)
        o, o32, lse = attn_fwd(limit[:, None].astype(jnp.int32), q, kt, raw, hd)

        attn_seq = to_seq(o)
        proj_out = dot(attn_seq, w_out).astype(BF16)
        y_loc, post_pull = jax.vjp(post_residual, merged, proj_out, post32)
        d_resid, d_proj, g_post = post_pull(grad_y)
        d_attn = dot_nt(d_proj, w_out).astype(BF16)
        d_o = to_heads(d_attn)
        d_proj_all = gather_rows(d_proj)

        dq, dk, dv = attn_bwd(limit.astype(jnp.int32).reshape(seq // BQ, 1, BQ), q, k, kt, raw, d_o, o32, lse, hd)
        d_qkv, g_q_gain, g_k_gain = rope_bwd(raw, dq, dk, dv, cos_t, sin_t, gq32, gk32, hd, n_q)

        dq_seq = to_seq(d_qkv[:, :wq_loc])
        dk_seq = to_seq(d_qkv[:, wq_loc:wq_loc + wk_loc])
        dv_seq = to_seq(d_qkv[:, wq_loc + wk_loc:])
        d_hidden = dot_nt(dq_seq, w_query) + dot_nt(dk_seq, w_key)
        d_hidden = (d_hidden + dot_nt(dv_seq, w_value)).astype(BF16)
        d_merged_attn, g_pre = pre_pull(d_hidden)
        d_merged = (d_resid.astype(F32) + d_merged_attn.astype(F32)).astype(BF16)
        grad_text = jnp.where(img_mask, 0.0, d_merged).astype(BF16)

        d_soft_rows = jnp.where(img_mask, d_merged, 0.0).astype(BF16)
        d_normed_rows = dot_nt(d_soft_rows, w_proj).astype(BF16)
        d_normed_all = dot_tn(select, d_normed_rows).astype(BF16)
        d_normed = lax.psum_scatter(d_normed_all, 'cp', scatter_dimension=0, tiled=True)
        d_pooled, g_pn = norm_pull(d_normed)
        spread = (d_pooled.astype(F32) / (POOL * POOL)).astype(BF16).reshape(img_loc, SIDE, 1, SIDE, 1, dim_v)
        grad_vis = jnp.broadcast_to(spread, (img_loc, SIDE, POOL, SIDE, POOL, dim_v)).reshape(img_loc, patches, dim_v)

        g_proj_part = dot_tn(normed_rows, d_soft_rows)
        g_proj = gather_rows(lax.psum_scatter(g_proj_part, 'cp', scatter_dimension=0, tiled=True).astype(BF16))

        g_out = gather_rows(dot_tn(o, d_proj_all).astype(BF16))
        g_query = lax.all_gather(dot_tn(hidden_all, d_qkv[:, :wq_loc]).astype(BF16), 'cp', axis=1, tiled=True)
        g_key = lax.all_gather(dot_tn(hidden_all, d_qkv[:, wq_loc:wq_loc + wk_loc]).astype(BF16), 'cp', axis=1, tiled=True)
        g_value = lax.all_gather(dot_tn(hidden_all, d_qkv[:, wq_loc + wk_loc:]).astype(BF16), 'cp', axis=1, tiled=True)
        small = lax.psum((g_pn, g_pre, g_q_gain[0], g_k_gain[0], g_post), 'cp')
        g_pn, g_pre, g_q_gain, g_k_gain, g_post = [part.astype(BF16) for part in small]
        return (y_loc, grad_text, grad_vis, g_pn, g_proj, g_pre, g_query, g_key, g_value, g_q_gain, g_k_gain, g_out, g_post)

    in_specs = (seq_spec, seq_spec, part_spec, seq_spec) + (rep_spec,) * 10
    out_specs = (seq_spec, seq_spec, seq_spec) + (part_spec,) * 10
    return jax.shard_map(device_body, mesh=mesh, in_specs=in_specs, out_specs=out_specs, check_vma=False)
```

time: 3600 us -> 1670 us (0.46)
  blocking collectives: 2220 us -> 23.8 us
  waiting for transfers between devices: 158 us -> 948 us
  matrix products: 818 us -> 274 us
  other arithmetic: 255 us -> 41.3 us
  Pallas kernels: 0 us -> 191 us
    psum x1, blocking collectives: 2220 us -> 23.8 us  [device_body(): small = lax.psum((g_pn, g_pre, g_q_gain[0], g_k_gain[0], g_post), 'cp')]
    all_gather x3 -> x8, waiting for transfers between devices: 75 us -> 713 us  [the longest x5 454 us: gather_rows(): return lax.all_gather(x, 'cp', tiled=True)]
    dot_general x21 -> x16, matrix products: 818 us -> 274 us  [the longest x5 101 us: dot_nt(): lax.dot_general(a, b, (((1,), (1,)), ((), ())), preferred_element_type=F32)]
    pallas_call x0 -> x4, Pallas kernels: none -> 191 us  [the longest x1 87.4 us: attn_bwd(): pl.pallas_call(functools.partial(attn_bwd_kernel, hd), grid=(seq // BQ,),...]
    all_to_all x0 -> x5, waiting for transfers between devices: none -> 149 us  [the longest x4 100 us: to_seq(): return lax.all_to_all(x, 'cp', split_axis=0, concat_axis=1, tiled=True)]
    sub x1 -> x0, other arithmetic: 129 us -> none  [attn_forward(): probs_hi = jax.nn.softmax(jnp.where(visible, scores, NEG_BIG), axis=-1)]
    unnamed x133 -> x89, local copies, waits for them, and re-layouts: 25.8 us -> 87.9 us
    convert_element_type x4 -> x0, local copies, waits for them, and re-layouts: 39.4 us -> none  [the longest x1 17.8 us: pool_patches(): pooled = jnp.sum(patch_grid, axis=(2, 4), dtype=jnp.float32) / (POOL * POOL)]
  transfers between devices with their start and end apart: 6 -> 15, of which waited for: 3 -> 15; matrix products, arithmetic and copies ran while one was open for 19% -> 11% of each run, Pallas kernels for 0% -> 0%
where the time goes in v1:
time: 1670 us; the launch traced here: 1660 us
  waiting for transfers between devices  948 us (57%)
  matrix products  274 us (16%)
  Pallas kernels  191 us (11%)
  local copies, waits for them, and re-layouts  151 us (9%)
  other arithmetic  41.3 us (2%)
  blocking collectives  23.8 us (1%)
    all_gather x5, waiting for transfers between devices, gather_rows(): return lax.all_gather(x, 'cp', tiled=True)  454 us
    all_gather x1, waiting for transfers between devices, device_body(): lax.all_gather(dot_tn(hidden_all, d_qkv[:, :wq_loc]).astype(BF16), 'cp',...  146 us
    dot_general x5, matrix products, dot_nt(): lax.dot_general(a, b, (((1,), (1,)), ((), ())), preferred_element_type=F32)  101 us
    all_to_all x4, waiting for transfers between devices, to_seq(): return lax.all_to_all(x, 'cp', split_axis=0, concat_axis=1, tiled=True)  100 us
    dot_general x6, matrix products, dot_tn(): lax.dot_general(a, b, (((0,), (0,)), ((), ())), preferred_element_type=F32)  90.4 us
    unnamed x89, local copies, waits for them, and re-layouts  87.9 us
    pallas_call x1, Pallas kernels, attn_bwd(): pl.pallas_call(functools.partial(attn_bwd_kernel, hd), grid=(seq // BQ,),...  87.4 us
    all_gather x1, waiting for transfers between devices, device_body(): lax.all_gather(dot_tn(hidden_all, d_qkv[:, wq_loc + wk_loc:]).astype(BF16...  79.9 us
  transfers between devices with their start and end apart: 15, of which 15 were waited for; matrix products, arithmetic and copies ran while one was open for 11% of the time, Pallas kernels for 0%

profile of v1, /device:TPU:0, one launch (start us, length us, event | category | flops | bytes accessed | tf_op | source)
XLA Modules:
  0.0 1660.3 jit_solution(8366592821896073729)
XLA Ops:
  7.9 6.8 multiply_reduce_fusion
  17.1 35.6 %all-gather.9.cloned.1.call-done = bf16[2048,1152]{1,0:T(8,128)(2,1)} async-done(((bf16[256,1152]{1,0:T(8,128)(2,1)}), bf16[2048,1152]{1,0:T(8,128)(2,1)}) %all-gather.9.cloned.1.call-update) | async-done | bytes 4718608 | tf_op jit(solution)/shard_map/all_gather | solution.py:304
  52.7 5.5 fusion.24
  58.3 9.3 fusion.14
  69.5 3.2 fusion.6
  76.0 4.1 constant_dynamic-slice_fusion.1
  80.1 4.3 constant_dynamic-slice_fusion
  84.5 9.3 multiply_sine_fusion
  93.8 116.5 %all-gather.11.cloned.1.call-done = bf16[4096,3584]{1,0:T(8,128)(2,1)} async-done(((bf16[512,3584]{1,0:T(8,128)(2,1)}), bf16[4096,3584]{1,0:T(8,128)(2,1)}) %all-gather.11.cloned.1.call-update) | async-done | bytes 29360144 | tf_op jit(solution)/shard_map/all_gather | solution.py:304
  210.3 37.4 %convolution_convert_fusion.1.raw_ref.v_ref = bf16[4096,1024]{1,0:T(8,128)(2,1)} fusion(bf16[4096,3584]{1,0:T(8,128)(2,1)} %all-gather.11.cloned.1.call-done, bf16[3584,256]{1,0:T(8,128)(2,1)} %get-tuple-element.64, bf16[3584,256]{1,0:T(8,128)(2,1)} %get-tuple-element.63, bf16[3584,512]{1,0:T(8,128)(2,1)} %constant_dynamic-slice_fusion.1), kind=kOutput, calls=%fused_computation.23 | convolution fusion | flops 30090985472 | bytes 45088768 | tf_op jit(solution)/shard_map/dot_general | solution.py:38
  247.7 11.4 rope_fwd.1
  259.1 2.2 copy-done.3
  262.9 76.8 %attn_fwd.1 = (bf16[4096,512]{1,0:T(8,128)(2,1)S(1)}, f32[4096,512]{1,0:T(8,128)}, f32[16,8,512]{2,1,0:T(8,128)S(1)}) custom-call(s32[4096,1]{1,0:T(8,128)S(1)} %iota_add_fusion.lim_ref, bf16[4096,512]{1,0:T(8,128)(2,1)S(1)} %copy-done.3, bf16[256,4096]{1,0:T(8,128)(2,1)S(1)} %copy-done.4, bf16[4096,1024]{1,0:T(8,128)(2,1)} %convolution_convert_fusion.1.raw_ref.v_ref), custom_call_target="tpu_custom_call" | custom-call | flops 18897856512 | bytes 16777216 | tf_op jit(solution)/shard_map/attn_fwd/pallas_call | solution.py:214
  341.7 6.4 copy.35
  348.1 3.9 all-to-all-start
  352.1 49.0 %all-to-all-done = bf16[8,512,512]{1,2,0:T(8,128)(2,1)} async-done(((bf16[8,512,512]{1,2,0:T(8,128)(2,1)}), bf16[8,512,512]{1,2,0:T(8,128)(2,1)}, u32[]{:S(2)}, u32[]{:S(2)}) %all-to-all-start) | async-done | bytes 4194336 | tf_op jit(solution)/shard_map/all_to_all | solution.py:307
  401.0 23.6 %fusion.12 = (f32[512]{0:T(512)S(1)}, bf16[512,3584]{1,0:T(8,128)(2,1)}) fusion(bf16[512,4096]{0,1:T(8,128)(2,1)} %bitcast.6, bf16[4096,3584]{1,0:T(8,128)(2,1)} %param.26), kind=kOutput, calls=%fused_computation.30 | convolution fusion | flops 15039725568 | bytes 37226496 | tf_op jit(solution)/shard_map/dot_general | solution.py:38
  424.6 6.8 fusion.9
  431.4 5.7 fusion.10
  437.1 23.8 %convolution_convert_fusion.4 = bf16[512,4096]{1,0:T(8,128)(2,1)} fusion(bf16[512,3584]{1,0:T(8,128)(2,1)} %get-tuple-element.52, bf16[4096,3584]{1,0:T(8,128)(2,1)} %param.26), kind=kOutput, calls=%fused_computation.43 | convolution fusion | flops 15034482688 | bytes 37224448 | tf_op jit(solution)/shard_map/dot_general | solution.py:42
  460.9 4.6 copy.42
  465.5 3.4 all-to-all-start.1
  469.0 49.0 %all-to-all-done.1 = bf16[512,8,512]{2,0,1:T(8,128)(2,1)} async-done(((bf16[512,8,512]{2,0,1:T(8,128)(2,1)}), bf16[512,8,512]{2,0,1:T(8,128)(2,1)}, u32[]{:S(2)}, u32[]{:S(2)}) %all-to-all-start.1) | async-done | bytes 4194336 | tf_op jit(solution)/shard_map/all_to_all | solution.py:310
  517.9 87.4 %attn_bwd.1 = (bf16[4096,512]{1,0:T(8,128)(2,1)}, bf16[4096,256]{1,0:T(8,128)(2,1)S(1)}, bf16[4096,256]{1,0:T(8,128)(2,1)S(1)}) custom-call(s32[16,1,256]{2,1,0:T(1,128)S(1)} %add_add_fusion.3.lim_ref, bf16[4096,512]{1,0:T(8,128)(2,1)} %get-tuple-element.25.q_ref, bf16[4096,256]{1,0:T(8,128)(2,1)} %get-tuple-element.28.k_ref, ...), custom_call_target="tpu_custom_call" | custom-call | flops 47244640256 | bytes 25165824 | tf_op jit(solution)/shard_map/attn_bwd/pallas_call | solution.py:283
  608.0 14.9 rope_bwd.1
  623.0 3.8 fusion.75
  626.8 3.9 copy.38
  630.7 3.1 all-to-all-start.3
  633.8 4.5 slice.12
  638.4 6.4 copy.37
  644.8 15.5 all-to-all-done.3
  660.3 3.3 all-to-all-start.2
  663.6 2.4 copy.39
  666.0 13.5 fusion.77
  679.6 33.1 %all-to-all-done.2 = bf16[8,512,512]{1,2,0:T(8,128)(2,1)} async-done(((bf16[8,512,512]{1,2,0:T(8,128)(2,1)}), bf16[8,512,512]{1,2,0:T(8,128)(2,1)}, u32[]{:S(2)}, u32[]{:S(2)}) %all-to-all-start.2) | async-done | bytes 4194336 | tf_op jit(solution)/shard_map/all_to_all | solution.py:307
  712.6 2.3 all-to-all-start.4
  715.0 23.9 %fusion.76 = f32[512,3584]{1,0:T(8,128)} fusion(bf16[512,4096]{0,1:T(8,128)(2,1)} %bitcast.12, bf16[3584,4096]{1,0:T(8,128)(2,1)} %param.21), kind=kOutput, calls=%fused_computation.142 | convolution fusion | flops 15032385536 | bytes 40894464 | tf_op jit(solution)/shard_map/dot_general | solution.py:42
  738.9 2.6 all-to-all-done.4
  741.5 30.0 %fusion.7 = (f32[3584]{0:T(1024)S(1)}, f32[512]{0:T(512)S(1)}, bf16[512,3584]{1,0:T(8,128)(2,1)}) fusion(bf16[512,3584]{1,0:T(8,128)(2,1)} %copy-done.6, f32[512]{0:T(512)S(1)} %copy-done.21, f32[3584]{0:T(1024)S(1)} %copy-done.14, bf16[512,2048]{0,1:T(8,128)(2,1)S(1)} %bitcast.70, bf16[3584,2048]{1,0:T(8,128)(2,1)} %param.23, f32[512,3584]{1,0:T(8,128)} %fusion.76, ...), kind=kOutput, calls=%fused_computation.25 | convolution fusion | flops 7536373760 | bytes 38830080 | tf_op jit(solution)/shard_map/dot_general | solution.py:42
  771.5 7.5 broadcast_select_fusion.1
  780.8 8.6 fusion.37
  790.1 9.4 convolution_convert_fusion.9
  799.6 4.8 convolution_convert_fusion
  804.4 14.9 convolution_convert_fusion.8
  819.4 15.2 convolution_convert_fusion.7
  834.6 59.7 %reduce-scatter.5.cloned.1.call-done = f32[144,3584]{1,0:T(8,128)} async-done(((f32[1152,3584]{1,0:T(8,128)}), f32[144,3584]{1,0:T(8,128)}) %reduce-scatter.5.cloned.1.call-update) | async-done | bytes 2064400 | tf_op jit(solution)/shard_map/reduce_scatter | solution.py:391
  894.4 2.6 convert_element_type.188
  897.1 23.3 %convolution_convert_fusion.3 = bf16[3584,512]{1,0:T(8,128)(2,1)} fusion(bf16[4096,3584]{1,0:T(8,128)(2,1)} %all-gather.11.cloned.1.call-done, bf16[4096,1024]{1,0:T(8,128)(2,1)} %get-tuple-element.34), kind=kOutput, calls=%fused_computation.42 | convolution fusion | flops 15034220544 | bytes 37224448 | tf_op jit(solution)/shard_map/dot_general | solution.py:46
  920.5 113.0 %all-gather.21.cloned.1.call-done = bf16[4096,3584]{1,0:T(8,128)(2,1)} async-done(((bf16[512,3584]{1,0:T(8,128)(2,1)}), bf16[4096,3584]{1,0:T(8,128)(2,1)}) %all-gather.21.cloned.1.call-update) | async-done | bytes 29360144 | tf_op jit(solution)/shard_map/all_gather | solution.py:304
  1033.5 23.6 %convolution_convert_fusion.2 = bf16[512,3584]{1,0:T(8,128)(2,1)} fusion(bf16[4096,512]{1,0:T(8,128)(2,1)} %copy-done, bf16[4096,3584]{1,0:T(8,128)(2,1)} %all-gather.21.cloned.1.call-done), kind=kOutput, calls=%fused_computation.41 | convolution fusion | flops 15034220544 | bytes 37224448 | tf_op jit(solution)/shard_map/dot_general | solution.py:46
  1057.1 25.2 %reduce-scatter.3.cloned.1.call-done = bf16[256,1152]{1,0:T(8,128)(2,1)} async-done(((bf16[2048,1152]{1,0:T(8,128)(2,1)}), bf16[256,1152]{1,0:T(8,128)(2,1)}) %reduce-scatter.3.cloned.1.call-update) | async-done | bytes 589840 | tf_op jit(solution)/shard_map/reduce_scatter | solution.py:385
  1085.2 5.6 broadcast_in_dim.92
  1090.8 15.5 broadcast_in_dim.93
  1106.3 23.8 %all-reduce = (bf16[1152]{0:T(1024)(128)(2,1)}, bf16[3584]{0:T(1024)(128)(2,1)}, bf16[256]{0:T(256)(128)(2,1)}, bf16[256]{0:T(256)(128)(2,1)}, bf16[3584]{0:T(1024)(128)(2,1)}) all-reduce(f32[1152]{0:T(1024)S(1)} %get-tuple-element.41, f32[3584]{0:T(1024)S(1)} %get-tuple-element.39, ...), channel_id=1, replica_groups=mesh['dp'=1,'cp'=8] {'cp'}, use_global_device_ids=true, to_apply=%region_11.12 | all-reduce | flops 8832 | bytes 52992 | tf_op jit(solution)/shard_map/psum | solution.py:397
  1130.1 33.4 %all-gather.17.cloned.1.call-done = bf16[3584,2048]{1,0:T(8,128)(2,1)} async-done(((bf16[3584,256]{1,0:T(8,128)(2,1)}), bf16[3584,2048]{1,0:T(8,128)(2,1)}) %all-gather.17.cloned.1.call-update) | async-done | bytes 14680080 | tf_op jit(solution)/shard_map/all_gather | solution.py:395
  1163.5 79.9 %all-gather.19.cloned.1.call-done = bf16[3584,2048]{1,0:T(8,128)(2,1)} async-done(((bf16[3584,256]{1,0:T(8,128)(2,1)}), bf16[3584,2048]{1,0:T(8,128)(2,1)}) %all-gather.19.cloned.1.call-update) | async-done | bytes 14680080 | tf_op jit(solution)/shard_map/all_gather | solution.py:396
  1243.4 49.6 %all-gather.13.cloned.1.call-done = bf16[1152,3584]{1,0:T(8,128)(2,1)} async-done(((bf16[144,3584]{1,0:T(8,128)(2,1)}), bf16[1152,3584]{1,0:T(8,128)(2,1)}) %all-gather.13.cloned.1.call-update) | async-done | bytes 8257552 | tf_op jit(solution)/shard_map/all_gather | solution.py:304
  1293.0 145.7 %all-gather.15.cloned.1.call-done = bf16[3584,4096]{1,0:T(8,128)(2,1)} async-done(((bf16[3584,512]{1,0:T(8,128)(2,1)}), bf16[3584,4096]{1,0:T(8,128)(2,1)}) %all-gather.15.cloned.1.call-update) | async-done | bytes 29360144 | tf_op jit(solution)/shard_map/all_gather | solution.py:394
  1438.7 139.7 %all-gather.23.cloned.1.call-done = bf16[4096,3584]{1,0:T(8,128)(2,1)} async-done(((bf16[512,3584]{1,0:T(8,128)(2,1)}), bf16[4096,3584]{1,0:T(8,128)(2,1)}) %all-gather.23.cloned.1.call-update) | async-done | bytes 29360144 | tf_op jit(solution)/shard_map/all_gather | solution.py:304
  1578.4 7.2 copy.48
  1585.6 20.0 %copy.49 = bf16[3584,4096]{1,0:T(8,128)(2,1)} copy(bf16[3584,4096]{1,0:T(8,128)(2,1)} %all-gather.15.cloned.1.call-done) | data formatting | bytes 58720256
  1605.7 13.5 copy.50
  1619.1 13.5 copy.51
  1632.6 20.4 %copy.52 = bf16[4096,3584]{1,0:T(8,128)(2,1)} copy(bf16[4096,3584]{1,0:T(8,128)(2,1)} %all-gather.23.cloned.1.call-done) | data formatting | bytes 58720256
  (129 shorter events, 20.3 us)
Async XLA Ops:
  7.2 45.5 %all-gather.9.cloned.1.call-start = ((), (), s32[]{:S(2)}) async-start(), calls=%async_computation.7 | async-start | bytes 5308416 | tf_op jit(solution)/shard_map/all_gather | solution.py:304
  7.9 6.9 copy-start.17
  7.9 9.0 copy-start.30
  7.9 9.2 copy-start.24
  14.8 1.0 copy-start.9
  14.8 2.1 copy-start.31
  14.8 1.0 copy-start.22
  16.8 193.5 %all-gather.11.cloned.1.call-start = ((), (), s32[]{:S(2)}) async-start(), calls=%async_computation.8 | async-start | bytes 33030144 | tf_op jit(solution)/shard_map/all_gather | solution.py:304
  17.0 41.3 %copy-start.28 = (pred[512]{0:T(512)(128)(4,1)}, pred[512]{0:T(512)(128)(4,1)S(1)}, u32[]{:S(2)}) copy-start(pred[512]{0:T(512)(128)(4,1)S(1)} %fusion.64) | copy-start | bytes 1540
  17.1 41.2 %copy-start.33 = (s32[512]{0:T(512)}, s32[512]{0:T(512)S(1)}, u32[]{:S(2)}) copy-start(s32[512]{0:T(512)S(1)} %broadcast_select_fusion.4) | copy-start | bytes 6148
  17.1 51.0 %copy-start.13 = (f32[3584]{0:T(1024)}, f32[3584]{0:T(1024)S(1)}, u32[]{:S(2)}) copy-start(f32[3584]{0:T(1024)S(1)} %convert_add_fusion.3) | copy-start | bytes 43012
  52.7 5.5 copy-start.37
  58.3 9.3 copy-start.40
  67.6 0.6 copy-start.26
  67.6 1.9 copy-start.6
  68.2 1.3 copy-start.20
  69.5 3.2 copy-start.38
  69.5 3.7 copy-start.39
  74.0 6.1 copy-start.15
  80.1 4.3 copy-start.11
  259.1 2.2 copy-start.3
  261.3 1.6 copy-start.4
  339.7 2.0 copy-start
  348.1 3.9 copy-start.25
  348.1 52.9 %all-to-all-start = ((bf16[8,512,512]{1,2,0:T(8,128)(2,1)}), bf16[8,512,512]{1,2,0:T(8,128)(2,1)}, u32[]{:S(2)}, u32[]{:S(2)}) async-start(bf16[8,512,512]{1,2,0:T(8,128)(2,1)} %copy.35), calls=%async_computation | async-start | bytes 8388608 | tf_op jit(solution)/shard_map/all_to_all | solution.py:307
  401.0 23.6 %copy-start.5 = (bf16[512,3584]{1,0:T(8,128)(2,1)S(1)}, bf16[512,3584]{1,0:T(8,128)(2,1)}, u32[]{:S(2)}) copy-start(bf16[512,3584]{1,0:T(8,128)(2,1)} %param.17) | copy-start | bytes 11010052
  424.6 6.8 copy-start.7
  424.6 6.8 copy-start.8
  465.5 3.4 copy-start.16
  465.5 52.4 %all-to-all-start.1 = ((bf16[512,8,512]{2,0,1:T(8,128)(2,1)}), bf16[512,8,512]{2,0,1:T(8,128)(2,1)}, u32[]{:S(2)}, u32[]{:S(2)}) async-start(bf16[512,8,512]{2,0,1:T(8,128)(2,1)} %bitcast.64), calls=%async_computation.1 | async-start | bytes 8388608 | tf_op jit(solution)/shard_map/all_to_all | solution.py:310
  605.4 1.3 copy-start.1
  606.7 1.3 copy-start.2
  630.7 29.6 %all-to-all-start.3 = ((bf16[8,512,256]{1,2,0:T(8,128)(2,1)}), bf16[8,512,256]{1,2,0:T(8,128)(2,1)}, u32[]{:S(2)}, u32[]{:S(2)}) async-start(bf16[8,512,256]{1,2,0:T(8,128)(2,1)} %copy.38), calls=%async_computation.3 | async-start | bytes 4194304 | tf_op jit(solution)/shard_map/all_to_all | solution.py:307
  660.3 52.3 %all-to-all-start.2 = ((bf16[8,512,512]{1,2,0:T(8,128)(2,1)}), bf16[8,512,512]{1,2,0:T(8,128)(2,1)}, u32[]{:S(2)}, u32[]{:S(2)}) async-start(bf16[8,512,512]{1,2,0:T(8,128)(2,1)} %copy.37), calls=%async_computation.2 | async-start | bytes 8388608 | tf_op jit(solution)/shard_map/all_to_all | solution.py:307
  712.6 28.9 %all-to-all-start.4 = ((bf16[8,512,256]{1,2,0:T(8,128)(2,1)}), bf16[8,512,256]{1,2,0:T(8,128)(2,1)S(1)}, u32[]{:S(2)}, u32[]{:S(2)}) async-start(bf16[8,512,256]{1,2,0:T(8,128)(2,1)} %copy.39), calls=%async_computation.4 | async-start | bytes 4194304 | tf_op jit(solution)/shard_map/all_to_all | solution.py:307
  715.0 179.4 %reduce-scatter.5.cloned.1.call-start = ((), (), s32[]{:S(2)}) async-start(), calls=%async_computation.10 | async-start | bytes 18579456 | tf_op jit(solution)/shard_map/reduce_scatter | solution.py:391
  715.0 26.5 %copy-start.14 = (f32[3584]{0:T(1024)S(1)}, f32[3584]{0:T(1024)}, u32[]{:S(2)}) copy-start(f32[3584]{0:T(1024)} %copy-done.13) | copy-start | bytes 43012
  715.0 26.5 %copy-start.21 = (f32[512]{0:T(512)S(1)}, f32[512]{0:T(512)}, u32[]{:S(2)}) copy-start(f32[512]{0:T(512)} %copy-done.20) | copy-start | bytes 6148
  741.5 30.0 %copy-start.27 = (f32[512]{0:T(512)S(1)}, f32[512]{0:T(512)}, u32[]{:S(2)}) copy-start(f32[512]{0:T(512)} %copy-done.26) | copy-start | bytes 6148
  741.5 30.0 %copy-start.29 = (pred[512]{0:T(512)(128)(4,1)S(1)}, pred[512]{0:T(512)(128)(4,1)}, u32[]{:S(2)}) copy-start(pred[512]{0:T(512)(128)(4,1)} %copy-done.28) | copy-start | bytes 1540
  771.5 9.4 copy-start.41
  779.0 1.8 copy-start.12
  789.5 244.0 %all-gather.21.cloned.1.call-start = ((), (), s32[]{:S(2)}) async-start(), calls=%async_computation.15 | async-start | bytes 33030144 | tf_op jit(solution)/shard_map/all_gather | solution.py:304
  790.1 9.5 copy-start.34
  790.1 292.3 %reduce-scatter.3.cloned.1.call-start = ((), (), s32[]{:S(2)}) async-start(), calls=%async_computation.9 | async-start | bytes 5308416 | tf_op jit(solution)/shard_map/reduce_scatter | solution.py:385
  804.4 359.2 %all-gather.17.cloned.1.call-start = ((), (), s32[]{:S(2)}) async-start(), calls=%async_computation.13 | async-start | bytes 16515072 | tf_op jit(solution)/shard_map/all_gather | solution.py:395
  819.4 424.0 %all-gather.19.cloned.1.call-start = ((), (), s32[]{:S(2)}) async-start(), calls=%async_computation.14 | async-start | bytes 16515072 | tf_op jit(solution)/shard_map/all_gather | solution.py:396
  834.6 458.4 %all-gather.13.cloned.1.call-start = ((), (), s32[]{:S(2)}) async-start(), calls=%async_computation.11 | async-start | bytes 9289728 | tf_op jit(solution)/shard_map/all_gather | solution.py:304
  897.0 541.7 %all-gather.15.cloned.1.call-start = ((), (), s32[]{:S(2)}) async-start(), calls=%async_computation.12 | async-start | bytes 33030144 | tf_op jit(solution)/shard_map/all_gather | solution.py:394
  920.4 161.9 %copy-start.18 = (f32[1152]{0:T(1024)S(1)}, f32[1152]{0:T(1024)}, u32[]{:S(2)}) copy-start(f32[1152]{0:T(1024)} %copy-done.17) | copy-start | bytes 13828
  920.4 161.9 %copy-start.23 = (f32[256]{0:T(256)S(1)}, f32[256]{0:T(256)}, u32[]{:S(2)}) copy-start(f32[256]{0:T(256)} %copy-done.22) | copy-start | bytes 3076
  920.4 658.0 %all-gather.23.cloned.1.call-start = ((), (), s32[]{:S(2)}) async-start(), calls=%async_computation.16 | async-start | bytes 33030144 | tf_op jit(solution)/shard_map/all_gather | solution.py:304
  1057.1 25.3 %copy-start.10 = (f32[256,1152]{1,0:T(8,128)S(1)}, f32[256,1152]{1,0:T(8,128)}, u32[]{:S(2)}) copy-start(f32[256,1152]{1,0:T(8,128)} %copy-done.9) | copy-start | bytes 3538948
  1057.1 26.7 %copy-start.32 = (f32[256]{0:T(256)S(1)}, f32[256]{0:T(256)}, u32[]{:S(2)}) copy-start(f32[256]{0:T(256)} %copy-done.31) | copy-start | bytes 3076
  1090.8 15.5 copy-start.19
  1090.8 15.5 copy-start.35
  1090.8 15.5 copy-start.36
Sparse Core Ops, SparseCore 0:
  16.9 35.7 all-gather.8
  72.8 137.4 all-gather.10
  789.6 104.6 reduce-scatter.4
  896.0 137.4 all-gather.20
  1037.3 45.0 reduce-scatter.2
  1084.0 79.4 all-gather.16
  1165.3 78.0 all-gather.18
  1245.2 47.7 all-gather.12
  1295.4 143.2 all-gather.14
  1441.0 137.4 all-gather.22

commit v2 on v1

v2 whole, which is shorter than its diff:
```python
import functools
import math
import jax
import jax.numpy as jnp
from jax import lax
from jax.experimental import pallas as pl
from jax.experimental.pallas import tpu as pltpu
from jax.sharding import PartitionSpec as P

GRID = 64
POOL = 4
SIDE = GRID // POOL
BLOCK = SIDE * SIDE
EPS = 1e-6
ROPE_BASE = 1000000.0
ROPE_SCALE = 8.0
NEG_BIG = -1e30
F32 = jnp.float32
BF16 = jnp.bfloat16
LOG2E = math.log2(math.e)


def rms_scale(values, gain_vec):
    wide_vals = values.astype(F32)
    mean_sq = jnp.mean(wide_vals * wide_vals, axis=-1, keepdims=True)
    return wide_vals * lax.rsqrt(mean_sq + EPS) * (1.0 + gain_vec)


def gain_norm(values, gain_vec):
    return rms_scale(values, gain_vec).astype(BF16)


def post_residual(merged, proj_out, gain_vec):
    return (merged.astype(F32) + rms_scale(proj_out, gain_vec)).astype(BF16)


def dot(a, b):
    return jnp.dot(a, b, preferred_element_type=F32)


def dot_nt(a, b):
    return lax.dot_general(a, b, (((1,), (1,)), ((), ())), preferred_element_type=F32)


def dot_tn(a, b):
    return lax.dot_general(a, b, (((0,), (0,)), ((), ())), preferred_element_type=F32)


def rope_tables(seq, head_dim):
    inv_freq = ROPE_BASE ** (-jnp.arange(0, head_dim, 2).astype(F32) / head_dim)
    rot_angle = (jnp.arange(seq).astype(F32) / ROPE_SCALE)[:, None] * inv_freq[None, :]
    return jnp.cos(rot_angle), jnp.sin(rot_angle)


def rope_fwd_kernel(hd, raw_ref, cos_ref, sin_ref, gq_ref, gk_ref, q_ref, k_ref, kt_ref, vt_ref):
    cos, sin = cos_ref[...], sin_ref[...]
    half = hd // 2
    n_q = q_ref.shape[1] // hd

    def one(col, gain):
        x = raw_ref[:, col:col + hd].astype(F32)
        r = lax.rsqrt(jnp.mean(x * x, axis=-1, keepdims=True) + EPS)
        x = x * r * (1.0 + gain)
        a, b = x[:, :half], x[:, half:]
        return (a * cos - b * sin), (b * cos + a * sin)

    for h in range(n_q):
        a, b = one(h * hd, gq_ref[...])
        q_ref[:, h * hd:h * hd + half] = a.astype(BF16)
        q_ref[:, h * hd + half:(h + 1) * hd] = b.astype(BF16)
    a, b = one(n_q * hd, gk_ref[...])
    k_ref[:, :half] = a.astype(BF16)
    k_ref[:, half:] = b.astype(BF16)
    kt_ref[:half, :] = a.T.astype(BF16)
    kt_ref[half:, :] = b.T.astype(BF16)
    vt_ref[...] = raw_ref[:, (n_q + 1) * hd:].T


def rope_fwd(raw, cos, sin, gq, gk, hd, n_q):
    seq, width = raw.shape
    bm = 512
    row = lambda w: pl.BlockSpec((bm, w), lambda i: (i, 0))
    fix = pl.BlockSpec((1, hd), lambda i: (0, 0))
    return pl.pallas_call(
        functools.partial(rope_fwd_kernel, hd),
        grid=(seq // bm,),
        in_specs=[row(width), row(hd // 2), row(hd // 2), fix, fix],
        out_specs=[row(n_q * hd), row(hd), pl.BlockSpec((hd, bm), lambda i: (0, i)), pl.BlockSpec((hd, bm), lambda i: (0, i))],
        out_shape=[jax.ShapeDtypeStruct((seq, n_q * hd), BF16), jax.ShapeDtypeStruct((seq, hd), BF16)] + [jax.ShapeDtypeStruct((hd, seq), BF16)] * 2,
        cost_estimate=pl.CostEstimate(flops=20 * seq * width, bytes_accessed=4 * seq * width, transcendentals=0),
        name="rope_fwd",
    )(raw, cos, sin, gq, gk)


def rope_bwd_kernel(hd, raw_ref, dq_ref, dk_ref, dv_ref, cos_ref, sin_ref, gq_ref, gk_ref, out_ref, qt_ref, kt_ref, vt_ref, sq_ref, sk_ref):
    cos, sin = cos_ref[...], sin_ref[...]
    half = hd // 2
    n_q = dq_ref.shape[1] // hd

    @pl.when(pl.program_id(0) == 0)
    def _():
        sq_ref[...] = jnp.zeros_like(sq_ref)
        sk_ref[...] = jnp.zeros_like(sk_ref)

    def one(col, d_ref, dcol, gain, acc_ref, t_ref):
        da = d_ref[:, dcol:dcol + half].astype(F32)
        db = d_ref[:, dcol + half:dcol + hd].astype(F32)
        d = jnp.concatenate([da * cos + db * sin, db * cos - da * sin], axis=1)
        x = raw_ref[:, col:col + hd].astype(F32)
        r = lax.rsqrt(jnp.mean(x * x, axis=-1, keepdims=True) + EPS)
        xr = x * r
        acc_ref[...] += jnp.sum(d * xr, axis=0, keepdims=True)
        gd = d * (1.0 + gain)
        dx = r * (gd - xr * jnp.mean(xr * gd, axis=-1, keepdims=True))
        dx = dx.astype(BF16)
        out_ref[:, col:col + hd] = dx
        t_ref[0, dcol:dcol + hd, :] = dx.T

    for h in range(n_q):
        one(h * hd, dq_ref, h * hd, gq_ref[...], sq_ref, qt_ref)
    one(n_q * hd, dk_ref, 0, gk_ref[...], sk_ref, kt_ref)
    out_ref[:, (n_q + 1) * hd:] = dv_ref[...]
    vt_ref[0] = dv_ref[...].T


def rope_bwd(raw, dq, dk, dv, cos, sin, gq, gk, hd, n_q, bm):
    seq, width = raw.shape
    tall = lambda w: pl.BlockSpec((1, w, bm), lambda i: (i, 0, 0))
    tshape = lambda w: jax.ShapeDtypeStruct((seq // bm, w, bm), BF16)
    row = lambda w: pl.BlockSpec((bm, w), lambda i: (i, 0))
    fix = pl.BlockSpec((1, hd), lambda i: (0, 0))
    return pl.pallas_call(
        functools.partial(rope_bwd_kernel, hd),
        grid=(seq // bm,),
        in_specs=[row(width), row(n_q * hd), row(hd), row(hd), row(hd // 2), row(hd // 2), fix, fix],
        out_specs=[row(width), tall(n_q * hd), tall(hd), tall(hd), fix, fix],
        out_shape=[jax.ShapeDtypeStruct((seq, width), BF16), tshape(n_q * hd), tshape(hd), tshape(hd), jax.ShapeDtypeStruct((1, hd), F32), jax.ShapeDtypeStruct((1, hd), F32)],
        cost_estimate=pl.CostEstimate(flops=30 * seq * width, bytes_accessed=6 * seq * width, transcendentals=0),
        name="rope_bwd",
    )(raw, dq, dk, dv, cos, sin, gq, gk)


BQ = 256
KB = 512


def stack_heads(blk, hd):
    return jnp.concatenate([blk[:, h * hd:(h + 1) * hd] for h in range(blk.shape[1] // hd)], axis=0)


def fold_rows(x, op):
    out = x[:8]
    for c in range(1, x.shape[0] // 8):
        out = op(out, x[c * 8:(c + 1) * 8])
    return out


def wide(blk, hd):
    return jnp.concatenate([blk[h * hd:(h + 1) * hd] for h in range(blk.shape[0] // hd)], axis=1)


def attn_fwd_kernel(hd, nkb_ref, lim_ref, q_ref, k_ref, vt_ref, o_ref, o32_ref, lse_ref, s_ref):
    qb = pl.program_id(0)
    coef = hd ** -0.5 * LOG2E
    n_q = q_ref.shape[1] // hd
    rows = n_q * BQ
    qt = stack_heads(q_ref[...], hd).T
    lim2 = jnp.concatenate([lim_ref[0]] * n_q, axis=1)
    n_full = (qb * BQ) // KB
    n_all = nkb_ref[qb]

    def score(kb):
        keys = pl.ds(pl.multiple_of(kb * KB, KB), KB)
        return dot(k_ref[keys, :], qt), keys

    def full_body(kb, m):
        s, keys = score(kb)
        s_ref[keys, :] = s
        return jnp.maximum(m, fold_rows(s, jnp.maximum))

    def mask_body(kb, m):
        s, keys = score(kb)
        key = kb * KB + lax.broadcasted_iota(jnp.int32, s.shape, 0)
        s = jnp.where(key <= lim2, s, NEG_BIG)
        s_ref[keys, :] = s
        return jnp.maximum(m, fold_rows(s, jnp.maximum))

    m = lax.fori_loop(0, n_full, full_body, jnp.full((8, rows), NEG_BIG, F32))
    m = lax.fori_loop(n_full, n_all, mask_body, m)
    m = jnp.max(m, axis=0, keepdims=True)

    def exp_body(kb, l):
        keys = pl.ds(pl.multiple_of(kb * KB, KB), KB)
        e = jnp.exp2((s_ref[keys, :] - m) * coef)
        s_ref[keys, :] = e
        return l + fold_rows(e, jnp.add)

    l = lax.fori_loop(0, n_all, exp_body, jnp.zeros((8, rows), F32))
    l = jnp.sum(l, axis=0, keepdims=True)
    inv = 1.0 / l

    def pv_body(kb, acc):
        keys = pl.ds(pl.multiple_of(kb * KB, KB), KB)
        p = (s_ref[keys, :] * inv).astype(BF16)
        return acc + dot(vt_ref[:, keys], p)

    acc = lax.fori_loop(0, n_all, pv_body, jnp.zeros((hd, rows), F32))
    for h in range(n_q):
        part = acc[:, h * BQ:(h + 1) * BQ]
        o32_ref[0, h * hd:(h + 1) * hd, :] = part
        o_ref[0, h * hd:(h + 1) * hd, :] = part.astype(BF16)
    lse_ref[0] = jnp.broadcast_to(m * coef + jnp.log2(l), (8, rows))


def attn_fwd(nkb, lim, q, k, vt, hd, seq_loc):
    seq, width = q.shape
    n_q = width // hd
    per = seq_loc // BQ
    tall = pl.BlockSpec((1, width, BQ), lambda i, *_: (i // per, 0, i % per))
    return pl.pallas_call(
        functools.partial(attn_fwd_kernel, hd),
        grid_spec=pltpu.PrefetchScalarGridSpec(
            num_scalar_prefetch=1,
            grid=(seq // BQ,),
            in_specs=[pl.BlockSpec((1, 1, BQ), lambda i, *_: (i, 0, 0)), pl.BlockSpec((BQ, width), lambda i, *_: (i, 0)),
                      pl.BlockSpec((seq, hd), lambda i, *_: (0, 0)), pl.BlockSpec((hd, seq), lambda i, *_: (0, 0))],
            out_specs=[tall, tall, pl.BlockSpec((1, 8, n_q * BQ), lambda i, *_: (i, 0, 0))],
            scratch_shapes=[pltpu.VMEM((seq, n_q * BQ), F32)]),
        out_shape=[jax.ShapeDtypeStruct((seq // seq_loc, width, seq_loc), BF16), jax.ShapeDtypeStruct((seq // seq_loc, width, seq_loc), F32),
                   jax.ShapeDtypeStruct((seq // BQ, 8, n_q * BQ), F32)],
        cost_estimate=pl.CostEstimate(flops=int(2.2 * seq * seq * width), bytes_accessed=8 * seq * width, transcendentals=seq * seq),
        compiler_params=pltpu.CompilerParams(vmem_limit_bytes=40 * 1024 * 1024),
        name="attn_fwd",
    )(nkb, lim, q, k, vt)


def attn_bwd_kernel(hd, nkb_ref, lim_ref, q_ref, k_ref, kt_ref, v_ref, do_ref, o32_ref, lse_ref, dq_ref, dk_ref, dv_ref, dk_acc, dv_acc):
    qb = pl.program_id(0)
    scale = hd ** -0.5
    coef = scale * LOG2E
    n_q = q_ref.shape[1] // hd
    rows = n_q * BQ

    @pl.when(qb == 0)
    def _():
        dk_acc[...] = jnp.zeros_like(dk_acc)
        dv_acc[...] = jnp.zeros_like(dv_acc)

    q2 = stack_heads(q_ref[...], hd)
    qt = q2.T
    dot_ = wide(do_ref[0], hd)
    do2 = dot_.T
    delta = jnp.sum(dot_.astype(F32) * wide(o32_ref[0], hd), axis=0, keepdims=True)
    lse = lse_ref[0][0:1, :]
    lim2 = jnp.concatenate([lim_ref[0]] * n_q, axis=1)
    n_full = (qb * BQ) // KB
    n_all = nkb_ref[qb]

    def body(masked, kb, dqt):
        keys = pl.ds(pl.multiple_of(kb * KB, KB), KB)
        st = dot(k_ref[keys, :], qt)
        pt = jnp.exp2(st * coef - lse)
        if masked:
            key = kb * KB + lax.broadcasted_iota(jnp.int32, st.shape, 0)
            pt = jnp.where(key <= lim2, pt, 0.0)
        dpt = dot(v_ref[keys, :], dot_)
        dst = (pt * (dpt - delta) * scale).astype(BF16)
        dv_acc[keys, :] += dot(pt.astype(BF16), do2)
        dk_acc[keys, :] += dot(dst, q2)
        return dqt + dot(kt_ref[:, keys], dst)

    dqt = lax.fori_loop(0, n_full, functools.partial(body, False), jnp.zeros((hd, rows), F32))
    dqt = lax.fori_loop(n_full, n_all, functools.partial(body, True), dqt)
    dq = dqt.T.astype(BF16)
    for h in range(n_q):
        dq_ref[:, h * hd:(h + 1) * hd] = dq[h * BQ:(h + 1) * BQ]

    @pl.when(qb == pl.num_programs(0) - 1)
    def _():
        dk_ref[...] = dk_acc[...].astype(BF16)
        dv_ref[...] = dv_acc[...].astype(BF16)


def attn_bwd(nkb, lim, q, k, kt, raw, d_o, o32, lse, hd):
    seq, width = q.shape
    n_q = width // hd
    v_col = raw.shape[1] // hd - 1
    per = d_o.shape[2] // BQ
    row = lambda w: pl.BlockSpec((BQ, w), lambda i, *_: (i, 0))
    tall = pl.BlockSpec((1, width, BQ), lambda i, *_: (i // per, 0, i % per))
    whole = pl.BlockSpec((seq, hd), lambda i, *_: (0, 0))
    return pl.pallas_call(
        functools.partial(attn_bwd_kernel, hd),
        grid_spec=pltpu.PrefetchScalarGridSpec(
            num_scalar_prefetch=1,
            grid=(seq // BQ,),
            in_specs=[pl.BlockSpec((1, 1, BQ), lambda i, *_: (i, 0, 0)), row(width), whole, pl.BlockSpec((hd, seq), lambda i, *_: (0, 0)),
                      pl.BlockSpec((seq, hd), lambda i, *_: (0, v_col)), tall, tall, pl.BlockSpec((1, 8, n_q * BQ), lambda i, *_: (i, 0, 0))],
            out_specs=[row(width), whole, whole],
            scratch_shapes=[pltpu.VMEM((seq, hd), F32), pltpu.VMEM((seq, hd), F32)]),
        out_shape=[jax.ShapeDtypeStruct((seq, width), BF16), jax.ShapeDtypeStruct((seq, hd), BF16), jax.ShapeDtypeStruct((seq, hd), BF16)],
        cost_estimate=pl.CostEstimate(flops=int(5.5 * seq * seq * width), bytes_accessed=12 * seq * width, transcendentals=seq * seq),
        compiler_params=pltpu.CompilerParams(vmem_limit_bytes=48 * 1024 * 1024),
        name="attn_bwd",
    )(nkb, lim, q, k, kt, raw, d_o, o32, lse)


def copy_kernel(x_ref, o_ref):
    o_ref[...] = x_ref[...]


def copy_out(x, cols):
    rows = x.shape[0]
    bm = 128
    spec = pl.BlockSpec((bm, cols), lambda i: (i, 0))
    return pl.pallas_call(
        copy_kernel,
        grid=(rows // bm,),
        in_specs=[spec],
        out_specs=spec,
        out_shape=jax.ShapeDtypeStruct((rows, cols), x.dtype),
        cost_estimate=pl.CostEstimate(flops=rows * cols, bytes_accessed=4 * rows * cols, transcendentals=0),
        name="copy_out",
    )(x)


def solution(mesh):
    n_dev = mesh.shape['cp']
    seq_spec = P(('dp', 'cp'))
    part_spec = P('dp')
    rep_spec = P()

    def gather(x, axis=0):
        return lax.all_gather(x, 'cp', axis=axis, tiled=True)

    def exchange(x):
        return lax.all_to_all(x, 'cp', split_axis=0, concat_axis=0, tiled=True)

    def device_step(vis_loc, text_loc, img_pos, grad_y, pn_gain, w_proj, pre_gain, w_query, w_key, w_value, q_gain, k_gain, w_out, post_gain):
        rank = lax.axis_index('cp')
        seq_loc, d_model = text_loc.shape
        seq = seq_loc * n_dev
        img_loc, patches, dim_v = vis_loc.shape
        n_img = img_pos.shape[0]
        hd = q_gain.shape[0]
        wq_loc = w_query.shape[1] // n_dev
        wk_loc = w_key.shape[1] // n_dev
        n_q = wq_loc // hd
        pn32, pre32, post32 = pn_gain.astype(F32), pre_gain.astype(F32), post_gain.astype(F32)
        gq32 = q_gain.astype(F32)[None, :]
        gk32 = k_gain.astype(F32)[None, :]

        patch = jnp.arange(patches)
        patch_cell = (patch // (GRID * POOL)) * SIDE + (patch % GRID) // POOL
        pool_mat = (jnp.arange(BLOCK)[:, None] == patch_cell[None, :]).astype(BF16)
        pooled = jnp.einsum('cp,npd->ncd', pool_mat, vis_loc, preferred_element_type=F32) / (POOL * POOL)
        pooled = pooled.astype(BF16).reshape(img_loc * BLOCK, dim_v)
        normed, norm_pull = jax.vjp(gain_norm, pooled, pn32)
        normed_all = gather(normed)

        q_pos = rank * seq_loc + jnp.arange(seq_loc)
        offset = q_pos[:, None] - img_pos[None, :]
        in_blk = (offset >= 0) & (offset < BLOCK)
        is_img = jnp.any(in_blk, axis=1)
        img_mask = is_img[:, None]
        flat_row = jnp.sum(jnp.where(in_blk, jnp.arange(n_img)[None, :] * BLOCK + offset, 0), axis=1)
        flat_row = jnp.where(is_img, flat_row, -1)
        select = (flat_row[:, None] == jnp.arange(n_img * BLOCK)[None, :]).astype(BF16)
        all_pos = jnp.arange(seq)
        all_off = all_pos[:, None] - img_pos[None, :]
        all_in = (all_off >= 0) & (all_off < BLOCK)
        limit = (all_pos + jnp.sum(jnp.where(all_in, BLOCK - 1 - all_off, 0), axis=1)).astype(jnp.int32).reshape(seq // BQ, 1, BQ)
        n_kb = (jnp.max(limit, axis=(1, 2)) // KB + 1).astype(jnp.int32)
        all_flat = jnp.sum(jnp.where(all_in, jnp.arange(n_img)[None, :] * BLOCK + all_off + 1, 0), axis=1) - 1
        select_all = (all_flat[:, None] == jnp.arange(n_img * BLOCK)[None, :]).astype(BF16)

        normed_rows = dot(select, normed_all).astype(BF16)
        soft_rows = dot(normed_rows, w_proj).astype(BF16)
        merged = jnp.where(img_mask, soft_rows, text_loc)
        hidden, pre_pull = jax.vjp(gain_norm, merged, pre32)
        hidden_all = gather(hidden)

        w_qkv = jnp.concatenate([
            lax.dynamic_slice_in_dim(w_query, rank * wq_loc, wq_loc, 1),
            lax.dynamic_slice_in_dim(w_key, rank * wk_loc, wk_loc, 1),
            lax.dynamic_slice_in_dim(w_value, rank * wk_loc, wk_loc, 1)], axis=1)
        raw = dot(hidden_all, w_qkv).astype(BF16)
        cos_t, sin_t = rope_tables(seq, hd)
        q, k, kt, vt = rope_fwd(raw, cos_t, sin_t, gq32, gk32, hd, n_q)
        o_t, o32_t, lse = attn_fwd(n_kb, limit, q, k, vt, hd, seq_loc)

        attn_t = exchange(o_t).reshape(n_dev * wq_loc, seq_loc)
        proj_out = dot_tn(attn_t, w_out).astype(BF16)
        y_loc, post_pull = jax.vjp(post_residual, merged, proj_out, post32)
        d_resid, d_proj, g_post = post_pull(grad_y)
        d_attn_t = dot_nt(w_out, d_proj).astype(BF16).reshape(n_dev, wq_loc, seq_loc)
        d_o = exchange(d_attn_t)
        d_proj_all = gather(d_proj)

        dq, dk, dv = attn_bwd(n_kb, limit, q, k, kt, raw, d_o, o32_t, lse, hd)
        d_qkv, dq_t, dk_t, dv_t, g_q_gain, g_k_gain = rope_bwd(raw, dq, dk, dv, cos_t, sin_t, gq32, gk32, hd, n_q, seq_loc)

        dk_seq = exchange(dk_t).reshape(-1, seq_loc)
        dv_seq = exchange(dv_t).reshape(-1, seq_loc)
        dq_seq = exchange(dq_t).reshape(-1, seq_loc)
        d_hidden = sum(lax.dot_general(d, w, (((0,), (1,)), ((), ())), preferred_element_type=F32)
                       for d, w in ((dk_seq, w_key), (dv_seq, w_value), (dq_seq, w_query))).astype(BF16)
        d_merged_attn, g_pre = pre_pull(d_hidden)
        d_merged = (d_resid.astype(F32) + d_merged_attn.astype(F32)).astype(BF16)
        grad_text = jnp.where(img_mask, 0.0, d_merged).astype(BF16)

        d_soft_rows = jnp.where(img_mask, d_merged, 0.0).astype(BF16)
        d_normed_rows = dot_nt(d_soft_rows, w_proj).astype(BF16)
        d_normed_all = dot_tn(select, d_normed_rows).astype(BF16)
        d_normed = lax.psum_scatter(d_normed_all, 'cp', scatter_dimension=0, tiled=True)
        d_pooled, g_pn = norm_pull(d_normed)
        spread = (d_pooled.astype(F32) / (POOL * POOL)).astype(BF16).reshape(img_loc, SIDE, 1, SIDE, 1, dim_v)
        grad_vis = jnp.broadcast_to(spread, (img_loc, SIDE, POOL, SIDE, POOL, dim_v)).reshape(img_loc, patches, dim_v)

        pad_cols = -(-d_model // (n_dev * 128)) * n_dev * 128
        d_soft_blk = jnp.pad(d_soft_rows, ((0, 0), (0, pad_cols - d_model))).T.reshape(n_dev, pad_cols // n_dev, seq_loc)
        d_soft_t = exchange(d_soft_blk)
        normed_pos = dot(select_all, normed_all).astype(BF16).reshape(n_dev, seq_loc, dim_v)
        g_proj = sum(lax.dot_general(normed_pos[i], d_soft_t[i], (((0,), (1,)), ((), ())), preferred_element_type=F32) for i in range(n_dev))
        g_proj = gather(g_proj.astype(BF16), 1)

        g_query = gather(dot_tn(hidden_all, d_qkv[:, :wq_loc]).astype(BF16), 1)
        o_rows = o_t.transpose(0, 2, 1).reshape(seq, wq_loc)
        g_out = gather(dot_tn(o_rows, d_proj_all).astype(BF16))
        g_value = gather(dot_tn(hidden_all, d_qkv[:, wq_loc + wk_loc:]).astype(BF16), 1)
        g_key = gather(dot_tn(hidden_all, d_qkv[:, wq_loc:wq_loc + wk_loc]).astype(BF16), 1)
        g_proj, g_query, g_out, g_value, g_key = [copy_out(g, c) for g, c in (
            (g_proj, d_model), (g_query, n_dev * wq_loc), (g_out, d_model), (g_value, n_dev * wk_loc), (g_key, n_dev * wk_loc))]
        small = lax.psum((g_pn, g_pre, g_q_gain[0], g_k_gain[0], g_post), 'cp')
        g_pn, g_pre, g_q_gain, g_k_gain, g_post = [part.astype(BF16) for part in small]
        return (y_loc, grad_text, grad_vis, g_pn, g_proj, g_pre, g_query, g_key, g_value, g_q_gain, g_k_gain, g_out, g_post)

    in_specs = (seq_spec, seq_spec, part_spec, seq_spec) + (rep_spec,) * 10
    out_specs = (seq_spec, seq_spec, seq_spec) + (part_spec,) * 10
    return jax.shard_map(device_step, mesh=mesh, in_specs=in_specs, out_specs=out_specs, check_vma=False)
```

time: 1670 us -> 1450 us (0.87)
  waiting for transfers between devices: 948 us -> 557 us
  blocking collectives: 23.8 us -> 131 us
  Pallas kernels: 191 us -> 297 us
  local copies, waits for them, and re-layouts: 151 us -> 66.5 us
  matrix products: 274 us -> 316 us
    all_gather x8, waiting for transfers between devices: 713 us -> 431 us  [gather(): return lax.all_gather(x, 'cp', axis=axis, tiled=True)]
    all_to_all x0 -> x2, blocking collectives: none -> 108 us  [exchange(): return lax.all_to_all(x, 'cp', split_axis=0, concat_axis=0, tiled=True)]
    pallas_call x2 -> x7, Pallas kernels: 164 us -> 267 us  [the longest x5 113 us: copy_out(): pl.pallas_call(copy_kernel, grid=(rows // bm,), in_specs=[spec], out_spec...]
    reduce_scatter x2 -> x1, waiting for transfers between devices: 84.9 us -> 0.01 us  [device_step(): lax.psum_scatter(d_normed_all, 'cp', scatter_dimension=0, tiled=True)]
    dot_general x1 -> x12, matrix products: 6.83 us -> 91.4 us  [the longest x3 67.1 us: device_step(): lax.dot_general(d, w, (((0,), (1,)), ((), ())), preferred_element_type=F32)]
    unnamed x89 -> x80, local copies, waits for them, and re-layouts: 87.9 us -> 11.7 us
    dot_general x5 -> x2, matrix products: 101 us -> 34.3 us  [dot_nt(): lax.dot_general(a, b, (((1,), (1,)), ((), ())), preferred_element_type=F32)]
    all_to_all x5 -> x0, local copies, waits for them, and re-layouts: 23.8 us -> none  [the longest x4 19.2 us: to_seq(): return lax.all_to_all(x, 'cp', split_axis=0, concat_axis=1, tiled=True)]
  transfers between devices with their start and end apart: 15 -> 13, of which waited for: 15 -> 9; matrix products, arithmetic and copies ran while one was open for 11% -> 22% of each run, Pallas kernels for 0% -> 13%
where the time goes in v2:
time: 1450 us; the launch traced here: 1440 us
  waiting for transfers between devices  557 us (38%)
  matrix products  316 us (22%)
  Pallas kernels  297 us (20%)
  blocking collectives  131 us (9%)
  local copies, waits for them, and re-layouts  66.5 us (5%)
  other arithmetic  46.8 us (3%)
  between operations  14.8 us (1%)
    all_gather x8, waiting for transfers between devices, gather(): return lax.all_gather(x, 'cp', axis=axis, tiled=True)  431 us
    all_to_all x4, waiting for transfers between devices, exchange(): return lax.all_to_all(x, 'cp', split_axis=0, concat_axis=0, tiled=True)  125 us
    pallas_call x5, Pallas kernels, copy_out(): pl.pallas_call(copy_kernel, grid=(rows // bm,), in_specs=[spec], out_spec...  113 us
    dot_general x6, matrix products, dot_tn(): lax.dot_general(a, b, (((0,), (0,)), ((), ())), preferred_element_type=F32)  109 us
    all_to_all x2, blocking collectives, exchange(): return lax.all_to_all(x, 'cp', split_axis=0, concat_axis=0, tiled=True)  108 us
    pallas_call x1, Pallas kernels, attn_bwd(): pl.pallas_call(functools.partial(attn_bwd_kernel, hd), grid_spec=pltpu.Pr...  84.9 us
    dot_general x3, matrix products, dot(): return jnp.dot(a, b, preferred_element_type=F32)  80.8 us
    pallas_call x1, Pallas kernels, attn_fwd(): pl.pallas_call(functools.partial(attn_fwd_kernel, hd), grid_spec=pltpu.Pr...  68.8 us
  transfers between devices with their start and end apart: 13, of which 9 were waited for; matrix products, arithmetic and copies ran while one was open for 22% of the time, Pallas kernels for 13%

profile of v2, /device:TPU:0, one launch (start us, length us, event | category | flops | bytes accessed | tf_op | source)
XLA Modules:
  0.0 1441.7 jit_solution(6785716222233591689)
XLA Ops:
  7.9 6.8 multiply_reduce_fusion
  17.4 35.6 %all-gather.9.cloned.1.call-done = bf16[2048,1152]{1,0:T(8,128)(2,1)} async-done(((bf16[256,1152]{1,0:T(8,128)(2,1)}), bf16[2048,1152]{1,0:T(8,128)(2,1)}) %all-gather.9.cloned.1.call-update) | async-done | bytes 4718608 | tf_op jit(solution)/shard_map/all_gather | solution.py:334
  53.0 15.6 %fusion.17 = (f32[512]{0:T(512)S(1)}, bf16[512,3584]{1,0:T(8,128)(2,1)}) fusion(bf16[512,3584]{1,0:T(8,128)(2,1)} %param.15, bf16[1152,3584]{1,0:T(8,128)(2,1)} %param.19, bf16[2048,1152]{1,0:T(8,128)(2,1)} %all-gather.9.cloned.1.call-done, s32[512]{0:T(512)S(1)} %broadcast_select_fusion.2, pred[512]{0:T(512)(128)(4,1)S(1)} %fusion.80), kind=kOutput, calls=%fused_computation.36 | convolution fusion | flops 6654590464 | bytes 20320768 | tf_op jit(solution)/shard_map/dot_general | solution.py:38
  69.3 5.1 fusion.9
  76.7 4.9 constant_dynamic-slice_fusion.2
  81.6 4.1 constant_dynamic-slice_fusion
  85.7 9.3 multiply_sine_fusion
  95.0 116.9 %all-gather.11.cloned.1.call-done = bf16[4096,3584]{1,0:T(8,128)(2,1)} async-done(((bf16[512,3584]{1,0:T(8,128)(2,1)}), bf16[4096,3584]{1,0:T(8,128)(2,1)}) %all-gather.11.cloned.1.call-update) | async-done | bytes 29360144 | tf_op jit(solution)/shard_map/all_gather | solution.py:334
  211.9 36.9 %convolution_convert_fusion.1.raw_ref.v_ref = bf16[4096,1024]{1,0:T(8,128)(2,1)} fusion(bf16[4096,3584]{1,0:T(8,128)(2,1)} %all-gather.11.cloned.1.call-done, bf16[3584,256]{1,0:T(8,128)(2,1)S(1)} %get-tuple-element.73, bf16[3584,256]{1,0:T(8,128)(2,1)} %get-tuple-element.74, bf16[3584,512]{1,0:T(8,128)(2,1)} %constant_dynamic-slice_fusion.2), kind=kOutput, calls=%fused_computation.27 | convolution fusion | flops 30090985472 | bytes 45088768 | tf_op jit(solution)/shard_map/dot_general | solution.py:38
  248.9 12.3 rope_fwd.1
  261.1 2.2 copy-done.3
  266.5 68.8 %attn_fwd.1 = (bf16[8,512,512]{2,1,0:T(8,128)(2,1)S(1)}, f32[8,512,512]{2,1,0:T(8,128)}, f32[16,8,512]{2,1,0:T(8,128)S(1)}) custom-call(s32[16]{0:T(128)S(1)} %fusion.84.nkb_ref, s32[16,1,256]{2,1,0:T(1,128)S(1)} %get-tuple-element.61.lim_ref, bf16[4096,512]{1,0:T(8,128)(2,1)S(1)} %copy-done.3, bf16[4096,256]{1,0:T(8,128)(2,1)S(1)} %copy-done.4, ...), custom_call_target="tpu_custom_call" | custom-call | flops 18897856512 | bytes 16777216 | tf_op jit(solution)/shard_map/attn_fwd/pallas_call | solution.py:220
  335.3 2.0 copy-done
  337.3 3.5 all-to-all-start
  340.9 49.0 %all-to-all-done = bf16[8,512,512]{2,1,0:T(8,128)(2,1)} async-done(((bf16[8,512,512]{2,1,0:T(8,128)(2,1)}), bf16[8,512,512]{2,1,0:T(8,128)(2,1)}, u32[]{:S(2)}, u32[]{:S(2)}) %all-to-all-start) | async-done | bytes 4194336 | tf_op jit(solution)/shard_map/all_to_all | solution.py:337
  389.9 24.1 %fusion.15 = (f32[512]{0:T(512)S(1)}, bf16[512,3584]{1,0:T(8,128)(2,1)}) fusion(bf16[4096,512]{1,0:T(8,128)(2,1)} %bitcast.4, bf16[4096,3584]{1,0:T(8,128)(2,1)} %param.26), kind=kOutput, calls=%fused_computation.34 | convolution fusion | flops 15039725568 | bytes 37226496 | tf_op jit(solution)/shard_map/dot_general | solution.py:46
  414.0 6.8 fusion.12
  420.8 5.7 fusion.13
  426.5 25.5 %fusion.25 = bf16[4096,512]{0,1:T(8,128)(2,1)} fusion(bf16[512,3584]{1,0:T(8,128)(2,1)} %get-tuple-element.62, bf16[4096,3584]{1,0:T(8,128)(2,1)} %param.26), kind=kOutput, calls=%fused_computation.50 | convolution fusion | flops 15034482688 | bytes 37224448 | tf_op jit(solution)/shard_map/dot_general | solution.py:42
  452.1 6.4 copy.31
  458.5 78.8 %all_to_all.30.do_ref = bf16[8,512,512]{2,1,0:T(8,128)(2,1)} all-to-all(bf16[8,512,512]{2,1,0:T(8,128)(2,1)} %bitcast.77), channel_id=1, replica_groups=mesh['dp'=1,'cp'=8] {'cp'}, dimensions={0} | all-to-all | bytes 8388608 | tf_op jit(solution)/shard_map/all_to_all | solution.py:337
  537.3 84.9 %attn_bwd.1 = (bf16[4096,512]{1,0:T(8,128)(2,1)}, bf16[4096,256]{1,0:T(8,128)(2,1)S(1)}, bf16[4096,256]{1,0:T(8,128)(2,1)S(1)}) custom-call(s32[16]{0:T(128)S(1)} %fusion.84.nkb_ref, s32[16,1,256]{2,1,0:T(1,128)S(1)} %get-tuple-element.61.lim_ref, bf16[4096,512]{1,0:T(8,128)(2,1)} %get-tuple-element.29.q_ref, bf16[4096,256]{1,0:T(8,128)(2,1)} %get-tuple-element.30.k_ref, ...), custom_call_target="tpu_custom_call" | custom-call | flops 47244640256 | bytes 25165824 | tf_op jit(solution)/shard_map/attn_bwd/pallas_call | solution.py:292
  624.8 17.8 %rope_bwd.1 = (bf16[4096,1024]{1,0:T(8,128)(2,1)}, bf16[8,512,512]{2,1,0:T(8,128)(2,1)}, bf16[8,256,512]{2,1,0:T(8,128)(2,1)}, bf16[8,256,512]{2,1,0:T(8,128)(2,1)}, f32[1,256]{1,0:T(1,128)}, /*index=5*/f32[1,256]{1,0:T(1,128)}) custom-call(bf16[4096,1024]{1,0:T(8,128)(2,1)} %convolution_convert_fusion.1.raw_ref.v_ref, ...), custom_call_target="tpu_custom_call" | custom-call | flops 125829120 | bytes 25165824 | tf_op jit(solution)/shard_map/rope_bwd/pallas_call | solution.py:132
  642.6 28.9 %all_to_all.31 = bf16[8,256,512]{2,1,0:T(8,128)(2,1)S(1)} all-to-all(bf16[8,256,512]{2,1,0:T(8,128)(2,1)} %get-tuple-element.39), channel_id=1, replica_groups=mesh['dp'=1,'cp'=8] {'cp'}, dimensions={0} | all-to-all | bytes 4194304 | tf_op jit(solution)/shard_map/all_to_all | solution.py:337
  671.4 3.4 all-to-all-start.4
  674.9 13.0 fusion.88
  687.9 36.1 %all-to-all-done.4 = bf16[8,512,512]{2,1,0:T(8,128)(2,1)} async-done(((bf16[8,512,512]{2,1,0:T(8,128)(2,1)}), bf16[8,512,512]{2,1,0:T(8,128)(2,1)}, u32[]{:S(2)}, u32[]{:S(2)}) %all-to-all-start.4) | async-done | bytes 4194336 | tf_op jit(solution)/shard_map/all_to_all | solution.py:337
  724.0 2.3 all-to-all-start.3
  726.4 23.6 %fusion.89 = f32[512,3584]{1,0:T(8,128)} fusion(bf16[4096,512]{1,0:T(8,128)(2,1)} %bitcast.9, bf16[3584,4096]{1,0:T(8,128)(2,1)} %param.21), kind=kOutput, calls=%fused_computation.176 | convolution fusion | flops 15032385536 | bytes 40894464 | tf_op jit(solution)/shard_map/dot_general | solution.py:406
  750.0 2.8 all-to-all-done.3
  752.9 30.4 %fusion.10 = (f32[3584]{0:T(1024)}, f32[512]{0:T(512)S(1)}, bf16[512,3584]{1,0:T(8,128)(2,1)}) fusion(bf16[512,3584]{1,0:T(8,128)(2,1)} %get-tuple-element.69, f32[512]{0:T(512)S(1)} %copy-done.20, f32[3584]{0:T(1024)S(1)} %copy-done.14, f32[512,3584]{1,0:T(8,128)} %fusion.89, f32[512,3584]{1,0:T(8,128)} %fusion.88, bf16[2048,512]{1,0:T(8,128)(2,1)S(1)} %bitcast.80, ...), kind=kOutput, calls=%fused_computation.29 | convolution fusion | flops 7536373760 | bytes 38830080 | tf_op jit(solution)/shard_map/dot_general | solution.py:406
  783.4 7.4 broadcast_select_fusion
  790.8 8.7 convolution_convert_fusion.9
  799.6 4.7 convolution_convert_fusion
  804.3 4.9 pad_bitcast_fusion
  809.2 6.6 copy.34
  815.8 3.3 all-to-all-start.5
  819.1 28.2 %fusion.2 = bf16[4096,1152]{1,0:T(8,128)(2,1)} fusion(bf16[2048,1152]{1,0:T(8,128)(2,1)} %all-gather.9.cloned.1.call-done, s32[4096]{0:T(1024)S(1)} %broadcast_add_fusion), kind=kOutput, calls=%fused_computation.3 | convolution fusion | flops 19340460032 | bytes 14172160 | tf_op jit(solution)/shard_map/dot_general | solution.py:38
  847.4 37.5 %all-to-all-done.5 = bf16[8,512,512]{2,1,0:T(8,128)(2,1)} async-done(((bf16[8,512,512]{2,1,0:T(8,128)(2,1)}), bf16[8,512,512]{2,1,0:T(8,128)(2,1)}, u32[]{:S(2)}, u32[]{:S(2)}) %all-to-all-start.5) | async-done | bytes 4194336 | tf_op jit(solution)/shard_map/all_to_all | solution.py:337
  884.9 2.4 fusion.57
  887.3 2.9 convolution_add_fusion.6
  890.2 1.9 convolution_add_fusion.5
  892.1 1.9 convolution_add_fusion.4
  893.9 1.9 convolution_add_fusion.3
  895.8 1.9 convolution_add_fusion.2
  897.7 1.9 convolution_add_fusion.1
  899.6 2.9 fusion.30
  902.6 16.1 %convolution_convert_fusion.8 = bf16[3584,256]{1,0:T(8,128)(2,1)} fusion(bf16[4096,3584]{1,0:T(8,128)(2,1)} %all-gather.11.cloned.1.call-done, bf16[4096,1024]{1,0:T(8,128)(2,1)} %get-tuple-element.42), kind=kOutput, calls=%fused_computation.52 | convolution fusion | flops 7517110272 | bytes 33292288 | tf_op jit(solution)/shard_map/dot_general | solution.py:46
  918.8 16.9 %convolution_convert_fusion.7 = bf16[3584,256]{1,0:T(8,128)(2,1)} fusion(bf16[4096,3584]{1,0:T(8,128)(2,1)} %all-gather.11.cloned.1.call-done, bf16[4096,1024]{1,0:T(8,128)(2,1)} %get-tuple-element.42), kind=kOutput, calls=%fused_computation.51 | convolution fusion | flops 7517110272 | bytes 33292288 | tf_op jit(solution)/shard_map/dot_general | solution.py:46
  935.7 23.4 %convolution_convert_fusion.3 = bf16[3584,512]{1,0:T(8,128)(2,1)} fusion(bf16[4096,3584]{1,0:T(8,128)(2,1)} %all-gather.11.cloned.1.call-done, bf16[4096,1024]{1,0:T(8,128)(2,1)} %get-tuple-element.42), kind=kOutput, calls=%fused_computation.46 | convolution fusion | flops 15034220544 | bytes 37224448 | tf_op jit(solution)/shard_map/dot_general | solution.py:46
  959.2 6.8 copy.33
  966.1 23.9 %convolution_convert_fusion.2 = bf16[512,3584]{1,0:T(8,128)(2,1)} fusion(bf16[4096,512]{1,0:T(8,128)(2,1)} %bitcast.78, bf16[4096,3584]{1,0:T(8,128)(2,1)} %all-gather.21.cloned.1.call-done), kind=kOutput, calls=%fused_computation.45 | convolution fusion | flops 15034220544 | bytes 37224448 | tf_op jit(solution)/shard_map/dot_general | solution.py:46
  990.0 5.4 broadcast_select_fusion.1
  998.3 5.6 broadcast_in_dim.95
  1004.0 15.5 %broadcast_in_dim.96 = bf16[1,4096,1152]{2,1,0:T(8,128)(2,1)} reshape(bf16[16,4,16,4,1152]{4,3,2,1,0:T(4,128)(2,1)} %broadcast_in_dim.95) | data formatting | bytes 18874368 | tf_op jit(solution)/shard_map/broadcast_in_dim | solution.py:418
  1019.5 23.7 %all-reduce.1 = (bf16[1152]{0:T(1024)(128)(2,1)}, bf16[3584]{0:T(1024)(128)(2,1)}, bf16[256]{0:T(256)(128)(2,1)}, bf16[256]{0:T(256)(128)(2,1)}, bf16[3584]{0:T(1024)(128)(2,1)}) all-reduce(f32[1152]{0:T(1024)S(1)} %get-tuple-element.49, f32[3584]{0:T(1024)S(1)} %copy-done.23, ...), channel_id=1, replica_groups=mesh['dp'=1,'cp'=8] {'cp'}, use_global_device_ids=true, to_apply=%region_12.13 | all-reduce | flops 8832 | bytes 52992 | tf_op jit(solution)/shard_map/psum | solution.py:434
  1043.2 10.3 copy_out.5
  1053.5 19.9 %copy_out.7 = bf16[3584,2048]{1,0:T(8,128)(2,1)} custom-call(bf16[3584,2048]{1,0:T(8,128)(2,1)} %all-gather.17.cloned.1.call-done.x_ref), custom_call_target="tpu_custom_call" | custom-call | flops 7340032 | bytes 29360128 | tf_op jit(solution)/shard_map/copy_out/pallas_call | solution.py:316
  1073.4 44.6 %all-gather.19.cloned.1.call-done.x_ref = bf16[3584,2048]{1,0:T(8,128)(2,1)} async-done(((bf16[3584,256]{1,0:T(8,128)(2,1)}), bf16[3584,2048]{1,0:T(8,128)(2,1)}) %all-gather.19.cloned.1.call-update) | async-done | bytes 14680080 | tf_op jit(solution)/shard_map/all_gather | solution.py:334
  1118.0 20.4 %copy_out.8 = bf16[3584,2048]{1,0:T(8,128)(2,1)} custom-call(bf16[3584,2048]{1,0:T(8,128)(2,1)} %all-gather.19.cloned.1.call-done.x_ref), custom_call_target="tpu_custom_call" | custom-call | flops 7340032 | bytes 29360128 | tf_op jit(solution)/shard_map/copy_out/pallas_call | solution.py:316
  1138.4 125.2 %all-gather.15.cloned.1.call-done.x_ref = bf16[3584,4096]{1,0:T(8,128)(2,1)} async-done(((bf16[3584,512]{1,0:T(8,128)(2,1)}), bf16[3584,4096]{1,0:T(8,128)(2,1)}) %all-gather.15.cloned.1.call-update) | async-done | bytes 29360144 | tf_op jit(solution)/shard_map/all_gather | solution.py:334
  1263.6 30.6 %copy_out.6 = bf16[3584,4096]{1,0:T(8,128)(2,1)} custom-call(bf16[3584,4096]{1,0:T(8,128)(2,1)} %all-gather.15.cloned.1.call-done.x_ref), custom_call_target="tpu_custom_call" | custom-call | flops 14680064 | bytes 58720256 | tf_op jit(solution)/shard_map/copy_out/pallas_call | solution.py:316
  1294.2 108.6 %all-gather.23.cloned.1.call-done.x_ref = bf16[4096,3584]{1,0:T(8,128)(2,1)} async-done(((bf16[512,3584]{1,0:T(8,128)(2,1)}), bf16[4096,3584]{1,0:T(8,128)(2,1)}) %all-gather.23.cloned.1.call-update) | async-done | bytes 29360144 | tf_op jit(solution)/shard_map/all_gather | solution.py:334
  1402.9 31.9 %copy_out.9 = bf16[4096,3584]{1,0:T(8,128)(2,1)} custom-call(bf16[4096,3584]{1,0:T(8,128)(2,1)} %all-gather.23.cloned.1.call-done.x_ref), custom_call_target="tpu_custom_call" | custom-call | flops 14680064 | bytes 58720256 | tf_op jit(solution)/shard_map/copy_out/pallas_call | solution.py:316
  (126 shorter events, 15.4 us)
Async XLA Ops:
  7.2 45.8 %all-gather.9.cloned.1.call-start = ((), (), s32[]{:S(2)}) async-start(), calls=%async_computation.7 | async-start | bytes 5308416 | tf_op jit(solution)/shard_map/all_gather | solution.py:334
  7.9 7.4 copy-start.15
  7.9 9.2 copy-start.31
  7.9 9.4 copy-start.27
  14.8 0.5 copy-start.32
  14.8 1.0 copy-start.10
  15.3 0.5 copy-start.21
  16.9 195.1 %all-gather.11.cloned.1.call-start = ((), (), s32[]{:S(2)}) async-start(), calls=%async_computation.8 | async-start | bytes 33030144 | tf_op jit(solution)/shard_map/all_gather | solution.py:334
  17.2 51.4 %copy-start.24 = (pred[512]{0:T(512)(128)(4,1)}, pred[512]{0:T(512)(128)(4,1)S(1)}, u32[]{:S(2)}) copy-start(pred[512]{0:T(512)(128)(4,1)S(1)} %fusion.80) | copy-start | bytes 1540
  17.4 51.3 %copy-start.34 = (s32[512]{0:T(512)}, s32[512]{0:T(512)S(1)}, u32[]{:S(2)}) copy-start(s32[512]{0:T(512)S(1)} %broadcast_select_fusion.2) | copy-start | bytes 6148
  17.4 51.3 %copy-start.13 = (f32[3584]{0:T(1024)}, f32[3584]{0:T(1024)S(1)}, u32[]{:S(2)}) copy-start(f32[3584]{0:T(1024)S(1)} %convert_add_fusion.3) | copy-start | bytes 43012
  68.7 5.8 copy-start.29
  68.7 0.6 copy-start.19
  69.3 5.2 copy-start.38
  69.3 5.7 copy-start.39
  261.1 2.2 copy-start.3
  263.3 1.6 copy-start.4
  264.9 1.6 copy-start.5
  335.3 2.0 copy-start
  337.3 3.5 copy-start.28
  337.3 52.6 %all-to-all-start = ((bf16[8,512,512]{2,1,0:T(8,128)(2,1)}), bf16[8,512,512]{2,1,0:T(8,128)(2,1)}, u32[]{:S(2)}, u32[]{:S(2)}) async-start(bf16[8,512,512]{2,1,0:T(8,128)(2,1)} %copy-done), calls=%async_computation | async-start | bytes 8388608 | tf_op jit(solution)/shard_map/all_to_all | solution.py:337
  340.8 625.3 %all-gather.21.cloned.1.call-start = ((), (), s32[]{:S(2)}) async-start(), calls=%async_computation.14 | async-start | bytes 33030144 | tf_op jit(solution)/shard_map/all_gather | solution.py:334
  389.9 24.1 %copy-start.6 = (bf16[512,3584]{1,0:T(8,128)(2,1)S(1)}, bf16[512,3584]{1,0:T(8,128)(2,1)}, u32[]{:S(2)}) copy-start(bf16[512,3584]{1,0:T(8,128)(2,1)} %param.17) | copy-start | bytes 11010052
  414.0 6.8 copy-start.7
  414.0 6.8 copy-start.9
  622.1 1.3 copy-start.1
  623.5 1.3 copy-start.2
  671.4 3.5 copy-start.18
  671.4 52.5 %all-to-all-start.4 = ((bf16[8,512,512]{2,1,0:T(8,128)(2,1)}), bf16[8,512,512]{2,1,0:T(8,128)(2,1)}, u32[]{:S(2)}, u32[]{:S(2)}) async-start(bf16[8,512,512]{2,1,0:T(8,128)(2,1)} %get-tuple-element.41), calls=%async_computation.4 | async-start | bytes 8388608 | tf_op jit(solution)/shard_map/all_to_all | solution.py:337
  724.0 28.9 %all-to-all-start.3 = ((bf16[8,256,512]{2,1,0:T(8,128)(2,1)}), bf16[8,256,512]{2,1,0:T(8,128)(2,1)S(1)}, u32[]{:S(2)}, u32[]{:S(2)}) async-start(bf16[8,256,512]{2,1,0:T(8,128)(2,1)} %get-tuple-element.40), calls=%async_computation.3 | async-start | bytes 4194304 | tf_op jit(solution)/shard_map/all_to_all | solution.py:337
  726.3 269.1 %reduce-scatter.2.cloned.1.call-start = ((), (), s32[]{:S(2)}) async-start(), calls=%async_computation.9 | async-start | bytes 5308416 | tf_op jit(solution)/shard_map/reduce_scatter | solution.py:415
  726.4 26.5 %copy-start.14 = (f32[3584]{0:T(1024)S(1)}, f32[3584]{0:T(1024)}, u32[]{:S(2)}) copy-start(f32[3584]{0:T(1024)} %copy-done.13) | copy-start | bytes 43012
  726.4 26.5 %copy-start.20 = (f32[512]{0:T(512)S(1)}, f32[512]{0:T(512)}, u32[]{:S(2)}) copy-start(f32[512]{0:T(512)} %copy-done.19) | copy-start | bytes 6148
  752.9 30.5 %copy-start.30 = (f32[512]{0:T(512)S(1)}, f32[512]{0:T(512)}, u32[]{:S(2)}) copy-start(f32[512]{0:T(512)} %copy-done.29) | copy-start | bytes 6148
  752.9 30.5 %copy-start.25 = (pred[512]{0:T(512)(128)(4,1)S(1)}, pred[512]{0:T(512)(128)(4,1)}, u32[]{:S(2)}) copy-start(pred[512]{0:T(512)(128)(4,1)} %copy-done.24) | copy-start | bytes 1540
  790.8 8.8 copy-start.8
  790.8 8.8 copy-start.35
  815.8 69.1 %all-to-all-start.5 = ((bf16[8,512,512]{2,1,0:T(8,128)(2,1)}), bf16[8,512,512]{2,1,0:T(8,128)(2,1)}, u32[]{:S(2)}, u32[]{:S(2)}) async-start(bf16[8,512,512]{2,1,0:T(8,128)(2,1)} %bitcast.76), calls=%async_computation.6 | async-start | bytes 8388608 | tf_op jit(solution)/shard_map/all_to_all | solution.py:337
  819.1 224.1 %all-gather.13.cloned.1.call-start = ((), (), s32[]{:S(2)}) async-start(), calls=%async_computation.10 | async-start | bytes 10616832 | tf_op jit(solution)/shard_map/all_gather | solution.py:334
  884.9 5.3 copy-start.12
  902.5 151.0 %all-gather.17.cloned.1.call-start = ((), (), s32[]{:S(2)}) async-start(), calls=%async_computation.12 | async-start | bytes 16515072 | tf_op jit(solution)/shard_map/all_gather | solution.py:334
  918.7 199.3 %all-gather.19.cloned.1.call-start = ((), (), s32[]{:S(2)}) async-start(), calls=%async_computation.13 | async-start | bytes 16515072 | tf_op jit(solution)/shard_map/all_gather | solution.py:334
  935.7 328.0 %all-gather.15.cloned.1.call-start = ((), (), s32[]{:S(2)}) async-start(), calls=%async_computation.11 | async-start | bytes 33030144 | tf_op jit(solution)/shard_map/all_gather | solution.py:334
  959.2 443.7 %all-gather.23.cloned.1.call-start = ((), (), s32[]{:S(2)}) async-start(), calls=%async_computation.15 | async-start | bytes 33030144 | tf_op jit(solution)/shard_map/all_gather | solution.py:334
  966.1 23.9 %copy-start.26 = (pred[512]{0:T(512)(128)(4,1)S(1)}, pred[512]{0:T(512)(128)(4,1)}, u32[]{:S(2)}) copy-start(pred[512]{0:T(512)(128)(4,1)} %copy-done.24) | copy-start | bytes 1540
  990.0 5.5 copy-start.11
  990.0 5.5 copy-start.16
  990.0 5.4 copy-start.22
  990.0 6.9 copy-start.33
  1004.0 15.5 %copy-start.17 = (f32[3584]{0:T(1024)S(1)}, f32[3584]{0:T(1024)}, u32[]{:S(2)}) copy-start(f32[3584]{0:T(1024)} %get-tuple-element.45) | copy-start | bytes 43012
  1004.0 15.5 %copy-start.23 = (f32[3584]{0:T(1024)S(1)}, f32[3584]{0:T(1024)}, u32[]{:S(2)}) copy-start(f32[3584]{0:T(1024)} %get-tuple-element.47) | copy-start | bytes 43012
  1004.0 15.5 %copy-start.36 = (f32[1,256]{1,0:T(1,128)S(1)}, f32[1,256]{1,0:T(1,128)}, u32[]{:S(2)}) copy-start(f32[1,256]{1,0:T(1,128)} %get-tuple-element.43) | copy-start | bytes 3076
  1004.0 15.5 %copy-start.37 = (f32[1,256]{1,0:T(1,128)S(1)}, f32[1,256]{1,0:T(1,128)}, u32[]{:S(2)}) copy-start(f32[1,256]{1,0:T(1,128)} %get-tuple-element.44) | copy-start | bytes 3076
Sparse Core Ops, SparseCore 0:
  17.0 36.0 all-gather.8
  74.5 137.3 all-gather.10
  426.6 176.6 all-gather.20
  804.4 83.7 reduce-scatter.1
  902.6 54.1 all-gather.12
  959.1 78.7 all-gather.16
  1039.7 78.2 all-gather.18
  1120.4 143.1 all-gather.14
  1265.4 137.3 all-gather.22

commit v3 on v2

--- a/solution.py
+++ b/solution.py
@@ -92,19 +92,22 @@
     )(raw, cos, sin, gq, gk)
 
 
-def rope_bwd_kernel(hd, raw_ref, dq_ref, dk_ref, dv_ref, cos_ref, sin_ref, gq_ref, gk_ref, out_ref, qt_ref, kt_ref, vt_ref, sq_ref, sk_ref):
+def rope_bwd_kernel(hd, raw_ref, dq0_ref, dq1_ref, dk_ref, dv_ref, cos_ref, sin_ref, gq_ref, gk_ref, out_ref, qt_ref, kt_ref, vt_ref, sq_ref, sk_ref):
     cos, sin = cos_ref[...], sin_ref[...]
     half = hd // 2
-    n_q = dq_ref.shape[1] // hd
+    n_q = dq0_ref.shape[1] // hd
 
     @pl.when(pl.program_id(0) == 0)
     def _():
         sq_ref[...] = jnp.zeros_like(sq_ref)
         sk_ref[...] = jnp.zeros_like(sk_ref)
 
-    def one(col, d_ref, dcol, gain, acc_ref, t_ref):
-        da = d_ref[:, dcol:dcol + half].astype(F32)
-        db = d_ref[:, dcol + half:dcol + hd].astype(F32)
+    def load(refs, lo, hi):
+        return jnp.concatenate([ref[:, lo:hi] for ref in refs], axis=0).astype(F32)
+
+    def one(col, refs, dcol, gain, acc_ref, t_ref):
+        da = load(refs, dcol, dcol + half)
+        db = load(refs, dcol + half, dcol + hd)
         d = jnp.concatenate([da * cos + db * sin, db * cos - da * sin], axis=1)
         x = raw_ref[:, col:col + hd].astype(F32)
         r = lax.rsqrt(jnp.mean(x * x, axis=-1, keepdims=True) + EPS)
@@ -117,13 +120,13 @@
         t_ref[0, dcol:dcol + hd, :] = dx.T
 
     for h in range(n_q):
-        one(h * hd, dq_ref, h * hd, gq_ref[...], sq_ref, qt_ref)
-    one(n_q * hd, dk_ref, 0, gk_ref[...], sk_ref, kt_ref)
+        one(h * hd, (dq0_ref, dq1_ref), h * hd, gq_ref[...], sq_ref, qt_ref)
+    one(n_q * hd, (dk_ref,), 0, gk_ref[...], sk_ref, kt_ref)
     out_ref[:, (n_q + 1) * hd:] = dv_ref[...]
     vt_ref[0] = dv_ref[...].T
 
 
-def rope_bwd(raw, dq, dk, dv, cos, sin, gq, gk, hd, n_q, bm):
+def rope_bwd(raw, dq_halves, dk, dv, cos, sin, gq, gk, hd, n_q, bm):
     seq, width = raw.shape
     tall = lambda w: pl.BlockSpec((1, w, bm), lambda i: (i, 0, 0))
     tshape = lambda w: jax.ShapeDtypeStruct((seq // bm, w, bm), BF16)
@@ -132,16 +135,18 @@
     return pl.pallas_call(
         functools.partial(rope_bwd_kernel, hd),
         grid=(seq // bm,),
-        in_specs=[row(width), row(n_q * hd), row(hd), row(hd), row(hd // 2), row(hd // 2), fix, fix],
+        in_specs=[row(width)] + [pl.BlockSpec((bm // 2, n_q * hd), lambda i: (i, 0))] * 2 + [row(hd), row(hd), row(hd // 2), row(hd // 2), fix, fix],
         out_specs=[row(width), tall(n_q * hd), tall(hd), tall(hd), fix, fix],
         out_shape=[jax.ShapeDtypeStruct((seq, width), BF16), tshape(n_q * hd), tshape(hd), tshape(hd), jax.ShapeDtypeStruct((1, hd), F32), jax.ShapeDtypeStruct((1, hd), F32)],
         cost_estimate=pl.CostEstimate(flops=30 * seq * width, bytes_accessed=6 * seq * width, transcendentals=0),
         name="rope_bwd",
-    )(raw, dq, dk, dv, cos, sin, gq, gk)
+    )(raw, *dq_halves, dk, dv, cos, sin, gq, gk)
 
 
 BQ = 256
 KB = 512
+HALVES = 2
+HALF_DEV = 4
 
 
 def stack_heads(blk, hd):
@@ -159,8 +164,8 @@
     return jnp.concatenate([blk[h * hd:(h + 1) * hd] for h in range(blk.shape[0] // hd)], axis=1)
 
 
-def attn_fwd_kernel(hd, nkb_ref, lim_ref, q_ref, k_ref, vt_ref, o_ref, o32_ref, lse_ref, s_ref):
-    qb = pl.program_id(0)
+def attn_fwd_kernel(hd, part, nkb_ref, lim_ref, q_ref, k_ref, vt_ref, o_ref, o32_ref, lse_ref, s_ref):
+    qb = HALVES * pl.program_id(0) + part
     coef = hd ** -0.5 * LOG2E
     n_q = q_ref.shape[1] // hd
     rows = n_q * BQ
@@ -212,39 +217,45 @@
     lse_ref[0] = jnp.broadcast_to(m * coef + jnp.log2(l), (8, rows))
 
 
-def attn_fwd(nkb, lim, q, k, vt, hd, seq_loc):
+def attn_fwd(part, nkb, lim, q, k, vt, hd, n_dev):
     seq, width = q.shape
     n_q = width // hd
-    per = seq_loc // BQ
-    tall = pl.BlockSpec((1, width, BQ), lambda i, *_: (i // per, 0, i % per))
+    tall = pl.BlockSpec((1, width, BQ), lambda i, *_: (i, 0, 0))
+    at = lambda i, *_: HALVES * i + part
     return pl.pallas_call(
-        functools.partial(attn_fwd_kernel, hd),
+        functools.partial(attn_fwd_kernel, hd, part),
         grid_spec=pltpu.PrefetchScalarGridSpec(
             num_scalar_prefetch=1,
-            grid=(seq // BQ,),
-            in_specs=[pl.BlockSpec((1, 1, BQ), lambda i, *_: (i, 0, 0)), pl.BlockSpec((BQ, width), lambda i, *_: (i, 0)),
+            grid=(n_dev,),
+            in_specs=[pl.BlockSpec((1, 1, BQ), lambda i, *_: (at(i), 0, 0)), pl.BlockSpec((BQ, width), lambda i, *_: (at(i), 0)),
                       pl.BlockSpec((seq, hd), lambda i, *_: (0, 0)), pl.BlockSpec((hd, seq), lambda i, *_: (0, 0))],
             out_specs=[tall, tall, pl.BlockSpec((1, 8, n_q * BQ), lambda i, *_: (i, 0, 0))],
             scratch_shapes=[pltpu.VMEM((seq, n_q * BQ), F32)]),
-        out_shape=[jax.ShapeDtypeStruct((seq // seq_loc, width, seq_loc), BF16), jax.ShapeDtypeStruct((seq // seq_loc, width, seq_loc), F32),
-                   jax.ShapeDtypeStruct((seq // BQ, 8, n_q * BQ), F32)],
-        cost_estimate=pl.CostEstimate(flops=int(2.2 * seq * seq * width), bytes_accessed=8 * seq * width, transcendentals=seq * seq),
+        out_shape=[jax.ShapeDtypeStruct((n_dev, width, BQ), BF16), jax.ShapeDtypeStruct((n_dev, width, BQ), F32),
+                   jax.ShapeDtypeStruct((n_dev, 8, n_q * BQ), F32)],
+        cost_estimate=pl.CostEstimate(flops=int(1.1 * seq * seq * width), bytes_accessed=4 * seq * width, transcendentals=seq * seq),
         compiler_params=pltpu.CompilerParams(vmem_limit_bytes=40 * 1024 * 1024),
         name="attn_fwd",
     )(nkb, lim, q, k, vt)
 
 
-def attn_bwd_kernel(hd, nkb_ref, lim_ref, q_ref, k_ref, kt_ref, v_ref, do_ref, o32_ref, lse_ref, dq_ref, dk_ref, dv_ref, dk_acc, dv_acc):
-    qb = pl.program_id(0)
+def attn_bwd_kernel(hd, part, nkb_ref, lim_ref, q_ref, k_ref, kt_ref, v_ref, do_ref, o32_ref, lse_ref, *refs):
+    step = pl.program_id(0)
+    qb = HALVES * step + part
     scale = hd ** -0.5
     coef = scale * LOG2E
     n_q = q_ref.shape[1] // hd
     rows = n_q * BQ
-
-    @pl.when(qb == 0)
+    first, last = part == 0, part == HALVES - 1
+    if not first:
+        dk_in, dv_in, *refs = refs
+    dq_ref, dk_ref, dv_ref, *refs = refs
+    dk_acc, dv_acc = refs if last else (dk_ref, dv_ref)
+
+    @pl.when(step == 0)
     def _():
-        dk_acc[...] = jnp.zeros_like(dk_acc)
-        dv_acc[...] = jnp.zeros_like(dv_acc)
+        dk_acc[...] = jnp.zeros_like(dk_acc) if first else dk_in[...]
+        dv_acc[...] = jnp.zeros_like(dv_acc) if first else dv_in[...]
 
     q2 = stack_heads(q_ref[...], hd)
     qt = q2.T
@@ -275,53 +286,108 @@
     for h in range(n_q):
         dq_ref[:, h * hd:(h + 1) * hd] = dq[h * BQ:(h + 1) * BQ]
 
-    @pl.when(qb == pl.num_programs(0) - 1)
-    def _():
-        dk_ref[...] = dk_acc[...].astype(BF16)
-        dv_ref[...] = dv_acc[...].astype(BF16)
-
-
-def attn_bwd(nkb, lim, q, k, kt, raw, d_o, o32, lse, hd):
+    if last:
+        @pl.when(step == pl.num_programs(0) - 1)
+        def _():
+            dk_ref[...] = dk_acc[...].astype(BF16)
+            dv_ref[...] = dv_acc[...].astype(BF16)
+
+
+def attn_bwd(part, nkb, lim, q, k, kt, raw, d_o, o32, lse, carried, hd, n_dev):
     seq, width = q.shape
     n_q = width // hd
     v_col = raw.shape[1] // hd - 1
-    per = d_o.shape[2] // BQ
-    row = lambda w: pl.BlockSpec((BQ, w), lambda i, *_: (i, 0))
-    tall = pl.BlockSpec((1, width, BQ), lambda i, *_: (i // per, 0, i % per))
+    at = lambda i, *_: HALVES * i + part
+    tall = pl.BlockSpec((1, width, BQ), lambda i, *_: (i, 0, 0))
     whole = pl.BlockSpec((seq, hd), lambda i, *_: (0, 0))
+    last = part == HALVES - 1
+    acc_type = BF16 if last else F32
     return pl.pallas_call(
-        functools.partial(attn_bwd_kernel, hd),
+        functools.partial(attn_bwd_kernel, hd, part),
         grid_spec=pltpu.PrefetchScalarGridSpec(
             num_scalar_prefetch=1,
-            grid=(seq // BQ,),
-            in_specs=[pl.BlockSpec((1, 1, BQ), lambda i, *_: (i, 0, 0)), row(width), whole, pl.BlockSpec((hd, seq), lambda i, *_: (0, 0)),
-                      pl.BlockSpec((seq, hd), lambda i, *_: (0, v_col)), tall, tall, pl.BlockSpec((1, 8, n_q * BQ), lambda i, *_: (i, 0, 0))],
-            out_specs=[row(width), whole, whole],
-            scratch_shapes=[pltpu.VMEM((seq, hd), F32), pltpu.VMEM((seq, hd), F32)]),
-        out_shape=[jax.ShapeDtypeStruct((seq, width), BF16), jax.ShapeDtypeStruct((seq, hd), BF16), jax.ShapeDtypeStruct((seq, hd), BF16)],
-        cost_estimate=pl.CostEstimate(flops=int(5.5 * seq * seq * width), bytes_accessed=12 * seq * width, transcendentals=seq * seq),
-        compiler_params=pltpu.CompilerParams(vmem_limit_bytes=48 * 1024 * 1024),
+            grid=(n_dev,),
+            in_specs=[pl.BlockSpec((1, 1, BQ), lambda i, *_: (at(i), 0, 0)), pl.BlockSpec((BQ, width), lambda i, *_: (at(i), 0)), whole,
+                      pl.BlockSpec((hd, seq), lambda i, *_: (0, 0)), pl.BlockSpec((seq, hd), lambda i, *_: (0, v_col)), tall, tall,
+                      pl.BlockSpec((1, 8, n_q * BQ), lambda i, *_: (i, 0, 0))] + [whole] * len(carried),
+            out_specs=[pl.BlockSpec((BQ, width), lambda i, *_: (i, 0)), whole, whole],
+            scratch_shapes=[pltpu.VMEM((seq, hd), F32)] * 2 if last else []),
+        out_shape=[jax.ShapeDtypeStruct((n_dev * BQ, width), BF16), jax.ShapeDtypeStruct((seq, hd), acc_type), jax.ShapeDtypeStruct((seq, hd), acc_type)],
+        cost_estimate=pl.CostEstimate(flops=int(2.7 * seq * seq * width), bytes_accessed=6 * seq * width, transcendentals=seq * seq),
+        compiler_params=pltpu.CompilerParams(vmem_limit_bytes=56 * 1024 * 1024),
         name="attn_bwd",
-    )(nkb, lim, q, k, kt, raw, d_o, o32, lse)
-
-
-def copy_kernel(x_ref, o_ref):
-    o_ref[...] = x_ref[...]
-
-
-def copy_out(x, cols):
-    rows = x.shape[0]
-    bm = 128
-    spec = pl.BlockSpec((bm, cols), lambda i: (i, 0))
+    )(nkb, lim, q, k, kt, raw, d_o, o32, lse, *carried)
+
+
+def by_core(core_ref, own_ref, par_ref, store):
+    @pl.when(core_ref[0] == 0)
+    def _():
+        store(own_ref, par_ref)
+
+    @pl.when(core_ref[0] != 0)
+    def _():
+        store(par_ref, own_ref)
+
+
+def merge_cols_kernel(core_ref, own_ref, par_ref, o_ref):
+    n = HALF_DEV
+    w = own_ref.shape[1] // n
+
+    def store(even, odd):
+        for j in range(n):
+            o_ref[:, 2 * j * w:(2 * j + 1) * w] = even[:, j * w:(j + 1) * w]
+            o_ref[:, (2 * j + 1) * w:(2 * j + 2) * w] = odd[:, j * w:(j + 1) * w]
+
+    by_core(core_ref, own_ref, par_ref, store)
+
+
+def merge_rows_kernel(core_ref, own_ref, par_ref, o_ref):
+    b = own_ref.shape[0]
+
+    def store(even, odd):
+        o_ref[:b] = even[...]
+        o_ref[b:] = odd[...]
+
+    by_core(core_ref, own_ref, par_ref, store)
+
+
+def merge_rows_t_kernel(core_ref, own_ref, par_ref, o_ref):
+    def store(even, odd):
+        o_ref[...] = jnp.concatenate([even[...], odd[...]], axis=0).T
+
+    by_core(core_ref, own_ref, par_ref, store)
+
+
+def merge_call(body, core, own, par, grid, in_block, in_map, out_shape, out_block, out_map):
     return pl.pallas_call(
-        copy_kernel,
-        grid=(rows // bm,),
-        in_specs=[spec],
-        out_specs=spec,
-        out_shape=jax.ShapeDtypeStruct((rows, cols), x.dtype),
-        cost_estimate=pl.CostEstimate(flops=rows * cols, bytes_accessed=4 * rows * cols, transcendentals=0),
-        name="copy_out",
-    )(x)
+        body,
+        grid_spec=pltpu.PrefetchScalarGridSpec(
+            num_scalar_prefetch=1, grid=(grid,),
+            in_specs=[pl.BlockSpec(in_block, in_map)] * 2,
+            out_specs=pl.BlockSpec(out_block, out_map)),
+        out_shape=jax.ShapeDtypeStruct(out_shape, own.dtype),
+        cost_estimate=pl.CostEstimate(flops=out_shape[0] * out_shape[1], bytes_accessed=4 * out_shape[0] * out_shape[1], transcendentals=0),
+        compiler_params=pltpu.CompilerParams(vmem_limit_bytes=40 * 1024 * 1024),
+        name="merge",
+    )(core, own, par)
+
+
+def merge_cols(core, own, par):
+    rows, cols = own.shape
+    bm = 512
+    return merge_call(merge_cols_kernel, core, own, par, rows // bm, (bm, cols), lambda i, *_: (i, 0), (rows, 2 * cols), (bm, 2 * cols), lambda i, *_: (i, 0))
+
+
+def merge_rows(core, own, par, n):
+    rows, cols = own.shape
+    bm = rows // n
+    return merge_call(merge_rows_kernel, core, own, par, n, (bm, cols), lambda i, *_: (i, 0), (2 * rows, cols), (2 * bm, cols), lambda i, *_: (i, 0))
+
+
+def merge_rows_t(core, own, par, n):
+    rows, cols = own.shape
+    bm = rows // n
+    return merge_call(merge_rows_t_kernel, core, own, par, n, (bm, cols), lambda i, *_: (i, 0), (cols, 2 * rows), (cols, 2 * bm), lambda i, *_: (0, i))
 
 
 def solution(mesh):
@@ -333,8 +399,14 @@
     def gather(x, axis=0):
         return lax.all_gather(x, 'cp', axis=axis, tiled=True)
 
-    def exchange(x):
+    def exchange(x, after=None):
+        if after is not None:
+            x, _ = lax.optimization_barrier((x, after))
         return lax.all_to_all(x, 'cp', split_axis=0, concat_axis=0, tiled=True)
+
+    def gather_pair(x, axis=0):
+        own = lax.all_gather(x, 'cp', axis=axis, tiled=True, axis_index_groups=[list(range(c, n_dev, 2)) for c in range(2)])
+        return own, lax.ppermute(own, 'cp', [(i, i ^ 1) for i in range(n_dev)])
 
     def device_step(vis_loc, text_loc, img_pos, grad_y, pn_gain, w_proj, pre_gain, w_query, w_key, w_value, q_gain, k_gain, w_out, post_gain):
         rank = lax.axis_index('cp')
@@ -387,26 +459,47 @@
         raw = dot(hidden_all, w_qkv).astype(BF16)
         cos_t, sin_t = rope_tables(seq, hd)
         q, k, kt, vt = rope_fwd(raw, cos_t, sin_t, gq32, gk32, hd, n_q)
-        o_t, o32_t, lse = attn_fwd(n_kb, limit, q, k, vt, hd, seq_loc)
-
-        attn_t = exchange(o_t).reshape(n_dev * wq_loc, seq_loc)
-        proj_out = dot_tn(attn_t, w_out).astype(BF16)
-        y_loc, post_pull = jax.vjp(post_residual, merged, proj_out, post32)
-        d_resid, d_proj, g_post = post_pull(grad_y)
-        d_attn_t = dot_nt(w_out, d_proj).astype(BF16).reshape(n_dev, wq_loc, seq_loc)
-        d_o = exchange(d_attn_t)
-        d_proj_all = gather(d_proj)
-
-        dq, dk, dv = attn_bwd(n_kb, limit, q, k, kt, raw, d_o, o32_t, lse, hd)
-        d_qkv, dq_t, dk_t, dv_t, g_q_gain, g_k_gain = rope_bwd(raw, dq, dk, dv, cos_t, sin_t, gq32, gk32, hd, n_q, seq_loc)
-
-        dk_seq = exchange(dk_t).reshape(-1, seq_loc)
-        dv_seq = exchange(dv_t).reshape(-1, seq_loc)
-        dq_seq = exchange(dq_t).reshape(-1, seq_loc)
+        core = rank % 2
+        rows_of = lambda x, c: x[c * BQ:(c + 1) * BQ]
+        fwd = []
+        for c in range(HALVES):
+            fwd.append(attn_fwd(c, n_kb, limit, q, k, vt, hd, n_dev))
+        y_parts, d_o, d_proj_all, g_post = [], [], [], 0.0
+        attn_t = []
+        for c in range(HALVES):
+            attn_t.append(exchange(fwd[c][0], attn_t[-1] if c else None))
+        prev = attn_t[-1]
+        for c in range(HALVES):
+            attn_c = attn_t[c]
+            if c:
+                attn_c, _ = lax.optimization_barrier((attn_c, d_attn_t))
+            proj_out = dot_tn(attn_c.reshape(n_dev * wq_loc, BQ), w_out).astype(BF16)
+            y_part, post_pull = jax.vjp(post_residual, rows_of(merged, c), proj_out, post32)
+            _, d_proj, g_post_part = post_pull(rows_of(grad_y, c))
+            d_attn_t = dot_nt(w_out, d_proj).astype(BF16).reshape(n_dev, wq_loc, BQ)
+            y_parts.append(y_part)
+            g_post = g_post + g_post_part
+            prev = exchange(d_attn_t, prev)
+            d_o.append(prev)
+            d_proj_all.append(gather_pair(d_proj))
+        y_loc = jnp.concatenate(y_parts, axis=0)
+
+        dq_halves, carried = [], []
+        for c in range(HALVES):
+            dq, *carried = attn_bwd(c, n_kb, limit, q, k, kt, raw, d_o[c], fwd[c][1], fwd[c][2], carried, hd, n_dev)
+            dq_halves.append(dq)
+        dk, dv = carried
+        g_value = gather_pair(dot_tn(hidden_all, dv).astype(BF16), 1)
+        d_qkv, dq_t, dk_t, dv_t, g_q_gain, g_k_gain = rope_bwd(raw, dq_halves, dk, dv, cos_t, sin_t, gq32, gk32, hd, n_q, seq_loc)
+
+        dk_seq = exchange(dk_t, prev)
+        dv_seq = exchange(dv_t, dk_seq)
+        dq_seq = exchange(dq_t, dv_seq)
+        dk_seq, dv_seq, dq_last = [x.reshape(-1, seq_loc) for x in (dk_seq, dv_seq, dq_seq)]
         d_hidden = sum(lax.dot_general(d, w, (((0,), (1,)), ((), ())), preferred_element_type=F32)
-                       for d, w in ((dk_seq, w_key), (dv_seq, w_value), (dq_seq, w_query))).astype(BF16)
+                       for d, w in ((dk_seq, w_key), (dv_seq, w_value), (dq_last, w_query))).astype(BF16)
         d_merged_attn, g_pre = pre_pull(d_hidden)
-        d_merged = (d_resid.astype(F32) + d_merged_attn.astype(F32)).astype(BF16)
+        d_merged = (grad_y.astype(F32) + d_merged_attn.astype(F32)).astype(BF16)
         grad_text = jnp.where(img_mask, 0.0, d_merged).astype(BF16)
 
         d_soft_rows = jnp.where(img_mask, d_merged, 0.0).astype(BF16)
@@ -417,20 +510,25 @@
         spread = (d_pooled.astype(F32) / (POOL * POOL)).astype(BF16).reshape(img_loc, SIDE, 1, SIDE, 1, dim_v)
         grad_vis = jnp.broadcast_to(spread, (img_loc, SIDE, POOL, SIDE, POOL, dim_v)).reshape(img_loc, patches, dim_v)
 
-        pad_cols = -(-d_model // (n_dev * 128)) * n_dev * 128
-        d_soft_blk = jnp.pad(d_soft_rows, ((0, 0), (0, pad_cols - d_model))).T.reshape(n_dev, pad_cols // n_dev, seq_loc)
-        d_soft_t = exchange(d_soft_blk)
+        d_soft_t = exchange(d_soft_rows.T.reshape(n_dev, d_model // n_dev, seq_loc), dq_seq)
         normed_pos = dot(select_all, normed_all).astype(BF16).reshape(n_dev, seq_loc, dim_v)
-        g_proj = sum(lax.dot_general(normed_pos[i], d_soft_t[i], (((0,), (1,)), ((), ())), preferred_element_type=F32) for i in range(n_dev))
-        g_proj = gather(g_proj.astype(BF16), 1)
-
-        g_query = gather(dot_tn(hidden_all, d_qkv[:, :wq_loc]).astype(BF16), 1)
-        o_rows = o_t.transpose(0, 2, 1).reshape(seq, wq_loc)
-        g_out = gather(dot_tn(o_rows, d_proj_all).astype(BF16))
-        g_value = gather(dot_tn(hidden_all, d_qkv[:, wq_loc + wk_loc:]).astype(BF16), 1)
-        g_key = gather(dot_tn(hidden_all, d_qkv[:, wq_loc:wq_loc + wk_loc]).astype(BF16), 1)
-        g_proj, g_query, g_out, g_value, g_key = [copy_out(g, c) for g, c in (
-            (g_proj, d_model), (g_query, n_dev * wq_loc), (g_out, d_model), (g_value, n_dev * wk_loc), (g_key, n_dev * wk_loc))]
+        g_proj = sum(dot(d_soft_t[i], normed_pos[i]) for i in range(n_dev)).astype(BF16)
+        g_proj = gather_pair(g_proj)
+
+        g_query = gather_pair(dot_tn(hidden_all, d_qkv[:, :wq_loc]).astype(BF16), 1)
+        g_key = gather_pair(dot_tn(hidden_all, d_qkv[:, wq_loc:wq_loc + wk_loc]).astype(BF16), 1)
+        g_out = 0.0
+        for c in range(HALVES):
+            o_rows = fwd[c][0].transpose(0, 2, 1).reshape(HALF_DEV, 2, BQ, wq_loc)
+            for side, d_part in zip((core, 1 - core), d_proj_all[c]):
+                g_out = g_out + dot_tn(lax.dynamic_index_in_dim(o_rows, side, 1, False).reshape(-1, wq_loc), d_part)
+        g_out = gather_pair(g_out.astype(BF16))
+        core_arr = core.astype(jnp.int32).reshape(1)
+        g_value = merge_cols(core_arr, *g_value)
+        g_key = merge_cols(core_arr, *g_key)
+        g_query = merge_cols(core_arr, *g_query)
+        g_out = merge_rows(core_arr, *g_out, HALF_DEV)
+        g_proj = merge_rows_t(core_arr, *g_proj, HALF_DEV)
         small = lax.psum((g_pn, g_pre, g_q_gain[0], g_k_gain[0], g_post), 'cp')
         g_pn, g_pre, g_q_gain, g_k_gain, g_post = [part.astype(BF16) for part in small]
         return (y_loc, grad_text, grad_vis, g_pn, g_proj, g_pre, g_query, g_key, g_value, g_q_gain, g_k_gain, g_out, g_post)

time: 1450 us -> 1420 us (0.979)
  blocking collectives: 131 us -> 74.7 us
  Pallas kernels: 297 us -> 268 us
  waiting for transfers between devices: 557 us -> 582 us
  matrix products: 316 us -> 339 us
    all_gather x8 -> x2, waiting for transfers between devices: 431 us -> 152 us  [gather(): return lax.all_gather(x, 'cp', axis=axis, tiled=True)]
    all_gather x0 -> x7, waiting for transfers between devices: none -> 166 us  [gather_pair(): lax.all_gather(x, 'cp', axis=axis, tiled=True, axis_index_groups=[list(ra...]
    all_to_all x4 -> x7, waiting for transfers between devices: 125 us -> 221 us  [exchange(): return lax.all_to_all(x, 'cp', split_axis=0, concat_axis=0, tiled=True)]
    all_to_all x2 -> x1, blocking collectives: 108 us -> 51.4 us  [exchange(): return lax.all_to_all(x, 'cp', split_axis=0, concat_axis=0, tiled=True)]
    reduce_scatter x1, waiting for transfers between devices: 0.01 us -> 43.3 us  [device_step(): lax.psum_scatter(d_normed_all, 'cp', scatter_dimension=0, tiled=True)]
    pallas_call x7 -> x9, Pallas kernels: 267 us -> 238 us  [the longest x2 97 us: attn_bwd(): pl.pallas_call(functools.partial(attn_bwd_kernel, hd, part), grid_spec=pl...]
    dot_general x8 -> x0, matrix products: 17.6 us -> none  [device_step(): lax.dot_general(normed_pos[i], d_soft_t[i], (((0,), (1,)), ((), ())), pre...]
    dot_general x3 -> x11, matrix products: 80.8 us -> 97.7 us  [dot(): return jnp.dot(a, b, preferred_element_type=F32)]
  transfers between devices with their start and end apart: 13 -> 24, of which waited for: 9 -> 13; matrix products, arithmetic and copies ran while one was open for 22% -> 25% of each run, Pallas kernels for 13% -> 14%
where the time goes in v3:
time: 1420 us
  waiting for transfers between devices  582 us (41%)
  matrix products  339 us (24%)
  Pallas kernels  268 us (19%)
  blocking collectives  74.7 us (5%)
  local copies, waits for them, and re-layouts  72 us (5%)
  other arithmetic  47.3 us (3%)
  starting transfers between devices  21.4 us (2%)
  between operations  15.1 us (1%)
    all_to_all x7, waiting for transfers between devices, exchange(): return lax.all_to_all(x, 'cp', split_axis=0, concat_axis=0, tiled=True)  221 us
    all_gather x7, waiting for transfers between devices, gather_pair(): lax.all_gather(x, 'cp', axis=axis, tiled=True, axis_index_groups=[list(ra...  166 us
    all_gather x2, waiting for transfers between devices, gather(): return lax.all_gather(x, 'cp', axis=axis, tiled=True)  152 us
    dot_general x10, matrix products, dot_tn(): lax.dot_general(a, b, (((0,), (0,)), ((), ())), preferred_element_type=F32)  125 us
    dot_general x11, matrix products, dot(): return jnp.dot(a, b, preferred_element_type=F32)  97.7 us
    pallas_call x2, Pallas kernels, attn_bwd(): pl.pallas_call(functools.partial(attn_bwd_kernel, hd, part), grid_spec=pl...  97 us
    pallas_call x2, Pallas kernels, attn_fwd(): pl.pallas_call(functools.partial(attn_fwd_kernel, hd, part), grid_spec=pl...  71.8 us
    pallas_call x5, Pallas kernels, merge_call(): pl.pallas_call(body, grid_spec=pltpu.PrefetchScalarGridSpec(num_scalar_pr...  68.9 us
  transfers between devices with their start and end apart: 24, of which 13 were waited for; matrix products, arithmetic and copies ran while one was open for 25% of the time, Pallas kernels for 14%

profile of v3, /device:TPU:0, one launch (start us, length us, event | category | flops | bytes accessed | tf_op | source)
XLA Modules:
  0.0 1419.2 jit_solution(692094681395712331)
XLA Ops:
  7.9 6.8 multiply_reduce_fusion
  17.5 35.6 %all-gather.10.cloned.1.call-done = bf16[2048,1152]{1,0:T(8,128)(2,1)} async-done(((bf16[256,1152]{1,0:T(8,128)(2,1)}), bf16[2048,1152]{1,0:T(8,128)(2,1)}) %all-gather.10.cloned.1.call-update) | async-done | bytes 4718608 | tf_op jit(solution)/shard_map/all_gather | solution.py:400
  53.0 15.6 %fusion.10 = (f32[512]{0:T(512)S(1)}, bf16[512,3584]{1,0:T(8,128)(2,1)}) fusion(bf16[512,3584]{1,0:T(8,128)(2,1)} %param.15, bf16[1152,3584]{1,0:T(8,128)(2,1)} %param.19, bf16[2048,1152]{1,0:T(8,128)(2,1)} %all-gather.10.cloned.1.call-done, s32[512]{0:T(512)S(1)} %broadcast_select_fusion.3, pred[512]{0:T(512)(128)(4,1)S(1)} %fusion.89), kind=kOutput, calls=%fused_computation.20 | convolution fusion | flops 6654590464 | bytes 20320768 | tf_op jit(solution)/shard_map/dot_general | solution.py:38
  69.3 5.1 fusion.7
  77.3 5.0 constant_dynamic-slice_fusion.5
  82.3 4.0 constant_dynamic-slice_fusion.3
  86.3 9.3 multiply_sine_fusion
  95.6 116.3 %all-gather.12.cloned.1.call-done = bf16[4096,3584]{1,0:T(8,128)(2,1)} async-done(((bf16[512,3584]{1,0:T(8,128)(2,1)}), bf16[4096,3584]{1,0:T(8,128)(2,1)}) %all-gather.12.cloned.1.call-update) | async-done | bytes 29360144 | tf_op jit(solution)/shard_map/all_gather | solution.py:400
  211.9 36.9 %convolution_convert_fusion.1.raw_ref.v_ref = bf16[4096,1024]{1,0:T(8,128)(2,1)} fusion(bf16[4096,3584]{1,0:T(8,128)(2,1)} %all-gather.12.cloned.1.call-done, bf16[3584,256]{1,0:T(8,128)(2,1)S(1)} %get-tuple-element.110, bf16[3584,256]{1,0:T(8,128)(2,1)} %get-tuple-element.111, bf16[3584,512]{1,0:T(8,128)(2,1)} %constant_dynamic-slice_fusion.5), kind=kOutput, calls=%fused_computation.16 | convolution fusion | flops 30090985472 | bytes 45088768 | tf_op jit(solution)/shard_map/dot_general | solution.py:38
  248.8 12.3 rope_fwd.1
  264.3 34.5 %attn_fwd.2 = (bf16[8,512,256]{2,1,0:T(8,128)(2,1)}, f32[8,512,256]{2,1,0:T(8,128)S(1)}, f32[8,8,512]{2,1,0:T(8,128)S(1)}) custom-call(s32[16]{0:T(128)S(1)} %fusion.94.nkb_ref, s32[16,1,256]{2,1,0:T(1,128)S(1)} %get-tuple-element.91.lim_ref, bf16[4096,512]{1,0:T(8,128)(2,1)} %get-tuple-element.43.q_ref, bf16[4096,256]{1,0:T(8,128)(2,1)S(1)} %copy-done.3, ...), custom_call_target="tpu_custom_call" | custom-call | flops 9448928256 | bytes 8388608 | tf_op jit(solution)/shard_map/attn_fwd/pallas_call | solution.py:225
  303.3 26.5 %all-to-all-done = bf16[8,512,256]{2,1,0:T(8,128)(2,1)S(1)} async-done(((bf16[8,512,256]{2,1,0:T(8,128)(2,1)}), bf16[8,512,256]{2,1,0:T(8,128)(2,1)S(1)}, u32[]{:S(2)}, u32[]{:S(2)}) %all-to-all-start) | async-done | bytes 2097184 | tf_op jit(solution)/shard_map/all_to_all | solution.py:405
  329.8 13.9 fusion.34
  350.5 37.3 %attn_fwd.3 = (bf16[8,512,256]{2,1,0:T(8,128)(2,1)}, f32[8,512,256]{2,1,0:T(8,128)S(1)}, f32[8,8,512]{2,1,0:T(8,128)S(1)}) custom-call(s32[16]{0:T(128)S(1)} %fusion.94.nkb_ref, s32[16,1,256]{2,1,0:T(1,128)S(1)} %get-tuple-element.91.lim_ref, bf16[4096,512]{1,0:T(8,128)(2,1)} %get-tuple-element.43.q_ref, bf16[4096,256]{1,0:T(8,128)(2,1)S(1)} %copy-done.4, ...), custom_call_target="tpu_custom_call" | custom-call | flops 9448928256 | bytes 8388608 | tf_op jit(solution)/shard_map/attn_fwd/pallas_call | solution.py:225
  392.9 15.3 %fusion.18 = bf16[4096,256]{0,1:T(8,128)(2,1)} fusion(bf16[256,3584]{1,0:T(8,128)(2,1)} %fusion.32, bf16[4096,3584]{1,0:T(8,128)(2,1)} %param.26), kind=kOutput, calls=%fused_computation.49 | convolution fusion | flops 7517241344 | bytes 33292288 | tf_op jit(solution)/shard_map/dot_general | solution.py:42
  408.3 4.1 copy.36
  412.3 29.9 %all-to-all-done.1 = bf16[8,512,256]{2,1,0:T(8,128)(2,1)S(1)} async-done(((bf16[8,512,256]{2,1,0:T(8,128)(2,1)}), bf16[8,512,256]{2,1,0:T(8,128)(2,1)S(1)}, u32[]{:S(2)}, u32[]{:S(2)}) %all-to-all-start.1) | async-done | bytes 2097184 | tf_op jit(solution)/shard_map/all_to_all | solution.py:405
  442.3 13.9 fusion.36
  458.8 4.2 fusion.29
  463.1 3.4 all-to-all-start.2
  466.5 16.0 %fusion.19 = bf16[4096,256]{0,1:T(8,128)(2,1)} fusion(bf16[256,3584]{1,0:T(8,128)(2,1)S(1)} %copy-done.22, bf16[4096,3584]{1,0:T(8,128)(2,1)} %param.26), kind=kOutput, calls=%fused_computation.50 | convolution fusion | flops 7517241344 | bytes 33292288 | tf_op jit(solution)/shard_map/dot_general | solution.py:42
  482.6 4.1 copy.37
  486.7 26.1 %all-to-all-done.2.do_ref = bf16[8,512,256]{2,1,0:T(8,128)(2,1)} async-done(((bf16[8,512,256]{2,1,0:T(8,128)(2,1)}), bf16[8,512,256]{2,1,0:T(8,128)(2,1)}, u32[]{:S(2)}, u32[]{:S(2)}) %all-to-all-start.2) | async-done | bytes 2097184 | tf_op jit(solution)/shard_map/all_to_all | solution.py:405
  515.2 45.7 %attn_bwd.2 = (bf16[2048,512]{1,0:T(8,128)(2,1)}, f32[4096,256]{1,0:T(8,128)}, f32[4096,256]{1,0:T(8,128)}) custom-call(s32[16]{0:T(128)} %copy-done.7, s32[16,1,256]{2,1,0:T(1,128)} %copy-done.2, bf16[4096,512]{1,0:T(8,128)(2,1)} %get-tuple-element.43.q_ref, bf16[4096,256]{1,0:T(8,128)(2,1)} %get-tuple-element.44.k_ref, ...), custom_call_target="tpu_custom_call" | custom-call | flops 23192823808 | bytes 12582912 | tf_op jit(solution)/shard_map/attn_bwd/pallas_call | solution.py:305
  560.9 3.6 all-to-all-done.3.do_ref
  565.8 51.3 %attn_bwd.3 = (bf16[2048,512]{1,0:T(8,128)(2,1)}, bf16[4096,256]{1,0:T(8,128)(2,1)}, bf16[4096,256]{1,0:T(8,128)(2,1)}) custom-call(s32[16]{0:T(128)} %copy-done.7, s32[16,1,256]{2,1,0:T(1,128)} %copy-done.2, bf16[4096,512]{1,0:T(8,128)(2,1)} %get-tuple-element.43.q_ref, bf16[4096,256]{1,0:T(8,128)(2,1)} %get-tuple-element.44.k_ref, ...), custom_call_target="tpu_custom_call" | custom-call | flops 23192823808 | bytes 12582912 | tf_op jit(solution)/shard_map/attn_bwd/pallas_call | solution.py:305
  617.2 17.7 %rope_bwd.1 = (bf16[4096,1024]{1,0:T(8,128)(2,1)}, bf16[8,512,512]{2,1,0:T(8,128)(2,1)}, bf16[8,256,512]{2,1,0:T(8,128)(2,1)}, bf16[8,256,512]{2,1,0:T(8,128)(2,1)}, f32[1,256]{1,0:T(1,128)}, /*index=5*/f32[1,256]{1,0:T(1,128)}) custom-call(bf16[4096,1024]{1,0:T(8,128)(2,1)} %convolution_convert_fusion.1.raw_ref.v_ref, ...), custom_call_target="tpu_custom_call" | custom-call | flops 125829120 | bytes 25165824 | tf_op jit(solution)/shard_map/rope_bwd/pallas_call | solution.py:135
  634.9 23.9 %convolution_convert_fusion.2 = bf16[3584,512]{1,0:T(8,128)(2,1)} fusion(bf16[4096,3584]{1,0:T(8,128)(2,1)} %all-gather.12.cloned.1.call-done, bf16[4096,1024]{1,0:T(8,128)(2,1)} %get-tuple-element.70), kind=kOutput, calls=%fused_computation.38 | convolution fusion | flops 15034220544 | bytes 37224448 | tf_op jit(solution)/shard_map/dot_general | solution.py:46
  663.9 3.1 constant_dynamic-slice_fusion.1
  670.7 10.9 fusion.100
  681.7 6.1 fusion.102
  687.9 9.3 fusion.101
  697.2 11.3 add_convert_fusion
  708.6 16.4 %convolution_convert_fusion.7 = bf16[3584,256]{1,0:T(8,128)(2,1)} fusion(bf16[4096,3584]{1,0:T(8,128)(2,1)} %all-gather.12.cloned.1.call-done, bf16[4096,1024]{1,0:T(8,128)(2,1)} %get-tuple-element.70), kind=kOutput, calls=%fused_computation.45 | convolution fusion | flops 7517110272 | bytes 33292288 | tf_op jit(solution)/shard_map/dot_general | solution.py:46
  725.0 51.4 %all_to_all.40 = bf16[8,256,512]{2,1,0:T(8,128)(2,1)} all-to-all(bf16[8,256,512]{2,1,0:T(8,128)(2,1)S(1)} %copy-done.25), channel_id=1, replica_groups=mesh['dp'=1,'cp'=8] {'cp'}, dimensions={0} | all-to-all | bytes 4194304 | tf_op jit(solution)/shard_map/all_to_all | solution.py:405
  778.8 49.4 %all-to-all-done.5 = bf16[8,256,512]{2,1,0:T(8,128)(2,1)S(1)} async-done(((bf16[8,256,512]{2,1,0:T(8,128)(2,1)}), bf16[8,256,512]{2,1,0:T(8,128)(2,1)S(1)}, u32[]{:S(2)}, u32[]{:S(2)}) %all-to-all-start.5) | async-done | bytes 2097184 | tf_op jit(solution)/shard_map/all_to_all | solution.py:405
  828.2 3.3 all-to-all-start.6
  831.5 14.9 %convolution_convert_fusion.6 = bf16[3584,256]{1,0:T(8,128)(2,1)} fusion(bf16[4096,3584]{1,0:T(8,128)(2,1)} %all-gather.12.cloned.1.call-done, bf16[4096,256]{1,0:T(8,128)(2,1)} %get-tuple-element.62.dv_ref), kind=kOutput, calls=%fused_computation.44 | convolution fusion | flops 7517110272 | bytes 33292288 | tf_op jit(solution)/shard_map/dot_general | solution.py:46
  846.5 13.6 fusion.98
  860.1 41.4 %all-to-all-done.6 = bf16[8,512,512]{2,1,0:T(8,128)(2,1)} async-done(((bf16[8,512,512]{2,1,0:T(8,128)(2,1)}), bf16[8,512,512]{2,1,0:T(8,128)(2,1)}, u32[]{:S(2)}, u32[]{:S(2)}) %all-to-all-start.6) | async-done | bytes 4194336 | tf_op jit(solution)/shard_map/all_to_all | solution.py:405
  901.6 23.9 %fusion.99 = f32[512,3584]{1,0:T(8,128)} fusion(bf16[4096,512]{1,0:T(8,128)(2,1)} %bitcast.12, bf16[3584,4096]{1,0:T(8,128)(2,1)} %param.21), kind=kOutput, calls=%fused_computation.201 | convolution fusion | flops 15032385536 | bytes 40894464 | tf_op jit(solution)/shard_map/dot_general | solution.py:499
  925.5 31.1 %fusion.8 = (f32[3584]{0:T(1024)S(1)}, f32[512]{0:T(512)S(1)}, bf16[512,3584]{1,0:T(8,128)(2,1)}) fusion(bf16[512,3584]{1,0:T(8,128)(2,1)} %get-tuple-element.104, f32[512]{0:T(512)S(1)} %copy-done.36, f32[3584]{0:T(1024)S(1)} %copy-done.29, f32[512,3584]{1,0:T(8,128)} %fusion.99, f32[512,3584]{1,0:T(8,128)} %fusion.98, ...), kind=kOutput, calls=%fused_computation.18 | convolution fusion | flops 7536373760 | bytes 38830080 | tf_op jit(solution)/shard_map/dot_general | solution.py:499
  956.6 8.1 fusion.53
  964.7 6.1 copy.38
  970.7 3.2 all-to-all-start.7
  974.0 27.3 %fusion.2 = bf16[4096,1152]{1,0:T(8,128)(2,1)} fusion(bf16[2048,1152]{1,0:T(8,128)(2,1)} %all-gather.10.cloned.1.call-done, s32[4096]{0:T(1024)S(1)} %broadcast_add_fusion), kind=kOutput, calls=%fused_computation.3 | convolution fusion | flops 19340460032 | bytes 14172160 | tf_op jit(solution)/shard_map/dot_general | solution.py:38
  1001.4 43.6 %all-to-all-done.7 = bf16[8,448,512]{2,1,0:T(8,128)(2,1)} async-done(((bf16[8,448,512]{2,1,0:T(8,128)(2,1)}), bf16[8,448,512]{2,1,0:T(8,128)(2,1)}, u32[]{:S(2)}, u32[]{:S(2)}) %all-to-all-start.7) | async-done | bytes 3670048 | tf_op jit(solution)/shard_map/all_to_all | solution.py:405
  1060.2 3.2 fusion.39
  1063.7 9.4 convolution_convert_fusion.10
  1073.1 4.8 convolution_convert_fusion
  1077.9 41.8 %all-gather.18.cloned.1.call-done.own_ref = bf16[3584,1024]{1,0:T(8,128)(2,1)} async-done(((bf16[3584,256]{1,0:T(8,128)(2,1)}), bf16[3584,1024]{1,0:T(8,128)(2,1)}) %all-gather.18.cloned.1.call-update) | async-done | bytes 7340048 | tf_op jit(solution)/shard_map/all_gather | solution.py:408
  1119.7 74.9 %all-gather.20.cloned.1.call-done.own_ref = bf16[3584,1024]{1,0:T(8,128)(2,1)} async-done(((bf16[3584,256]{1,0:T(8,128)(2,1)}), bf16[3584,1024]{1,0:T(8,128)(2,1)}) %all-gather.20.cloned.1.call-update) | async-done | bytes 7340048 | tf_op jit(solution)/shard_map/all_gather | solution.py:408
  1194.6 48.9 %all-gather.14.cloned.1.call-done.own_ref = bf16[1792,1152]{1,0:T(8,128)(2,1)} async-done(((bf16[448,1152]{1,0:T(8,128)(2,1)}), bf16[1792,1152]{1,0:T(8,128)(2,1)}) %all-gather.14.cloned.1.call-update) | async-done | bytes 4128784 | tf_op jit(solution)/shard_map/all_gather | solution.py:408
  1243.5 3.7 pad_maximum_fusion
  1249.4 43.3 %reduce-scatter.2.cloned.1.call-done = bf16[256,1152]{1,0:T(8,128)(2,1)} async-done(((bf16[2048,1152]{1,0:T(8,128)(2,1)}), bf16[256,1152]{1,0:T(8,128)(2,1)}) %reduce-scatter.2.cloned.1.call-update) | async-done | bytes 589840 | tf_op jit(solution)/shard_map/reduce_scatter | solution.py:508
  1295.6 5.6 broadcast_in_dim.101
  1301.2 15.6 %broadcast_in_dim.102 = bf16[1,4096,1152]{2,1,0:T(8,128)(2,1)} reshape(bf16[16,4,16,4,1152]{4,3,2,1,0:T(4,128)(2,1)} %broadcast_in_dim.101) | data formatting | bytes 18874368 | tf_op jit(solution)/shard_map/broadcast_in_dim | solution.py:511
  1316.8 23.3 %all-reduce = (bf16[1152]{0:T(1024)(128)(2,1)}, bf16[3584]{0:T(1024)(128)(2,1)}, bf16[256]{0:T(256)(128)(2,1)}, bf16[256]{0:T(256)(128)(2,1)}, bf16[3584]{0:T(1024)(128)(2,1)}) all-reduce(f32[1152]{0:T(1024)S(1)} %get-tuple-element.79, f32[3584]{0:T(1024)S(1)} %get-tuple-element.73, ...), channel_id=1, replica_groups=mesh['dp'=1,'cp'=8] {'cp'}, use_global_device_ids=true, to_apply=%region_14.15 | all-reduce | flops 8832 | bytes 52992 | tf_op jit(solution)/shard_map/psum | solution.py:532
  1340.1 3.1 copy-done
  1343.2 10.7 merge.7
  1353.9 10.6 merge.8
  1364.5 6.8 merge.5
  1371.3 21.5 %merge.6 = bf16[3584,4096]{1,0:T(8,128)(2,1)} custom-call(s32[1]{0:T(128)} %bitcast.14.core_ref, bf16[3584,2048]{1,0:T(8,128)(2,1)} %all-gather.16.cloned.1.call-done.own_ref, bf16[3584,2048]{1,0:T(8,128)(2,1)} %collective-permute-done.1.par_ref), custom_call_target="tpu_custom_call" | custom-call | flops 14680064 | bytes 58720256 | tf_op jit(solution)/shard_map/merge/pallas_call | solution.py:362
  1392.7 19.4 %merge.9 = bf16[4096,3584]{1,0:T(8,128)(2,1)} custom-call(s32[1]{0:T(128)} %bitcast.14.core_ref, bf16[2048,3584]{1,0:T(8,128)(2,1)} %all-gather.26.cloned.1.call-done.own_ref, bf16[2048,3584]{1,0:T(8,128)(2,1)} %collective-permute-done.6.par_ref), custom_call_target="tpu_custom_call" | custom-call | flops 14680064 | bytes 58720256 | tf_op jit(solution)/shard_map/merge/pallas_call | solution.py:362
  (209 shorter events, 64.7 us)
Async XLA Ops:
  7.2 45.9 %all-gather.10.cloned.1.call-start = ((), (), s32[]{:S(2)}) async-start(), calls=%async_computation.9 | async-start | bytes 5308416 | tf_op jit(solution)/shard_map/all_gather | solution.py:400
  7.9 7.4 copy-start.30
  7.9 9.3 copy-start.45
  7.9 9.5 copy-start.41
  16.9 195.0 %all-gather.12.cloned.1.call-start = ((), (), s32[]{:S(2)}) async-start(), calls=%async_computation.10 | async-start | bytes 33030144 | tf_op jit(solution)/shard_map/all_gather | solution.py:400
  17.3 51.3 %copy-start.39 = (pred[512]{0:T(512)(128)(4,1)}, pred[512]{0:T(512)(128)(4,1)S(1)}, u32[]{:S(2)}) copy-start(pred[512]{0:T(512)(128)(4,1)S(1)} %fusion.89) | copy-start | bytes 1540
  17.4 51.2 %copy-start.48 = (s32[512]{0:T(512)}, s32[512]{0:T(512)S(1)}, u32[]{:S(2)}) copy-start(s32[512]{0:T(512)S(1)} %broadcast_select_fusion.3) | copy-start | bytes 6148
  17.5 51.2 %copy-start.28 = (f32[3584]{0:T(1024)}, f32[3584]{0:T(1024)S(1)}, u32[]{:S(2)}) copy-start(f32[3584]{0:T(1024)S(1)} %convert_add_fusion.1) | copy-start | bytes 43012
  68.7 5.7 copy-start.43
  77.3 271.6 %copy-start.2 = (s32[16,1,256]{2,1,0:T(1,128)}, s32[16,1,256]{2,1,0:T(1,128)S(1)}, u32[]{:S(2)}) copy-start(s32[16,1,256]{2,1,0:T(1,128)S(1)} %get-tuple-element.91.lim_ref) | copy-start | bytes 49156
  77.3 271.6 %copy-start.7 = (s32[16]{0:T(128)}, s32[16]{0:T(128)S(1)}, u32[]{:S(2)}) copy-start(s32[16]{0:T(128)S(1)} %fusion.94.nkb_ref) | copy-start | bytes 196
  300.8 42.9 %copy-start.10 = (f32[8,8,512]{2,1,0:T(8,128)}, f32[8,8,512]{2,1,0:T(8,128)S(1)}, u32[]{:S(2)}) copy-start(f32[8,8,512]{2,1,0:T(8,128)S(1)} %get-tuple-element.53.lse_ref) | copy-start | bytes 393220
  300.8 29.0 %all-to-all-start = ((bf16[8,512,256]{2,1,0:T(8,128)(2,1)}), bf16[8,512,256]{2,1,0:T(8,128)(2,1)S(1)}, u32[]{:S(2)}, u32[]{:S(2)}) async-start(bf16[8,512,256]{2,1,0:T(8,128)(2,1)} %get-tuple-element.46), calls=%async_computation | async-start | bytes 4194304 | tf_op jit(solution)/shard_map/all_to_all | solution.py:405
  303.3 355.5 %all-gather.22.cloned.1.call-start = ((), (), s32[]{:S(2)}) async-start(), calls=%async_computation.16 | async-start | bytes 9175040 | tf_op jit(solution)/shard_map/all_gather | solution.py:408
  329.8 13.9 copy-start.12
  390.5 51.7 %all-to-all-start.1 = ((bf16[8,512,256]{2,1,0:T(8,128)(2,1)}), bf16[8,512,256]{2,1,0:T(8,128)(2,1)S(1)}, u32[]{:S(2)}, u32[]{:S(2)}) async-start(bf16[8,512,256]{2,1,0:T(8,128)(2,1)} %get-tuple-element.48), calls=%async_computation.1 | async-start | bytes 4194304 | tf_op jit(solution)/shard_map/all_to_all | solution.py:405
  392.9 266.0 %all-gather.24.cloned.1.call-start = ((), (), s32[]{:S(2)}) async-start(), calls=%async_computation.17 | async-start | bytes 9175040 | tf_op jit(solution)/shard_map/all_gather | solution.py:408
  442.3 13.9 copy-start.13
  442.3 16.6 %copy-start.16 = (bf16[256,3584]{1,0:T(8,128)(2,1)S(1)}, bf16[256,3584]{1,0:T(8,128)(2,1)}, u32[]{:S(2)}) copy-start(bf16[256,3584]{1,0:T(8,128)(2,1)} %copy-done.15) | copy-start | bytes 5505028
  463.1 49.7 %all-to-all-start.2 = ((bf16[8,512,256]{2,1,0:T(8,128)(2,1)}), bf16[8,512,256]{2,1,0:T(8,128)(2,1)}, u32[]{:S(2)}, u32[]{:S(2)}) async-start(bf16[8,512,256]{2,1,0:T(8,128)(2,1)} %bitcast.6), calls=%async_computation.2 | async-start | bytes 4194304 | tf_op jit(solution)/shard_map/all_to_all | solution.py:405
  512.8 51.7 %all-to-all-start.3 = ((bf16[8,512,256]{2,1,0:T(8,128)(2,1)}), bf16[8,512,256]{2,1,0:T(8,128)(2,1)S(1)}, u32[]{:S(2)}, u32[]{:S(2)}) async-start(bf16[8,512,256]{2,1,0:T(8,128)(2,1)} %bitcast.9), calls=%async_computation.3 | async-start | bytes 4194304 | tf_op jit(solution)/shard_map/all_to_all | solution.py:405
  515.1 542.4 %all-gather.16.cloned.1.call-start = ((), (), s32[]{:S(2)}) async-start(), calls=%async_computation.13 | async-start | bytes 18350080 | tf_op jit(solution)/shard_map/all_gather | solution.py:408
  658.8 398.8 %all-gather.26.cloned.1.call-start = ((), (), s32[]{:S(2)}) async-start(), calls=%async_computation.18 | async-start | bytes 18350080 | tf_op jit(solution)/shard_map/all_gather | solution.py:408
  658.8 29.0 %collective-permute-start.4 = (bf16[1024,3584]{1,0:T(8,128)(2,1)}, bf16[1024,3584]{1,0:T(8,128)(2,1)}, u32[]{:S(2)}, u32[]{:S(2)}) collective-permute-start(bf16[1024,3584]{1,0:T(8,128)(2,1)} %all-gather.22.cloned.1.call-done), channel_id=1, source_target_pairs={{0,1},{1,0},{2,3},{3,2},{4,5},{5,4},{6,7},{7,6}} | collective-permute-start | bytes 22020104 | tf_op jit(solution)/shard_map/ppermute | solution.py:409
  658.9 38.3 %collective-permute-start.5 = (bf16[1024,3584]{1,0:T(8,128)(2,1)}, bf16[1024,3584]{1,0:T(8,128)(2,1)}, u32[]{:S(2)}, u32[]{:S(2)}) collective-permute-start(bf16[1024,3584]{1,0:T(8,128)(2,1)} %all-gather.24.cloned.1.call-done), channel_id=1, source_target_pairs={{0,1},{1,0},{2,3},{3,2},{4,5},{5,4},{6,7},{7,6}} | collective-permute-start | bytes 22020104 | tf_op jit(solution)/shard_map/ppermute | solution.py:409
  668.3 13.4 slice-start.2
  670.7 11.0 slice-start.3
  670.7 11.0 copy-start.23
  681.7 6.2 copy-start.24
  681.7 15.5 %slice-start.4 = ((s8[7340032]{0:T(1024)(128)(4,1)}), s8[4194304]{0:T(1024)(128)(4,1)S(1)}, s32[]{:S(2)}) async-start(s8[7340032]{0:T(1024)(128)(4,1)} %bitcast.105), calls=%async_computation.23 | async-start | bytes 8388608
  687.9 9.3 slice-start.5
  687.9 9.3 copy-start.27
  708.6 16.5 %copy-start.25 = (bf16[8,256,512]{2,1,0:T(8,128)(2,1)S(1)}, bf16[8,256,512]{2,1,0:T(8,128)(2,1)}, u32[]{:S(2)}) copy-start(bf16[8,256,512]{2,1,0:T(8,128)(2,1)} %get-tuple-element.64) | copy-start | bytes 6291460
  708.6 411.2 %all-gather.18.cloned.1.call-start = ((), (), s32[]{:S(2)}) async-start(), calls=%async_computation.14 | async-start | bytes 9175040 | tf_op jit(solution)/shard_map/all_gather | solution.py:408
  725.0 53.8 %copy-start.34 = (s32[4096]{0:T(1024)S(1)}, s32[4096]{0:T(1024)}, u32[]{:S(2)}) copy-start(s32[4096]{0:T(1024)} %get-tuple-element.81) | copy-start | bytes 49156
  776.4 51.7 %all-to-all-start.5 = ((bf16[8,256,512]{2,1,0:T(8,128)(2,1)}), bf16[8,256,512]{2,1,0:T(8,128)(2,1)S(1)}, u32[]{:S(2)}, u32[]{:S(2)}) async-start(bf16[8,256,512]{2,1,0:T(8,128)(2,1)} %get-tuple-element.66), calls=%async_computation.5 | async-start | bytes 4194304 | tf_op jit(solution)/shard_map/all_to_all | solution.py:405
  828.2 73.4 %all-to-all-start.6 = ((bf16[8,512,512]{2,1,0:T(8,128)(2,1)}), bf16[8,512,512]{2,1,0:T(8,128)(2,1)}, u32[]{:S(2)}, u32[]{:S(2)}) async-start(bf16[8,512,512]{2,1,0:T(8,128)(2,1)} %get-tuple-element.68), calls=%async_computation.6 | async-start | bytes 8388608 | tf_op jit(solution)/shard_map/all_to_all | solution.py:405
  831.5 363.1 %all-gather.20.cloned.1.call-start = ((), (), s32[]{:S(2)}) async-start(), calls=%async_computation.15 | async-start | bytes 9175040 | tf_op jit(solution)/shard_map/all_gather | solution.py:408
  901.6 23.9 %copy-start.29 = (f32[3584]{0:T(1024)S(1)}, f32[3584]{0:T(1024)}, u32[]{:S(2)}) copy-start(f32[3584]{0:T(1024)} %copy-done.28) | copy-start | bytes 43012
  901.6 23.9 %copy-start.36 = (f32[512]{0:T(512)S(1)}, f32[512]{0:T(512)}, u32[]{:S(2)}) copy-start(f32[512]{0:T(512)} %copy-done.35) | copy-start | bytes 6148
  925.5 31.1 %copy-start.44 = (f32[512]{0:T(512)S(1)}, f32[512]{0:T(512)}, u32[]{:S(2)}) copy-start(f32[512]{0:T(512)} %copy-done.43) | copy-start | bytes 6148
  925.5 31.1 %copy-start.40 = (pred[512]{0:T(512)(128)(4,1)S(1)}, pred[512]{0:T(512)(128)(4,1)}, u32[]{:S(2)}) copy-start(pred[512]{0:T(512)(128)(4,1)} %copy-done.39) | copy-start | bytes 1540
  970.7 74.2 %all-to-all-start.7 = ((bf16[8,448,512]{2,1,0:T(8,128)(2,1)}), bf16[8,448,512]{2,1,0:T(8,128)(2,1)}, u32[]{:S(2)}, u32[]{:S(2)}) async-start(bf16[8,448,512]{2,1,0:T(8,128)(2,1)} %bitcast.100), calls=%async_computation.8 | async-start | bytes 7340032 | tf_op jit(solution)/shard_map/all_to_all | solution.py:405
  974.0 269.4 %all-gather.14.cloned.1.call-start = ((), (), s32[]{:S(2)}) async-start(), calls=%async_computation.12 | async-start | bytes 5160960 | tf_op jit(solution)/shard_map/all_gather | solution.py:408
  1045.0 5.1 copy-start.20
  1057.5 313.8 %collective-permute-start.1 = (bf16[3584,2048]{1,0:T(8,128)(2,1)}, bf16[3584,2048]{1,0:T(8,128)(2,1)}, u32[]{:S(2)}, u32[]{:S(2)}) collective-permute-start(bf16[3584,2048]{1,0:T(8,128)(2,1)} %all-gather.16.cloned.1.call-done.own_ref), channel_id=1, source_target_pairs={{0,1},{1,0},{2,3},{3,2},{4,5},{5,4},{6,7},{7,6}} | collective-permute-start | bytes 44040200 | tf_op jit(solution)/shard_map/ppermute | solution.py:409
  1057.6 335.2 %collective-permute-start.6 = (bf16[2048,3584]{1,0:T(8,128)(2,1)}, bf16[2048,3584]{1,0:T(8,128)(2,1)}, u32[]{:S(2)}, u32[]{:S(2)}) collective-permute-start(bf16[2048,3584]{1,0:T(8,128)(2,1)} %all-gather.26.cloned.1.call-done.own_ref), channel_id=1, source_target_pairs={{0,1},{1,0},{2,3},{3,2},{4,5},{5,4},{6,7},{7,6}} | collective-permute-start | bytes 44040200 | tf_op jit(solution)/shard_map/ppermute | solution.py:409
  1063.4 229.3 %reduce-scatter.2.cloned.1.call-start = ((), (), s32[]{:S(2)}) async-start(), calls=%async_computation.11 | async-start | bytes 5308416 | tf_op jit(solution)/shard_map/reduce_scatter | solution.py:508
  1063.7 9.4 copy-start.49
  1077.9 165.5 %copy-start.32 = (f32[3584]{0:T(1024)S(1)}, f32[3584]{0:T(1024)}, u32[]{:S(2)}) copy-start(f32[3584]{0:T(1024)} %get-tuple-element.77) | copy-start | bytes 43012
  1077.9 165.5 %copy-start.33 = (f32[3584]{0:T(1024)S(1)}, f32[3584]{0:T(1024)}, u32[]{:S(2)}) copy-start(f32[3584]{0:T(1024)} %get-tuple-element.75) | copy-start | bytes 43012
  1077.9 165.5 %copy-start.21 = (bf16[256,3584]{1,0:T(8,128)(2,1)S(1)}, bf16[256,3584]{1,0:T(8,128)(2,1)}, u32[]{:S(2)}) copy-start(bf16[256,3584]{1,0:T(8,128)(2,1)} %get-tuple-element.92) | copy-start | bytes 5505028
  1119.7 220.4 %collective-permute-start.2 = (bf16[3584,1024]{1,0:T(8,128)(2,1)}, bf16[3584,1024]{1,0:T(8,128)(2,1)}, u32[]{:S(2)}, u32[]{:S(2)}) collective-permute-start(bf16[3584,1024]{1,0:T(8,128)(2,1)} %all-gather.18.cloned.1.call-done.own_ref), channel_id=1, source_target_pairs={{0,1},{1,0},{2,3},{3,2},{4,5},{5,4},{6,7},{7,6}} | collective-permute-start | bytes 22020104 | tf_op jit(solution)/shard_map/ppermute | solution.py:409
  1194.6 159.3 %collective-permute-start.3 = (bf16[3584,1024]{1,0:T(8,128)(2,1)}, bf16[3584,1024]{1,0:T(8,128)(2,1)}, u32[]{:S(2)}, u32[]{:S(2)}) collective-permute-start(bf16[3584,1024]{1,0:T(8,128)(2,1)} %all-gather.20.cloned.1.call-done.own_ref), channel_id=1, source_target_pairs={{0,1},{1,0},{2,3},{3,2},{4,5},{5,4},{6,7},{7,6}} | collective-permute-start | bytes 22020104 | tf_op jit(solution)/shard_map/ppermute | solution.py:409
  1243.4 121.0 %collective-permute-start = (bf16[1792,1152]{1,0:T(8,128)(2,1)}, bf16[1792,1152]{1,0:T(8,128)(2,1)}, u32[]{:S(2)}, u32[]{:S(2)}) collective-permute-start(bf16[1792,1152]{1,0:T(8,128)(2,1)} %all-gather.14.cloned.1.call-done.own_ref), channel_id=1, source_target_pairs={{0,1},{1,0},{2,3},{3,2},{4,5},{5,4},{6,7},{7,6}} | collective-permute-start | bytes 12386312 | tf_op jit(solution)/shard_map/ppermute | solution.py:409
  1247.2 45.5 %copy-start.19 = (f32[256,1152]{1,0:T(8,128)S(1)}, f32[256,1152]{1,0:T(8,128)}, u32[]{:S(2)}) copy-start(f32[256,1152]{1,0:T(8,128)} %copy-done.18) | copy-start | bytes 3538948
  1247.2 45.5 %copy-start.31 = (f32[1152]{0:T(1024)S(1)}, f32[1152]{0:T(1024)}, u32[]{:S(2)}) copy-start(f32[1152]{0:T(1024)} %copy-done.30) | copy-start | bytes 13828
  1247.2 45.5 %copy-start.38 = (f32[256]{0:T(256)S(1)}, f32[256]{0:T(256)}, u32[]{:S(2)}) copy-start(f32[256]{0:T(256)} %copy-done.37) | copy-start | bytes 3076
  1247.2 46.9 %copy-start.47 = (f32[256]{0:T(256)S(1)}, f32[256]{0:T(256)}, u32[]{:S(2)}) copy-start(f32[256]{0:T(256)} %copy-done.46) | copy-start | bytes 3076
  1301.2 15.6 %copy-start.50 = (f32[1,256]{1,0:T(1,128)S(1)}, f32[1,256]{1,0:T(1,128)}, u32[]{:S(2)}) copy-start(f32[1,256]{1,0:T(1,128)} %get-tuple-element.71) | copy-start | bytes 3076
  1301.2 15.6 %copy-start.51 = (f32[1,256]{1,0:T(1,128)S(1)}, f32[1,256]{1,0:T(1,128)}, u32[]{:S(2)}) copy-start(f32[1,256]{1,0:T(1,128)} %get-tuple-element.72) | copy-start | bytes 3076
  1301.2 52.7 %slice-start = ((s8[7340032]{0:T(1024)(128)(4,1)}), s8[3145728]{0:T(1024)(128)(4,1)S(1)}, s32[]{:S(2)}) async-start(s8[7340032]{0:T(1024)(128)(4,1)} %bitcast.98), calls=%async_computation.19 | async-start | bytes 6291456
  1343.2 10.7 slice-start.1
  1353.8 10.6 copy-start.1
  (20 other events, 36.0 us)
Sparse Core Ops, SparseCore 0:
  17.0 36.0 all-gather.9
  74.5 137.3 all-gather.11
  349.0 94.7 all-gather.21
  463.2 115.3 all-gather.23
  658.9 180.5 all-gather.15
  841.1 193.2 all-gather.25
  1036.8 82.8 all-gather.17
  1121.5 73.0 all-gather.19
  1196.9 46.4 all-gather.13
  1247.2 45.4 reduce-scatter.1

commit v4 on v3

--- a/solution.py
+++ b/solution.py
@@ -146,18 +146,10 @@
 BQ = 256
 KB = 512
 HALVES = 2
-HALF_DEV = 4
 
 
 def stack_heads(blk, hd):
     return jnp.concatenate([blk[:, h * hd:(h + 1) * hd] for h in range(blk.shape[1] // hd)], axis=0)
-
-
-def fold_rows(x, op):
-    out = x[:8]
-    for c in range(1, x.shape[0] // 8):
-        out = op(out, x[c * 8:(c + 1) * 8])
-    return out
 
 
 def wide(blk, hd):
@@ -174,39 +166,27 @@
     n_full = (qb * BQ) // KB
     n_all = nkb_ref[qb]
 
-    def score(kb):
+    def body(masked, kb, stats):
+        m, l = stats
         keys = pl.ds(pl.multiple_of(kb * KB, KB), KB)
-        return dot(k_ref[keys, :], qt), keys
-
-    def full_body(kb, m):
-        s, keys = score(kb)
-        s_ref[keys, :] = s
-        return jnp.maximum(m, fold_rows(s, jnp.maximum))
-
-    def mask_body(kb, m):
-        s, keys = score(kb)
-        key = kb * KB + lax.broadcasted_iota(jnp.int32, s.shape, 0)
-        s = jnp.where(key <= lim2, s, NEG_BIG)
-        s_ref[keys, :] = s
-        return jnp.maximum(m, fold_rows(s, jnp.maximum))
-
-    m = lax.fori_loop(0, n_full, full_body, jnp.full((8, rows), NEG_BIG, F32))
-    m = lax.fori_loop(n_full, n_all, mask_body, m)
-    m = jnp.max(m, axis=0, keepdims=True)
-
-    def exp_body(kb, l):
-        keys = pl.ds(pl.multiple_of(kb * KB, KB), KB)
-        e = jnp.exp2((s_ref[keys, :] - m) * coef)
-        s_ref[keys, :] = e
-        return l + fold_rows(e, jnp.add)
-
-    l = lax.fori_loop(0, n_all, exp_body, jnp.zeros((8, rows), F32))
-    l = jnp.sum(l, axis=0, keepdims=True)
-    inv = 1.0 / l
+        t = dot(k_ref[keys, :], qt) * coef
+        if masked:
+            key = kb * KB + lax.broadcasted_iota(jnp.int32, t.shape, 0)
+            t = jnp.where(key <= lim2, t, NEG_BIG)
+        s_ref[keys, :] = t
+        t = t.reshape(KB // 8, 8, rows)
+        m_new = jnp.maximum(m, jnp.max(t, axis=0))
+        return m_new, l * jnp.exp2(m - m_new) + jnp.sum(jnp.exp2(t - m_new), axis=0)
+
+    stats = (jnp.full((8, rows), NEG_BIG, F32), jnp.zeros((8, rows), F32))
+    stats = lax.fori_loop(0, n_full, functools.partial(body, False), stats)
+    m8, l8 = lax.fori_loop(n_full, n_all, functools.partial(body, True), stats)
+    m = jnp.max(m8, axis=0, keepdims=True)
+    lse = m + jnp.log2(jnp.sum(l8 * jnp.exp2(m8 - m), axis=0, keepdims=True))
 
     def pv_body(kb, acc):
         keys = pl.ds(pl.multiple_of(kb * KB, KB), KB)
-        p = (s_ref[keys, :] * inv).astype(BF16)
+        p = jnp.exp2(s_ref[keys, :] - lse).astype(BF16)
         return acc + dot(vt_ref[:, keys], p)
 
     acc = lax.fori_loop(0, n_all, pv_body, jnp.zeros((hd, rows), F32))
@@ -214,7 +194,7 @@
         part = acc[:, h * BQ:(h + 1) * BQ]
         o32_ref[0, h * hd:(h + 1) * hd, :] = part
         o_ref[0, h * hd:(h + 1) * hd, :] = part.astype(BF16)
-    lse_ref[0] = jnp.broadcast_to(m * coef + jnp.log2(l), (8, rows))
+    lse_ref[0] = jnp.broadcast_to(lse, (8, rows))
 
 
 def attn_fwd(part, nkb, lim, q, k, vt, hd, n_dev):
@@ -275,21 +255,21 @@
             key = kb * KB + lax.broadcasted_iota(jnp.int32, st.shape, 0)
             pt = jnp.where(key <= lim2, pt, 0.0)
         dpt = dot(v_ref[keys, :], dot_)
-        dst = (pt * (dpt - delta) * scale).astype(BF16)
+        dst = (pt * (dpt - delta)).astype(BF16)
         dv_acc[keys, :] += dot(pt.astype(BF16), do2)
         dk_acc[keys, :] += dot(dst, q2)
         return dqt + dot(kt_ref[:, keys], dst)
 
     dqt = lax.fori_loop(0, n_full, functools.partial(body, False), jnp.zeros((hd, rows), F32))
     dqt = lax.fori_loop(n_full, n_all, functools.partial(body, True), dqt)
-    dq = dqt.T.astype(BF16)
+    dq = (dqt * scale).T.astype(BF16)
     for h in range(n_q):
         dq_ref[:, h * hd:(h + 1) * hd] = dq[h * BQ:(h + 1) * BQ]
 
     if last:
         @pl.when(step == pl.num_programs(0) - 1)
         def _():
-            dk_ref[...] = dk_acc[...].astype(BF16)
+            dk_ref[...] = (dk_acc[...] * scale).astype(BF16)
             dv_ref[...] = dv_acc[...].astype(BF16)
 
 
@@ -319,75 +299,51 @@
     )(nkb, lim, q, k, kt, raw, d_o, o32, lse, *carried)
 
 
-def by_core(core_ref, own_ref, par_ref, store):
-    @pl.when(core_ref[0] == 0)
-    def _():
-        store(own_ref, par_ref)
-
-    @pl.when(core_ref[0] != 0)
-    def _():
-        store(par_ref, own_ref)
-
-
-def merge_cols_kernel(core_ref, own_ref, par_ref, o_ref):
-    n = HALF_DEV
-    w = own_ref.shape[1] // n
-
-    def store(even, odd):
-        for j in range(n):
-            o_ref[:, 2 * j * w:(2 * j + 1) * w] = even[:, j * w:(j + 1) * w]
-            o_ref[:, (2 * j + 1) * w:(2 * j + 2) * w] = odd[:, j * w:(j + 1) * w]
-
-    by_core(core_ref, own_ref, par_ref, store)
-
-
-def merge_rows_kernel(core_ref, own_ref, par_ref, o_ref):
-    b = own_ref.shape[0]
-
-    def store(even, odd):
-        o_ref[:b] = even[...]
-        o_ref[b:] = odd[...]
-
-    by_core(core_ref, own_ref, par_ref, store)
-
-
-def merge_rows_t_kernel(core_ref, own_ref, par_ref, o_ref):
-    def store(even, odd):
-        o_ref[...] = jnp.concatenate([even[...], odd[...]], axis=0).T
-
-    by_core(core_ref, own_ref, par_ref, store)
-
-
-def merge_call(body, core, own, par, grid, in_block, in_map, out_shape, out_block, out_map):
+def split_kernel(n_dev, x_ref, *o_refs):
+    width = x_ref.shape[1] // n_dev
+    for g in range(n_dev):
+        col = g * width
+        for o_ref in o_refs:
+            w = o_ref.shape[1] // n_dev
+            o_ref[:, g * w:(g + 1) * w] = x_ref[:, col:col + w]
+            col += w
+
+
+def copy_kernel(x_ref, o_ref):
+    o_ref[...] = x_ref[...]
+
+
+def transpose_kernel(x_ref, o_ref):
+    o_ref[...] = x_ref[...].T
+
+
+def stream(body, x, in_spec, shapes, out_specs, grid):
     return pl.pallas_call(
         body,
-        grid_spec=pltpu.PrefetchScalarGridSpec(
-            num_scalar_prefetch=1, grid=(grid,),
-            in_specs=[pl.BlockSpec(in_block, in_map)] * 2,
-            out_specs=pl.BlockSpec(out_block, out_map)),
-        out_shape=jax.ShapeDtypeStruct(out_shape, own.dtype),
-        cost_estimate=pl.CostEstimate(flops=out_shape[0] * out_shape[1], bytes_accessed=4 * out_shape[0] * out_shape[1], transcendentals=0),
+        grid=(grid,),
+        in_specs=[in_spec],
+        out_specs=out_specs,
+        out_shape=[jax.ShapeDtypeStruct(shape, x.dtype) for shape in shapes],
+        cost_estimate=pl.CostEstimate(flops=x.size, bytes_accessed=4 * x.size, transcendentals=0),
         compiler_params=pltpu.CompilerParams(vmem_limit_bytes=40 * 1024 * 1024),
-        name="merge",
-    )(core, own, par)
-
-
-def merge_cols(core, own, par):
-    rows, cols = own.shape
-    bm = 512
-    return merge_call(merge_cols_kernel, core, own, par, rows // bm, (bm, cols), lambda i, *_: (i, 0), (rows, 2 * cols), (bm, 2 * cols), lambda i, *_: (i, 0))
-
-
-def merge_rows(core, own, par, n):
-    rows, cols = own.shape
-    bm = rows // n
-    return merge_call(merge_rows_kernel, core, own, par, n, (bm, cols), lambda i, *_: (i, 0), (2 * rows, cols), (2 * bm, cols), lambda i, *_: (i, 0))
-
-
-def merge_rows_t(core, own, par, n):
-    rows, cols = own.shape
-    bm = rows // n
-    return merge_call(merge_rows_t_kernel, core, own, par, n, (bm, cols), lambda i, *_: (i, 0), (cols, 2 * rows), (cols, 2 * bm), lambda i, *_: (0, i))
+        name="copy_out",
+    )(x)
+
+
+def split_cols(x, n_dev, widths):
+    bm = 256
+    row = lambda w: pl.BlockSpec((bm, w), lambda i: (i, 0))
+    return stream(functools.partial(split_kernel, n_dev), x, row(x.shape[1]), [(x.shape[0], w) for w in widths], [row(w) for w in widths], x.shape[0] // bm)
+
+
+def copy_rows(x):
+    spec = pl.BlockSpec((512, x.shape[1]), lambda i: (i, 0))
+    return stream(copy_kernel, x, spec, [x.shape], [spec], x.shape[0] // 512)[0]
+
+
+def transpose_rows(x):
+    rows, cols = x.shape
+    return stream(transpose_kernel, x, pl.BlockSpec((512, cols), lambda i: (i, 0)), [(cols, rows)], [pl.BlockSpec((cols, 512), lambda i: (0, i))], rows // 512)[0]
 
 
 def solution(mesh):
@@ -403,10 +359,6 @@
         if after is not None:
             x, _ = lax.optimization_barrier((x, after))
         return lax.all_to_all(x, 'cp', split_axis=0, concat_axis=0, tiled=True)
-
-    def gather_pair(x, axis=0):
-        own = lax.all_gather(x, 'cp', axis=axis, tiled=True, axis_index_groups=[list(range(c, n_dev, 2)) for c in range(2)])
-        return own, lax.ppermute(own, 'cp', [(i, i ^ 1) for i in range(n_dev)])
 
     def device_step(vis_loc, text_loc, img_pos, grad_y, pn_gain, w_proj, pre_gain, w_query, w_key, w_value, q_gain, k_gain, w_out, post_gain):
         rank = lax.axis_index('cp')
@@ -459,12 +411,11 @@
         raw = dot(hidden_all, w_qkv).astype(BF16)
         cos_t, sin_t = rope_tables(seq, hd)
         q, k, kt, vt = rope_fwd(raw, cos_t, sin_t, gq32, gk32, hd, n_q)
-        core = rank % 2
         rows_of = lambda x, c: x[c * BQ:(c + 1) * BQ]
         fwd = []
         for c in range(HALVES):
             fwd.append(attn_fwd(c, n_kb, limit, q, k, vt, hd, n_dev))
-        y_parts, d_o, d_proj_all, g_post = [], [], [], 0.0
+        y_parts, d_o, d_proj_parts, g_post = [], [], [], 0.0
         attn_t = []
         for c in range(HALVES):
             attn_t.append(exchange(fwd[c][0], attn_t[-1] if c else None))
@@ -481,7 +432,8 @@
             g_post = g_post + g_post_part
             prev = exchange(d_attn_t, prev)
             d_o.append(prev)
-            d_proj_all.append(gather_pair(d_proj))
+            d_proj_parts.append(d_proj)
+        d_proj_all = gather(jnp.concatenate(d_proj_parts, axis=0))
         y_loc = jnp.concatenate(y_parts, axis=0)
 
         dq_halves, carried = [], []
@@ -489,15 +441,17 @@
             dq, *carried = attn_bwd(c, n_kb, limit, q, k, kt, raw, d_o[c], fwd[c][1], fwd[c][2], carried, hd, n_dev)
             dq_halves.append(dq)
         dk, dv = carried
-        g_value = gather_pair(dot_tn(hidden_all, dv).astype(BF16), 1)
         d_qkv, dq_t, dk_t, dv_t, g_q_gain, g_k_gain = rope_bwd(raw, dq_halves, dk, dv, cos_t, sin_t, gq32, gk32, hd, n_q, seq_loc)
 
-        dk_seq = exchange(dk_t, prev)
-        dv_seq = exchange(dv_t, dk_seq)
-        dq_seq = exchange(dq_t, dv_seq)
-        dk_seq, dv_seq, dq_last = [x.reshape(-1, seq_loc) for x in (dk_seq, dv_seq, dq_seq)]
+        g_qkv = dot_tn(hidden_all, d_qkv).astype(BF16)
+        g_qkv = gather(g_qkv, 1)
+
+        dq_seq = exchange(dq_t, prev)
+        dk_seq = exchange(dk_t, dq_seq)
+        dv_last = exchange(dv_t, dk_seq)
+        dq_seq, dk_seq, dv_seq = [x.reshape(-1, seq_loc) for x in (dq_seq, dk_seq, dv_last)]
         d_hidden = sum(lax.dot_general(d, w, (((0,), (1,)), ((), ())), preferred_element_type=F32)
-                       for d, w in ((dk_seq, w_key), (dv_seq, w_value), (dq_last, w_query))).astype(BF16)
+                       for d, w in ((dq_seq, w_query), (dk_seq, w_key), (dv_seq, w_value))).astype(BF16)
         d_merged_attn, g_pre = pre_pull(d_hidden)
         d_merged = (grad_y.astype(F32) + d_merged_attn.astype(F32)).astype(BF16)
         grad_text = jnp.where(img_mask, 0.0, d_merged).astype(BF16)
@@ -510,25 +464,17 @@
         spread = (d_pooled.astype(F32) / (POOL * POOL)).astype(BF16).reshape(img_loc, SIDE, 1, SIDE, 1, dim_v)
         grad_vis = jnp.broadcast_to(spread, (img_loc, SIDE, POOL, SIDE, POOL, dim_v)).reshape(img_loc, patches, dim_v)
 
-        d_soft_t = exchange(d_soft_rows.T.reshape(n_dev, d_model // n_dev, seq_loc), dq_seq)
+        d_soft_t = exchange(d_soft_rows.T.reshape(n_dev, d_model // n_dev, seq_loc), dv_last)
         normed_pos = dot(select_all, normed_all).astype(BF16).reshape(n_dev, seq_loc, dim_v)
         g_proj = sum(dot(d_soft_t[i], normed_pos[i]) for i in range(n_dev)).astype(BF16)
-        g_proj = gather_pair(g_proj)
-
-        g_query = gather_pair(dot_tn(hidden_all, d_qkv[:, :wq_loc]).astype(BF16), 1)
-        g_key = gather_pair(dot_tn(hidden_all, d_qkv[:, wq_loc:wq_loc + wk_loc]).astype(BF16), 1)
-        g_out = 0.0
-        for c in range(HALVES):
-            o_rows = fwd[c][0].transpose(0, 2, 1).reshape(HALF_DEV, 2, BQ, wq_loc)
-            for side, d_part in zip((core, 1 - core), d_proj_all[c]):
-                g_out = g_out + dot_tn(lax.dynamic_index_in_dim(o_rows, side, 1, False).reshape(-1, wq_loc), d_part)
-        g_out = gather_pair(g_out.astype(BF16))
-        core_arr = core.astype(jnp.int32).reshape(1)
-        g_value = merge_cols(core_arr, *g_value)
-        g_key = merge_cols(core_arr, *g_key)
-        g_query = merge_cols(core_arr, *g_query)
-        g_out = merge_rows(core_arr, *g_out, HALF_DEV)
-        g_proj = merge_rows_t(core_arr, *g_proj, HALF_DEV)
+        g_proj = gather(g_proj)
+
+        o_rows = jnp.stack([part[0] for part in fwd], axis=1).transpose(0, 1, 3, 2).reshape(seq, wq_loc)
+        g_out = dot_tn(o_rows, d_proj_all).astype(BF16)
+        g_out = gather(g_out)
+        g_query, g_key, g_value = split_cols(g_qkv, n_dev, (n_dev * wq_loc, n_dev * wk_loc, n_dev * wk_loc))
+        g_out = copy_rows(g_out)
+        g_proj = transpose_rows(g_proj)
         small = lax.psum((g_pn, g_pre, g_q_gain[0], g_k_gain[0], g_post), 'cp')
         g_pn, g_pre, g_q_gain, g_k_gain, g_post = [part.astype(BF16) for part in small]
         return (y_loc, grad_text, grad_vis, g_pn, g_proj, g_pre, g_query, g_key, g_value, g_q_gain, g_k_gain, g_out, g_post)

time: 1420 us -> 1330 us (0.937)
  waiting for transfers between devices: 582 us -> 511 us
  matrix products: 339 us -> 296 us
    all_gather x2 -> x6, waiting for transfers between devices: 152 us -> 442 us  [gather(): return lax.all_gather(x, 'cp', axis=axis, tiled=True)]
    all_gather x7 -> x0, waiting for transfers between devices: 166 us -> none  [gather_pair(): lax.all_gather(x, 'cp', axis=axis, tiled=True, axis_index_groups=[list(ra...]
    all_to_all x7, waiting for transfers between devices: 221 us -> 68.6 us  [exchange(): return lax.all_to_all(x, 'cp', split_axis=0, concat_axis=0, tiled=True)]
    reduce_scatter x1, waiting for transfers between devices: 43.3 us -> 0.01 us  [device_step(): lax.psum_scatter(d_normed_all, 'cp', scatter_dimension=0, tiled=True)]
    dot_general x10 -> x5, matrix products: 125 us -> 95.1 us  [dot_tn(): lax.dot_general(a, b, (((0,), (0,)), ((), ())), preferred_element_type=F32)]
    pallas_call x5 -> x3, Pallas kernels: 68.9 us -> 69.5 us  [stream(): pl.pallas_call(body, grid=(grid,), in_specs=[in_spec], out_specs=out_spec...]
  transfers between devices with their start and end apart: 24 -> 14, of which waited for: 13 -> 9; matrix products, arithmetic and copies ran while one was open for 25% -> 22% of each run, Pallas kernels for 14% -> 14%
where the time goes in v4:
time: 1330 us; the launch traced here: 1320 us
  waiting for transfers between devices  511 us (38%)
  matrix products  296 us (22%)
  Pallas kernels  276 us (21%)
  blocking collectives  77.1 us (6%)
  local copies, waits for them, and re-layouts  73 us (5%)
  other arithmetic  53.2 us (4%)
  starting transfers between devices  21.3 us (2%)
  between operations  15.1 us (1%)
    all_gather x6, waiting for transfers between devices, gather(): return lax.all_gather(x, 'cp', axis=axis, tiled=True)  442 us
    pallas_call x2, Pallas kernels, attn_bwd(): pl.pallas_call(functools.partial(attn_bwd_kernel, hd, part), grid_spec=pl...  99.7 us
    dot_general x11, matrix products, dot(): return jnp.dot(a, b, preferred_element_type=F32)  96.9 us
    dot_general x5, matrix products, dot_tn(): lax.dot_general(a, b, (((0,), (0,)), ((), ())), preferred_element_type=F32)  95.1 us
    pallas_call x2, Pallas kernels, attn_fwd(): pl.pallas_call(functools.partial(attn_fwd_kernel, hd, part), grid_spec=pl...  76.6 us
    pallas_call x3, Pallas kernels, stream(): pl.pallas_call(body, grid=(grid,), in_specs=[in_spec], out_specs=out_spec...  69.5 us
    all_to_all x7, waiting for transfers between devices, exchange(): return lax.all_to_all(x, 'cp', split_axis=0, concat_axis=0, tiled=True)  68.6 us
    dot_general x3, matrix products, device_step(): lax.dot_general(d, w, (((0,), (1,)), ((), ())), preferred_element_type=F32)  54.6 us
  transfers between devices with their start and end apart: 14, of which 9 were waited for; matrix products, arithmetic and copies ran while one was open for 22% of the time, Pallas kernels for 14%

profile of v4, /device:TPU:0, one launch (start us, length us, event | category | flops | bytes accessed | tf_op | source)
XLA Modules:
  0.0 1322.6 jit_solution(13935132677020745847)
XLA Ops:
  7.9 6.8 multiply_reduce_fusion
  17.5 35.6 %all-gather.7.cloned.1.call-done = bf16[2048,1152]{1,0:T(8,128)(2,1)} async-done(((bf16[256,1152]{1,0:T(8,128)(2,1)}), bf16[2048,1152]{1,0:T(8,128)(2,1)}) %all-gather.7.cloned.1.call-update) | async-done | bytes 4718608 | tf_op jit(solution)/shard_map/all_gather | solution.py:356
  53.1 15.6 %fusion.10 = (f32[512]{0:T(512)S(1)}, bf16[512,3584]{1,0:T(8,128)(2,1)}) fusion(bf16[512,3584]{1,0:T(8,128)(2,1)} %param.15, bf16[1152,3584]{1,0:T(8,128)(2,1)} %param.19, bf16[2048,1152]{1,0:T(8,128)(2,1)} %all-gather.7.cloned.1.call-done, s32[512]{0:T(512)S(1)} %broadcast_select_fusion.3, pred[512]{0:T(512)(128)(4,1)S(1)} %fusion.87), kind=kOutput, calls=%fused_computation.21 | convolution fusion | flops 6654590464 | bytes 20320768 | tf_op jit(solution)/shard_map/dot_general | solution.py:38
  69.4 5.1 fusion.7
  77.4 5.0 constant_dynamic-slice_fusion.2
  82.5 4.0 constant_dynamic-slice_fusion
  86.4 9.3 multiply_sine_fusion
  95.7 116.3 %all-gather.9.cloned.1.call-done = bf16[4096,3584]{1,0:T(8,128)(2,1)} async-done(((bf16[512,3584]{1,0:T(8,128)(2,1)}), bf16[4096,3584]{1,0:T(8,128)(2,1)}) %all-gather.9.cloned.1.call-update) | async-done | bytes 29360144 | tf_op jit(solution)/shard_map/all_gather | solution.py:356
  212.0 36.9 %convolution_convert_fusion.2.raw_ref.v_ref = bf16[4096,1024]{1,0:T(8,128)(2,1)} fusion(bf16[4096,3584]{1,0:T(8,128)(2,1)} %all-gather.9.cloned.1.call-done, bf16[3584,256]{1,0:T(8,128)(2,1)S(1)} %get-tuple-element.112, bf16[3584,256]{1,0:T(8,128)(2,1)} %get-tuple-element.113, bf16[3584,512]{1,0:T(8,128)(2,1)} %constant_dynamic-slice_fusion.2), kind=kOutput, calls=%fused_computation.17 | convolution fusion | flops 30090985472 | bytes 45088768 | tf_op jit(solution)/shard_map/dot_general | solution.py:38
  248.9 12.3 rope_fwd.1
  264.4 36.6 %attn_fwd.2 = (bf16[8,512,256]{2,1,0:T(8,128)(2,1)}, f32[8,512,256]{2,1,0:T(8,128)S(1)}, f32[8,8,512]{2,1,0:T(8,128)S(1)}) custom-call(s32[16]{0:T(128)S(1)} %fusion.92.nkb_ref, s32[16,1,256]{2,1,0:T(1,128)S(1)} %get-tuple-element.97.lim_ref, bf16[4096,512]{1,0:T(8,128)(2,1)} %get-tuple-element.46.q_ref, bf16[4096,256]{1,0:T(8,128)(2,1)S(1)} %copy-done.2, ...), custom_call_target="tpu_custom_call" | custom-call | flops 9448928256 | bytes 8388608 | tf_op jit(solution)/shard_map/attn_fwd/pallas_call | solution.py:205
  303.6 3.2 all-to-all-start
  308.5 40.0 %attn_fwd.3 = (bf16[8,512,256]{2,1,0:T(8,128)(2,1)}, f32[8,512,256]{2,1,0:T(8,128)S(1)}, f32[8,8,512]{2,1,0:T(8,128)S(1)}) custom-call(s32[16]{0:T(128)S(1)} %fusion.92.nkb_ref, s32[16,1,256]{2,1,0:T(1,128)S(1)} %get-tuple-element.97.lim_ref, bf16[4096,512]{1,0:T(8,128)(2,1)} %get-tuple-element.46.q_ref, bf16[4096,256]{1,0:T(8,128)(2,1)S(1)} %copy-done.3, ...), custom_call_target="tpu_custom_call" | custom-call | flops 9448928256 | bytes 8388608 | tf_op jit(solution)/shard_map/attn_fwd/pallas_call | solution.py:205
  348.5 2.0 copy-done.7
  351.2 14.3 %fusion.33 = (f32[256]{0:T(256)S(1)}, bf16[256,3584]{1,0:T(8,128)(2,1)S(1)}) fusion(bf16[4096,256]{1,0:T(8,128)(2,1)} %bitcast.4, bf16[4096,3584]{1,0:T(8,128)(2,1)} %param.26), kind=kOutput, calls=%fused_computation.69 | convolution fusion | flops 7519862784 | bytes 33293312 | tf_op jit(solution)/shard_map/dot_general | solution.py:46
  365.5 3.1 all-to-all-start.1
  368.7 4.3 fusion.29
  375.4 15.4 %fusion.18 = bf16[4096,256]{0,1:T(8,128)(2,1)} fusion(bf16[256,3584]{1,0:T(8,128)(2,1)S(1)} %fusion.31, bf16[4096,3584]{1,0:T(8,128)(2,1)} %param.26), kind=kOutput, calls=%fused_computation.47 | convolution fusion | flops 7517241344 | bytes 33292288 | tf_op jit(solution)/shard_map/dot_general | solution.py:42
  390.8 4.1 copy.33
  395.3 14.3 %fusion.35 = (f32[256]{0:T(256)S(1)}, bf16[256,3584]{1,0:T(8,128)(2,1)S(1)}) fusion(bf16[4096,256]{1,0:T(8,128)(2,1)} %bitcast.7, bf16[4096,3584]{1,0:T(8,128)(2,1)} %param.26), kind=kOutput, calls=%fused_computation.71 | convolution fusion | flops 7519862784 | bytes 33293312 | tf_op jit(solution)/shard_map/dot_general | solution.py:46
  409.6 2.6 fusion.30
  412.2 3.8 fusion.28
  417.2 2.1 pad_maximum_fusion.1
  419.3 3.4 all-to-all-start.2
  422.8 18.1 %fusion.19 = bf16[4096,256]{0,1:T(8,128)(2,1)} fusion(bf16[256,3584]{1,0:T(8,128)(2,1)S(1)} %copy-done.21, bf16[4096,3584]{1,0:T(8,128)(2,1)} %param.26), kind=kOutput, calls=%fused_computation.48 | convolution fusion | flops 7517241344 | bytes 33292288 | tf_op jit(solution)/shard_map/dot_general | solution.py:42
  440.9 4.1 copy.34
  445.0 22.0 %all-to-all-done.2.do_ref = bf16[8,512,256]{2,1,0:T(8,128)(2,1)} async-done(((bf16[8,512,256]{2,1,0:T(8,128)(2,1)}), bf16[8,512,256]{2,1,0:T(8,128)(2,1)}, u32[]{:S(2)}, u32[]{:S(2)}) %all-to-all-start.2) | async-done | bytes 2097184 | tf_op jit(solution)/shard_map/all_to_all | solution.py:361
  467.0 2.3 all-to-all-start.3
  469.4 47.1 %attn_bwd.2 = (bf16[2048,512]{1,0:T(8,128)(2,1)}, f32[4096,256]{1,0:T(8,128)}, f32[4096,256]{1,0:T(8,128)}) custom-call(s32[16]{0:T(128)} %copy-done.6, s32[16,1,256]{2,1,0:T(1,128)} %copy-done.1, bf16[4096,512]{1,0:T(8,128)(2,1)} %get-tuple-element.46.q_ref, bf16[4096,256]{1,0:T(8,128)(2,1)} %get-tuple-element.47.k_ref, ...), custom_call_target="tpu_custom_call" | custom-call | flops 23192823808 | bytes 12582912 | tf_op jit(solution)/shard_map/attn_bwd/pallas_call | solution.py:285
  517.9 52.6 %attn_bwd.3 = (bf16[2048,512]{1,0:T(8,128)(2,1)}, bf16[4096,256]{1,0:T(8,128)(2,1)}, bf16[4096,256]{1,0:T(8,128)(2,1)}) custom-call(s32[16]{0:T(128)} %copy-done.6, s32[16,1,256]{2,1,0:T(1,128)} %copy-done.1, bf16[4096,512]{1,0:T(8,128)(2,1)} %get-tuple-element.46.q_ref, bf16[4096,256]{1,0:T(8,128)(2,1)} %get-tuple-element.47.k_ref, ...), custom_call_target="tpu_custom_call" | custom-call | flops 23192823808 | bytes 12582912 | tf_op jit(solution)/shard_map/attn_bwd/pallas_call | solution.py:285
  570.5 17.9 %rope_bwd.1 = (bf16[4096,1024]{1,0:T(8,128)(2,1)}, bf16[8,512,512]{2,1,0:T(8,128)(2,1)}, bf16[8,256,512]{2,1,0:T(8,128)(2,1)}, bf16[8,256,512]{2,1,0:T(8,128)(2,1)}, f32[1,256]{1,0:T(1,128)}, /*index=5*/f32[1,256]{1,0:T(1,128)}) custom-call(bf16[4096,1024]{1,0:T(8,128)(2,1)} %convolution_convert_fusion.2.raw_ref.v_ref, ...), custom_call_target="tpu_custom_call" | custom-call | flops 125829120 | bytes 25165824 | tf_op jit(solution)/shard_map/rope_bwd/pallas_call | solution.py:135
  588.4 52.5 %all_to_all.40 = bf16[8,512,512]{2,1,0:T(8,128)(2,1)} all-to-all(bf16[8,512,512]{2,1,0:T(8,128)(2,1)} %get-tuple-element.67), channel_id=1, replica_groups=mesh['dp'=1,'cp'=8] {'cp'}, dimensions={0} | all-to-all | bytes 8388608 | tf_op jit(solution)/shard_map/all_to_all | solution.py:361
  640.9 2.3 all-to-all-start.5
  643.3 23.4 %fusion.96 = f32[512,3584]{1,0:T(8,128)} fusion(bf16[4096,512]{1,0:T(8,128)(2,1)} %bitcast.85, bf16[3584,4096]{1,0:T(8,128)(2,1)} %param.21), kind=kOutput, calls=%fused_computation.194 | convolution fusion | flops 15032385536 | bytes 40894464 | tf_op jit(solution)/shard_map/dot_general | solution.py:453
  666.7 3.1 all-to-all-done.5
  669.8 3.1 all-to-all-start.6
  673.0 13.4 %fusion.97 = f32[512,3584]{1,0:T(8,128)} fusion(bf16[2048,512]{1,0:T(8,128)(2,1)S(1)} %bitcast.88, bf16[3584,2048]{1,0:T(8,128)(2,1)} %param.22), kind=kOutput, calls=%fused_computation.195 | convolution fusion | flops 7516192768 | bytes 24117248 | tf_op jit(solution)/shard_map/dot_general | solution.py:453
  686.4 13.2 all-to-all-done.6
  699.6 17.7 %fusion.8 = (f32[3584]{0:T(1024)S(1)}, f32[512]{0:T(512)S(1)}, bf16[512,3584]{1,0:T(8,128)(2,1)}) fusion(bf16[512,3584]{1,0:T(8,128)(2,1)} %get-tuple-element.106, f32[512]{0:T(512)S(1)} %copy-done.33, f32[3584]{0:T(1024)S(1)} %copy-done.26, bf16[2048,512]{1,0:T(8,128)(2,1)} %bitcast.12, bf16[3584,2048]{1,0:T(8,128)(2,1)} %param.23, ...), kind=kOutput, calls=%fused_computation.19 | convolution fusion | flops 7536373760 | bytes 38830080 | tf_op jit(solution)/shard_map/dot_general | solution.py:453
  717.3 7.4 fusion.51
  724.8 8.9 convolution_convert_fusion.9
  733.6 4.8 convolution_convert_fusion
  739.1 5.9 copy.35
  745.0 3.3 all-to-all-start.7
  748.4 27.4 %fusion.2 = bf16[4096,1152]{1,0:T(8,128)(2,1)} fusion(bf16[2048,1152]{1,0:T(8,128)(2,1)} %all-gather.7.cloned.1.call-done, s32[4096]{0:T(1024)S(1)} %broadcast_add_fusion), kind=kOutput, calls=%fused_computation.3 | convolution fusion | flops 19340460032 | bytes 14172160 | tf_op jit(solution)/shard_map/dot_general | solution.py:38
  775.8 29.9 %all-to-all-done.7 = bf16[8,448,512]{2,1,0:T(8,128)(2,1)} async-done(((bf16[8,448,512]{2,1,0:T(8,128)(2,1)}), bf16[8,448,512]{2,1,0:T(8,128)(2,1)}, u32[]{:S(2)}, u32[]{:S(2)}) %all-to-all-start.7) | async-done | bytes 3670048 | tf_op jit(solution)/shard_map/all_to_all | solution.py:361
  805.7 2.3 fusion.64
  808.0 2.8 convolution_add_fusion.6
  819.9 2.8 fusion.38
  822.8 4.6 maximum_bitcast_fusion
  827.4 6.7 copy.36
  834.1 23.4 %convolution_convert_fusion.3 = bf16[512,3584]{1,0:T(8,128)(2,1)} fusion(bf16[4096,512]{1,0:T(8,128)(2,1)} %bitcast.86, bf16[4096,3584]{1,0:T(8,128)(2,1)} %all-gather.15.cloned.1.call-done), kind=kOutput, calls=%fused_computation.38 | convolution fusion | flops 15034220544 | bytes 37224448 | tf_op jit(solution)/shard_map/dot_general | solution.py:46
  857.5 38.5 %convolution_convert_fusion.1 = bf16[3584,1024]{1,0:T(8,128)(2,1)} fusion(bf16[4096,3584]{1,0:T(8,128)(2,1)} %all-gather.9.cloned.1.call-done, bf16[4096,1024]{1,0:T(8,128)(2,1)} %get-tuple-element.73), kind=kOutput, calls=%fused_computation.16 | convolution fusion | flops 30068441088 | bytes 45088768 | tf_op jit(solution)/shard_map/dot_general | solution.py:46
  897.5 3.7 pad_maximum_fusion
  901.2 2.1 broadcast_select_fusion.1
  906.3 5.6 broadcast_in_dim.101
  911.9 15.6 %broadcast_in_dim.102 = bf16[1,4096,1152]{2,1,0:T(8,128)(2,1)} reshape(bf16[16,4,16,4,1152]{4,3,2,1,0:T(4,128)(2,1)} %broadcast_in_dim.101) | data formatting | bytes 18874368 | tf_op jit(solution)/shard_map/broadcast_in_dim | solution.py:465
  927.5 24.6 %all-reduce = (bf16[1152]{0:T(1024)(128)(2,1)}, bf16[3584]{0:T(1024)(128)(2,1)}, bf16[256]{0:T(256)(128)(2,1)}, bf16[256]{0:T(256)(128)(2,1)}, bf16[3584]{0:T(1024)(128)(2,1)}) all-reduce(f32[1152]{0:T(1024)S(1)} %get-tuple-element.85, f32[3584]{0:T(1024)S(1)} %get-tuple-element.79, ...), channel_id=1, replica_groups=mesh['dp'=1,'cp'=8] {'cp'}, use_global_device_ids=true, to_apply=%region_14.15 | all-reduce | flops 8832 | bytes 52992 | tf_op jit(solution)/shard_map/psum | solution.py:478
  952.1 3.3 copy-done
  955.4 5.5 copy_out.3
  960.9 50.4 %all-gather.17.cloned.1.call-done.x_ref = bf16[4096,3584]{1,0:T(8,128)(2,1)} async-done(((bf16[512,3584]{1,0:T(8,128)(2,1)}), bf16[4096,3584]{1,0:T(8,128)(2,1)}) %all-gather.17.cloned.1.call-update) | async-done | bytes 29360144 | tf_op jit(solution)/shard_map/all_gather | solution.py:356
  1011.3 24.2 %copy_out.5 = bf16[4096,3584]{1,0:T(8,128)(2,1)} custom-call(bf16[4096,3584]{1,0:T(8,128)(2,1)} %all-gather.17.cloned.1.call-done.x_ref), custom_call_target="tpu_custom_call" | custom-call | flops 14680064 | bytes 58720256 | tf_op jit(solution)/shard_map/copy_out/pallas_call | solution.py:321
  1035.5 240.0 %all-gather.13.cloned.1.call-done.x_ref = bf16[3584,8192]{1,0:T(8,128)(2,1)} async-done(((bf16[3584,1024]{1,0:T(8,128)(2,1)}), bf16[3584,8192]{1,0:T(8,128)(2,1)}) %all-gather.13.cloned.1.call-update) | async-done | bytes 58720272 | tf_op jit(solution)/shard_map/all_gather | solution.py:356
  1275.4 39.8 %copy_out.4 = (bf16[3584,4096]{1,0:T(8,128)(2,1)}, bf16[3584,2048]{1,0:T(8,128)(2,1)}, bf16[3584,2048]{1,0:T(8,128)(2,1)}) custom-call(bf16[3584,8192]{1,0:T(8,128)(2,1)} %all-gather.13.cloned.1.call-done.x_ref), custom_call_target="tpu_custom_call" | custom-call | flops 29360128 | bytes 117440512 | tf_op jit(solution)/shard_map/copy_out/pallas_call | solution.py:321
  (155 shorter events, 34.9 us)
Async XLA Ops:
  7.2 46.0 %all-gather.7.cloned.1.call-start = ((), (), s32[]{:S(2)}) async-start(), calls=%async_computation.9 | async-start | bytes 5308416 | tf_op jit(solution)/shard_map/all_gather | solution.py:356
  7.9 7.4 copy-start.27
  7.9 9.3 copy-start.42
  7.9 9.5 copy-start.38
  14.8 0.6 copy-start.43
  14.8 1.0 copy-start.16
  15.4 0.6 copy-start.34
  17.0 195.1 %all-gather.9.cloned.1.call-start = ((), (), s32[]{:S(2)}) async-start(), calls=%async_computation.10 | async-start | bytes 33030144 | tf_op jit(solution)/shard_map/all_gather | solution.py:356
  17.4 51.4 %copy-start.36 = (pred[512]{0:T(512)(128)(4,1)}, pred[512]{0:T(512)(128)(4,1)S(1)}, u32[]{:S(2)}) copy-start(pred[512]{0:T(512)(128)(4,1)S(1)} %fusion.87) | copy-start | bytes 1540
  17.5 51.3 %copy-start.45 = (s32[512]{0:T(512)}, s32[512]{0:T(512)S(1)}, u32[]{:S(2)}) copy-start(s32[512]{0:T(512)S(1)} %broadcast_select_fusion.3) | copy-start | bytes 6148
  17.5 51.3 %copy-start.25 = (f32[3584]{0:T(1024)}, f32[3584]{0:T(1024)S(1)}, u32[]{:S(2)}) copy-start(f32[3584]{0:T(1024)S(1)} %convert_add_fusion.1) | copy-start | bytes 43012
  68.8 5.7 copy-start.40
  74.5 0.7 copy-start.49
  74.5 1.2 copy-start.50
  77.4 229.5 %copy-start.1 = (s32[16,1,256]{2,1,0:T(1,128)}, s32[16,1,256]{2,1,0:T(1,128)S(1)}, u32[]{:S(2)}) copy-start(s32[16,1,256]{2,1,0:T(1,128)S(1)} %get-tuple-element.97.lim_ref) | copy-start | bytes 49156
  77.4 229.5 %copy-start.6 = (s32[16]{0:T(128)}, s32[16]{0:T(128)S(1)}, u32[]{:S(2)}) copy-start(s32[16]{0:T(128)S(1)} %fusion.92.nkb_ref) | copy-start | bytes 196
  261.2 1.6 copy-start.2
  262.8 1.6 copy-start.4
  301.0 2.0 copy-start.8
  303.0 0.6 copy-start.10
  303.6 3.3 copy-start.39
  303.6 3.3 copy-start.3
  303.6 47.6 %all-to-all-start = ((bf16[8,512,256]{2,1,0:T(8,128)(2,1)}), bf16[8,512,256]{2,1,0:T(8,128)(2,1)}, u32[]{:S(2)}, u32[]{:S(2)}) async-start(bf16[8,512,256]{2,1,0:T(8,128)(2,1)} %get-tuple-element.49), calls=%async_computation | async-start | bytes 4194304 | tf_op jit(solution)/shard_map/all_to_all | solution.py:361
  306.9 1.6 copy-start.5
  348.5 2.0 copy-start.7
  350.5 0.7 copy-start.9
  365.5 29.8 %all-to-all-start.1 = ((bf16[8,512,256]{2,1,0:T(8,128)(2,1)}), bf16[8,512,256]{2,1,0:T(8,128)(2,1)}, u32[]{:S(2)}, u32[]{:S(2)}) async-start(bf16[8,512,256]{2,1,0:T(8,128)(2,1)} %get-tuple-element.51), calls=%async_computation.1 | async-start | bytes 4194304 | tf_op jit(solution)/shard_map/all_to_all | solution.py:361
  368.6 465.4 %all-gather.15.cloned.1.call-start = ((), (), s32[]{:S(2)}) async-start(), calls=%async_computation.14 | async-start | bytes 33030144 | tf_op jit(solution)/shard_map/all_gather | solution.py:356
  368.7 4.3 copy-start.11
  374.1 1.3 copy-start.22
  395.3 14.3 %copy-start.12 = (bf16[512,3584]{1,0:T(8,128)(2,1)S(1)}, bf16[512,3584]{1,0:T(8,128)(2,1)}, u32[]{:S(2)}) copy-start(bf16[512,3584]{1,0:T(8,128)(2,1)} %param.17) | copy-start | bytes 11010052
  409.6 2.7 copy-start.13
  412.2 5.0 copy-start.23
  416.0 1.2 copy-start.20
  419.3 3.5 copy-start.21
  419.3 47.7 %all-to-all-start.2 = ((bf16[8,512,256]{2,1,0:T(8,128)(2,1)}), bf16[8,512,256]{2,1,0:T(8,128)(2,1)}, u32[]{:S(2)}, u32[]{:S(2)}) async-start(bf16[8,512,256]{2,1,0:T(8,128)(2,1)} %bitcast.6), calls=%async_computation.2 | async-start | bytes 4194304 | tf_op jit(solution)/shard_map/all_to_all | solution.py:361
  467.0 49.5 %all-to-all-start.3 = ((bf16[8,512,256]{2,1,0:T(8,128)(2,1)}), bf16[8,512,256]{2,1,0:T(8,128)(2,1)S(1)}, u32[]{:S(2)}, u32[]{:S(2)}) async-start(bf16[8,512,256]{2,1,0:T(8,128)(2,1)} %bitcast.9), calls=%async_computation.3 | async-start | bytes 4194304 | tf_op jit(solution)/shard_map/all_to_all | solution.py:361
  516.5 1.4 copy-start.24
  640.9 28.9 %all-to-all-start.5 = ((bf16[8,256,512]{2,1,0:T(8,128)(2,1)}), bf16[8,256,512]{2,1,0:T(8,128)(2,1)S(1)}, u32[]{:S(2)}, u32[]{:S(2)}) async-start(bf16[8,256,512]{2,1,0:T(8,128)(2,1)} %get-tuple-element.69), calls=%async_computation.5 | async-start | bytes 4194304 | tf_op jit(solution)/shard_map/all_to_all | solution.py:361
  669.8 29.7 %all-to-all-start.6 = ((bf16[8,256,512]{2,1,0:T(8,128)(2,1)}), bf16[8,256,512]{2,1,0:T(8,128)(2,1)}, u32[]{:S(2)}, u32[]{:S(2)}) async-start(bf16[8,256,512]{2,1,0:T(8,128)(2,1)} %get-tuple-element.71), calls=%async_computation.6 | async-start | bytes 4194304 | tf_op jit(solution)/shard_map/all_to_all | solution.py:361
  672.9 230.4 %reduce-scatter.2.cloned.1.call-start = ((), (), s32[]{:S(2)}) async-start(), calls=%async_computation.11 | async-start | bytes 5308416 | tf_op jit(solution)/shard_map/reduce_scatter | solution.py:462
  673.0 26.6 %copy-start.26 = (f32[3584]{0:T(1024)S(1)}, f32[3584]{0:T(1024)}, u32[]{:S(2)}) copy-start(f32[3584]{0:T(1024)} %copy-done.25) | copy-start | bytes 43012
  673.0 26.6 %copy-start.33 = (f32[512]{0:T(512)S(1)}, f32[512]{0:T(512)}, u32[]{:S(2)}) copy-start(f32[512]{0:T(512)} %copy-done.32) | copy-start | bytes 6148
  699.6 17.8 %copy-start.41 = (f32[512]{0:T(512)S(1)}, f32[512]{0:T(512)}, u32[]{:S(2)}) copy-start(f32[512]{0:T(512)} %copy-done.40) | copy-start | bytes 6148
  699.6 17.8 %copy-start.37 = (pred[512]{0:T(512)(128)(4,1)S(1)}, pred[512]{0:T(512)(128)(4,1)}, u32[]{:S(2)}) copy-start(pred[512]{0:T(512)(128)(4,1)} %copy-done.36) | copy-start | bytes 1540
  724.8 8.9 copy-start.14
  724.8 8.9 copy-start.46
  738.4 0.7 copy-start.31
  745.0 60.7 %all-to-all-start.7 = ((bf16[8,448,512]{2,1,0:T(8,128)(2,1)}), bf16[8,448,512]{2,1,0:T(8,128)(2,1)}, u32[]{:S(2)}, u32[]{:S(2)}) async-start(bf16[8,448,512]{2,1,0:T(8,128)(2,1)} %bitcast.84), calls=%async_computation.8 | async-start | bytes 7340032 | tf_op jit(solution)/shard_map/all_to_all | solution.py:361
  748.3 203.8 %all-gather.11.cloned.1.call-start = ((), (), s32[]{:S(2)}) async-start(), calls=%async_computation.12 | async-start | bytes 9289728 | tf_op jit(solution)/shard_map/all_gather | solution.py:356
  805.7 5.2 copy-start.18
  822.7 188.6 %all-gather.17.cloned.1.call-start = ((), (), s32[]{:S(2)}) async-start(), calls=%async_computation.15 | async-start | bytes 33030144 | tf_op jit(solution)/shard_map/all_gather | solution.py:356
  857.4 418.0 %all-gather.13.cloned.1.call-start = ((), (), s32[]{:S(2)}) async-start(), calls=%async_computation.13 | async-start | bytes 66060288 | tf_op jit(solution)/shard_map/all_gather | solution.py:356
  896.0 0.7 copy-start.29
  896.0 0.7 copy-start.30
  896.0 1.5 copy-start.19
  897.5 3.7 copy-start.15
  901.2 2.2 copy-start.17
  901.2 2.2 copy-start.28
  901.2 2.2 copy-start.35
  901.2 3.6 copy-start.44
  911.9 15.6 %copy-start.47 = (f32[1,256]{1,0:T(1,128)S(1)}, f32[1,256]{1,0:T(1,128)}, u32[]{:S(2)}) copy-start(f32[1,256]{1,0:T(1,128)} %get-tuple-element.77) | copy-start | bytes 3076
  911.9 15.6 %copy-start.48 = (f32[1,256]{1,0:T(1,128)S(1)}, f32[1,256]{1,0:T(1,128)}, u32[]{:S(2)}) copy-start(f32[1,256]{1,0:T(1,128)} %get-tuple-element.78) | copy-start | bytes 3076
  952.1 3.3 copy-start
  (1 other events, 0.6 us)
Sparse Core Ops, SparseCore 0:
  17.1 36.0 all-gather.6
  74.6 137.3 all-gather.8
  419.4 177.4 all-gather.14
  738.5 73.2 reduce-scatter.1
  822.8 47.3 all-gather.10
  872.5 138.7 all-gather.16
  1013.7 261.6 all-gather.12

commit v5 on v4

--- a/solution.py
+++ b/solution.py
@@ -156,7 +156,7 @@
     return jnp.concatenate([blk[h * hd:(h + 1) * hd] for h in range(blk.shape[0] // hd)], axis=1)
 
 
-def attn_fwd_kernel(hd, part, nkb_ref, lim_ref, q_ref, k_ref, vt_ref, o_ref, o32_ref, lse_ref, s_ref):
+def attn_fwd_kernel(hd, part, nkb_ref, lim_ref, q_ref, k_ref, vt_ref, o_ref, o32_ref, lse_ref, s_ref, p_ref):
     qb = HALVES * pl.program_id(0) + part
     coef = hd ** -0.5 * LOG2E
     n_q = q_ref.shape[1] // hd
@@ -166,30 +166,47 @@
     n_full = (qb * BQ) // KB
     n_all = nkb_ref[qb]
 
+    @pl.when(pl.program_id(0) == 0)
+    def _():
+        s_ref[:KB, :] = jnp.full((KB, rows), NEG_BIG, F32)
+
+    def add_sum(m_prev, m, l, t):
+        return l * jnp.exp2(m_prev - m) + jnp.sum(jnp.exp2(t.reshape(KB // 8, 8, rows) - m), axis=0)
+
     def body(masked, kb, stats):
-        m, l = stats
-        keys = pl.ds(pl.multiple_of(kb * KB, KB), KB)
-        t = dot(k_ref[keys, :], qt) * coef
+        m_prev, m, l = stats
+        pair = s_ref.at[pl.ds(pl.multiple_of(kb * KB, KB), 2 * KB)]
+        l = add_sum(m_prev, m, l, pair[:KB])
+        t = dot(k_ref[pl.ds(pl.multiple_of(kb * KB, KB), KB), :], qt) * coef
         if masked:
             key = kb * KB + lax.broadcasted_iota(jnp.int32, t.shape, 0)
             t = jnp.where(key <= lim2, t, NEG_BIG)
-        s_ref[keys, :] = t
-        t = t.reshape(KB // 8, 8, rows)
-        m_new = jnp.maximum(m, jnp.max(t, axis=0))
-        return m_new, l * jnp.exp2(m - m_new) + jnp.sum(jnp.exp2(t - m_new), axis=0)
-
-    stats = (jnp.full((8, rows), NEG_BIG, F32), jnp.zeros((8, rows), F32))
-    stats = lax.fori_loop(0, n_full, functools.partial(body, False), stats)
-    m8, l8 = lax.fori_loop(n_full, n_all, functools.partial(body, True), stats)
+        pair[KB:] = t
+        return m, jnp.maximum(m, jnp.max(t.reshape(KB // 8, 8, rows), axis=0)), l
+
+    low = s_ref[:8, :]
+    stats = lax.fori_loop(0, n_full, functools.partial(body, False), (low, low, jnp.zeros((8, rows), F32)))
+    m_prev, m8, l8 = lax.fori_loop(n_full, n_all, functools.partial(body, True), stats)
+    l8 = add_sum(m_prev, m8, l8, s_ref[pl.ds(pl.multiple_of(n_all * KB, KB), KB), :])
     m = jnp.max(m8, axis=0, keepdims=True)
     lse = m + jnp.log2(jnp.sum(l8 * jnp.exp2(m8 - m), axis=0, keepdims=True))
 
+    def prob(kb):
+        return jnp.exp2(s_ref[pl.ds(pl.multiple_of((kb + 1) * KB, KB), KB), :] - lse).astype(BF16)
+
+    def pv(kb, p):
+        return dot(vt_ref[:, pl.ds(pl.multiple_of(kb * KB, KB), KB)], p)
+
+    p_ref[:KB] = prob(0)
+
     def pv_body(kb, acc):
-        keys = pl.ds(pl.multiple_of(kb * KB, KB), KB)
-        p = jnp.exp2(s_ref[keys, :] - lse).astype(BF16)
-        return acc + dot(vt_ref[:, keys], p)
-
-    acc = lax.fori_loop(0, n_all, pv_body, jnp.zeros((hd, rows), F32))
+        pair = p_ref.at[pl.ds(pl.multiple_of((kb - 1) * KB, KB), 2 * KB)]
+        acc = acc + pv(kb - 1, pair[:KB])
+        pair[KB:] = prob(kb)
+        return acc
+
+    acc = lax.fori_loop(1, n_all, pv_body, jnp.zeros((hd, rows), F32))
+    acc = acc + pv(n_all - 1, p_ref[pl.ds(pl.multiple_of((n_all - 1) * KB, KB), KB), :])
     for h in range(n_q):
         part = acc[:, h * BQ:(h + 1) * BQ]
         o32_ref[0, h * hd:(h + 1) * hd, :] = part
@@ -210,7 +227,7 @@
             in_specs=[pl.BlockSpec((1, 1, BQ), lambda i, *_: (at(i), 0, 0)), pl.BlockSpec((BQ, width), lambda i, *_: (at(i), 0)),
                       pl.BlockSpec((seq, hd), lambda i, *_: (0, 0)), pl.BlockSpec((hd, seq), lambda i, *_: (0, 0))],
             out_specs=[tall, tall, pl.BlockSpec((1, 8, n_q * BQ), lambda i, *_: (i, 0, 0))],
-            scratch_shapes=[pltpu.VMEM((seq, n_q * BQ), F32)]),
+            scratch_shapes=[pltpu.VMEM((seq + KB, n_q * BQ), F32), pltpu.VMEM((seq, n_q * BQ), BF16)]),
         out_shape=[jax.ShapeDtypeStruct((n_dev, width, BQ), BF16), jax.ShapeDtypeStruct((n_dev, width, BQ), F32),
                    jax.ShapeDtypeStruct((n_dev, 8, n_q * BQ), F32)],
         cost_estimate=pl.CostEstimate(flops=int(1.1 * seq * seq * width), bytes_accessed=4 * seq * width, transcendentals=seq * seq),
@@ -432,8 +449,7 @@
             g_post = g_post + g_post_part
             prev = exchange(d_attn_t, prev)
             d_o.append(prev)
-            d_proj_parts.append(d_proj)
-        d_proj_all = gather(jnp.concatenate(d_proj_parts, axis=0))
+            d_proj_parts.append(gather(d_proj))
         y_loc = jnp.concatenate(y_parts, axis=0)
 
         dq_halves, carried = [], []
@@ -469,8 +485,7 @@
         g_proj = sum(dot(d_soft_t[i], normed_pos[i]) for i in range(n_dev)).astype(BF16)
         g_proj = gather(g_proj)
 
-        o_rows = jnp.stack([part[0] for part in fwd], axis=1).transpose(0, 1, 3, 2).reshape(seq, wq_loc)
-        g_out = dot_tn(o_rows, d_proj_all).astype(BF16)
+        g_out = sum(dot_tn(fwd[c][0].transpose(0, 2, 1).reshape(-1, wq_loc), d_proj_parts[c]) for c in range(HALVES)).astype(BF16)
         g_out = gather(g_out)
         g_query, g_key, g_value = split_cols(g_qkv, n_dev, (n_dev * wq_loc, n_dev * wk_loc, n_dev * wk_loc))
         g_out = copy_rows(g_out)

time: 1330 us -> 1380 us (1.038)
  waiting for transfers between devices: 511 us -> 572 us
    all_to_all x7, waiting for transfers between devices: 68.6 us -> 132 us  [exchange(): return lax.all_to_all(x, 'cp', split_axis=0, concat_axis=0, tiled=True)]
    dot_general x5 -> x6, matrix products: 95.1 us -> 101 us  [dot_tn(): lax.dot_general(a, b, (((0,), (0,)), ((), ())), preferred_element_type=F32)]
    all_gather x6 -> x7, waiting for transfers between devices: 442 us -> 439 us  [gather(): return lax.all_gather(x, 'cp', axis=axis, tiled=True)]
  transfers between devices with their start and end apart: 14 -> 15, of which waited for: 9 -> 11; matrix products, arithmetic and copies ran while one was open for 22% -> 23% of each run, Pallas kernels for 14% -> 13%
where the time goes in v5:
time: 1380 us; the launch traced here: 1370 us
  waiting for transfers between devices  572 us (41%)
  matrix products  300 us (22%)
  Pallas kernels  271 us (20%)
  blocking collectives  76.8 us (6%)
  local copies, waits for them, and re-layouts  70.3 us (5%)
  other arithmetic  46.7 us (3%)
  starting transfers between devices  19.8 us (1%)
  between operations  15 us (1%)
    all_gather x7, waiting for transfers between devices, gather(): return lax.all_gather(x, 'cp', axis=axis, tiled=True)  439 us
    all_to_all x7, waiting for transfers between devices, exchange(): return lax.all_to_all(x, 'cp', split_axis=0, concat_axis=0, tiled=True)  132 us
    dot_general x6, matrix products, dot_tn(): lax.dot_general(a, b, (((0,), (0,)), ((), ())), preferred_element_type=F32)  101 us
    pallas_call x2, Pallas kernels, attn_bwd(): pl.pallas_call(functools.partial(attn_bwd_kernel, hd, part), grid_spec=pl...  97.5 us
    dot_general x11, matrix products, dot(): return jnp.dot(a, b, preferred_element_type=F32)  97 us
    pallas_call x2, Pallas kernels, attn_fwd(): pl.pallas_call(functools.partial(attn_fwd_kernel, hd, part), grid_spec=pl...  73.7 us
    pallas_call x3, Pallas kernels, stream(): pl.pallas_call(body, grid=(grid,), in_specs=[in_spec], out_specs=out_spec...  69.5 us
    dot_general x3, matrix products, device_step(): lax.dot_general(d, w, (((0,), (1,)), ((), ())), preferred_element_type=F32)  54.5 us
  transfers between devices with their start and end apart: 15, of which 11 were waited for; matrix products, arithmetic and copies ran while one was open for 23% of the time, Pallas kernels for 13%

profile of v5, /device:TPU:0, one launch (start us, length us, event | category | flops | bytes accessed | tf_op | source)
XLA Modules:
  0.0 1370.8 jit_solution(14936653511513550588)
XLA Ops:
  7.9 6.8 multiply_reduce_fusion
  17.4 35.7 %all-gather.8.cloned.1.call-done = bf16[2048,1152]{1,0:T(8,128)(2,1)} async-done(((bf16[256,1152]{1,0:T(8,128)(2,1)}), bf16[2048,1152]{1,0:T(8,128)(2,1)}) %all-gather.8.cloned.1.call-update) | async-done | bytes 4718608 | tf_op jit(solution)/shard_map/all_gather | solution.py:373
  53.1 15.6 %fusion.10 = (f32[512]{0:T(512)S(1)}, bf16[512,3584]{1,0:T(8,128)(2,1)}) fusion(bf16[512,3584]{1,0:T(8,128)(2,1)} %param.15, bf16[1152,3584]{1,0:T(8,128)(2,1)} %param.19, bf16[2048,1152]{1,0:T(8,128)(2,1)} %all-gather.8.cloned.1.call-done, s32[512]{0:T(512)S(1)} %broadcast_select_fusion.3, pred[512]{0:T(512)(128)(4,1)S(1)} %fusion.87), kind=kOutput, calls=%fused_computation.21 | convolution fusion | flops 6654590464 | bytes 20320768 | tf_op jit(solution)/shard_map/dot_general | solution.py:38
  69.3 5.1 fusion.7
  77.5 5.0 constant_dynamic-slice_fusion.2
  82.5 4.0 constant_dynamic-slice_fusion
  86.4 9.3 multiply_sine_fusion
  95.7 116.3 %all-gather.10.cloned.1.call-done = bf16[4096,3584]{1,0:T(8,128)(2,1)} async-done(((bf16[512,3584]{1,0:T(8,128)(2,1)}), bf16[4096,3584]{1,0:T(8,128)(2,1)}) %all-gather.10.cloned.1.call-update) | async-done | bytes 29360144 | tf_op jit(solution)/shard_map/all_gather | solution.py:373
  212.0 36.9 %convolution_convert_fusion.2.raw_ref.v_ref = bf16[4096,1024]{1,0:T(8,128)(2,1)} fusion(bf16[4096,3584]{1,0:T(8,128)(2,1)} %all-gather.10.cloned.1.call-done, bf16[3584,256]{1,0:T(8,128)(2,1)S(1)} %get-tuple-element.112, bf16[3584,256]{1,0:T(8,128)(2,1)} %get-tuple-element.113, bf16[3584,512]{1,0:T(8,128)(2,1)} %constant_dynamic-slice_fusion.2), kind=kOutput, calls=%fused_computation.17 | convolution fusion | flops 30090985472 | bytes 45088768 | tf_op jit(solution)/shard_map/dot_general | solution.py:38
  248.9 12.3 rope_fwd.1
  264.4 35.1 %attn_fwd.2 = (bf16[8,512,256]{2,1,0:T(8,128)(2,1)}, f32[8,512,256]{2,1,0:T(8,128)S(1)}, f32[8,8,512]{2,1,0:T(8,128)S(1)}) custom-call(s32[16]{0:T(128)S(1)} %fusion.92.nkb_ref, s32[16,1,256]{2,1,0:T(1,128)S(1)} %get-tuple-element.97.lim_ref, bf16[4096,512]{1,0:T(8,128)(2,1)} %get-tuple-element.46.q_ref, bf16[4096,256]{1,0:T(8,128)(2,1)S(1)} %copy-done.2, ...), custom_call_target="tpu_custom_call" | custom-call | flops 9448928256 | bytes 8388608 | tf_op jit(solution)/shard_map/attn_fwd/pallas_call | solution.py:222
  301.5 2.5 all-to-all-start
  304.0 26.5 %all-to-all-done = bf16[8,512,256]{2,1,0:T(8,128)(2,1)S(1)} async-done(((bf16[8,512,256]{2,1,0:T(8,128)(2,1)}), bf16[8,512,256]{2,1,0:T(8,128)(2,1)S(1)}, u32[]{:S(2)}, u32[]{:S(2)}) %all-to-all-start) | async-done | bytes 2097184 | tf_op jit(solution)/shard_map/all_to_all | solution.py:378
  330.5 13.9 %fusion.33 = (f32[256]{0:T(256)S(1)}, bf16[256,3584]{1,0:T(8,128)(2,1)S(1)}) fusion(bf16[4096,256]{1,0:T(8,128)(2,1)S(1)} %bitcast.87, bf16[4096,3584]{1,0:T(8,128)(2,1)} %param.26), kind=kOutput, calls=%fused_computation.68 | convolution fusion | flops 7519862784 | bytes 33293312 | tf_op jit(solution)/shard_map/dot_general | solution.py:46
  344.4 2.6 fusion.29
  347.1 2.4 fusion.31
  351.1 38.6 %attn_fwd.3 = (bf16[8,512,256]{2,1,0:T(8,128)(2,1)}, f32[8,512,256]{2,1,0:T(8,128)S(1)}, f32[8,8,512]{2,1,0:T(8,128)S(1)}) custom-call(s32[16]{0:T(128)S(1)} %fusion.92.nkb_ref, s32[16,1,256]{2,1,0:T(1,128)S(1)} %get-tuple-element.97.lim_ref, bf16[4096,512]{1,0:T(8,128)(2,1)} %get-tuple-element.46.q_ref, bf16[4096,256]{1,0:T(8,128)(2,1)S(1)} %copy-done.3, ...), custom_call_target="tpu_custom_call" | custom-call | flops 9448928256 | bytes 8388608 | tf_op jit(solution)/shard_map/attn_fwd/pallas_call | solution.py:222
  392.4 2.4 all-to-all-start.1
  394.8 15.7 %fusion.18 = bf16[4096,256]{0,1:T(8,128)(2,1)} fusion(bf16[256,3584]{1,0:T(8,128)(2,1)} %fusion.31, bf16[4096,3584]{1,0:T(8,128)(2,1)} %param.26), kind=kOutput, calls=%fused_computation.47 | convolution fusion | flops 7517241344 | bytes 33292288 | tf_op jit(solution)/shard_map/dot_general | solution.py:42
  410.5 4.1 copy.34
  414.6 29.6 %all-to-all-done.1 = bf16[8,512,256]{2,1,0:T(8,128)(2,1)S(1)} async-done(((bf16[8,512,256]{2,1,0:T(8,128)(2,1)}), bf16[8,512,256]{2,1,0:T(8,128)(2,1)S(1)}, u32[]{:S(2)}, u32[]{:S(2)}) %all-to-all-start.1) | async-done | bytes 2097184 | tf_op jit(solution)/shard_map/all_to_all | solution.py:378
  444.2 14.1 %fusion.35 = (f32[256]{0:T(256)S(1)}, bf16[256,3584]{1,0:T(8,128)(2,1)S(1)}) fusion(bf16[4096,256]{1,0:T(8,128)(2,1)S(1)} %bitcast.86, bf16[4096,3584]{1,0:T(8,128)(2,1)} %param.26), kind=kOutput, calls=%fused_computation.70 | convolution fusion | flops 7519862784 | bytes 33293312 | tf_op jit(solution)/shard_map/dot_general | solution.py:46
  458.3 2.6 fusion.30
  461.0 4.2 fusion.28
  465.2 3.4 all-to-all-start.2
  468.7 16.1 %fusion.19 = bf16[4096,256]{0,1:T(8,128)(2,1)} fusion(bf16[256,3584]{1,0:T(8,128)(2,1)S(1)} %copy-done.22, bf16[4096,3584]{1,0:T(8,128)(2,1)} %param.26), kind=kOutput, calls=%fused_computation.48 | convolution fusion | flops 7517241344 | bytes 33292288 | tf_op jit(solution)/shard_map/dot_general | solution.py:42
  484.7 4.1 copy.35
  488.8 26.1 %all-to-all-done.2.do_ref = bf16[8,512,256]{2,1,0:T(8,128)(2,1)} async-done(((bf16[8,512,256]{2,1,0:T(8,128)(2,1)}), bf16[8,512,256]{2,1,0:T(8,128)(2,1)}, u32[]{:S(2)}, u32[]{:S(2)}) %all-to-all-start.2) | async-done | bytes 2097184 | tf_op jit(solution)/shard_map/all_to_all | solution.py:378
  517.2 45.8 %attn_bwd.2 = (bf16[2048,512]{1,0:T(8,128)(2,1)}, f32[4096,256]{1,0:T(8,128)}, f32[4096,256]{1,0:T(8,128)}) custom-call(s32[16]{0:T(128)} %copy-done.6, s32[16,1,256]{2,1,0:T(1,128)} %copy-done.1, bf16[4096,512]{1,0:T(8,128)(2,1)} %get-tuple-element.46.q_ref, bf16[4096,256]{1,0:T(8,128)(2,1)} %get-tuple-element.47.k_ref, ...), custom_call_target="tpu_custom_call" | custom-call | flops 23192823808 | bytes 12582912 | tf_op jit(solution)/shard_map/attn_bwd/pallas_call | solution.py:302
  563.0 3.6 all-to-all-done.3.do_ref
  567.9 51.8 %attn_bwd.3 = (bf16[2048,512]{1,0:T(8,128)(2,1)}, bf16[4096,256]{1,0:T(8,128)(2,1)}, bf16[4096,256]{1,0:T(8,128)(2,1)}) custom-call(s32[16]{0:T(128)} %copy-done.6, s32[16,1,256]{2,1,0:T(1,128)} %copy-done.1, bf16[4096,512]{1,0:T(8,128)(2,1)} %get-tuple-element.46.q_ref, bf16[4096,256]{1,0:T(8,128)(2,1)} %get-tuple-element.47.k_ref, ...), custom_call_target="tpu_custom_call" | custom-call | flops 23192823808 | bytes 12582912 | tf_op jit(solution)/shard_map/attn_bwd/pallas_call | solution.py:302
  619.7 17.7 %rope_bwd.1 = (bf16[4096,1024]{1,0:T(8,128)(2,1)}, bf16[8,512,512]{2,1,0:T(8,128)(2,1)}, bf16[8,256,512]{2,1,0:T(8,128)(2,1)}, bf16[8,256,512]{2,1,0:T(8,128)(2,1)}, f32[1,256]{1,0:T(1,128)}, /*index=5*/f32[1,256]{1,0:T(1,128)}) custom-call(bf16[4096,1024]{1,0:T(8,128)(2,1)} %convolution_convert_fusion.2.raw_ref.v_ref, ...), custom_call_target="tpu_custom_call" | custom-call | flops 125829120 | bytes 25165824 | tf_op jit(solution)/shard_map/rope_bwd/pallas_call | solution.py:135
  637.4 52.3 %all_to_all.40 = bf16[8,512,512]{2,1,0:T(8,128)(2,1)} all-to-all(bf16[8,512,512]{2,1,0:T(8,128)(2,1)} %get-tuple-element.67), channel_id=1, replica_groups=mesh['dp'=1,'cp'=8] {'cp'}, dimensions={0} | all-to-all | bytes 8388608 | tf_op jit(solution)/shard_map/all_to_all | solution.py:378
  689.7 2.3 all-to-all-start.5
  692.1 23.4 %fusion.96 = f32[512,3584]{1,0:T(8,128)} fusion(bf16[4096,512]{1,0:T(8,128)(2,1)} %bitcast.88, bf16[3584,4096]{1,0:T(8,128)(2,1)} %param.21), kind=kOutput, calls=%fused_computation.192 | convolution fusion | flops 15032385536 | bytes 40894464 | tf_op jit(solution)/shard_map/dot_general | solution.py:469
  715.5 3.1 all-to-all-done.5
  718.6 3.1 all-to-all-start.6
  721.8 13.4 fusion.97
  735.2 13.2 all-to-all-done.6
  748.4 17.8 %fusion.8 = (f32[3584]{0:T(1024)S(1)}, f32[512]{0:T(512)S(1)}, bf16[512,3584]{1,0:T(8,128)(2,1)}) fusion(bf16[512,3584]{1,0:T(8,128)(2,1)} %get-tuple-element.106, f32[512]{0:T(512)S(1)} %copy-done.32, f32[3584]{0:T(1024)S(1)} %copy-done.25, bf16[2048,512]{1,0:T(8,128)(2,1)} %bitcast.12, bf16[3584,2048]{1,0:T(8,128)(2,1)} %param.23, ...), kind=kOutput, calls=%fused_computation.19 | convolution fusion | flops 7536373760 | bytes 38830080 | tf_op jit(solution)/shard_map/dot_general | solution.py:469
  766.2 7.4 fusion.51
  773.6 8.9 convolution_convert_fusion.8
  782.5 4.8 convolution_convert_fusion
  787.9 5.9 copy.36
  793.8 3.3 all-to-all-start.7
  797.2 27.4 %fusion.2 = bf16[4096,1152]{1,0:T(8,128)(2,1)} fusion(bf16[2048,1152]{1,0:T(8,128)(2,1)} %all-gather.8.cloned.1.call-done, s32[4096]{0:T(1024)S(1)} %broadcast_add_fusion), kind=kOutput, calls=%fused_computation.3 | convolution fusion | flops 19340460032 | bytes 14172160 | tf_op jit(solution)/shard_map/dot_general | solution.py:38
  824.6 29.9 %all-to-all-done.7 = bf16[8,448,512]{2,1,0:T(8,128)(2,1)} async-done(((bf16[8,448,512]{2,1,0:T(8,128)(2,1)}), bf16[8,448,512]{2,1,0:T(8,128)(2,1)}, u32[]{:S(2)}, u32[]{:S(2)}) %all-to-all-start.7) | async-done | bytes 3670048 | tf_op jit(solution)/shard_map/all_to_all | solution.py:378
  856.8 2.8 convolution_add_fusion.6
  868.8 2.8 fusion.38
  871.6 4.2 copy.37
  875.8 3.0 copy.38
  878.7 13.6 fusion.98
  892.4 16.3 %add_convert_fusion = bf16[512,3584]{1,0:T(8,128)(2,1)} fusion(f32[512,3584]{1,0:T(8,128)} %fusion.98, bf16[2048,512]{1,0:T(8,128)(2,1)S(1)} %bitcast.91, bf16[2048,3584]{1,0:T(8,128)(2,1)} %all-gather.18.cloned.1.call-done), kind=kOutput, calls=%fused_computation.28 | convolution fusion | flops 7519862784 | bytes 27787264 | tf_op jit(solution)/shard_map/dot_general | solution.py:46
  908.7 38.5 %convolution_convert_fusion.1 = bf16[3584,1024]{1,0:T(8,128)(2,1)} fusion(bf16[4096,3584]{1,0:T(8,128)(2,1)} %all-gather.10.cloned.1.call-done, bf16[4096,1024]{1,0:T(8,128)(2,1)} %get-tuple-element.73), kind=kOutput, calls=%fused_computation.16 | convolution fusion | flops 30068441088 | bytes 45088768 | tf_op jit(solution)/shard_map/dot_general | solution.py:46
  948.7 3.7 pad_maximum_fusion
  957.5 5.6 broadcast_in_dim.101
  963.1 15.8 %broadcast_in_dim.102 = bf16[1,4096,1152]{2,1,0:T(8,128)(2,1)} reshape(bf16[16,4,16,4,1152]{4,3,2,1,0:T(4,128)(2,1)} %broadcast_in_dim.101) | data formatting | bytes 18874368 | tf_op jit(solution)/shard_map/broadcast_in_dim | solution.py:481
  978.9 24.5 %all-reduce = (bf16[1152]{0:T(1024)(128)(2,1)}, bf16[3584]{0:T(1024)(128)(2,1)}, bf16[256]{0:T(256)(128)(2,1)}, bf16[256]{0:T(256)(128)(2,1)}, bf16[3584]{0:T(1024)(128)(2,1)}) all-reduce(f32[1152]{0:T(1024)S(1)} %get-tuple-element.85, f32[3584]{0:T(1024)S(1)} %get-tuple-element.79, ...), channel_id=1, replica_groups=mesh['dp'=1,'cp'=8] {'cp'}, use_global_device_ids=true, to_apply=%region_14.15 | all-reduce | flops 8832 | bytes 52992 | tf_op jit(solution)/shard_map/psum | solution.py:493
  1003.4 3.3 copy-done
  1006.7 5.5 copy_out.3
  1012.2 47.5 %all-gather.20.cloned.1.call-done.x_ref = bf16[4096,3584]{1,0:T(8,128)(2,1)} async-done(((bf16[512,3584]{1,0:T(8,128)(2,1)}), bf16[4096,3584]{1,0:T(8,128)(2,1)}) %all-gather.20.cloned.1.call-update) | async-done | bytes 29360144 | tf_op jit(solution)/shard_map/all_gather | solution.py:373
  1059.7 24.2 %copy_out.5 = bf16[4096,3584]{1,0:T(8,128)(2,1)} custom-call(bf16[4096,3584]{1,0:T(8,128)(2,1)} %all-gather.20.cloned.1.call-done.x_ref), custom_call_target="tpu_custom_call" | custom-call | flops 14680064 | bytes 58720256 | tf_op jit(solution)/shard_map/copy_out/pallas_call | solution.py:338
  1083.9 240.0 %all-gather.14.cloned.1.call-done.x_ref = bf16[3584,8192]{1,0:T(8,128)(2,1)} async-done(((bf16[3584,1024]{1,0:T(8,128)(2,1)}), bf16[3584,8192]{1,0:T(8,128)(2,1)}) %all-gather.14.cloned.1.call-update) | async-done | bytes 58720272 | tf_op jit(solution)/shard_map/all_gather | solution.py:373
  1323.9 39.8 %copy_out.4 = (bf16[3584,4096]{1,0:T(8,128)(2,1)}, bf16[3584,2048]{1,0:T(8,128)(2,1)}, bf16[3584,2048]{1,0:T(8,128)(2,1)}) custom-call(bf16[3584,8192]{1,0:T(8,128)(2,1)} %all-gather.14.cloned.1.call-done.x_ref), custom_call_target="tpu_custom_call" | custom-call | flops 29360128 | bytes 117440512 | tf_op jit(solution)/shard_map/copy_out/pallas_call | solution.py:338
  (156 shorter events, 39.0 us)
Async XLA Ops:
  7.2 45.9 %all-gather.8.cloned.1.call-start = ((), (), s32[]{:S(2)}) async-start(), calls=%async_computation.9 | async-start | bytes 5308416 | tf_op jit(solution)/shard_map/all_gather | solution.py:373
  7.9 7.4 copy-start.26
  7.9 9.3 copy-start.41
  7.9 9.5 copy-start.37
  14.8 0.6 copy-start.42
  14.8 1.0 copy-start.18
  16.9 195.1 %all-gather.10.cloned.1.call-start = ((), (), s32[]{:S(2)}) async-start(), calls=%async_computation.10 | async-start | bytes 33030144 | tf_op jit(solution)/shard_map/all_gather | solution.py:373
  17.3 51.4 %copy-start.35 = (pred[512]{0:T(512)(128)(4,1)}, pred[512]{0:T(512)(128)(4,1)S(1)}, u32[]{:S(2)}) copy-start(pred[512]{0:T(512)(128)(4,1)S(1)} %fusion.87) | copy-start | bytes 1540
  17.4 51.3 %copy-start.44 = (s32[512]{0:T(512)}, s32[512]{0:T(512)S(1)}, u32[]{:S(2)}) copy-start(s32[512]{0:T(512)S(1)} %broadcast_select_fusion.3) | copy-start | bytes 6148
  17.4 51.4 %copy-start.24 = (f32[3584]{0:T(1024)}, f32[3584]{0:T(1024)S(1)}, u32[]{:S(2)}) copy-start(f32[3584]{0:T(1024)S(1)} %convert_add_fusion.1) | copy-start | bytes 43012
  68.7 5.7 copy-start.39
  68.8 0.6 copy-start.31
  74.4 0.7 copy-start.48
  74.4 1.2 copy-start.49
  77.4 272.1 %copy-start.1 = (s32[16,1,256]{2,1,0:T(1,128)}, s32[16,1,256]{2,1,0:T(1,128)S(1)}, u32[]{:S(2)}) copy-start(s32[16,1,256]{2,1,0:T(1,128)S(1)} %get-tuple-element.97.lim_ref) | copy-start | bytes 49156
  77.4 272.1 %copy-start.6 = (s32[16]{0:T(128)}, s32[16]{0:T(128)S(1)}, u32[]{:S(2)}) copy-start(s32[16]{0:T(128)S(1)} %fusion.92.nkb_ref) | copy-start | bytes 196
  261.2 1.6 copy-start.2
  262.8 1.6 copy-start.4
  299.4 2.0 copy-start.7
  301.5 42.9 %copy-start.9 = (f32[8,8,512]{2,1,0:T(8,128)}, f32[8,8,512]{2,1,0:T(8,128)S(1)}, u32[]{:S(2)}) copy-start(f32[8,8,512]{2,1,0:T(8,128)S(1)} %get-tuple-element.56.lse_ref) | copy-start | bytes 393220
  301.5 2.5 copy-start.38
  301.5 29.0 %all-to-all-start = ((bf16[8,512,256]{2,1,0:T(8,128)(2,1)}), bf16[8,512,256]{2,1,0:T(8,128)(2,1)S(1)}, u32[]{:S(2)}, u32[]{:S(2)}) async-start(bf16[8,512,256]{2,1,0:T(8,128)(2,1)} %get-tuple-element.49), calls=%async_computation | async-start | bytes 4194304 | tf_op jit(solution)/shard_map/all_to_all | solution.py:378
  303.9 574.8 %all-gather.16.cloned.1.call-start = ((), (), s32[]{:S(2)}) async-start(), calls=%async_computation.14 | async-start | bytes 16515072 | tf_op jit(solution)/shard_map/all_gather | solution.py:373
  330.5 13.9 %copy-start.11 = (bf16[512,3584]{1,0:T(8,128)(2,1)S(1)}, bf16[512,3584]{1,0:T(8,128)(2,1)}, u32[]{:S(2)}) copy-start(bf16[512,3584]{1,0:T(8,128)(2,1)} %param.17) | copy-start | bytes 11010052
  344.4 2.7 copy-start.14
  347.1 2.4 copy-start.3
  349.5 1.6 copy-start.5
  389.7 2.0 copy-start.8
  391.7 0.6 copy-start.10
  392.4 51.8 %all-to-all-start.1 = ((bf16[8,512,256]{2,1,0:T(8,128)(2,1)}), bf16[8,512,256]{2,1,0:T(8,128)(2,1)S(1)}, u32[]{:S(2)}, u32[]{:S(2)}) async-start(bf16[8,512,256]{2,1,0:T(8,128)(2,1)} %get-tuple-element.51), calls=%async_computation.1 | async-start | bytes 4194304 | tf_op jit(solution)/shard_map/all_to_all | solution.py:378
  394.8 497.6 %all-gather.18.cloned.1.call-start = ((), (), s32[]{:S(2)}) async-start(), calls=%async_computation.15 | async-start | bytes 16515072 | tf_op jit(solution)/shard_map/all_gather | solution.py:373
  444.2 14.2 %copy-start.12 = (bf16[512,3584]{1,0:T(8,128)(2,1)S(1)}, bf16[512,3584]{1,0:T(8,128)(2,1)}, u32[]{:S(2)}) copy-start(bf16[512,3584]{1,0:T(8,128)(2,1)} %param.17) | copy-start | bytes 11010052
  444.2 16.8 %copy-start.15 = (bf16[256,3584]{1,0:T(8,128)(2,1)S(1)}, bf16[256,3584]{1,0:T(8,128)(2,1)}, u32[]{:S(2)}) copy-start(bf16[256,3584]{1,0:T(8,128)(2,1)} %copy-done.14) | copy-start | bytes 5505028
  458.3 2.7 copy-start.13
  465.2 3.4 copy-start.22
  465.2 49.7 %all-to-all-start.2 = ((bf16[8,512,256]{2,1,0:T(8,128)(2,1)}), bf16[8,512,256]{2,1,0:T(8,128)(2,1)}, u32[]{:S(2)}, u32[]{:S(2)}) async-start(bf16[8,512,256]{2,1,0:T(8,128)(2,1)} %bitcast.6), calls=%async_computation.2 | async-start | bytes 4194304 | tf_op jit(solution)/shard_map/all_to_all | solution.py:378
  514.9 51.7 %all-to-all-start.3 = ((bf16[8,512,256]{2,1,0:T(8,128)(2,1)}), bf16[8,512,256]{2,1,0:T(8,128)(2,1)S(1)}, u32[]{:S(2)}, u32[]{:S(2)}) async-start(bf16[8,512,256]{2,1,0:T(8,128)(2,1)} %bitcast.9), calls=%async_computation.3 | async-start | bytes 4194304 | tf_op jit(solution)/shard_map/all_to_all | solution.py:378
  566.6 1.3 copy-start.23
  689.7 28.9 %all-to-all-start.5 = ((bf16[8,256,512]{2,1,0:T(8,128)(2,1)}), bf16[8,256,512]{2,1,0:T(8,128)(2,1)S(1)}, u32[]{:S(2)}, u32[]{:S(2)}) async-start(bf16[8,256,512]{2,1,0:T(8,128)(2,1)} %get-tuple-element.69), calls=%async_computation.5 | async-start | bytes 4194304 | tf_op jit(solution)/shard_map/all_to_all | solution.py:378
  718.6 29.7 %all-to-all-start.6 = ((bf16[8,256,512]{2,1,0:T(8,128)(2,1)}), bf16[8,256,512]{2,1,0:T(8,128)(2,1)}, u32[]{:S(2)}, u32[]{:S(2)}) async-start(bf16[8,256,512]{2,1,0:T(8,128)(2,1)} %get-tuple-element.71), calls=%async_computation.6 | async-start | bytes 4194304 | tf_op jit(solution)/shard_map/all_to_all | solution.py:378
  721.7 232.9 %reduce-scatter.2.cloned.1.call-start = ((), (), s32[]{:S(2)}) async-start(), calls=%async_computation.11 | async-start | bytes 5308416 | tf_op jit(solution)/shard_map/reduce_scatter | solution.py:478
  721.8 26.6 %copy-start.25 = (f32[3584]{0:T(1024)S(1)}, f32[3584]{0:T(1024)}, u32[]{:S(2)}) copy-start(f32[3584]{0:T(1024)} %copy-done.24) | copy-start | bytes 43012
  721.8 26.6 %copy-start.32 = (f32[512]{0:T(512)S(1)}, f32[512]{0:T(512)}, u32[]{:S(2)}) copy-start(f32[512]{0:T(512)} %copy-done.31) | copy-start | bytes 6148
  748.4 17.8 %copy-start.40 = (f32[512]{0:T(512)S(1)}, f32[512]{0:T(512)}, u32[]{:S(2)}) copy-start(f32[512]{0:T(512)} %copy-done.39) | copy-start | bytes 6148
  748.4 17.8 %copy-start.36 = (pred[512]{0:T(512)(128)(4,1)S(1)}, pred[512]{0:T(512)(128)(4,1)}, u32[]{:S(2)}) copy-start(pred[512]{0:T(512)(128)(4,1)} %copy-done.35) | copy-start | bytes 1540
  773.6 8.9 copy-start.16
  773.6 8.9 copy-start.45
  787.2 0.7 copy-start.30
  793.8 60.7 %all-to-all-start.7 = ((bf16[8,448,512]{2,1,0:T(8,128)(2,1)}), bf16[8,448,512]{2,1,0:T(8,128)(2,1)}, u32[]{:S(2)}, u32[]{:S(2)}) async-start(bf16[8,448,512]{2,1,0:T(8,128)(2,1)} %bitcast.85), calls=%async_computation.8 | async-start | bytes 7340032 | tf_op jit(solution)/shard_map/all_to_all | solution.py:378
  797.1 206.3 %all-gather.12.cloned.1.call-start = ((), (), s32[]{:S(2)}) async-start(), calls=%async_computation.12 | async-start | bytes 9289728 | tf_op jit(solution)/shard_map/all_gather | solution.py:373
  854.5 5.2 copy-start.20
  871.6 188.2 %all-gather.20.cloned.1.call-start = ((), (), s32[]{:S(2)}) async-start(), calls=%async_computation.16 | async-start | bytes 33030144 | tf_op jit(solution)/shard_map/all_gather | solution.py:373
  908.7 415.2 %all-gather.14.cloned.1.call-start = ((), (), s32[]{:S(2)}) async-start(), calls=%async_computation.13 | async-start | bytes 66060288 | tf_op jit(solution)/shard_map/all_gather | solution.py:373
  947.2 0.7 copy-start.28
  947.2 0.7 copy-start.29
  947.2 1.5 copy-start.21
  948.7 3.7 copy-start.17
  952.4 2.2 copy-start.19
  952.4 2.2 copy-start.27
  952.4 2.2 copy-start.34
  952.4 3.6 copy-start.43
  963.1 15.8 %copy-start.46 = (f32[1,256]{1,0:T(1,128)S(1)}, f32[1,256]{1,0:T(1,128)}, u32[]{:S(2)}) copy-start(f32[1,256]{1,0:T(1,128)} %get-tuple-element.77) | copy-start | bytes 3076
  963.1 15.8 %copy-start.47 = (f32[1,256]{1,0:T(1,128)S(1)}, f32[1,256]{1,0:T(1,128)}, u32[]{:S(2)}) copy-start(f32[1,256]{1,0:T(1,128)} %get-tuple-element.78) | copy-start | bytes 3076
  1003.4 3.3 copy-start
  (1 other events, 0.6 us)
Sparse Core Ops, SparseCore 0:
  17.1 36.0 all-gather.7
  74.6 137.3 all-gather.9
  349.6 96.8 all-gather.15
  465.4 117.4 all-gather.17
  787.4 73.2 reduce-scatter.1
  871.7 47.3 all-gather.11
  920.9 138.7 all-gather.19
  1062.1 261.6 all-gather.13

commit v6 on v5

--- a/solution.py
+++ b/solution.py
@@ -156,7 +156,7 @@
     return jnp.concatenate([blk[h * hd:(h + 1) * hd] for h in range(blk.shape[0] // hd)], axis=1)
 
 
-def attn_fwd_kernel(hd, part, nkb_ref, lim_ref, q_ref, k_ref, vt_ref, o_ref, o32_ref, lse_ref, s_ref, p_ref):
+def attn_fwd_kernel(hd, part, nkb_ref, lim_ref, q_ref, k_ref, vt_ref, o_ref, o32_ref, lse_ref, s_ref, p_ref, acc_ref):
     qb = HALVES * pl.program_id(0) + part
     coef = hd ** -0.5 * LOG2E
     n_q = q_ref.shape[1] // hd
@@ -198,15 +198,16 @@
         return dot(vt_ref[:, pl.ds(pl.multiple_of(kb * KB, KB), KB)], p)
 
     p_ref[:KB] = prob(0)
-
-    def pv_body(kb, acc):
+    acc_ref[...] = jnp.zeros_like(acc_ref)
+
+    def pv_body(kb, carry):
         pair = p_ref.at[pl.ds(pl.multiple_of((kb - 1) * KB, KB), 2 * KB)]
-        acc = acc + pv(kb - 1, pair[:KB])
+        acc_ref[...] += pv(kb - 1, pair[:KB])
         pair[KB:] = prob(kb)
-        return acc
-
-    acc = lax.fori_loop(1, n_all, pv_body, jnp.zeros((hd, rows), F32))
-    acc = acc + pv(n_all - 1, p_ref[pl.ds(pl.multiple_of((n_all - 1) * KB, KB), KB), :])
+        return carry
+
+    lax.fori_loop(1, n_all, pv_body, 0)
+    acc = acc_ref[...] + pv(n_all - 1, p_ref[pl.ds(pl.multiple_of((n_all - 1) * KB, KB), KB), :])
     for h in range(n_q):
         part = acc[:, h * BQ:(h + 1) * BQ]
         o32_ref[0, h * hd:(h + 1) * hd, :] = part
@@ -227,7 +228,7 @@
             in_specs=[pl.BlockSpec((1, 1, BQ), lambda i, *_: (at(i), 0, 0)), pl.BlockSpec((BQ, width), lambda i, *_: (at(i), 0)),
                       pl.BlockSpec((seq, hd), lambda i, *_: (0, 0)), pl.BlockSpec((hd, seq), lambda i, *_: (0, 0))],
             out_specs=[tall, tall, pl.BlockSpec((1, 8, n_q * BQ), lambda i, *_: (i, 0, 0))],
-            scratch_shapes=[pltpu.VMEM((seq + KB, n_q * BQ), F32), pltpu.VMEM((seq, n_q * BQ), BF16)]),
+            scratch_shapes=[pltpu.VMEM((seq + KB, n_q * BQ), F32), pltpu.VMEM((seq, n_q * BQ), BF16), pltpu.VMEM((hd, n_q * BQ), F32)]),
         out_shape=[jax.ShapeDtypeStruct((n_dev, width, BQ), BF16), jax.ShapeDtypeStruct((n_dev, width, BQ), F32),
                    jax.ShapeDtypeStruct((n_dev, 8, n_q * BQ), F32)],
         cost_estimate=pl.CostEstimate(flops=int(1.1 * seq * seq * width), bytes_accessed=4 * seq * width, transcendentals=seq * seq),
@@ -376,6 +377,21 @@
         if after is not None:
             x, _ = lax.optimization_barrier((x, after))
         return lax.all_to_all(x, 'cp', split_axis=0, concat_axis=0, tiled=True)
+
+    def reduce_to_owner(x, rank):
+        bits = [rank // 4, (rank // 2) % 2, rank % 2]
+
+        def halve(x, dim, bit):
+            pick = lambda b: lax.dynamic_index_in_dim(x, b, dim, keepdims=False)
+            got = lax.ppermute(pick(1 - bits[bit]), 'cp', [(i, i ^ (4 >> bit)) for i in range(n_dev)])
+            return pick(bits[bit]) + got
+
+        rows, cols = x.shape[0] // n_dev, x.shape[1]
+        x = halve(x.reshape(2, 2, 2, rows, cols), 2, 2)
+        cut = cols // 256 * 128
+        first = halve(halve(x[..., :cut], 1, 1), 0, 0)
+        second = halve(halve(x[..., cut:], 0, 0), 0, 1)
+        return jnp.concatenate([first, second], axis=-1)
 
     def device_step(vis_loc, text_loc, img_pos, grad_y, pn_gain, w_proj, pre_gain, w_query, w_key, w_value, q_gain, k_gain, w_out, post_gain):
         rank = lax.axis_index('cp')
@@ -475,7 +491,7 @@
         d_soft_rows = jnp.where(img_mask, d_merged, 0.0).astype(BF16)
         d_normed_rows = dot_nt(d_soft_rows, w_proj).astype(BF16)
         d_normed_all = dot_tn(select, d_normed_rows).astype(BF16)
-        d_normed = lax.psum_scatter(d_normed_all, 'cp', scatter_dimension=0, tiled=True)
+        d_normed = reduce_to_owner(d_normed_all, rank)
         d_pooled, g_pn = norm_pull(d_normed)
         spread = (d_pooled.astype(F32) / (POOL * POOL)).astype(BF16).reshape(img_loc, SIDE, 1, SIDE, 1, dim_v)
         grad_vis = jnp.broadcast_to(spread, (img_loc, SIDE, POOL, SIDE, POOL, dim_v)).reshape(img_loc, patches, dim_v)

time: 1380 us -> 1330 us (0.964)
  blocking collectives: 76.8 us -> 24.4 us
    all_to_all x1 -> x0, blocking collectives: 52.3 us -> none  [exchange(): return lax.all_to_all(x, 'cp', split_axis=0, concat_axis=0, tiled=True)]
    all_gather x7, waiting for transfers between devices: 439 us -> 396 us  [gather(): return lax.all_gather(x, 'cp', axis=axis, tiled=True)]
    ppermute x0 -> x5, waiting for transfers between devices: none -> 42.8 us  [halve(): lax.ppermute(pick(1 - bits[bit]), 'cp', [(i, i ^ 4 >> bit) for i in range...]
    all_to_all x7 -> x8, waiting for transfers between devices: 132 us -> 138 us  [exchange(): return lax.all_to_all(x, 'cp', split_axis=0, concat_axis=0, tiled=True)]
  transfers between devices with their start and end apart: 15 -> 20, of which waited for: 11 -> 15; matrix products, arithmetic and copies ran while one was open for 23% -> 23% of each run, Pallas kernels for 13% -> 14%
where the time goes in v6:
time: 1330 us; the launch traced here: 1320 us
  waiting for transfers between devices  577 us (43%)
  matrix products  296 us (22%)
  Pallas kernels  267 us (20%)
  local copies, waits for them, and re-layouts  69.9 us (5%)
  other arithmetic  46.3 us (3%)
  starting transfers between devices  27.8 us (2%)
  blocking collectives  24.4 us (2%)
  between operations  15.1 us (1%)
    all_gather x7, waiting for transfers between devices, gather(): return lax.all_gather(x, 'cp', axis=axis, tiled=True)  396 us
    all_to_all x8, waiting for transfers between devices, exchange(): return lax.all_to_all(x, 'cp', split_axis=0, concat_axis=0, tiled=True)  138 us
    dot_general x6, matrix products, dot_tn(): lax.dot_general(a, b, (((0,), (0,)), ((), ())), preferred_element_type=F32)  99.1 us
    pallas_call x2, Pallas kernels, attn_bwd(): pl.pallas_call(functools.partial(attn_bwd_kernel, hd, part), grid_spec=pl...  97.1 us
    dot_general x11, matrix products, dot(): return jnp.dot(a, b, preferred_element_type=F32)  96.7 us
    pallas_call x2, Pallas kernels, attn_fwd(): pl.pallas_call(functools.partial(attn_fwd_kernel, hd, part), grid_spec=pl...  70.1 us
    pallas_call x3, Pallas kernels, stream(): pl.pallas_call(body, grid=(grid,), in_specs=[in_spec], out_specs=out_spec...  69.5 us
    dot_general x3, matrix products, device_step(): lax.dot_general(d, w, (((0,), (1,)), ((), ())), preferred_element_type=F32)  54.1 us
  transfers between devices with their start and end apart: 20, of which 15 were waited for; matrix products, arithmetic and copies ran while one was open for 23% of the time, Pallas kernels for 14%

profile of v6, /device:TPU:0, one launch (start us, length us, event | category | flops | bytes accessed | tf_op | source)
XLA Modules:
  0.0 1324.2 jit_solution(15869690551491243847)
XLA Ops:
  7.9 6.8 multiply_reduce_fusion
  17.8 35.3 %all-gather.8.cloned.1.call-done = bf16[2048,1152]{1,0:T(8,128)(2,1)} async-done(((bf16[256,1152]{1,0:T(8,128)(2,1)}), bf16[2048,1152]{1,0:T(8,128)(2,1)}) %all-gather.8.cloned.1.call-update) | async-done | bytes 4718608 | tf_op jit(solution)/shard_map/all_gather | solution.py:374
  53.2 15.6 %fusion.10 = (f32[512]{0:T(512)S(1)}, bf16[512,3584]{1,0:T(8,128)(2,1)}) fusion(bf16[512,3584]{1,0:T(8,128)(2,1)} %param.15, bf16[1152,3584]{1,0:T(8,128)(2,1)} %param.19, bf16[2048,1152]{1,0:T(8,128)(2,1)} %all-gather.8.cloned.1.call-done, s32[512]{0:T(512)S(1)} %broadcast_select_fusion.3, pred[512]{0:T(512)(128)(4,1)S(1)} %fusion.86), kind=kOutput, calls=%fused_computation.21 | convolution fusion | flops 6654590464 | bytes 20320768 | tf_op jit(solution)/shard_map/dot_general | solution.py:38
  69.4 5.1 fusion.7
  77.4 5.0 constant_dynamic-slice_fusion.2
  82.4 4.0 constant_dynamic-slice_fusion
  86.4 9.3 multiply_sine_fusion
  95.7 116.4 %all-gather.10.cloned.1.call-done = bf16[4096,3584]{1,0:T(8,128)(2,1)} async-done(((bf16[512,3584]{1,0:T(8,128)(2,1)}), bf16[4096,3584]{1,0:T(8,128)(2,1)}) %all-gather.10.cloned.1.call-update) | async-done | bytes 29360144 | tf_op jit(solution)/shard_map/all_gather | solution.py:374
  212.1 36.9 %convolution_convert_fusion.2.raw_ref.v_ref = bf16[4096,1024]{1,0:T(8,128)(2,1)} fusion(bf16[4096,3584]{1,0:T(8,128)(2,1)} %all-gather.10.cloned.1.call-done, bf16[3584,256]{1,0:T(8,128)(2,1)S(1)} %get-tuple-element.116, bf16[3584,256]{1,0:T(8,128)(2,1)} %get-tuple-element.117, bf16[3584,512]{1,0:T(8,128)(2,1)} %constant_dynamic-slice_fusion.2), kind=kOutput, calls=%fused_computation.17 | convolution fusion | flops 30090985472 | bytes 45088768 | tf_op jit(solution)/shard_map/dot_general | solution.py:38
  249.0 12.3 rope_fwd.1
  264.4 33.4 %attn_fwd.2 = (bf16[8,512,256]{2,1,0:T(8,128)(2,1)}, f32[8,512,256]{2,1,0:T(8,128)S(1)}, f32[8,8,512]{2,1,0:T(8,128)S(1)}) custom-call(s32[16]{0:T(128)S(1)} %fusion.90.nkb_ref, s32[16,1,256]{2,1,0:T(1,128)S(1)} %get-tuple-element.97.lim_ref, bf16[4096,512]{1,0:T(8,128)(2,1)} %get-tuple-element.46.q_ref, bf16[4096,256]{1,0:T(8,128)(2,1)S(1)} %copy-done.2, ...), custom_call_target="tpu_custom_call" | custom-call | flops 9448928256 | bytes 8388608 | tf_op jit(solution)/shard_map/attn_fwd/pallas_call | solution.py:223
  302.3 26.5 %all-to-all-done = bf16[8,512,256]{2,1,0:T(8,128)(2,1)S(1)} async-done(((bf16[8,512,256]{2,1,0:T(8,128)(2,1)}), bf16[8,512,256]{2,1,0:T(8,128)(2,1)S(1)}, u32[]{:S(2)}, u32[]{:S(2)}) %all-to-all-start) | async-done | bytes 2097184 | tf_op jit(solution)/shard_map/all_to_all | solution.py:379
  328.8 13.9 %fusion.33 = (f32[256]{0:T(256)S(1)}, bf16[256,3584]{1,0:T(8,128)(2,1)S(1)}) fusion(bf16[4096,256]{1,0:T(8,128)(2,1)S(1)} %bitcast.117, bf16[4096,3584]{1,0:T(8,128)(2,1)} %param.26), kind=kOutput, calls=%fused_computation.68 | convolution fusion | flops 7519862784 | bytes 33293312 | tf_op jit(solution)/shard_map/dot_general | solution.py:46
  342.8 2.6 fusion.29
  349.5 36.8 %attn_fwd.3 = (bf16[8,512,256]{2,1,0:T(8,128)(2,1)}, f32[8,512,256]{2,1,0:T(8,128)S(1)}, f32[8,8,512]{2,1,0:T(8,128)S(1)}) custom-call(s32[16]{0:T(128)S(1)} %fusion.90.nkb_ref, s32[16,1,256]{2,1,0:T(1,128)S(1)} %get-tuple-element.97.lim_ref, bf16[4096,512]{1,0:T(8,128)(2,1)} %get-tuple-element.46.q_ref, bf16[4096,256]{1,0:T(8,128)(2,1)S(1)} %copy-done.3, ...), custom_call_target="tpu_custom_call" | custom-call | flops 9448928256 | bytes 8388608 | tf_op jit(solution)/shard_map/attn_fwd/pallas_call | solution.py:223
  388.9 2.6 all-to-all-start.1
  391.5 15.2 %fusion.18 = bf16[4096,256]{0,1:T(8,128)(2,1)} fusion(bf16[256,3584]{1,0:T(8,128)(2,1)} %fusion.31, bf16[4096,3584]{1,0:T(8,128)(2,1)} %param.26), kind=kOutput, calls=%fused_computation.47 | convolution fusion | flops 7517241344 | bytes 33292288 | tf_op jit(solution)/shard_map/dot_general | solution.py:42
  406.7 3.9 copy.34
  410.7 30.2 %all-to-all-done.1 = bf16[8,512,256]{2,1,0:T(8,128)(2,1)S(1)} async-done(((bf16[8,512,256]{2,1,0:T(8,128)(2,1)}), bf16[8,512,256]{2,1,0:T(8,128)(2,1)S(1)}, u32[]{:S(2)}, u32[]{:S(2)}) %all-to-all-start.1) | async-done | bytes 2097184 | tf_op jit(solution)/shard_map/all_to_all | solution.py:379
  440.8 3.1 all-to-all-start.2
  444.0 13.9 %fusion.35 = (f32[256]{0:T(256)S(1)}, bf16[256,3584]{1,0:T(8,128)(2,1)S(1)}) fusion(bf16[4096,256]{1,0:T(8,128)(2,1)S(1)} %bitcast.116, bf16[4096,3584]{1,0:T(8,128)(2,1)} %param.26), kind=kOutput, calls=%fused_computation.70 | convolution fusion | flops 7519862784 | bytes 33293312 | tf_op jit(solution)/shard_map/dot_general | solution.py:46
  457.9 2.6 fusion.30
  460.6 4.3 fusion.28
  464.9 15.1 %fusion.19 = bf16[4096,256]{0,1:T(8,128)(2,1)S(1)} fusion(bf16[256,3584]{1,0:T(8,128)(2,1)} %get-tuple-element.100, bf16[4096,3584]{1,0:T(8,128)(2,1)} %param.26), kind=kOutput, calls=%fused_computation.48 | convolution fusion | flops 7517241344 | bytes 33292288 | tf_op jit(solution)/shard_map/dot_general | solution.py:42
  482.4 2.8 all-to-all-start.3
  485.3 45.5 %attn_bwd.2 = (bf16[2048,512]{1,0:T(8,128)(2,1)}, f32[4096,256]{1,0:T(8,128)}, f32[4096,256]{1,0:T(8,128)}) custom-call(s32[16]{0:T(128)} %copy-done.6, s32[16,1,256]{2,1,0:T(1,128)} %copy-done.1, bf16[4096,512]{1,0:T(8,128)(2,1)} %get-tuple-element.46.q_ref, bf16[4096,256]{1,0:T(8,128)(2,1)} %get-tuple-element.47.k_ref, ...), custom_call_target="tpu_custom_call" | custom-call | flops 23192823808 | bytes 12582912 | tf_op jit(solution)/shard_map/attn_bwd/pallas_call | solution.py:303
  532.1 51.6 %attn_bwd.3 = (bf16[2048,512]{1,0:T(8,128)(2,1)}, bf16[4096,256]{1,0:T(8,128)(2,1)}, bf16[4096,256]{1,0:T(8,128)(2,1)}) custom-call(s32[16]{0:T(128)} %copy-done.6, s32[16,1,256]{2,1,0:T(1,128)} %copy-done.1, bf16[4096,512]{1,0:T(8,128)(2,1)} %get-tuple-element.46.q_ref, bf16[4096,256]{1,0:T(8,128)(2,1)} %get-tuple-element.47.k_ref, ...), custom_call_target="tpu_custom_call" | custom-call | flops 23192823808 | bytes 12582912 | tf_op jit(solution)/shard_map/attn_bwd/pallas_call | solution.py:303
  583.7 17.8 %rope_bwd.1 = (bf16[4096,1024]{1,0:T(8,128)(2,1)}, bf16[8,512,512]{2,1,0:T(8,128)(2,1)}, bf16[8,256,512]{2,1,0:T(8,128)(2,1)}, bf16[8,256,512]{2,1,0:T(8,128)(2,1)}, f32[1,256]{1,0:T(1,128)}, /*index=5*/f32[1,256]{1,0:T(1,128)}) custom-call(bf16[4096,1024]{1,0:T(8,128)(2,1)} %convolution_convert_fusion.2.raw_ref.v_ref, ...), custom_call_target="tpu_custom_call" | custom-call | flops 125829120 | bytes 25165824 | tf_op jit(solution)/shard_map/rope_bwd/pallas_call | solution.py:135
  601.5 3.3 all-to-all-start.4
  604.9 49.1 %all-to-all-done.4 = bf16[8,512,512]{2,1,0:T(8,128)(2,1)} async-done(((bf16[8,512,512]{2,1,0:T(8,128)(2,1)}), bf16[8,512,512]{2,1,0:T(8,128)(2,1)}, u32[]{:S(2)}, u32[]{:S(2)}) %all-to-all-start.4) | async-done | bytes 4194336 | tf_op jit(solution)/shard_map/all_to_all | solution.py:379
  656.3 23.4 %fusion.96 = f32[512,3584]{1,0:T(8,128)} fusion(bf16[4096,512]{1,0:T(8,128)(2,1)} %bitcast.10, bf16[3584,4096]{1,0:T(8,128)(2,1)} %param.21), kind=kOutput, calls=%fused_computation.203 | convolution fusion | flops 15032385536 | bytes 40894464 | tf_op jit(solution)/shard_map/dot_general | solution.py:485
  679.8 3.1 all-to-all-done.5
  682.9 3.3 all-to-all-start.6
  686.2 13.0 fusion.97
  699.1 13.7 %all-to-all-done.6 = bf16[8,256,512]{2,1,0:T(8,128)(2,1)} async-done(((bf16[8,256,512]{2,1,0:T(8,128)(2,1)}), bf16[8,256,512]{2,1,0:T(8,128)(2,1)}, u32[]{:S(2)}, u32[]{:S(2)}) %all-to-all-start.6) | async-done | bytes 2097184 | tf_op jit(solution)/shard_map/all_to_all | solution.py:379
  712.8 17.7 %fusion.8 = (f32[3584]{0:T(1024)S(1)}, f32[512]{0:T(512)S(1)}, bf16[512,3584]{1,0:T(8,128)(2,1)}) fusion(bf16[512,3584]{1,0:T(8,128)(2,1)} %get-tuple-element.110, f32[512]{0:T(512)S(1)} %copy-done.32, f32[3584]{0:T(1024)S(1)} %copy-done.25, bf16[2048,512]{1,0:T(8,128)(2,1)} %bitcast.12, bf16[3584,2048]{1,0:T(8,128)(2,1)} %param.23, ...), kind=kOutput, calls=%fused_computation.19 | convolution fusion | flops 7536373760 | bytes 38830080 | tf_op jit(solution)/shard_map/dot_general | solution.py:485
  730.6 8.1 fusion.51
  738.6 5.9 copy.36
  744.5 3.2 all-to-all-start.7
  748.0 27.3 %fusion.2 = bf16[4096,1152]{1,0:T(8,128)(2,1)} fusion(bf16[2048,1152]{1,0:T(8,128)(2,1)} %all-gather.8.cloned.1.call-done, s32[4096]{0:T(1024)S(1)} %broadcast_add_fusion), kind=kOutput, calls=%fused_computation.3 | convolution fusion | flops 19340460032 | bytes 14172160 | tf_op jit(solution)/shard_map/dot_general | solution.py:38
  775.4 15.9 %all-to-all-done.7 = bf16[8,448,512]{2,1,0:T(8,128)(2,1)} async-done(((bf16[8,448,512]{2,1,0:T(8,128)(2,1)}), bf16[8,448,512]{2,1,0:T(8,128)(2,1)}, u32[]{:S(2)}, u32[]{:S(2)}) %all-to-all-start.7) | async-done | bytes 3670048 | tf_op jit(solution)/shard_map/all_to_all | solution.py:379
  793.6 2.7 convolution_add_fusion.6
  805.4 2.8 fusion.38
  808.6 3.9 copy.37
  812.6 2.9 copy.38
  815.5 13.6 %fusion.98 = f32[512,3584]{1,0:T(8,128)} fusion(bf16[2048,512]{1,0:T(8,128)(2,1)} %bitcast.125, bf16[2048,3584]{1,0:T(8,128)(2,1)} %all-gather.16.cloned.1.call-done), kind=kOutput, calls=%fused_computation.205 | convolution fusion | flops 7516192768 | bytes 24117248 | tf_op jit(solution)/shard_map/dot_general | solution.py:46
  829.2 15.9 %add_convert_fusion = bf16[512,3584]{1,0:T(8,128)(2,1)} fusion(f32[512,3584]{1,0:T(8,128)} %fusion.98, bf16[2048,512]{1,0:T(8,128)(2,1)S(1)} %bitcast.124, bf16[2048,3584]{1,0:T(8,128)(2,1)} %all-gather.18.cloned.1.call-done), kind=kOutput, calls=%fused_computation.28 | convolution fusion | flops 7519862784 | bytes 27787264 | tf_op jit(solution)/shard_map/dot_general | solution.py:46
  845.3 38.2 %convolution_convert_fusion.1 = bf16[3584,1024]{1,0:T(8,128)(2,1)} fusion(bf16[4096,3584]{1,0:T(8,128)(2,1)} %all-gather.10.cloned.1.call-done, bf16[4096,1024]{1,0:T(8,128)(2,1)} %get-tuple-element.73), kind=kOutput, calls=%fused_computation.16 | convolution fusion | flops 30068441088 | bytes 45088768 | tf_op jit(solution)/shard_map/dot_general | solution.py:46
  883.6 9.4 convolution_convert_fusion.8
  893.0 3.6 convolution_convert_fusion
  900.5 4.6 collective-permute-done
  911.5 20.9 %collective-permute-done.1 = bf16[2,256,512]{2,1,0:T(8,128)(2,1)S(1)} collective-permute-done((bf16[2,256,512]{2,1,0:T(8,128)(2,1)S(1)}, bf16[2,256,512]{2,1,0:T(8,128)(2,1)S(1)}, u32[]{:S(2)}, u32[]{:S(2)}) %collective-permute-start.1) | collective-permute-done | bytes 524320 | tf_op jit(solution)/shard_map/ppermute | solution.py:386
  932.8 3.9 collective-permute-done.3
  939.9 7.3 collective-permute-done.2
  947.2 6.0 collective-permute-done.4
  954.1 5.6 broadcast_in_dim.98
  959.8 15.7 %broadcast_in_dim.99 = bf16[1,4096,1152]{2,1,0:T(8,128)(2,1)} reshape(bf16[16,4,16,4,1152]{4,3,2,1,0:T(4,128)(2,1)} %broadcast_in_dim.98) | data formatting | bytes 18874368 | tf_op jit(solution)/shard_map/broadcast_in_dim | solution.py:497
  975.4 24.4 %all-reduce = (bf16[1152]{0:T(1024)(128)(2,1)}, bf16[3584]{0:T(1024)(128)(2,1)}, bf16[256]{0:T(256)(128)(2,1)}, bf16[256]{0:T(256)(128)(2,1)}, bf16[3584]{0:T(1024)(128)(2,1)}) all-reduce(f32[1152]{0:T(1024)S(1)} %get-tuple-element.85, f32[3584]{0:T(1024)S(1)} %get-tuple-element.79, ...), channel_id=1, replica_groups=mesh['dp'=1,'cp'=8] {'cp'}, use_global_device_ids=true, to_apply=%region_13.14 | all-reduce | flops 8832 | bytes 52992 | tf_op jit(solution)/shard_map/psum | solution.py:509
  999.9 3.5 copy-done
  1003.4 5.5 copy_out.3
  1008.9 4.4 all-gather.20.cloned.1.call-done.x_ref
  1013.2 24.2 %copy_out.5 = bf16[4096,3584]{1,0:T(8,128)(2,1)} custom-call(bf16[4096,3584]{1,0:T(8,128)(2,1)} %all-gather.20.cloned.1.call-done.x_ref), custom_call_target="tpu_custom_call" | custom-call | flops 14680064 | bytes 58720256 | tf_op jit(solution)/shard_map/copy_out/pallas_call | solution.py:339
  1037.4 239.9 %all-gather.14.cloned.1.call-done.x_ref = bf16[3584,8192]{1,0:T(8,128)(2,1)} async-done(((bf16[3584,1024]{1,0:T(8,128)(2,1)}), bf16[3584,8192]{1,0:T(8,128)(2,1)}) %all-gather.14.cloned.1.call-update) | async-done | bytes 58720272 | tf_op jit(solution)/shard_map/all_gather | solution.py:374
  1277.3 39.8 %copy_out.4 = (bf16[3584,4096]{1,0:T(8,128)(2,1)}, bf16[3584,2048]{1,0:T(8,128)(2,1)}, bf16[3584,2048]{1,0:T(8,128)(2,1)}) custom-call(bf16[3584,8192]{1,0:T(8,128)(2,1)} %all-gather.14.cloned.1.call-done.x_ref), custom_call_target="tpu_custom_call" | custom-call | flops 29360128 | bytes 117440512 | tf_op jit(solution)/shard_map/copy_out/pallas_call | solution.py:339
  (176 shorter events, 54.8 us)
Async XLA Ops:
  7.2 46.0 %all-gather.8.cloned.1.call-start = ((), (), s32[]{:S(2)}) async-start(), calls=%async_computation.8 | async-start | bytes 5308416 | tf_op jit(solution)/shard_map/all_gather | solution.py:374
  7.9 7.5 copy-start.26
  7.9 9.7 copy-start.41
  7.9 9.9 copy-start.37
  17.0 195.1 %all-gather.10.cloned.1.call-start = ((), (), s32[]{:S(2)}) async-start(), calls=%async_computation.9 | async-start | bytes 33030144 | tf_op jit(solution)/shard_map/all_gather | solution.py:374
  17.7 51.1 %copy-start.35 = (pred[512]{0:T(512)(128)(4,1)}, pred[512]{0:T(512)(128)(4,1)S(1)}, u32[]{:S(2)}) copy-start(pred[512]{0:T(512)(128)(4,1)S(1)} %fusion.86) | copy-start | bytes 1540
  17.8 51.0 %copy-start.43 = (s32[512]{0:T(512)}, s32[512]{0:T(512)S(1)}, u32[]{:S(2)}) copy-start(s32[512]{0:T(512)S(1)} %broadcast_select_fusion.3) | copy-start | bytes 6148
  17.8 51.0 %copy-start.24 = (f32[3584]{0:T(1024)}, f32[3584]{0:T(1024)S(1)}, u32[]{:S(2)}) copy-start(f32[3584]{0:T(1024)S(1)} %convert_add_fusion.1) | copy-start | bytes 43012
  68.8 5.7 copy-start.39
  74.5 1.2 copy-start.48
  77.4 270.5 %copy-start.1 = (s32[16,1,256]{2,1,0:T(1,128)}, s32[16,1,256]{2,1,0:T(1,128)S(1)}, u32[]{:S(2)}) copy-start(s32[16,1,256]{2,1,0:T(1,128)S(1)} %get-tuple-element.97.lim_ref) | copy-start | bytes 49156
  77.4 270.5 %copy-start.6 = (s32[16]{0:T(128)}, s32[16]{0:T(128)S(1)}, u32[]{:S(2)}) copy-start(s32[16]{0:T(128)S(1)} %fusion.90.nkb_ref) | copy-start | bytes 196
  261.2 1.6 copy-start.2
  262.8 1.6 copy-start.4
  297.8 2.0 copy-start.7
  299.8 42.9 %copy-start.9 = (f32[8,8,512]{2,1,0:T(8,128)}, f32[8,8,512]{2,1,0:T(8,128)S(1)}, u32[]{:S(2)}) copy-start(f32[8,8,512]{2,1,0:T(8,128)S(1)} %get-tuple-element.56.lse_ref) | copy-start | bytes 393220
  299.8 2.5 copy-start.38
  299.8 29.0 %all-to-all-start = ((bf16[8,512,256]{2,1,0:T(8,128)(2,1)}), bf16[8,512,256]{2,1,0:T(8,128)(2,1)S(1)}, u32[]{:S(2)}, u32[]{:S(2)}) async-start(bf16[8,512,256]{2,1,0:T(8,128)(2,1)} %get-tuple-element.49), calls=%async_computation | async-start | bytes 4194304 | tf_op jit(solution)/shard_map/all_to_all | solution.py:379
  302.3 513.2 %all-gather.16.cloned.1.call-start = ((), (), s32[]{:S(2)}) async-start(), calls=%async_computation.12 | async-start | bytes 16515072 | tf_op jit(solution)/shard_map/all_gather | solution.py:374
  328.8 13.9 %copy-start.11 = (bf16[512,3584]{1,0:T(8,128)(2,1)S(1)}, bf16[512,3584]{1,0:T(8,128)(2,1)}, u32[]{:S(2)}) copy-start(bf16[512,3584]{1,0:T(8,128)(2,1)} %param.17) | copy-start | bytes 11010052
  342.7 2.7 copy-start.14
  345.4 2.5 copy-start.3
  347.9 1.6 copy-start.5
  386.2 2.0 copy-start.8
  388.9 51.9 %all-to-all-start.1 = ((bf16[8,512,256]{2,1,0:T(8,128)(2,1)}), bf16[8,512,256]{2,1,0:T(8,128)(2,1)S(1)}, u32[]{:S(2)}, u32[]{:S(2)}) async-start(bf16[8,512,256]{2,1,0:T(8,128)(2,1)} %get-tuple-element.51), calls=%async_computation.1 | async-start | bytes 4194304 | tf_op jit(solution)/shard_map/all_to_all | solution.py:379
  440.8 41.6 %all-to-all-start.2 = ((bf16[8,512,256]{2,1,0:T(8,128)(2,1)}), bf16[8,512,256]{2,1,0:T(8,128)(2,1)}, u32[]{:S(2)}, u32[]{:S(2)}) async-start(bf16[8,512,256]{2,1,0:T(8,128)(2,1)} %bitcast.118), calls=%async_computation.2 | async-start | bytes 4194304 | tf_op jit(solution)/shard_map/all_to_all | solution.py:379
  443.9 385.2 %all-gather.18.cloned.1.call-start = ((), (), s32[]{:S(2)}) async-start(), calls=%async_computation.13 | async-start | bytes 16515072 | tf_op jit(solution)/shard_map/all_gather | solution.py:374
  444.0 13.9 %copy-start.12 = (bf16[512,3584]{1,0:T(8,128)(2,1)S(1)}, bf16[512,3584]{1,0:T(8,128)(2,1)}, u32[]{:S(2)}) copy-start(bf16[512,3584]{1,0:T(8,128)(2,1)} %param.17) | copy-start | bytes 11010052
  444.0 16.6 %copy-start.15 = (bf16[256,3584]{1,0:T(8,128)(2,1)S(1)}, bf16[256,3584]{1,0:T(8,128)(2,1)}, u32[]{:S(2)}) copy-start(bf16[256,3584]{1,0:T(8,128)(2,1)} %copy-done.14) | copy-start | bytes 5505028
  457.9 2.7 copy-start.13
  482.4 48.3 %all-to-all-start.3 = ((bf16[8,512,256]{2,1,0:T(8,128)(2,1)}), bf16[8,512,256]{2,1,0:T(8,128)(2,1)S(1)}, u32[]{:S(2)}, u32[]{:S(2)}) async-start(bf16[8,512,256]{2,1,0:T(8,128)(2,1)} %bitcast.9), calls=%async_computation.3 | async-start | bytes 4194304 | tf_op jit(solution)/shard_map/all_to_all | solution.py:379
  530.8 1.3 copy-start.23
  601.5 3.3 copy-start.30
  601.5 52.5 %all-to-all-start.4 = ((bf16[8,512,512]{2,1,0:T(8,128)(2,1)}), bf16[8,512,512]{2,1,0:T(8,128)(2,1)}, u32[]{:S(2)}, u32[]{:S(2)}) async-start(bf16[8,512,512]{2,1,0:T(8,128)(2,1)} %get-tuple-element.67), calls=%async_computation.4 | async-start | bytes 8388608 | tf_op jit(solution)/shard_map/all_to_all | solution.py:379
  654.0 28.9 %all-to-all-start.5 = ((bf16[8,256,512]{2,1,0:T(8,128)(2,1)}), bf16[8,256,512]{2,1,0:T(8,128)(2,1)S(1)}, u32[]{:S(2)}, u32[]{:S(2)}) async-start(bf16[8,256,512]{2,1,0:T(8,128)(2,1)} %get-tuple-element.69), calls=%async_computation.5 | async-start | bytes 4194304 | tf_op jit(solution)/shard_map/all_to_all | solution.py:379
  682.9 29.9 %all-to-all-start.6 = ((bf16[8,256,512]{2,1,0:T(8,128)(2,1)}), bf16[8,256,512]{2,1,0:T(8,128)(2,1)}, u32[]{:S(2)}, u32[]{:S(2)}) async-start(bf16[8,256,512]{2,1,0:T(8,128)(2,1)} %get-tuple-element.71), calls=%async_computation.6 | async-start | bytes 4194304 | tf_op jit(solution)/shard_map/all_to_all | solution.py:379
  686.2 26.6 %copy-start.25 = (f32[3584]{0:T(1024)S(1)}, f32[3584]{0:T(1024)}, u32[]{:S(2)}) copy-start(f32[3584]{0:T(1024)} %copy-done.24) | copy-start | bytes 43012
  686.2 26.6 %copy-start.32 = (f32[512]{0:T(512)S(1)}, f32[512]{0:T(512)}, u32[]{:S(2)}) copy-start(f32[512]{0:T(512)} %copy-done.31) | copy-start | bytes 6148
  712.8 17.7 %copy-start.40 = (f32[512]{0:T(512)S(1)}, f32[512]{0:T(512)}, u32[]{:S(2)}) copy-start(f32[512]{0:T(512)} %copy-done.39) | copy-start | bytes 6148
  712.8 17.7 %copy-start.36 = (pred[512]{0:T(512)(128)(4,1)S(1)}, pred[512]{0:T(512)(128)(4,1)}, u32[]{:S(2)}) copy-start(pred[512]{0:T(512)(128)(4,1)} %copy-done.35) | copy-start | bytes 1540
  744.5 46.7 %all-to-all-start.7 = ((bf16[8,448,512]{2,1,0:T(8,128)(2,1)}), bf16[8,448,512]{2,1,0:T(8,128)(2,1)}, u32[]{:S(2)}, u32[]{:S(2)}) async-start(bf16[8,448,512]{2,1,0:T(8,128)(2,1)} %bitcast.114), calls=%async_computation.7 | async-start | bytes 7340032 | tf_op jit(solution)/shard_map/all_to_all | solution.py:379
  747.8 252.1 %all-gather.12.cloned.1.call-start = ((), (), s32[]{:S(2)}) async-start(), calls=%async_computation.10 | async-start | bytes 9289728 | tf_op jit(solution)/shard_map/all_gather | solution.py:374
  791.3 5.1 copy-start.19
  808.2 205.0 %all-gather.20.cloned.1.call-start = ((), (), s32[]{:S(2)}) async-start(), calls=%async_computation.14 | async-start | bytes 33030144 | tf_op jit(solution)/shard_map/all_gather | solution.py:374
  845.1 432.2 %all-gather.14.cloned.1.call-start = ((), (), s32[]{:S(2)}) async-start(), calls=%async_computation.11 | async-start | bytes 66060288 | tf_op jit(solution)/shard_map/all_gather | solution.py:374
  883.6 9.4 copy-start.44
  896.6 2.2 copy-start.22
  896.6 3.8 copy-start.42
  896.6 3.8 copy-start.28
  896.6 3.8 copy-start.29
  900.4 4.7 collective-permute-start
  907.1 2.4 copy-start.20
  907.1 2.4 copy-start.21
  907.4 29.3 %collective-permute-start.3 = (bf16[2,256,640]{2,1,0:T(8,128)(2,1)S(1)}, bf16[2,256,640]{2,1,0:T(8,128)(2,1)S(1)}, u32[]{:S(2)}, u32[]{:S(2)}) collective-permute-start(bf16[2,256,640]{2,1,0:T(8,128)(2,1)S(1)} %dynamic-slice_bitcast_fusion.1), channel_id=1, source_target_pairs={{0,4},{1,5},{2,6},{3,7},{4,0},{5,1},{6,2},{7,3}} | collective-permute-start | bytes 1966088 | tf_op jit(solution)/shard_map/ppermute | solution.py:386
  908.6 23.8 %collective-permute-start.1 = (bf16[2,256,512]{2,1,0:T(8,128)(2,1)S(1)}, bf16[2,256,512]{2,1,0:T(8,128)(2,1)S(1)}, u32[]{:S(2)}, u32[]{:S(2)}) collective-permute-start(bf16[2,256,512]{2,1,0:T(8,128)(2,1)S(1)} %dynamic-slice_bitcast_fusion.2), channel_id=1, source_target_pairs={{0,2},{1,3},{2,0},{3,1},{4,6},{5,7},{6,4},{7,5}} | collective-permute-start | bytes 1572872 | tf_op jit(solution)/shard_map/ppermute | solution.py:386
  911.5 26.2 %copy-start.16 = (bf16[512,3584]{1,0:T(8,128)(2,1)S(1)}, bf16[512,3584]{1,0:T(8,128)(2,1)}, u32[]{:S(2)}) copy-start(bf16[512,3584]{1,0:T(8,128)(2,1)} %get-tuple-element.95) | copy-start | bytes 11010052
  932.5 14.6 %collective-permute-start.2 = (bf16[256,512]{1,0:T(8,128)(2,1)S(1)}, bf16[256,512]{1,0:T(8,128)(2,1)S(1)}, u32[]{:S(2)}, u32[]{:S(2)}) collective-permute-start(bf16[256,512]{1,0:T(8,128)(2,1)S(1)} %dynamic-slice_bitcast_fusion.4), channel_id=1, source_target_pairs={{0,4},{1,5},{2,6},{3,7},{4,0},{5,1},{6,2},{7,3}} | collective-permute-start | bytes 786440 | tf_op jit(solution)/shard_map/ppermute | solution.py:386
  936.8 16.4 %copy-start.18 = (f32[256,1152]{1,0:T(8,128)S(1)}, f32[256,1152]{1,0:T(8,128)}, u32[]{:S(2)}) copy-start(f32[256,1152]{1,0:T(8,128)} %copy-done.17) | copy-start | bytes 3538948
  936.8 16.4 %copy-start.27 = (f32[1152]{0:T(1024)S(1)}, f32[1152]{0:T(1024)}, u32[]{:S(2)}) copy-start(f32[1152]{0:T(1024)} %copy-done.26) | copy-start | bytes 13828
  936.9 16.4 %copy-start.34 = (f32[256]{0:T(256)S(1)}, f32[256]{0:T(256)}, u32[]{:S(2)}) copy-start(f32[256]{0:T(256)} %copy-done.33) | copy-start | bytes 3076
  936.9 16.3 %collective-permute-start.4 = (bf16[256,640]{1,0:T(8,128)(2,1)S(1)}, bf16[256,640]{1,0:T(8,128)(2,1)S(1)}, u32[]{:S(2)}, u32[]{:S(2)}) collective-permute-start(bf16[256,640]{1,0:T(8,128)(2,1)S(1)} %dynamic-slice_bitcast_fusion.3), channel_id=1, source_target_pairs={{0,2},{1,3},{2,0},{3,1},{4,6},{5,7},{6,4},{7,5}} | collective-permute-start | bytes 983048 | tf_op jit(solution)/shard_map/ppermute | solution.py:386
  959.7 15.7 %copy-start.45 = (f32[1,256]{1,0:T(1,128)S(1)}, f32[1,256]{1,0:T(1,128)}, u32[]{:S(2)}) copy-start(f32[1,256]{1,0:T(1,128)} %get-tuple-element.77) | copy-start | bytes 3076
  959.8 15.7 %copy-start.46 = (f32[1,256]{1,0:T(1,128)S(1)}, f32[1,256]{1,0:T(1,128)}, u32[]{:S(2)}) copy-start(f32[1,256]{1,0:T(1,128)} %get-tuple-element.78) | copy-start | bytes 3076
  999.9 3.5 copy-start
  (5 other events, 3.5 us)
Sparse Core Ops, SparseCore 0:
  17.1 36.0 all-gather.7
  74.6 137.3 all-gather.9
  348.0 96.8 all-gather.15
  465.0 94.6 all-gather.17
  808.3 47.2 all-gather.11
  857.8 155.3 all-gather.19
  1015.6 261.6 all-gather.13

commit v7 on v6

--- a/solution.py
+++ b/solution.py
@@ -92,7 +92,7 @@
     )(raw, cos, sin, gq, gk)
 
 
-def rope_bwd_kernel(hd, raw_ref, dq0_ref, dq1_ref, dk_ref, dv_ref, cos_ref, sin_ref, gq_ref, gk_ref, out_ref, qt_ref, kt_ref, vt_ref, sq_ref, sk_ref):
+def rope_bwd_kernel(hd, raw_ref, dq0_ref, dq1_ref, dk_ref, cos_ref, sin_ref, gq_ref, gk_ref, q_ref, k_ref, qt_ref, sq_ref, sk_ref):
     cos, sin = cos_ref[...], sin_ref[...]
     half = hd // 2
     n_q = dq0_ref.shape[1] // hd
@@ -105,7 +105,7 @@
     def load(refs, lo, hi):
         return jnp.concatenate([ref[:, lo:hi] for ref in refs], axis=0).astype(F32)
 
-    def one(col, refs, dcol, gain, acc_ref, t_ref):
+    def one(col, refs, dcol, gain, acc_ref, out_ref, t_ref=None):
         da = load(refs, dcol, dcol + half)
         db = load(refs, dcol + half, dcol + hd)
         d = jnp.concatenate([da * cos + db * sin, db * cos - da * sin], axis=1)
@@ -116,17 +116,16 @@
         gd = d * (1.0 + gain)
         dx = r * (gd - xr * jnp.mean(xr * gd, axis=-1, keepdims=True))
         dx = dx.astype(BF16)
-        out_ref[:, col:col + hd] = dx
-        t_ref[0, dcol:dcol + hd, :] = dx.T
+        out_ref[:, dcol:dcol + hd] = dx
+        if t_ref is not None:
+            t_ref[0, dcol:dcol + hd, :] = dx.T
 
     for h in range(n_q):
-        one(h * hd, (dq0_ref, dq1_ref), h * hd, gq_ref[...], sq_ref, qt_ref)
-    one(n_q * hd, (dk_ref,), 0, gk_ref[...], sk_ref, kt_ref)
-    out_ref[:, (n_q + 1) * hd:] = dv_ref[...]
-    vt_ref[0] = dv_ref[...].T
-
-
-def rope_bwd(raw, dq_halves, dk, dv, cos, sin, gq, gk, hd, n_q, bm):
+        one(h * hd, (dq0_ref, dq1_ref), h * hd, gq_ref[...], sq_ref, q_ref, qt_ref)
+    one(n_q * hd, (dk_ref,), 0, gk_ref[...], sk_ref, k_ref)
+
+
+def rope_bwd(raw, dq_halves, dk, cos, sin, gq, gk, hd, n_q, bm):
     seq, width = raw.shape
     tall = lambda w: pl.BlockSpec((1, w, bm), lambda i: (i, 0, 0))
     tshape = lambda w: jax.ShapeDtypeStruct((seq // bm, w, bm), BF16)
@@ -135,12 +134,12 @@
     return pl.pallas_call(
         functools.partial(rope_bwd_kernel, hd),
         grid=(seq // bm,),
-        in_specs=[row(width)] + [pl.BlockSpec((bm // 2, n_q * hd), lambda i: (i, 0))] * 2 + [row(hd), row(hd), row(hd // 2), row(hd // 2), fix, fix],
-        out_specs=[row(width), tall(n_q * hd), tall(hd), tall(hd), fix, fix],
-        out_shape=[jax.ShapeDtypeStruct((seq, width), BF16), tshape(n_q * hd), tshape(hd), tshape(hd), jax.ShapeDtypeStruct((1, hd), F32), jax.ShapeDtypeStruct((1, hd), F32)],
+        in_specs=[row(width)] + [pl.BlockSpec((bm // 2, n_q * hd), lambda i: (i, 0))] * 2 + [row(hd), row(hd // 2), row(hd // 2), fix, fix],
+        out_specs=[row(n_q * hd), row(hd), tall(n_q * hd), fix, fix],
+        out_shape=[jax.ShapeDtypeStruct((seq, n_q * hd), BF16), jax.ShapeDtypeStruct((seq, hd), BF16), tshape(n_q * hd), jax.ShapeDtypeStruct((1, hd), F32), jax.ShapeDtypeStruct((1, hd), F32)],
         cost_estimate=pl.CostEstimate(flops=30 * seq * width, bytes_accessed=6 * seq * width, transcendentals=0),
         name="rope_bwd",
-    )(raw, *dq_halves, dk, dv, cos, sin, gq, gk)
+    )(raw, *dq_halves, dk, cos, sin, gq, gk)
 
 
 BQ = 256
@@ -317,16 +316,6 @@
     )(nkb, lim, q, k, kt, raw, d_o, o32, lse, *carried)
 
 
-def split_kernel(n_dev, x_ref, *o_refs):
-    width = x_ref.shape[1] // n_dev
-    for g in range(n_dev):
-        col = g * width
-        for o_ref in o_refs:
-            w = o_ref.shape[1] // n_dev
-            o_ref[:, g * w:(g + 1) * w] = x_ref[:, col:col + w]
-            col += w
-
-
 def copy_kernel(x_ref, o_ref):
     o_ref[...] = x_ref[...]
 
@@ -348,15 +337,23 @@
     )(x)
 
 
-def split_cols(x, n_dev, widths):
-    bm = 256
-    row = lambda w: pl.BlockSpec((bm, w), lambda i: (i, 0))
-    return stream(functools.partial(split_kernel, n_dev), x, row(x.shape[1]), [(x.shape[0], w) for w in widths], [row(w) for w in widths], x.shape[0] // bm)
-
-
 def copy_rows(x):
     spec = pl.BlockSpec((512, x.shape[1]), lambda i: (i, 0))
     return stream(copy_kernel, x, spec, [x.shape], [spec], x.shape[0] // 512)[0]
+
+
+def spread_kernel(x_ref, o_ref):
+    cell, col = (lax.broadcasted_iota(jnp.int32, (GRID, SIDE), d) for d in (0, 1))
+    y = dot((cell // POOL == col).astype(BF16), x_ref[...]).astype(BF16)
+    for t in range(POOL):
+        o_ref[t * GRID:(t + 1) * GRID, :] = y
+
+
+def spread_rows(x):
+    cols = x.shape[1]
+    step = GRID * POOL
+    n = x.shape[0] // SIDE
+    return stream(spread_kernel, x, pl.BlockSpec((SIDE, cols), lambda i: (i, 0)), [(n * step, cols)], [pl.BlockSpec((step, cols), lambda i: (i, 0))], n)[0]
 
 
 def transpose_rows(x):
@@ -473,17 +470,17 @@
             dq, *carried = attn_bwd(c, n_kb, limit, q, k, kt, raw, d_o[c], fwd[c][1], fwd[c][2], carried, hd, n_dev)
             dq_halves.append(dq)
         dk, dv = carried
-        d_qkv, dq_t, dk_t, dv_t, g_q_gain, g_k_gain = rope_bwd(raw, dq_halves, dk, dv, cos_t, sin_t, gq32, gk32, hd, n_q, seq_loc)
-
-        g_qkv = dot_tn(hidden_all, d_qkv).astype(BF16)
-        g_qkv = gather(g_qkv, 1)
-
-        dq_seq = exchange(dq_t, prev)
-        dk_seq = exchange(dk_t, dq_seq)
-        dv_last = exchange(dv_t, dk_seq)
-        dq_seq, dk_seq, dv_seq = [x.reshape(-1, seq_loc) for x in (dq_seq, dk_seq, dv_last)]
-        d_hidden = sum(lax.dot_general(d, w, (((0,), (1,)), ((), ())), preferred_element_type=F32)
-                       for d, w in ((dq_seq, w_query), (dk_seq, w_key), (dv_seq, w_value))).astype(BF16)
+        dv_all = gather(dv, 1)
+        dq, dk, dq_t, g_q_gain, g_k_gain = rope_bwd(raw, dq_halves, dk, cos_t, sin_t, gq32, gk32, hd, n_q, seq_loc)
+        dk_all = gather(dk, 1)
+        dq_last = exchange(dq_t, prev)
+        g_query = dot_tn(hidden_all, dq).astype(BF16)
+        g_query = gather(g_query, 1)
+
+        own_rows = lambda x: lax.dynamic_slice_in_dim(x, rank * seq_loc, seq_loc, 0)
+        d_hidden = lax.dot_general(dq_last.reshape(-1, seq_loc), w_query, (((0,), (1,)), ((), ())), preferred_element_type=F32)
+        d_hidden = d_hidden + dot_nt(own_rows(dv_all), w_value)
+        d_hidden = (d_hidden + dot_nt(own_rows(dk_all), w_key)).astype(BF16)
         d_merged_attn, g_pre = pre_pull(d_hidden)
         d_merged = (grad_y.astype(F32) + d_merged_attn.astype(F32)).astype(BF16)
         grad_text = jnp.where(img_mask, 0.0, d_merged).astype(BF16)
@@ -493,17 +490,18 @@
         d_normed_all = dot_tn(select, d_normed_rows).astype(BF16)
         d_normed = reduce_to_owner(d_normed_all, rank)
         d_pooled, g_pn = norm_pull(d_normed)
-        spread = (d_pooled.astype(F32) / (POOL * POOL)).astype(BF16).reshape(img_loc, SIDE, 1, SIDE, 1, dim_v)
-        grad_vis = jnp.broadcast_to(spread, (img_loc, SIDE, POOL, SIDE, POOL, dim_v)).reshape(img_loc, patches, dim_v)
-
-        d_soft_t = exchange(d_soft_rows.T.reshape(n_dev, d_model // n_dev, seq_loc), dv_last)
-        normed_pos = dot(select_all, normed_all).astype(BF16).reshape(n_dev, seq_loc, dim_v)
-        g_proj = sum(dot(d_soft_t[i], normed_pos[i]) for i in range(n_dev)).astype(BF16)
+        grad_vis = spread_rows((d_pooled.astype(F32) / (POOL * POOL)).astype(BF16)).reshape(img_loc, patches, dim_v)
+
+        d_soft_t = exchange(d_soft_rows.T.reshape(n_dev, d_model // n_dev, seq_loc), dq_last)
+        normed_pos = dot(select_all, normed_all).astype(BF16)
+        g_proj = dot(d_soft_t.transpose(1, 0, 2).reshape(-1, seq), normed_pos).astype(BF16)
         g_proj = gather(g_proj)
 
         g_out = sum(dot_tn(fwd[c][0].transpose(0, 2, 1).reshape(-1, wq_loc), d_proj_parts[c]) for c in range(HALVES)).astype(BF16)
         g_out = gather(g_out)
-        g_query, g_key, g_value = split_cols(g_qkv, n_dev, (n_dev * wq_loc, n_dev * wk_loc, n_dev * wk_loc))
+        g_key = dot_tn(hidden_all, dk_all).astype(BF16)
+        g_value = dot_tn(hidden_all, dv_all).astype(BF16)
+        g_query = copy_rows(g_query)
         g_out = copy_rows(g_out)
         g_proj = transpose_rows(g_proj)
         small = lax.psum((g_pn, g_pre, g_q_gain[0], g_k_gain[0], g_post), 'cp')

time: 1330 us -> 1330 us (level)
  waiting for transfers between devices: 577 us -> 412 us
  matrix products: 296 us -> 417 us
  blocking collectives: 24.4 us -> 104 us
  Pallas kernels: 267 us -> 250 us
    dot_general x6 -> x8, matrix products: 99.1 us -> 229 us  [dot_tn(): lax.dot_general(a, b, (((0,), (0,)), ((), ())), preferred_element_type=F32)]
    all_to_all x0 -> x1, blocking collectives: none -> 80.4 us  [exchange(): return lax.all_to_all(x, 'cp', split_axis=0, concat_axis=0, tiled=True)]
    all_gather x7 -> x9, waiting for transfers between devices: 396 us -> 323 us  [gather(): return lax.all_gather(x, 'cp', axis=axis, tiled=True)]
    all_to_all x8 -> x5, waiting for transfers between devices: 138 us -> 86.4 us  [exchange(): return lax.all_to_all(x, 'cp', split_axis=0, concat_axis=0, tiled=True)]
    ppermute x5, waiting for transfers between devices: 42.8 us -> 1.28 us  [halve(): lax.ppermute(pick(1 - bits[bit]), 'cp', [(i, i ^ 4 >> bit) for i in range...]
    dot_general x3 -> x5, matrix products: 39.7 us -> 72.3 us  [dot_nt(): lax.dot_general(a, b, (((1,), (1,)), ((), ())), preferred_element_type=F32)]
    dot_general x3 -> x1, matrix products: 54.1 us -> 23.4 us  [device_step(): lax.dot_general(dq_last.reshape(-1, seq_loc), w_query, (((0,), (1,)), (()...]
    broadcast_in_dim x2 -> x0, local copies, waits for them, and re-layouts: 21.3 us -> none  [device_step(): jnp.broadcast_to(spread, (img_loc, SIDE, POOL, SIDE, POOL, dim_v))]
  transfers between devices with their start and end apart: 20 -> 19, of which waited for: 15 -> 9; matrix products, arithmetic and copies ran while one was open for 23% -> 30% of each run, Pallas kernels for 14% -> 10%
where the time goes in v7:
time: 1330 us
  matrix products  417 us (31%)
  waiting for transfers between devices  412 us (31%)
  Pallas kernels  250 us (19%)
  blocking collectives  104 us (8%)
  local copies, waits for them, and re-layouts  56.7 us (4%)
  other arithmetic  50.1 us (4%)
  starting transfers between devices  20.6 us (2%)
  between operations  14.7 us (1%)
    all_gather x9, waiting for transfers between devices, gather(): return lax.all_gather(x, 'cp', axis=axis, tiled=True)  323 us
    dot_general x8, matrix products, dot_tn(): lax.dot_general(a, b, (((0,), (0,)), ((), ())), preferred_element_type=F32)  229 us
    pallas_call x2, Pallas kernels, attn_bwd(): pl.pallas_call(functools.partial(attn_bwd_kernel, hd, part), grid_spec=pl...  97.1 us
    all_to_all x5, waiting for transfers between devices, exchange(): return lax.all_to_all(x, 'cp', split_axis=0, concat_axis=0, tiled=True)  86.4 us
    dot_general x3, matrix products, dot(): return jnp.dot(a, b, preferred_element_type=F32)  86 us
    all_to_all x1, blocking collectives, exchange(): return lax.all_to_all(x, 'cp', split_axis=0, concat_axis=0, tiled=True)  80.4 us
    dot_general x5, matrix products, dot_nt(): lax.dot_general(a, b, (((1,), (1,)), ((), ())), preferred_element_type=F32)  72.3 us
    pallas_call x2, Pallas kernels, attn_fwd(): pl.pallas_call(functools.partial(attn_fwd_kernel, hd, part), grid_spec=pl...  70.1 us
  transfers between devices with their start and end apart: 19, of which 9 were waited for; matrix products, arithmetic and copies ran while one was open for 30% of the time, Pallas kernels for 10%

profile of v7, /device:TPU:0, one launch (start us, length us, event | category | flops | bytes accessed | tf_op | source)
XLA Modules:
  0.0 1325.1 jit_solution(17583353530437459452)
XLA Ops:
  7.9 6.8 multiply_reduce_fusion
  17.8 35.3 %all-gather.10.cloned.1.call-done = bf16[2048,1152]{1,0:T(8,128)(2,1)} async-done(((bf16[256,1152]{1,0:T(8,128)(2,1)}), bf16[2048,1152]{1,0:T(8,128)(2,1)}) %all-gather.10.cloned.1.call-update) | async-done | bytes 4718608 | tf_op jit(solution)/shard_map/all_gather | solution.py:371
  53.1 15.6 %fusion.10 = (f32[512]{0:T(512)S(1)}, bf16[512,3584]{1,0:T(8,128)(2,1)}) fusion(bf16[512,3584]{1,0:T(8,128)(2,1)} %param.15, bf16[1152,3584]{1,0:T(8,128)(2,1)} %param.19, bf16[2048,1152]{1,0:T(8,128)(2,1)} %all-gather.10.cloned.1.call-done, s32[512]{0:T(512)S(1)} %broadcast_select_fusion.3, pred[512]{0:T(512)(128)(4,1)S(1)} %fusion.82), kind=kOutput, calls=%fused_computation.22 | convolution fusion | flops 6654590464 | bytes 20320768 | tf_op jit(solution)/shard_map/dot_general | solution.py:38
  69.3 5.1 fusion.7
  77.4 5.0 constant_dynamic-slice_fusion.2
  82.4 4.0 constant_dynamic-slice_fusion
  86.4 9.3 multiply_sine_fusion
  95.7 116.3 %all-gather.12.cloned.1.call-done = bf16[4096,3584]{1,0:T(8,128)(2,1)} async-done(((bf16[512,3584]{1,0:T(8,128)(2,1)}), bf16[4096,3584]{1,0:T(8,128)(2,1)}) %all-gather.12.cloned.1.call-update) | async-done | bytes 29360144 | tf_op jit(solution)/shard_map/all_gather | solution.py:371
  212.0 36.9 %convolution_convert_fusion.3.raw_ref.v_ref = bf16[4096,1024]{1,0:T(8,128)(2,1)} fusion(bf16[4096,3584]{1,0:T(8,128)(2,1)} %all-gather.12.cloned.1.call-done, bf16[3584,256]{1,0:T(8,128)(2,1)S(1)} %get-tuple-element.100, bf16[3584,256]{1,0:T(8,128)(2,1)} %get-tuple-element.101, bf16[3584,512]{1,0:T(8,128)(2,1)} %constant_dynamic-slice_fusion.2), kind=kOutput, calls=%fused_computation.18 | convolution fusion | flops 30090985472 | bytes 45088768 | tf_op jit(solution)/shard_map/dot_general | solution.py:38
  248.9 12.3 rope_fwd.1
  264.4 33.4 %attn_fwd.2 = (bf16[8,512,256]{2,1,0:T(8,128)(2,1)}, f32[8,512,256]{2,1,0:T(8,128)S(1)}, f32[8,8,512]{2,1,0:T(8,128)S(1)}) custom-call(s32[16]{0:T(128)S(1)} %fusion.89.nkb_ref, s32[16,1,256]{2,1,0:T(1,128)S(1)} %get-tuple-element.85.lim_ref, bf16[4096,512]{1,0:T(8,128)(2,1)} %get-tuple-element.40.q_ref, bf16[4096,256]{1,0:T(8,128)(2,1)S(1)} %copy-done.2, ...), custom_call_target="tpu_custom_call" | custom-call | flops 9448928256 | bytes 8388608 | tf_op jit(solution)/shard_map/attn_fwd/pallas_call | solution.py:222
  297.8 2.0 copy-done.8
  300.4 3.2 all-to-all-start
  305.3 36.7 %attn_fwd.3 = (bf16[8,512,256]{2,1,0:T(8,128)(2,1)}, f32[8,512,256]{2,1,0:T(8,128)S(1)}, f32[8,8,512]{2,1,0:T(8,128)S(1)}) custom-call(s32[16]{0:T(128)S(1)} %fusion.89.nkb_ref, s32[16,1,256]{2,1,0:T(1,128)S(1)} %get-tuple-element.85.lim_ref, bf16[4096,512]{1,0:T(8,128)(2,1)} %get-tuple-element.40.q_ref, bf16[4096,256]{1,0:T(8,128)(2,1)S(1)} %copy-done.3, ...), custom_call_target="tpu_custom_call" | custom-call | flops 9448928256 | bytes 8388608 | tf_op jit(solution)/shard_map/attn_fwd/pallas_call | solution.py:222
  342.0 2.0 copy-done.7
  344.7 14.1 %fusion.34 = (f32[256]{0:T(256)S(1)}, bf16[256,3584]{1,0:T(8,128)(2,1)S(1)}) fusion(bf16[4096,256]{1,0:T(8,128)(2,1)} %bitcast.4, bf16[4096,3584]{1,0:T(8,128)(2,1)} %param.26), kind=kOutput, calls=%fused_computation.71 | convolution fusion | flops 7519862784 | bytes 33293312 | tf_op jit(solution)/shard_map/dot_general | solution.py:46
  358.8 3.3 all-to-all-start.1
  362.2 4.3 fusion.30
  366.5 2.4 fusion.32
  368.9 15.2 %fusion.18 = bf16[4096,256]{0,1:T(8,128)(2,1)} fusion(bf16[256,3584]{1,0:T(8,128)(2,1)} %fusion.32, bf16[4096,3584]{1,0:T(8,128)(2,1)} %param.26), kind=kOutput, calls=%fused_computation.49 | convolution fusion | flops 7517241344 | bytes 33292288 | tf_op jit(solution)/shard_map/dot_general | solution.py:42
  384.0 4.1 copy.35
  388.8 14.2 %fusion.36 = (f32[256]{0:T(256)S(1)}, bf16[256,3584]{1,0:T(8,128)(2,1)S(1)}) fusion(bf16[4096,256]{1,0:T(8,128)(2,1)} %bitcast.7, bf16[4096,3584]{1,0:T(8,128)(2,1)} %param.26), kind=kOutput, calls=%fused_computation.73 | convolution fusion | flops 7519862784 | bytes 33293312 | tf_op jit(solution)/shard_map/dot_general | solution.py:46
  403.0 2.6 fusion.31
  405.6 4.7 fusion.29
  410.3 3.2 all-to-all-start.2
  413.6 15.0 %fusion.19 = bf16[4096,256]{0,1:T(8,128)(2,1)} fusion(bf16[256,3584]{1,0:T(8,128)(2,1)S(1)} %copy-done.18, bf16[4096,3584]{1,0:T(8,128)(2,1)} %param.26), kind=kOutput, calls=%fused_computation.50 | convolution fusion | flops 7517241344 | bytes 33292288 | tf_op jit(solution)/shard_map/dot_general | solution.py:42
  428.5 4.1 copy.36
  432.6 7.6 all-to-all-done.2.do_ref
  440.2 2.3 all-to-all-start.3
  442.6 45.5 %attn_bwd.2 = (bf16[2048,512]{1,0:T(8,128)(2,1)}, f32[4096,256]{1,0:T(8,128)}, f32[4096,256]{1,0:T(8,128)}) custom-call(s32[16]{0:T(128)} %copy-done.6, s32[16,1,256]{2,1,0:T(1,128)} %copy-done.1, bf16[4096,512]{1,0:T(8,128)(2,1)} %get-tuple-element.40.q_ref, bf16[4096,256]{1,0:T(8,128)(2,1)} %get-tuple-element.41.k_ref, ...), custom_call_target="tpu_custom_call" | custom-call | flops 23192823808 | bytes 12582912 | tf_op jit(solution)/shard_map/attn_bwd/pallas_call | solution.py:302
  489.4 51.6 %attn_bwd.3 = (bf16[2048,512]{1,0:T(8,128)(2,1)}, bf16[4096,256]{1,0:T(8,128)(2,1)}, bf16[4096,256]{1,0:T(8,128)(2,1)}) custom-call(s32[16]{0:T(128)} %copy-done.6, s32[16,1,256]{2,1,0:T(1,128)} %copy-done.1, bf16[4096,512]{1,0:T(8,128)(2,1)} %get-tuple-element.40.q_ref, bf16[4096,256]{1,0:T(8,128)(2,1)} %get-tuple-element.41.k_ref, ...), custom_call_target="tpu_custom_call" | custom-call | flops 23192823808 | bytes 12582912 | tf_op jit(solution)/shard_map/attn_bwd/pallas_call | solution.py:302
  541.1 15.3 %rope_bwd.1 = (bf16[4096,512]{1,0:T(8,128)(2,1)}, bf16[4096,256]{1,0:T(8,128)(2,1)}, bf16[8,512,512]{2,1,0:T(8,128)(2,1)}, f32[1,256]{1,0:T(1,128)}, f32[1,256]{1,0:T(1,128)}) custom-call(bf16[4096,1024]{1,0:T(8,128)(2,1)} %convolution_convert_fusion.3.raw_ref.v_ref, bf16[2048,512]{1,0:T(8,128)(2,1)} %get-tuple-element.51.dq0_ref, ...), custom_call_target="tpu_custom_call" | custom-call | flops 125829120 | bytes 25165824 | tf_op jit(solution)/shard_map/rope_bwd/pallas_call | solution.py:134
  557.6 80.4 %all_to_all.30 = bf16[8,512,512]{2,1,0:T(8,128)(2,1)} all-to-all(bf16[8,512,512]{2,1,0:T(8,128)(2,1)} %get-tuple-element.60), channel_id=1, replica_groups=mesh['dp'=1,'cp'=8] {'cp'}, dimensions={0} | all-to-all | bytes 8388608 | tf_op jit(solution)/shard_map/all_to_all | solution.py:376
  637.9 23.4 %fusion.93 = f32[512,3584]{1,0:T(8,128)} fusion(bf16[4096,512]{1,0:T(8,128)(2,1)} %bitcast.91, bf16[3584,4096]{1,0:T(8,128)(2,1)} %param.21), kind=kOutput, calls=%fused_computation.187 | convolution fusion | flops 15032385536 | bytes 40894464 | tf_op jit(solution)/shard_map/dot_general | solution.py:481
  661.4 8.8 all-gather.14.cloned.1.call-done
  670.2 13.5 %fusion.50 = f32[512,3584]{1,0:T(8,128)} fusion(bf16[3584,2048]{1,0:T(8,128)(2,1)} %param.23, bf16[4096,2048]{1,0:T(8,128)(2,1)} %all-gather.14.cloned.1.call-done, s32[]{:T(128)S(6)} %select_n.124), kind=kOutput, calls=%fused_computation.89 | convolution fusion | flops 7516192768 | bytes 24117252 | tf_op jit(solution)/shard_map/dot_general | solution.py:42
  683.7 76.2 %all-gather.16.cloned.1.call-done = bf16[4096,2048]{1,0:T(8,128)(2,1)} async-done(((bf16[4096,256]{1,0:T(8,128)(2,1)}), bf16[4096,2048]{1,0:T(8,128)(2,1)}) %all-gather.16.cloned.1.call-update) | async-done | bytes 16777232 | tf_op jit(solution)/shard_map/all_gather | solution.py:371
  760.0 19.3 %fusion.8 = (f32[3584]{0:T(1024)}, f32[512]{0:T(512)S(1)}, bf16[512,3584]{1,0:T(8,128)(2,1)}) fusion(bf16[512,3584]{1,0:T(8,128)(2,1)} %get-tuple-element.94, f32[512]{0:T(512)S(1)} %copy-done.31, f32[3584]{0:T(1024)S(1)} %copy-done.23, bf16[3584,2048]{1,0:T(8,128)(2,1)} %param.22, bf16[4096,2048]{1,0:T(8,128)(2,1)} %all-gather.16.cloned.1.call-done, ...), kind=kOutput, calls=%fused_computation.20 | convolution fusion | flops 7536373760 | bytes 38830084 | tf_op jit(solution)/shard_map/dot_general | solution.py:42
  779.3 8.1 fusion.55
  787.3 5.9 copy.37
  793.2 3.5 all-to-all-start.5
  796.8 78.1 %all-to-all-done.5 = bf16[8,448,512]{2,1,0:T(8,128)(2,1)} async-done(((bf16[8,448,512]{2,1,0:T(8,128)(2,1)}), bf16[8,448,512]{2,1,0:T(8,128)(2,1)}, u32[]{:S(2)}, u32[]{:S(2)}) %all-to-all-start.5) | async-done | bytes 3670048 | tf_op jit(solution)/shard_map/all_to_all | solution.py:376
  874.9 4.4 copy.41
  879.3 33.4 %fusion.39 = bf16[448,1152]{1,0:T(8,128)(2,1)} fusion(bf16[448,4096]{1,0:T(8,128)(2,1)} %bitcast.92, bf16[2048,1152]{1,0:T(8,128)(2,1)} %all-gather.10.cloned.1.call-done, s32[4096]{0:T(1024)S(1)} %broadcast_add_fusion), kind=kOutput, calls=%fused_computation.82 | convolution fusion | flops 23568834560 | bytes 9437184 | tf_op jit(solution)/shard_map/dot_general | solution.py:38
  912.8 23.3 %convolution_convert_fusion.4 = bf16[3584,512]{1,0:T(8,128)(2,1)} fusion(bf16[4096,3584]{1,0:T(8,128)(2,1)} %all-gather.12.cloned.1.call-done, bf16[4096,512]{1,0:T(8,128)(2,1)} %get-tuple-element.64), kind=kOutput, calls=%fused_computation.40 | convolution fusion | flops 15034220544 | bytes 37224448 | tf_op jit(solution)/shard_map/dot_general | solution.py:46
  936.2 3.9 copy.39
  940.1 2.9 copy.40
  943.0 13.6 %fusion.94 = f32[512,3584]{1,0:T(8,128)} fusion(bf16[2048,512]{1,0:T(8,128)(2,1)} %bitcast.94, bf16[2048,3584]{1,0:T(8,128)(2,1)} %all-gather.22.cloned.1.call-done), kind=kOutput, calls=%fused_computation.188 | convolution fusion | flops 7516192768 | bytes 24117248 | tf_op jit(solution)/shard_map/dot_general | solution.py:46
  956.7 16.2 %add_convert_fusion = bf16[512,3584]{1,0:T(8,128)(2,1)} fusion(f32[512,3584]{1,0:T(8,128)} %fusion.94, bf16[2048,512]{1,0:T(8,128)(2,1)S(1)} %bitcast.93, bf16[2048,3584]{1,0:T(8,128)(2,1)} %all-gather.24.cloned.1.call-done), kind=kOutput, calls=%fused_computation.29 | convolution fusion | flops 7519862784 | bytes 27787264 | tf_op jit(solution)/shard_map/dot_general | solution.py:46
  972.9 9.4 convolution_convert_fusion.10
  982.3 3.8 convolution_convert_fusion.2
  986.2 2.2 copy-done.19
  990.6 3.7 pad_maximum_fusion
  999.5 71.3 %convolution_convert_fusion.1 = bf16[3584,2048]{1,0:T(8,128)(2,1)} fusion(bf16[4096,3584]{1,0:T(8,128)(2,1)} %all-gather.12.cloned.1.call-done, bf16[4096,2048]{1,0:T(8,128)(2,1)} %all-gather.16.cloned.1.call-done), kind=kOutput, calls=%fused_computation.5 | convolution fusion | flops 60136882176 | bytes 60817408 | tf_op jit(solution)/shard_map/dot_general | solution.py:46
  1071.5 2.0 collective-permute-start.4
  1073.5 72.1 %convolution_convert_fusion = bf16[3584,2048]{1,0:T(8,128)(2,1)} fusion(bf16[4096,3584]{1,0:T(8,128)(2,1)} %all-gather.12.cloned.1.call-done, bf16[4096,2048]{1,0:T(8,128)(2,1)} %all-gather.14.cloned.1.call-done), kind=kOutput, calls=%fused_computation.4 | convolution fusion | flops 60136882176 | bytes 60817408 | tf_op jit(solution)/shard_map/dot_general | solution.py:46
  1147.7 2.1 broadcast_select_fusion.1
  1149.8 8.2 copy_out.4
  1158.0 23.9 %all-reduce = (bf16[1152]{0:T(1024)(128)(2,1)}, bf16[3584]{0:T(1024)(128)(2,1)}, bf16[256]{0:T(256)(128)(2,1)}, bf16[256]{0:T(256)(128)(2,1)}, bf16[3584]{0:T(1024)(128)(2,1)}) all-reduce(f32[1152]{0:T(1024)S(1)} %get-tuple-element.73, f32[3584]{0:T(1024)S(1)} %copy-done.34, ...), channel_id=1, replica_groups=mesh['dp'=1,'cp'=8] {'cp'}, use_global_device_ids=true, to_apply=%region_13.14 | all-reduce | flops 8832 | bytes 52992 | tf_op jit(solution)/shard_map/psum | solution.py:507
  1182.0 3.3 copy-done
  1185.3 5.5 copy_out.5
  1190.8 21.1 %copy_out.6 = bf16[3584,4096]{1,0:T(8,128)(2,1)} custom-call(bf16[3584,4096]{1,0:T(8,128)(2,1)} %all-gather.20.cloned.1.call-done.x_ref), custom_call_target="tpu_custom_call" | custom-call | flops 14680064 | bytes 58720256 | tf_op jit(solution)/shard_map/copy_out/pallas_call | solution.py:328
  1211.9 86.0 %all-gather.26.cloned.1.call-done.x_ref = bf16[4096,3584]{1,0:T(8,128)(2,1)} async-done(((bf16[512,3584]{1,0:T(8,128)(2,1)}), bf16[4096,3584]{1,0:T(8,128)(2,1)}) %all-gather.26.cloned.1.call-update) | async-done | bytes 29360144 | tf_op jit(solution)/shard_map/all_gather | solution.py:371
  1297.9 20.5 %copy_out.7 = bf16[4096,3584]{1,0:T(8,128)(2,1)} custom-call(bf16[4096,3584]{1,0:T(8,128)(2,1)} %all-gather.26.cloned.1.call-done.x_ref), custom_call_target="tpu_custom_call" | custom-call | flops 14680064 | bytes 58720256 | tf_op jit(solution)/shard_map/copy_out/pallas_call | solution.py:328
  (173 shorter events, 26.9 us)
Async XLA Ops:
  7.2 45.9 %all-gather.10.cloned.1.call-start = ((), (), s32[]{:S(2)}) async-start(), calls=%async_computation.6 | async-start | bytes 5308416 | tf_op jit(solution)/shard_map/all_gather | solution.py:371
  7.9 7.4 copy-start.24
  7.9 9.6 copy-start.42
  7.9 9.8 copy-start.38
  14.8 1.1 copy-start.15
  16.9 195.1 %all-gather.12.cloned.1.call-start = ((), (), s32[]{:S(2)}) async-start(), calls=%async_computation.7 | async-start | bytes 33030144 | tf_op jit(solution)/shard_map/all_gather | solution.py:371
  17.6 51.1 %copy-start.35 = (pred[512]{0:T(512)(128)(4,1)}, pred[512]{0:T(512)(128)(4,1)S(1)}, u32[]{:S(2)}) copy-start(pred[512]{0:T(512)(128)(4,1)S(1)} %fusion.82) | copy-start | bytes 1540
  17.7 51.0 %copy-start.45 = (s32[512]{0:T(512)}, s32[512]{0:T(512)S(1)}, u32[]{:S(2)}) copy-start(s32[512]{0:T(512)S(1)} %broadcast_select_fusion.3) | copy-start | bytes 6148
  17.8 51.0 %copy-start.22 = (f32[3584]{0:T(1024)}, f32[3584]{0:T(1024)S(1)}, u32[]{:S(2)}) copy-start(f32[3584]{0:T(1024)S(1)} %convert_add_fusion.1) | copy-start | bytes 43012
  68.7 5.7 copy-start.40
  74.4 1.2 copy-start.50
  77.4 226.3 %copy-start.1 = (s32[16,1,256]{2,1,0:T(1,128)}, s32[16,1,256]{2,1,0:T(1,128)S(1)}, u32[]{:S(2)}) copy-start(s32[16,1,256]{2,1,0:T(1,128)S(1)} %get-tuple-element.85.lim_ref) | copy-start | bytes 49156
  77.4 226.3 %copy-start.6 = (s32[16]{0:T(128)}, s32[16]{0:T(128)S(1)}, u32[]{:S(2)}) copy-start(s32[16]{0:T(128)S(1)} %fusion.89.nkb_ref) | copy-start | bytes 196
  261.2 1.6 copy-start.2
  262.8 1.6 copy-start.4
  297.8 2.0 copy-start.8
  300.4 3.2 copy-start.39
  300.4 3.3 copy-start.3
  300.4 44.2 %all-to-all-start = ((bf16[8,512,256]{2,1,0:T(8,128)(2,1)}), bf16[8,512,256]{2,1,0:T(8,128)(2,1)}, u32[]{:S(2)}, u32[]{:S(2)}) async-start(bf16[8,512,256]{2,1,0:T(8,128)(2,1)} %get-tuple-element.43), calls=%async_computation | async-start | bytes 4194304 | tf_op jit(solution)/shard_map/all_to_all | solution.py:376
  303.7 1.6 copy-start.5
  342.0 2.0 copy-start.7
  358.8 29.9 %all-to-all-start.1 = ((bf16[8,512,256]{2,1,0:T(8,128)(2,1)}), bf16[8,512,256]{2,1,0:T(8,128)(2,1)}, u32[]{:S(2)}, u32[]{:S(2)}) async-start(bf16[8,512,256]{2,1,0:T(8,128)(2,1)} %get-tuple-element.45), calls=%async_computation.1 | async-start | bytes 4194304 | tf_op jit(solution)/shard_map/all_to_all | solution.py:376
  362.1 4.3 copy-start.11
  388.8 14.2 %copy-start.12 = (bf16[512,3584]{1,0:T(8,128)(2,1)S(1)}, bf16[512,3584]{1,0:T(8,128)(2,1)}, u32[]{:S(2)}) copy-start(bf16[512,3584]{1,0:T(8,128)(2,1)} %param.17) | copy-start | bytes 11010052
  403.0 2.7 copy-start.13
  410.3 3.2 copy-start.18
  410.3 29.8 %all-to-all-start.2 = ((bf16[8,512,256]{2,1,0:T(8,128)(2,1)}), bf16[8,512,256]{2,1,0:T(8,128)(2,1)}, u32[]{:S(2)}, u32[]{:S(2)}) async-start(bf16[8,512,256]{2,1,0:T(8,128)(2,1)} %bitcast.88), calls=%async_computation.2 | async-start | bytes 4194304 | tf_op jit(solution)/shard_map/all_to_all | solution.py:376
  440.2 47.9 %all-to-all-start.3 = ((bf16[8,512,256]{2,1,0:T(8,128)(2,1)}), bf16[8,512,256]{2,1,0:T(8,128)(2,1)S(1)}, u32[]{:S(2)}, u32[]{:S(2)}) async-start(bf16[8,512,256]{2,1,0:T(8,128)(2,1)} %bitcast.9), calls=%async_computation.3 | async-start | bytes 4194304 | tf_op jit(solution)/shard_map/all_to_all | solution.py:376
  442.5 227.7 %all-gather.14.cloned.1.call-start = ((), (), s32[]{:S(2)}) async-start(), calls=%async_computation.8 | async-start | bytes 18874368 | tf_op jit(solution)/shard_map/all_gather | solution.py:371
  488.1 1.3 copy-start.21
  541.0 218.9 %all-gather.16.cloned.1.call-start = ((), (), s32[]{:S(2)}) async-start(), calls=%async_computation.9 | async-start | bytes 18874368 | tf_op jit(solution)/shard_map/all_gather | solution.py:371
  556.4 386.6 %all-gather.22.cloned.1.call-start = ((), (), s32[]{:S(2)}) async-start(), calls=%async_computation.12 | async-start | bytes 16515072 | tf_op jit(solution)/shard_map/all_gather | solution.py:371
  557.0 399.7 %all-gather.24.cloned.1.call-start = ((), (), s32[]{:S(2)}) async-start(), calls=%async_computation.13 | async-start | bytes 16515072 | tf_op jit(solution)/shard_map/all_gather | solution.py:371
  661.4 98.6 %copy-start.23 = (f32[3584]{0:T(1024)S(1)}, f32[3584]{0:T(1024)}, u32[]{:S(2)}) copy-start(f32[3584]{0:T(1024)} %copy-done.22) | copy-start | bytes 43012
  661.4 98.6 %copy-start.31 = (f32[512]{0:T(512)S(1)}, f32[512]{0:T(512)}, u32[]{:S(2)}) copy-start(f32[512]{0:T(512)} %copy-done.30) | copy-start | bytes 6148
  683.7 95.5 %copy-start.41 = (f32[512]{0:T(512)S(1)}, f32[512]{0:T(512)}, u32[]{:S(2)}) copy-start(f32[512]{0:T(512)} %copy-done.40) | copy-start | bytes 6148
  683.7 95.5 %copy-start.36 = (pred[512]{0:T(512)(128)(4,1)S(1)}, pred[512]{0:T(512)(128)(4,1)}, u32[]{:S(2)}) copy-start(pred[512]{0:T(512)(128)(4,1)} %copy-done.35) | copy-start | bytes 1540
  793.2 3.6 copy-start.29
  793.2 81.7 %all-to-all-start.5 = ((bf16[8,448,512]{2,1,0:T(8,128)(2,1)}), bf16[8,448,512]{2,1,0:T(8,128)(2,1)}, u32[]{:S(2)}, u32[]{:S(2)}) async-start(bf16[8,448,512]{2,1,0:T(8,128)(2,1)} %bitcast.86), calls=%async_computation.5 | async-start | bytes 7340032 | tf_op jit(solution)/shard_map/all_to_all | solution.py:376
  796.7 385.2 %all-gather.18.cloned.1.call-start = ((), (), s32[]{:S(2)}) async-start(), calls=%async_computation.10 | async-start | bytes 9289728 | tf_op jit(solution)/shard_map/all_gather | solution.py:371
  912.8 278.0 %all-gather.20.cloned.1.call-start = ((), (), s32[]{:S(2)}) async-start(), calls=%async_computation.11 | async-start | bytes 33030144 | tf_op jit(solution)/shard_map/all_gather | solution.py:371
  936.2 361.7 %all-gather.26.cloned.1.call-start = ((), (), s32[]{:S(2)}) async-start(), calls=%async_computation.14 | async-start | bytes 33030144 | tf_op jit(solution)/shard_map/all_gather | solution.py:371
  972.9 9.4 copy-start.46
  986.1 2.3 copy-start.19
  986.1 3.9 copy-start.26
  986.1 3.9 copy-start.27
  986.1 4.5 copy-start.17
  990.0 5.6 collective-permute-start
  990.6 5.0 copy-start.20
  997.8 73.5 %collective-permute-start.3 = (bf16[2,256,640]{2,1,0:T(8,128)(2,1)S(1)}, bf16[2,256,640]{2,1,0:T(8,128)(2,1)S(1)}, u32[]{:S(2)}, u32[]{:S(2)}) collective-permute-start(bf16[2,256,640]{2,1,0:T(8,128)(2,1)S(1)} %dynamic-slice_bitcast_fusion.1), channel_id=1, source_target_pairs={{0,4},{1,5},{2,6},{3,7},{4,0},{5,1},{6,2},{7,3}} | collective-permute-start | bytes 1966088 | tf_op jit(solution)/shard_map/ppermute | solution.py:383
  998.0 72.7 %collective-permute-start.1 = (bf16[2,256,512]{2,1,0:T(8,128)(2,1)S(1)}, bf16[2,256,512]{2,1,0:T(8,128)(2,1)S(1)}, u32[]{:S(2)}, u32[]{:S(2)}) collective-permute-start(bf16[2,256,512]{2,1,0:T(8,128)(2,1)S(1)} %dynamic-slice_bitcast_fusion.2), channel_id=1, source_target_pairs={{0,2},{1,3},{2,0},{3,1},{4,6},{5,7},{6,4},{7,5}} | collective-permute-start | bytes 1572872 | tf_op jit(solution)/shard_map/ppermute | solution.py:383
  1070.8 74.8 %collective-permute-start.2 = (bf16[256,512]{1,0:T(8,128)(2,1)S(1)}, bf16[256,512]{1,0:T(8,128)(2,1)S(1)}, u32[]{:S(2)}, u32[]{:S(2)}) collective-permute-start(bf16[256,512]{1,0:T(8,128)(2,1)S(1)} %dynamic-slice_bitcast_fusion.4), channel_id=1, source_target_pairs={{0,4},{1,5},{2,6},{3,7},{4,0},{5,1},{6,2},{7,3}} | collective-permute-start | bytes 786440 | tf_op jit(solution)/shard_map/ppermute | solution.py:383
  1071.5 74.3 %copy-start.16 = (f32[256,1152]{1,0:T(8,128)S(1)}, f32[256,1152]{1,0:T(8,128)}, u32[]{:S(2)}) copy-start(f32[256,1152]{1,0:T(8,128)} %copy-done.15) | copy-start | bytes 3538948
  1071.5 74.3 %copy-start.25 = (f32[1152]{0:T(1024)S(1)}, f32[1152]{0:T(1024)}, u32[]{:S(2)}) copy-start(f32[1152]{0:T(1024)} %copy-done.24) | copy-start | bytes 13828
  1071.5 74.3 %copy-start.33 = (f32[256]{0:T(256)S(1)}, f32[256]{0:T(256)}, u32[]{:S(2)}) copy-start(f32[256]{0:T(256)} %copy-done.32) | copy-start | bytes 3076
  1071.5 74.7 %copy-start.44 = (f32[256]{0:T(256)S(1)}, f32[256]{0:T(256)}, u32[]{:S(2)}) copy-start(f32[256]{0:T(256)} %copy-done.43) | copy-start | bytes 3076
  1071.5 74.2 %collective-permute-start.4 = (bf16[256,640]{1,0:T(8,128)(2,1)S(1)}, bf16[256,640]{1,0:T(8,128)(2,1)S(1)}, u32[]{:S(2)}, u32[]{:S(2)}) collective-permute-start(bf16[256,640]{1,0:T(8,128)(2,1)S(1)} %dynamic-slice_bitcast_fusion.3), channel_id=1, source_target_pairs={{0,2},{1,3},{2,0},{3,1},{4,6},{5,7},{6,4},{7,5}} | collective-permute-start | bytes 983048 | tf_op jit(solution)/shard_map/ppermute | solution.py:383
  1145.6 2.0 copy-start.14
  1145.6 2.0 copy-start.37
  1149.8 8.2 copy-start.28
  1149.8 8.2 copy-start.34
  1149.8 8.2 copy-start.47
  1149.8 8.2 copy-start.48
  1182.0 3.3 copy-start
  (6 other events, 3.7 us)
Sparse Core Ops, SparseCore 0:
  17.0 36.0 all-gather.9
  74.6 137.3 all-gather.11
  541.1 129.0 all-gather.13
  672.4 87.4 all-gather.15
  761.6 109.4 all-gather.21
  872.8 80.4 all-gather.23
  955.7 49.3 all-gather.17
  1007.4 150.3 all-gather.19
  1159.7 138.1 all-gather.25

commit v8 on v6

--- a/solution.py
+++ b/solution.py
@@ -343,7 +343,7 @@
         out_specs=out_specs,
         out_shape=[jax.ShapeDtypeStruct(shape, x.dtype) for shape in shapes],
         cost_estimate=pl.CostEstimate(flops=x.size, bytes_accessed=4 * x.size, transcendentals=0),
-        compiler_params=pltpu.CompilerParams(vmem_limit_bytes=40 * 1024 * 1024),
+        compiler_params=pltpu.CompilerParams(vmem_limit_bytes=60 * 1024 * 1024),
         name="copy_out",
     )(x)
 
@@ -357,6 +357,20 @@
 def copy_rows(x):
     spec = pl.BlockSpec((512, x.shape[1]), lambda i: (i, 0))
     return stream(copy_kernel, x, spec, [x.shape], [spec], x.shape[0] // 512)[0]
+
+
+def spread_kernel(x_ref, o_ref):
+    cell, col = (lax.broadcasted_iota(jnp.int32, (GRID, SIDE), d) for d in (0, 1))
+    y = dot((cell // POOL == col).astype(BF16), x_ref[...]).astype(BF16)
+    for t in range(POOL):
+        o_ref[t * GRID:(t + 1) * GRID, :] = y
+
+
+def spread_rows(x):
+    cols = x.shape[1]
+    step = GRID * POOL
+    n = x.shape[0] // SIDE
+    return stream(spread_kernel, x, pl.BlockSpec((SIDE, cols), lambda i: (i, 0)), [(n * step, cols)], [pl.BlockSpec((step, cols), lambda i: (i, 0))], n)[0]
 
 
 def transpose_rows(x):
@@ -493,8 +507,7 @@
         d_normed_all = dot_tn(select, d_normed_rows).astype(BF16)
         d_normed = reduce_to_owner(d_normed_all, rank)
         d_pooled, g_pn = norm_pull(d_normed)
-        spread = (d_pooled.astype(F32) / (POOL * POOL)).astype(BF16).reshape(img_loc, SIDE, 1, SIDE, 1, dim_v)
-        grad_vis = jnp.broadcast_to(spread, (img_loc, SIDE, POOL, SIDE, POOL, dim_v)).reshape(img_loc, patches, dim_v)
+        grad_vis = spread_rows((d_pooled.astype(F32) / (POOL * POOL)).astype(BF16)).reshape(img_loc, patches, dim_v)
 
         d_soft_t = exchange(d_soft_rows.T.reshape(n_dev, d_model // n_dev, seq_loc), dv_last)
         normed_pos = dot(select_all, normed_all).astype(BF16).reshape(n_dev, seq_loc, dim_v)

time: 1330 us -> 1330 us (level)
  local copies, waits for them, and re-layouts: 69.9 us -> 46.8 us
  Pallas kernels: 267 us -> 282 us
    broadcast_in_dim x2 -> x0, local copies, waits for them, and re-layouts: 21.3 us -> none  [device_step(): jnp.broadcast_to(spread, (img_loc, SIDE, POOL, SIDE, POOL, dim_v))]
    pallas_call x3 -> x4, Pallas kernels: 69.5 us -> 84.7 us  [stream(): pl.pallas_call(body, grid=(grid,), in_specs=[in_spec], out_specs=out_spec...]
  transfers between devices with their start and end apart: 20 -> 20, of which waited for: 15 -> 15; matrix products, arithmetic and copies ran while one was open for 23% -> 22% of each run, Pallas kernels for 14% -> 15%
where the time goes in v8:
time: 1330 us
  waiting for transfers between devices  584 us (44%)
  matrix products  297 us (22%)
  Pallas kernels  282 us (21%)
  other arithmetic  49.6 us (4%)
  local copies, waits for them, and re-layouts  46.8 us (4%)
  starting transfers between devices  28.5 us (2%)
  blocking collectives  24.6 us (2%)
  between operations  15.2 us (1%)
    all_gather x7, waiting for transfers between devices, gather(): return lax.all_gather(x, 'cp', axis=axis, tiled=True)  398 us
    all_to_all x8, waiting for transfers between devices, exchange(): return lax.all_to_all(x, 'cp', split_axis=0, concat_axis=0, tiled=True)  138 us
    dot_general x6, matrix products, dot_tn(): lax.dot_general(a, b, (((0,), (0,)), ((), ())), preferred_element_type=F32)  99.1 us
    pallas_call x2, Pallas kernels, attn_bwd(): pl.pallas_call(functools.partial(attn_bwd_kernel, hd, part), grid_spec=pl...  97.1 us
    dot_general x11, matrix products, dot(): return jnp.dot(a, b, preferred_element_type=F32)  96.7 us
    pallas_call x4, Pallas kernels, stream(): pl.pallas_call(body, grid=(grid,), in_specs=[in_spec], out_specs=out_spec...  84.7 us
    pallas_call x2, Pallas kernels, attn_fwd(): pl.pallas_call(functools.partial(attn_fwd_kernel, hd, part), grid_spec=pl...  70.1 us
    dot_general x3, matrix products, device_step(): lax.dot_general(d, w, (((0,), (1,)), ((), ())), preferred_element_type=F32)  54.1 us
  transfers between devices with their start and end apart: 20, of which 15 were waited for; matrix products, arithmetic and copies ran while one was open for 22% of the time, Pallas kernels for 15%

profile of v8, /device:TPU:0, one launch (start us, length us, event | category | flops | bytes accessed | tf_op | source)
XLA Modules:
  0.0 1327.2 jit_solution(9417665612262343626)
XLA Ops:
  7.9 6.8 multiply_reduce_fusion
  17.7 35.3 %all-gather.8.cloned.1.call-done = bf16[2048,1152]{1,0:T(8,128)(2,1)} async-done(((bf16[256,1152]{1,0:T(8,128)(2,1)}), bf16[2048,1152]{1,0:T(8,128)(2,1)}) %all-gather.8.cloned.1.call-update) | async-done | bytes 4718608 | tf_op jit(solution)/shard_map/all_gather | solution.py:388
  53.1 15.6 %fusion.10 = (f32[512]{0:T(512)S(1)}, bf16[512,3584]{1,0:T(8,128)(2,1)}) fusion(bf16[512,3584]{1,0:T(8,128)(2,1)} %param.15, bf16[1152,3584]{1,0:T(8,128)(2,1)} %param.19, bf16[2048,1152]{1,0:T(8,128)(2,1)} %all-gather.8.cloned.1.call-done, s32[512]{0:T(512)S(1)} %broadcast_select_fusion.3, pred[512]{0:T(512)(128)(4,1)S(1)} %fusion.87), kind=kOutput, calls=%fused_computation.21 | convolution fusion | flops 6654590464 | bytes 20320768 | tf_op jit(solution)/shard_map/dot_general | solution.py:38
  69.3 5.1 fusion.7
  77.3 5.0 constant_dynamic-slice_fusion.2
  82.3 4.0 constant_dynamic-slice_fusion
  86.3 9.3 multiply_sine_fusion
  95.6 116.3 %all-gather.10.cloned.1.call-done = bf16[4096,3584]{1,0:T(8,128)(2,1)} async-done(((bf16[512,3584]{1,0:T(8,128)(2,1)}), bf16[4096,3584]{1,0:T(8,128)(2,1)}) %all-gather.10.cloned.1.call-update) | async-done | bytes 29360144 | tf_op jit(solution)/shard_map/all_gather | solution.py:388
  211.9 36.9 %convolution_convert_fusion.2.raw_ref.v_ref = bf16[4096,1024]{1,0:T(8,128)(2,1)} fusion(bf16[4096,3584]{1,0:T(8,128)(2,1)} %all-gather.10.cloned.1.call-done, bf16[3584,256]{1,0:T(8,128)(2,1)S(1)} %get-tuple-element.112, bf16[3584,256]{1,0:T(8,128)(2,1)} %get-tuple-element.113, bf16[3584,512]{1,0:T(8,128)(2,1)} %constant_dynamic-slice_fusion.2), kind=kOutput, calls=%fused_computation.17 | convolution fusion | flops 30090985472 | bytes 45088768 | tf_op jit(solution)/shard_map/dot_general | solution.py:38
  248.9 12.3 rope_fwd.1
  264.3 33.4 %attn_fwd.2 = (bf16[8,512,256]{2,1,0:T(8,128)(2,1)}, f32[8,512,256]{2,1,0:T(8,128)S(1)}, f32[8,8,512]{2,1,0:T(8,128)S(1)}) custom-call(s32[16]{0:T(128)S(1)} %fusion.92.nkb_ref, s32[16,1,256]{2,1,0:T(1,128)S(1)} %get-tuple-element.97.lim_ref, bf16[4096,512]{1,0:T(8,128)(2,1)} %get-tuple-element.46.q_ref, bf16[4096,256]{1,0:T(8,128)(2,1)S(1)} %copy-done.1, ...), custom_call_target="tpu_custom_call" | custom-call | flops 9448928256 | bytes 8388608 | tf_op jit(solution)/shard_map/attn_fwd/pallas_call | solution.py:223
  302.2 26.5 %all-to-all-done = bf16[8,512,256]{2,1,0:T(8,128)(2,1)S(1)} async-done(((bf16[8,512,256]{2,1,0:T(8,128)(2,1)}), bf16[8,512,256]{2,1,0:T(8,128)(2,1)S(1)}, u32[]{:S(2)}, u32[]{:S(2)}) %all-to-all-start) | async-done | bytes 2097184 | tf_op jit(solution)/shard_map/all_to_all | solution.py:393
  328.7 13.9 %fusion.33 = (f32[256]{0:T(256)S(1)}, bf16[256,3584]{1,0:T(8,128)(2,1)S(1)}) fusion(bf16[4096,256]{1,0:T(8,128)(2,1)S(1)} %bitcast.109, bf16[4096,3584]{1,0:T(8,128)(2,1)} %param.26), kind=kOutput, calls=%fused_computation.68 | convolution fusion | flops 7519862784 | bytes 33293312 | tf_op jit(solution)/shard_map/dot_general | solution.py:46
  342.7 2.6 fusion.29
  349.3 36.8 %attn_fwd.3 = (bf16[8,512,256]{2,1,0:T(8,128)(2,1)}, f32[8,512,256]{2,1,0:T(8,128)S(1)}, f32[8,8,512]{2,1,0:T(8,128)S(1)}) custom-call(s32[16]{0:T(128)S(1)} %fusion.92.nkb_ref, s32[16,1,256]{2,1,0:T(1,128)S(1)} %get-tuple-element.97.lim_ref, bf16[4096,512]{1,0:T(8,128)(2,1)} %get-tuple-element.46.q_ref, bf16[4096,256]{1,0:T(8,128)(2,1)S(1)} %copy-done.2, ...), custom_call_target="tpu_custom_call" | custom-call | flops 9448928256 | bytes 8388608 | tf_op jit(solution)/shard_map/attn_fwd/pallas_call | solution.py:223
  388.8 2.6 all-to-all-start.1
  391.3 15.2 %fusion.18 = bf16[4096,256]{0,1:T(8,128)(2,1)} fusion(bf16[256,3584]{1,0:T(8,128)(2,1)} %fusion.31, bf16[4096,3584]{1,0:T(8,128)(2,1)} %param.26), kind=kOutput, calls=%fused_computation.47 | convolution fusion | flops 7517241344 | bytes 33292288 | tf_op jit(solution)/shard_map/dot_general | solution.py:42
  406.6 3.9 copy.34
  410.5 30.2 %all-to-all-done.1 = bf16[8,512,256]{2,1,0:T(8,128)(2,1)S(1)} async-done(((bf16[8,512,256]{2,1,0:T(8,128)(2,1)}), bf16[8,512,256]{2,1,0:T(8,128)(2,1)S(1)}, u32[]{:S(2)}, u32[]{:S(2)}) %all-to-all-start.1) | async-done | bytes 2097184 | tf_op jit(solution)/shard_map/all_to_all | solution.py:393
  440.7 3.1 all-to-all-start.2
  443.9 13.9 %fusion.35 = (f32[256]{0:T(256)S(1)}, bf16[256,3584]{1,0:T(8,128)(2,1)S(1)}) fusion(bf16[4096,256]{1,0:T(8,128)(2,1)S(1)} %bitcast.108, bf16[4096,3584]{1,0:T(8,128)(2,1)} %param.26), kind=kOutput, calls=%fused_computation.70 | convolution fusion | flops 7519862784 | bytes 33293312 | tf_op jit(solution)/shard_map/dot_general | solution.py:46
  457.8 2.6 fusion.30
  460.5 4.3 fusion.28
  464.7 15.1 %fusion.19 = bf16[4096,256]{0,1:T(8,128)(2,1)S(1)} fusion(bf16[256,3584]{1,0:T(8,128)(2,1)} %get-tuple-element.100, bf16[4096,3584]{1,0:T(8,128)(2,1)} %param.26), kind=kOutput, calls=%fused_computation.48 | convolution fusion | flops 7517241344 | bytes 33292288 | tf_op jit(solution)/shard_map/dot_general | solution.py:42
  479.8 2.5 copy.35
  482.3 2.8 all-to-all-start.3
  485.2 45.5 %attn_bwd.2 = (bf16[2048,512]{1,0:T(8,128)(2,1)}, f32[4096,256]{1,0:T(8,128)}, f32[4096,256]{1,0:T(8,128)}) custom-call(s32[16]{0:T(128)} %copy-done.5, s32[16,1,256]{2,1,0:T(1,128)} %copy-done, bf16[4096,512]{1,0:T(8,128)(2,1)} %get-tuple-element.46.q_ref, bf16[4096,256]{1,0:T(8,128)(2,1)} %get-tuple-element.47.k_ref, ...), custom_call_target="tpu_custom_call" | custom-call | flops 23192823808 | bytes 12582912 | tf_op jit(solution)/shard_map/attn_bwd/pallas_call | solution.py:303
  532.0 51.6 %attn_bwd.3 = (bf16[2048,512]{1,0:T(8,128)(2,1)}, bf16[4096,256]{1,0:T(8,128)(2,1)}, bf16[4096,256]{1,0:T(8,128)(2,1)}) custom-call(s32[16]{0:T(128)} %copy-done.5, s32[16,1,256]{2,1,0:T(1,128)} %copy-done, bf16[4096,512]{1,0:T(8,128)(2,1)} %get-tuple-element.46.q_ref, bf16[4096,256]{1,0:T(8,128)(2,1)} %get-tuple-element.47.k_ref, ...), custom_call_target="tpu_custom_call" | custom-call | flops 23192823808 | bytes 12582912 | tf_op jit(solution)/shard_map/attn_bwd/pallas_call | solution.py:303
  583.6 17.8 %rope_bwd.1 = (bf16[4096,1024]{1,0:T(8,128)(2,1)}, bf16[8,512,512]{2,1,0:T(8,128)(2,1)}, bf16[8,256,512]{2,1,0:T(8,128)(2,1)}, bf16[8,256,512]{2,1,0:T(8,128)(2,1)}, f32[1,256]{1,0:T(1,128)}, /*index=5*/f32[1,256]{1,0:T(1,128)}) custom-call(bf16[4096,1024]{1,0:T(8,128)(2,1)} %convolution_convert_fusion.2.raw_ref.v_ref, ...), custom_call_target="tpu_custom_call" | custom-call | flops 125829120 | bytes 25165824 | tf_op jit(solution)/shard_map/rope_bwd/pallas_call | solution.py:135
  601.5 3.3 all-to-all-start.4
  604.8 49.1 %all-to-all-done.4 = bf16[8,512,512]{2,1,0:T(8,128)(2,1)} async-done(((bf16[8,512,512]{2,1,0:T(8,128)(2,1)}), bf16[8,512,512]{2,1,0:T(8,128)(2,1)}, u32[]{:S(2)}, u32[]{:S(2)}) %all-to-all-start.4) | async-done | bytes 4194336 | tf_op jit(solution)/shard_map/all_to_all | solution.py:393
  656.3 23.4 %fusion.96 = f32[512,3584]{1,0:T(8,128)} fusion(bf16[4096,512]{1,0:T(8,128)(2,1)} %bitcast.10, bf16[3584,4096]{1,0:T(8,128)(2,1)} %param.21), kind=kOutput, calls=%fused_computation.203 | convolution fusion | flops 15032385536 | bytes 40894464 | tf_op jit(solution)/shard_map/dot_general | solution.py:499
  679.7 3.1 all-to-all-done.5
  682.8 3.3 all-to-all-start.6
  686.1 13.0 fusion.97
  699.1 13.6 %all-to-all-done.6 = bf16[8,256,512]{2,1,0:T(8,128)(2,1)} async-done(((bf16[8,256,512]{2,1,0:T(8,128)(2,1)}), bf16[8,256,512]{2,1,0:T(8,128)(2,1)}, u32[]{:S(2)}, u32[]{:S(2)}) %all-to-all-start.6) | async-done | bytes 2097184 | tf_op jit(solution)/shard_map/all_to_all | solution.py:393
  712.7 17.7 %fusion.8 = (f32[3584]{0:T(1024)S(1)}, f32[512]{0:T(512)S(1)}, bf16[512,3584]{1,0:T(8,128)(2,1)}) fusion(bf16[512,3584]{1,0:T(8,128)(2,1)} %get-tuple-element.106, f32[512]{0:T(512)S(1)} %copy-done.32, f32[3584]{0:T(1024)S(1)} %copy-done.25, bf16[2048,512]{1,0:T(8,128)(2,1)} %bitcast.12, bf16[3584,2048]{1,0:T(8,128)(2,1)} %param.23, ...), kind=kOutput, calls=%fused_computation.19 | convolution fusion | flops 7536373760 | bytes 38830080 | tf_op jit(solution)/shard_map/dot_general | solution.py:499
  730.5 8.1 fusion.51
  738.5 5.9 copy.36
  744.5 3.2 all-to-all-start.7
  748.0 27.3 %fusion.2 = bf16[4096,1152]{1,0:T(8,128)(2,1)} fusion(bf16[2048,1152]{1,0:T(8,128)(2,1)} %all-gather.8.cloned.1.call-done, s32[4096]{0:T(1024)S(1)} %broadcast_add_fusion), kind=kOutput, calls=%fused_computation.3 | convolution fusion | flops 19340460032 | bytes 14172160 | tf_op jit(solution)/shard_map/dot_general | solution.py:38
  775.3 15.9 %all-to-all-done.7 = bf16[8,448,512]{2,1,0:T(8,128)(2,1)} async-done(((bf16[8,448,512]{2,1,0:T(8,128)(2,1)}), bf16[8,448,512]{2,1,0:T(8,128)(2,1)}, u32[]{:S(2)}, u32[]{:S(2)}) %all-to-all-start.7) | async-done | bytes 3670048 | tf_op jit(solution)/shard_map/all_to_all | solution.py:393
  793.5 2.7 convolution_add_fusion.6
  805.3 2.8 fusion.38
  808.6 3.9 copy.37
  812.5 2.9 copy.38
  815.5 13.6 %fusion.98 = f32[512,3584]{1,0:T(8,128)} fusion(bf16[2048,512]{1,0:T(8,128)(2,1)} %bitcast.115, bf16[2048,3584]{1,0:T(8,128)(2,1)} %all-gather.16.cloned.1.call-done), kind=kOutput, calls=%fused_computation.205 | convolution fusion | flops 7516192768 | bytes 24117248 | tf_op jit(solution)/shard_map/dot_general | solution.py:46
  829.1 15.9 %add_convert_fusion = bf16[512,3584]{1,0:T(8,128)(2,1)} fusion(f32[512,3584]{1,0:T(8,128)} %fusion.98, bf16[2048,512]{1,0:T(8,128)(2,1)S(1)} %bitcast.114, bf16[2048,3584]{1,0:T(8,128)(2,1)} %all-gather.18.cloned.1.call-done), kind=kOutput, calls=%fused_computation.28 | convolution fusion | flops 7519862784 | bytes 27787264 | tf_op jit(solution)/shard_map/dot_general | solution.py:46
  845.3 38.2 %convolution_convert_fusion.1 = bf16[3584,1024]{1,0:T(8,128)(2,1)} fusion(bf16[4096,3584]{1,0:T(8,128)(2,1)} %all-gather.10.cloned.1.call-done, bf16[4096,1024]{1,0:T(8,128)(2,1)} %get-tuple-element.73), kind=kOutput, calls=%fused_computation.16 | convolution fusion | flops 30068441088 | bytes 45088768 | tf_op jit(solution)/shard_map/dot_general | solution.py:46
  883.6 9.4 convolution_convert_fusion.8
  893.0 3.6 convolution_convert_fusion
  899.0 4.6 collective-permute-done
  903.6 2.6 bitcast_add_fusion
  911.2 19.2 %collective-permute-done.1 = bf16[2,256,512]{2,1,0:T(8,128)(2,1)} collective-permute-done((bf16[2,256,512]{2,1,0:T(8,128)(2,1)}, bf16[2,256,512]{2,1,0:T(8,128)(2,1)}, u32[]{:S(2)}, u32[]{:S(2)}) %collective-permute-start.1) | collective-permute-done | bytes 524320 | tf_op jit(solution)/shard_map/ppermute | solution.py:400
  932.4 9.7 collective-permute-done.3
  946.6 6.2 collective-permute-done.2
  952.9 7.5 collective-permute-done.4
  964.2 10.6 copy_out.4
  974.9 24.6 %all-reduce = (bf16[1152]{0:T(1024)(128)(2,1)}, bf16[3584]{0:T(1024)(128)(2,1)}, bf16[256]{0:T(256)(128)(2,1)}, bf16[256]{0:T(256)(128)(2,1)}, bf16[3584]{0:T(1024)(128)(2,1)}) all-reduce(f32[1152]{0:T(1024)S(1)} %get-tuple-element.85, f32[3584]{0:T(1024)S(1)} %get-tuple-element.79, ...), channel_id=1, replica_groups=mesh['dp'=1,'cp'=8] {'cp'}, use_global_device_ids=true, to_apply=%region_13.14 | all-reduce | flops 8832 | bytes 52992 | tf_op jit(solution)/shard_map/psum | solution.py:522
  999.4 10.1 copy_out.5
  1009.6 6.6 all-gather.20.cloned.1.call-done.x_ref
  1016.1 24.2 %copy_out.7 = bf16[4096,3584]{1,0:T(8,128)(2,1)} custom-call(bf16[4096,3584]{1,0:T(8,128)(2,1)} %all-gather.20.cloned.1.call-done.x_ref), custom_call_target="tpu_custom_call" | custom-call | flops 14680064 | bytes 58720256 | tf_op jit(solution)/shard_map/copy_out/pallas_call | solution.py:339
  1040.3 240.0 %all-gather.14.cloned.1.call-done.x_ref = bf16[3584,8192]{1,0:T(8,128)(2,1)} async-done(((bf16[3584,1024]{1,0:T(8,128)(2,1)}), bf16[3584,8192]{1,0:T(8,128)(2,1)}) %all-gather.14.cloned.1.call-update) | async-done | bytes 58720272 | tf_op jit(solution)/shard_map/all_gather | solution.py:388
  1280.3 39.8 %copy_out.6 = (bf16[3584,4096]{1,0:T(8,128)(2,1)}, bf16[3584,2048]{1,0:T(8,128)(2,1)}, bf16[3584,2048]{1,0:T(8,128)(2,1)}) custom-call(bf16[3584,8192]{1,0:T(8,128)(2,1)} %all-gather.14.cloned.1.call-done.x_ref), custom_call_target="tpu_custom_call" | custom-call | flops 29360128 | bytes 117440512 | tf_op jit(solution)/shard_map/copy_out/pallas_call | solution.py:339
  (175 shorter events, 55.3 us)
Async XLA Ops:
  7.2 45.9 %all-gather.8.cloned.1.call-start = ((), (), s32[]{:S(2)}) async-start(), calls=%async_computation.8 | async-start | bytes 5308416 | tf_op jit(solution)/shard_map/all_gather | solution.py:388
  7.9 7.4 copy-start.26
  7.9 9.5 copy-start.41
  7.9 9.8 copy-start.37
  16.9 195.1 %all-gather.10.cloned.1.call-start = ((), (), s32[]{:S(2)}) async-start(), calls=%async_computation.9 | async-start | bytes 33030144 | tf_op jit(solution)/shard_map/all_gather | solution.py:388
  17.6 51.1 %copy-start.35 = (pred[512]{0:T(512)(128)(4,1)}, pred[512]{0:T(512)(128)(4,1)S(1)}, u32[]{:S(2)}) copy-start(pred[512]{0:T(512)(128)(4,1)S(1)} %fusion.87) | copy-start | bytes 1540
  17.7 51.0 %copy-start.44 = (s32[512]{0:T(512)}, s32[512]{0:T(512)S(1)}, u32[]{:S(2)}) copy-start(s32[512]{0:T(512)S(1)} %broadcast_select_fusion.3) | copy-start | bytes 6148
  17.7 51.0 %copy-start.24 = (f32[3584]{0:T(1024)}, f32[3584]{0:T(1024)S(1)}, u32[]{:S(2)}) copy-start(f32[3584]{0:T(1024)S(1)} %convert_add_fusion.1) | copy-start | bytes 43012
  68.7 5.7 copy-start.39
  74.4 1.2 copy-start.49
  77.3 270.4 %copy-start = (s32[16,1,256]{2,1,0:T(1,128)}, s32[16,1,256]{2,1,0:T(1,128)S(1)}, u32[]{:S(2)}) copy-start(s32[16,1,256]{2,1,0:T(1,128)S(1)} %get-tuple-element.97.lim_ref) | copy-start | bytes 49156
  77.3 270.4 %copy-start.5 = (s32[16]{0:T(128)}, s32[16]{0:T(128)S(1)}, u32[]{:S(2)}) copy-start(s32[16]{0:T(128)S(1)} %fusion.92.nkb_ref) | copy-start | bytes 196
  261.1 1.6 copy-start.1
  262.7 1.6 copy-start.3
  297.7 2.0 copy-start.6
  299.7 42.9 %copy-start.8 = (f32[8,8,512]{2,1,0:T(8,128)}, f32[8,8,512]{2,1,0:T(8,128)S(1)}, u32[]{:S(2)}) copy-start(f32[8,8,512]{2,1,0:T(8,128)S(1)} %get-tuple-element.56.lse_ref) | copy-start | bytes 393220
  299.7 2.5 copy-start.38
  299.7 29.0 %all-to-all-start = ((bf16[8,512,256]{2,1,0:T(8,128)(2,1)}), bf16[8,512,256]{2,1,0:T(8,128)(2,1)S(1)}, u32[]{:S(2)}, u32[]{:S(2)}) async-start(bf16[8,512,256]{2,1,0:T(8,128)(2,1)} %get-tuple-element.49), calls=%async_computation | async-start | bytes 4194304 | tf_op jit(solution)/shard_map/all_to_all | solution.py:393
  302.2 513.3 %all-gather.16.cloned.1.call-start = ((), (), s32[]{:S(2)}) async-start(), calls=%async_computation.12 | async-start | bytes 16515072 | tf_op jit(solution)/shard_map/all_gather | solution.py:388
  328.7 13.9 %copy-start.10 = (bf16[512,3584]{1,0:T(8,128)(2,1)S(1)}, bf16[512,3584]{1,0:T(8,128)(2,1)}, u32[]{:S(2)}) copy-start(bf16[512,3584]{1,0:T(8,128)(2,1)} %param.17) | copy-start | bytes 11010052
  342.6 2.7 copy-start.13
  345.3 2.4 copy-start.2
  347.7 1.6 copy-start.4
  386.1 2.0 copy-start.7
  388.8 51.9 %all-to-all-start.1 = ((bf16[8,512,256]{2,1,0:T(8,128)(2,1)}), bf16[8,512,256]{2,1,0:T(8,128)(2,1)S(1)}, u32[]{:S(2)}, u32[]{:S(2)}) async-start(bf16[8,512,256]{2,1,0:T(8,128)(2,1)} %get-tuple-element.51), calls=%async_computation.1 | async-start | bytes 4194304 | tf_op jit(solution)/shard_map/all_to_all | solution.py:393
  440.7 41.6 %all-to-all-start.2 = ((bf16[8,512,256]{2,1,0:T(8,128)(2,1)}), bf16[8,512,256]{2,1,0:T(8,128)(2,1)}, u32[]{:S(2)}, u32[]{:S(2)}) async-start(bf16[8,512,256]{2,1,0:T(8,128)(2,1)} %bitcast.110), calls=%async_computation.2 | async-start | bytes 4194304 | tf_op jit(solution)/shard_map/all_to_all | solution.py:393
  443.8 385.3 %all-gather.18.cloned.1.call-start = ((), (), s32[]{:S(2)}) async-start(), calls=%async_computation.13 | async-start | bytes 16515072 | tf_op jit(solution)/shard_map/all_gather | solution.py:388
  443.8 13.9 %copy-start.11 = (bf16[512,3584]{1,0:T(8,128)(2,1)S(1)}, bf16[512,3584]{1,0:T(8,128)(2,1)}, u32[]{:S(2)}) copy-start(bf16[512,3584]{1,0:T(8,128)(2,1)} %param.17) | copy-start | bytes 11010052
  443.9 16.6 %copy-start.14 = (bf16[256,3584]{1,0:T(8,128)(2,1)S(1)}, bf16[256,3584]{1,0:T(8,128)(2,1)}, u32[]{:S(2)}) copy-start(bf16[256,3584]{1,0:T(8,128)(2,1)} %copy-done.13) | copy-start | bytes 5505028
  457.8 2.7 copy-start.12
  482.3 48.4 %all-to-all-start.3 = ((bf16[8,512,256]{2,1,0:T(8,128)(2,1)}), bf16[8,512,256]{2,1,0:T(8,128)(2,1)S(1)}, u32[]{:S(2)}, u32[]{:S(2)}) async-start(bf16[8,512,256]{2,1,0:T(8,128)(2,1)} %bitcast.9), calls=%async_computation.3 | async-start | bytes 4194304 | tf_op jit(solution)/shard_map/all_to_all | solution.py:393
  530.7 1.3 copy-start.23
  601.4 3.3 copy-start.30
  601.5 52.5 %all-to-all-start.4 = ((bf16[8,512,512]{2,1,0:T(8,128)(2,1)}), bf16[8,512,512]{2,1,0:T(8,128)(2,1)}, u32[]{:S(2)}, u32[]{:S(2)}) async-start(bf16[8,512,512]{2,1,0:T(8,128)(2,1)} %get-tuple-element.67), calls=%async_computation.4 | async-start | bytes 8388608 | tf_op jit(solution)/shard_map/all_to_all | solution.py:393
  653.9 28.9 %all-to-all-start.5 = ((bf16[8,256,512]{2,1,0:T(8,128)(2,1)}), bf16[8,256,512]{2,1,0:T(8,128)(2,1)S(1)}, u32[]{:S(2)}, u32[]{:S(2)}) async-start(bf16[8,256,512]{2,1,0:T(8,128)(2,1)} %get-tuple-element.69), calls=%async_computation.5 | async-start | bytes 4194304 | tf_op jit(solution)/shard_map/all_to_all | solution.py:393
  682.8 29.9 %all-to-all-start.6 = ((bf16[8,256,512]{2,1,0:T(8,128)(2,1)}), bf16[8,256,512]{2,1,0:T(8,128)(2,1)}, u32[]{:S(2)}, u32[]{:S(2)}) async-start(bf16[8,256,512]{2,1,0:T(8,128)(2,1)} %get-tuple-element.71), calls=%async_computation.6 | async-start | bytes 4194304 | tf_op jit(solution)/shard_map/all_to_all | solution.py:393
  686.1 26.6 %copy-start.25 = (f32[3584]{0:T(1024)S(1)}, f32[3584]{0:T(1024)}, u32[]{:S(2)}) copy-start(f32[3584]{0:T(1024)} %copy-done.24) | copy-start | bytes 43012
  686.1 26.6 %copy-start.32 = (f32[512]{0:T(512)S(1)}, f32[512]{0:T(512)}, u32[]{:S(2)}) copy-start(f32[512]{0:T(512)} %copy-done.31) | copy-start | bytes 6148
  712.7 17.7 %copy-start.40 = (f32[512]{0:T(512)S(1)}, f32[512]{0:T(512)}, u32[]{:S(2)}) copy-start(f32[512]{0:T(512)} %copy-done.39) | copy-start | bytes 6148
  712.7 17.8 %copy-start.36 = (pred[512]{0:T(512)(128)(4,1)S(1)}, pred[512]{0:T(512)(128)(4,1)}, u32[]{:S(2)}) copy-start(pred[512]{0:T(512)(128)(4,1)} %copy-done.35) | copy-start | bytes 1540
  744.5 46.7 %all-to-all-start.7 = ((bf16[8,448,512]{2,1,0:T(8,128)(2,1)}), bf16[8,448,512]{2,1,0:T(8,128)(2,1)}, u32[]{:S(2)}, u32[]{:S(2)}) async-start(bf16[8,448,512]{2,1,0:T(8,128)(2,1)} %bitcast.106), calls=%async_computation.7 | async-start | bytes 7340032 | tf_op jit(solution)/shard_map/all_to_all | solution.py:393
  747.7 251.7 %all-gather.12.cloned.1.call-start = ((), (), s32[]{:S(2)}) async-start(), calls=%async_computation.10 | async-start | bytes 9289728 | tf_op jit(solution)/shard_map/all_gather | solution.py:388
  791.2 5.1 copy-start.18
  808.1 208.0 %all-gather.20.cloned.1.call-start = ((), (), s32[]{:S(2)}) async-start(), calls=%async_computation.14 | async-start | bytes 33030144 | tf_op jit(solution)/shard_map/all_gather | solution.py:388
  845.1 435.2 %all-gather.14.cloned.1.call-start = ((), (), s32[]{:S(2)}) async-start(), calls=%async_computation.11 | async-start | bytes 66060288 | tf_op jit(solution)/shard_map/all_gather | solution.py:388
  883.6 9.4 copy-start.45
  896.6 2.2 copy-start.22
  898.9 4.7 collective-permute-start
  907.2 23.3 %collective-permute-start.1 = (bf16[2,256,512]{2,1,0:T(8,128)(2,1)}, bf16[2,256,512]{2,1,0:T(8,128)(2,1)}, u32[]{:S(2)}, u32[]{:S(2)}) collective-permute-start(bf16[2,256,512]{2,1,0:T(8,128)(2,1)} %dynamic-slice_bitcast_fusion.2), channel_id=1, source_target_pairs={{0,2},{1,3},{2,0},{3,1},{4,6},{5,7},{6,4},{7,5}} | collective-permute-start | bytes 1572872 | tf_op jit(solution)/shard_map/ppermute | solution.py:400
  908.4 1.1 copy-start.21
  909.5 35.0 %copy-start.19 = (bf16[256,3584]{1,0:T(8,128)(2,1)S(1)}, bf16[256,3584]{1,0:T(8,128)(2,1)}, u32[]{:S(2)}) copy-start(bf16[256,3584]{1,0:T(8,128)(2,1)} %get-tuple-element.98) | copy-start | bytes 5505028
  910.4 31.8 %collective-permute-start.3 = (bf16[2,256,640]{2,1,0:T(8,128)(2,1)}, bf16[2,256,640]{2,1,0:T(8,128)(2,1)}, u32[]{:S(2)}, u32[]{:S(2)}) collective-permute-start(bf16[2,256,640]{2,1,0:T(8,128)(2,1)} %dynamic-slice_bitcast_fusion.1), channel_id=1, source_target_pairs={{0,4},{1,5},{2,6},{3,7},{4,0},{5,1},{6,2},{7,3}} | collective-permute-start | bytes 1966088 | tf_op jit(solution)/shard_map/ppermute | solution.py:400
  911.2 33.3 %copy-start.20 = (bf16[256,3584]{1,0:T(8,128)(2,1)S(1)}, bf16[256,3584]{1,0:T(8,128)(2,1)}, u32[]{:S(2)}) copy-start(bf16[256,3584]{1,0:T(8,128)(2,1)} %get-tuple-element.99) | copy-start | bytes 5505028
  931.6 21.3 %collective-permute-start.2 = (bf16[256,512]{1,0:T(8,128)(2,1)S(1)}, bf16[256,512]{1,0:T(8,128)(2,1)S(1)}, u32[]{:S(2)}, u32[]{:S(2)}) collective-permute-start(bf16[256,512]{1,0:T(8,128)(2,1)S(1)} %dynamic-slice_bitcast_fusion.4), channel_id=1, source_target_pairs={{0,4},{1,5},{2,6},{3,7},{4,0},{5,1},{6,2},{7,3}} | collective-permute-start | bytes 786440 | tf_op jit(solution)/shard_map/ppermute | solution.py:400
  943.5 16.8 %collective-permute-start.4 = (bf16[256,640]{1,0:T(8,128)(2,1)S(1)}, bf16[256,640]{1,0:T(8,128)(2,1)S(1)}, u32[]{:S(2)}, u32[]{:S(2)}) collective-permute-start(bf16[256,640]{1,0:T(8,128)(2,1)S(1)} %dynamic-slice_bitcast_fusion.3), channel_id=1, source_target_pairs={{0,2},{1,3},{2,0},{3,1},{4,6},{5,7},{6,4},{7,5}} | collective-permute-start | bytes 983048 | tf_op jit(solution)/shard_map/ppermute | solution.py:400
  944.5 2.1 copy-start.28
  944.5 2.1 copy-start.29
  944.5 15.9 %copy-start.17 = (f32[256,1152]{1,0:T(8,128)S(1)}, f32[256,1152]{1,0:T(8,128)}, u32[]{:S(2)}) copy-start(f32[256,1152]{1,0:T(8,128)} %copy-done.16) | copy-start | bytes 3538948
  944.5 15.9 %copy-start.27 = (f32[1152]{0:T(1024)S(1)}, f32[1152]{0:T(1024)}, u32[]{:S(2)}) copy-start(f32[1152]{0:T(1024)} %copy-done.26) | copy-start | bytes 13828
  944.5 15.9 %copy-start.34 = (f32[256]{0:T(256)S(1)}, f32[256]{0:T(256)}, u32[]{:S(2)}) copy-start(f32[256]{0:T(256)} %copy-done.33) | copy-start | bytes 3076
  944.5 16.4 %copy-start.43 = (f32[256]{0:T(256)S(1)}, f32[256]{0:T(256)}, u32[]{:S(2)}) copy-start(f32[256]{0:T(256)} %copy-done.42) | copy-start | bytes 3076
  946.6 15.5 %copy-start.15 = (bf16[512,3584]{1,0:T(8,128)(2,1)S(1)}, bf16[512,3584]{1,0:T(8,128)(2,1)}, u32[]{:S(2)}) copy-start(bf16[512,3584]{1,0:T(8,128)(2,1)} %get-tuple-element.95) | copy-start | bytes 11010052
  964.2 10.6 copy-start.46
  964.2 10.6 copy-start.47
  (6 other events, 4.0 us)
Sparse Core Ops, SparseCore 0:
  17.0 36.0 all-gather.7
  74.5 137.3 all-gather.9
  347.8 96.8 all-gather.15
  464.8 94.6 all-gather.17
  808.3 47.2 all-gather.11
  857.8 158.2 all-gather.19
  1018.6 261.6 all-gather.13
